TPU v7x, 32 devices: a whole 2x2x4 slice. The times are simulated.
32 devices in a mesh: samp: 8 (over y, x, core), snp: 4 (over z).
Axes of the slice: x: 2, y: 2, z: 4, core: 2. Of those that a mesh axis runs over, the one named last changes fastest.
Arguments:
- genotypes: bfloat16 [8192, 16384], P('samp', 'snp'), may hold values from -6 to 6
- probes: bfloat16 [8, 8192], P(None, 'samp'), may hold values from -6 to 6
- env_label: int32 [8192], P('samp'), may hold values from 0 to 7
- variances: float32 [3], replicated, may hold values from 0.25 to 1
Outputs:
- first: float32 [8, 8192], P(None, 'samp')
- second: float32 [8, 8192], P(None, 'samp')
All inputs are finite; a program needn't handle non-finite values.
Results may differ from a plain program's by a relative error of at most 0.0018.
Values may be sent and summed in bfloat16 or wider, within the bound.
No kernel may reach another device: no remote copies, remote signals or barrier semaphores. Data moves between devices by JAX's collectives and lax.ppermute only.
A program may use at most 64 MiB of HBM per device.

v0:
```python
import jax
import jax.numpy as jnp
from jax import lax
from jax.sharding import PartitionSpec as P

SNPS = 16384
PROBES = 8
ENVS = 8


def local_image(snp_panel, genotypes):
    return lax.dot_general(
        snp_panel, genotypes, (((1,), (1,)), ((), ())), preferred_element_type=jnp.float32
    )


def apply_operator(current, genotypes, onehot, variances):
    rounded = current.astype(jnp.bfloat16)
    scaled = (onehot[:, None, :] * rounded[None, :, :]).reshape(ENVS * PROBES, -1)
    panel = jnp.concatenate([rounded, scaled], axis=0)
    partial_panel = jnp.dot(panel, genotypes, preferred_element_type=jnp.float32)
    snp_panel = lax.psum(partial_panel, "samp").astype(jnp.bfloat16)
    image = local_image(snp_panel, genotypes)
    additive = image[:PROBES]
    blocks = image[PROBES:].reshape(ENVS, PROBES, -1)
    interaction = jnp.sum(onehot.astype(jnp.float32)[:, None, :] * blocks, axis=0)
    weighted = variances[0] * additive / SNPS + variances[1] * interaction / SNPS
    totals = lax.psum(weighted, "snp")
    return totals + variances[2] * current


def per_device(genotypes, probes, env_label, variances):
    labels = jnp.arange(ENVS, dtype=jnp.int32)
    onehot = (env_label[None, :] == labels[:, None]).astype(jnp.bfloat16)
    first = apply_operator(probes.astype(jnp.float32), genotypes, onehot, variances)
    second = apply_operator(first, genotypes, onehot, variances)
    return (first, second)


def solution(mesh):
    return jax.shard_map(
        per_device,
        mesh=mesh,
        in_specs=(P("samp", "snp"), P(None, "samp"), P("samp"), P()),
        out_specs=(P(None, "samp"), P(None, "samp")),
        check_vma=False,
    )
```

profile of v0, /device:TPU:0, one launch (start us, length us, event | category | flops | bytes accessed | tf_op | source)
XLA Modules:
  0.0 167.7 jit_solution(6879203342592267592)
XLA Ops:
  0.6 1.4 fusion.25
  2.1 0.7 fusion.21
  2.8 0.7 multiply_bitcast_fusion.1
  3.5 5.0 %fusion.8 = f32[72,4096]{1,0:T(8,128)S(1)} fusion(bf16[1024,4096]{1,0:T(8,128)(2,1)} %param.4, bf16[64,1024]{1,0:T(8,128)(2,1)S(1)} %multiply_bitcast_fusion.1, bf16[8,1024]{1,0:T(8,128)(2,1)} %param.5), kind=kOutput, calls=%fused_computation.10 | convolution fusion | flops 604274688 | bytes 9715712 | tf_op jit(solution)/shard_map/dot_general | solution.py:21
  8.5 0.0 copy-start
  8.5 53.0 %all-reduce.2 = bf16[72,4096]{1,0:T(8,128)(2,1)S(1)} all-reduce(f32[72,4096]{1,0:T(8,128)S(1)} %fusion.8), channel_id=1, replica_groups=mesh['samp'=8,'snp'=4] {'samp'}, use_global_device_ids=true, to_apply=%region_0.0 | all-reduce | flops 294912 | bytes 1769472 | tf_op jit(solution)/shard_map/psum | solution.py:22
  61.5 6.0 %fusion.27 = f32[72,1024]{1,0:T(8,128)S(1)} fusion(bf16[72,4096]{1,0:T(8,128)(2,1)S(1)} %all-reduce.2, bf16[1024,4096]{1,0:T(8,128)(2,1)} %param.4), kind=kOutput, calls=%fused_computation.36 | convolution fusion | flops 603979776 | bytes 9273344 | tf_op jit(solution)/shard_map/dot_general | solution.py:12
  67.6 1.2 fusion.19
  68.8 19.5 %psum.29 = f32[8,1024]{1,0:T(8,128)S(1)} all-reduce(f32[8,1024]{1,0:T(8,128)S(1)} %fusion.19), channel_id=1, replica_groups=mesh['samp'=8,'snp'=4] {'snp'}, use_global_device_ids=true, to_apply=%region_2.0 | all-reduce | flops 8192 | bytes 65536 | tf_op jit(solution)/shard_map/psum | solution.py:28
  88.3 0.0 copy-done
  88.3 0.7 fusion.24
  89.0 0.0 copy-start.1
  89.1 5.0 %fusion.12 = f32[72,4096]{1,0:T(8,128)S(1)} fusion(bf16[1024,4096]{1,0:T(8,128)(2,1)} %param.4, bf16[64,1024]{1,0:T(8,128)(2,1)S(1)} %multiply_bitcast_fusion, bf16[8,1024]{1,0:T(8,128)(2,1)S(1)} %get-tuple-element.2), kind=kOutput, calls=%fused_computation.14 | convolution fusion | flops 604274688 | bytes 9715712 | tf_op jit(solution)/shard_map/dot_general | solution.py:21
  94.1 49.2 %all-reduce.3 = bf16[72,4096]{1,0:T(8,128)(2,1)S(1)} all-reduce(f32[72,4096]{1,0:T(8,128)S(1)} %fusion.12), channel_id=1, replica_groups=mesh['samp'=8,'snp'=4] {'samp'}, use_global_device_ids=true, to_apply=%region_3.0 | all-reduce | flops 294912 | bytes 1769472 | tf_op jit(solution)/shard_map/psum | solution.py:22
  143.3 6.0 %fusion.26 = f32[72,1024]{1,0:T(8,128)S(1)} fusion(bf16[72,4096]{1,0:T(8,128)(2,1)S(1)} %all-reduce.3, bf16[1024,4096]{1,0:T(8,128)(2,1)} %param.4), kind=kOutput, calls=%fused_computation.35 | convolution fusion | flops 603979776 | bytes 9273344 | tf_op jit(solution)/shard_map/dot_general | solution.py:12
  149.4 1.2 fusion.17
  150.6 15.8 %psum.31 = f32[8,1024]{1,0:T(8,128)S(1)} all-reduce(f32[8,1024]{1,0:T(8,128)S(1)} %fusion.17), channel_id=1, replica_groups=mesh['samp'=8,'snp'=4] {'snp'}, use_global_device_ids=true, to_apply=%region_5.0 | all-reduce | flops 8192 | bytes 65536 | tf_op jit(solution)/shard_map/psum | solution.py:28
  166.4 0.0 copy-done.1
  166.4 1.3 multiply_add_fusion
  (3 shorter events, 0.1 us)
Async XLA Ops:
  8.5 79.8 %copy-start = (bf16[8,1024]{1,0:T(8,128)(2,1)S(1)}, bf16[8,1024]{1,0:T(8,128)(2,1)}, u32[]{:S(2)}) copy-start(bf16[8,1024]{1,0:T(8,128)(2,1)} %param.5) | copy-start | bytes 49156
  89.0 77.4 %copy-start.1 = (f32[8,1024]{1,0:T(8,128)}, f32[8,1024]{1,0:T(8,128)S(1)}, u32[]{:S(2)}) copy-start(f32[8,1024]{1,0:T(8,128)S(1)} %get-tuple-element.3) | copy-start | bytes 98308
where the time goes:
time: 168 us
  blocking collectives  138 us (82%)
  matrix products  22.1 us (13%)
  other arithmetic  5.97 us (4%)
    psum x2, blocking collectives, apply_operator(): snp_panel = lax.psum(partial_panel, 'samp').astype(jnp.bfloat16)  102 us
    psum x2, blocking collectives, apply_operator(): totals = lax.psum(weighted, 'snp')  35.2 us
    dot_general x2, matrix products, local_image(): lax.dot_general(snp_panel, genotypes, (((1,), (1,)), ((), ())), preferred...  12.1 us
    dot_general x2, matrix products, apply_operator(): jnp.dot(panel, genotypes, preferred_element_type=jnp.float32)  9.96 us

commit v1 on v0

v1 whole, which is shorter than its diff:
```python
import jax
import jax.numpy as jnp
from jax import lax
from jax.sharding import PartitionSpec as P

ENVS = 8


def exchange(block, offset, devices):
    return lax.ppermute(block, "samp", [(k, k ^ offset) for k in range(devices)])


def make(mesh):
    samp = mesh.shape["samp"]
    snp = mesh.shape["snp"]
    chips = samp // 2

    def block_of(array, index, width):
        return lax.dynamic_slice_in_dim(array, index * width, width, axis=1)

    def apply_operator(current, genotypes, onehot, scale, noise, exact):
        probes = current.shape[0]
        wire = jnp.float32 if exact else jnp.bfloat16
        snps = genotypes.shape[1]
        half, width = snps // 2, snps // samp
        index = lax.axis_index("samp")
        core, chip = index % 2, index // 2
        rounded = current.astype(jnp.bfloat16)
        panel = (onehot[:, None, :] * rounded[None, :, :]).reshape(ENVS * probes, -1)
        partial = jnp.dot(panel, genotypes, preferred_element_type=jnp.float32)
        given = exchange(block_of(partial, 1 - core, half).astype(wire), 1, samp)
        pair = block_of(partial, core, half) + given.astype(jnp.float32)
        total = block_of(pair, chip, width)
        for step in range(1, chips):
            total = total + exchange(block_of(pair, chip ^ step, width).astype(wire), 2 * step, samp).astype(jnp.float32)
        if exact:
            total = jnp.concatenate([total.reshape(ENVS, probes, width).sum(0), total], axis=0)
        mine = total.astype(jnp.bfloat16)
        rows = mine.shape[0]
        gathered = jnp.zeros((rows, half), jnp.bfloat16)
        for step in range(chips):
            piece = exchange(mine, 2 * step, samp) if step else mine
            gathered = lax.dynamic_update_slice(gathered, piece, (0, (chip ^ step) * width))
        other = exchange(gathered, 1, samp)
        dims = (((1,), (1,)), ((), ()))
        image = lax.dot_general(gathered, block_of(genotypes, core, half), dims, preferred_element_type=jnp.float32)
        image = image + lax.dot_general(other, block_of(genotypes, 1 - core, half), dims, preferred_element_type=jnp.float32)
        blocks = image[rows - ENVS * probes:].reshape(ENVS, probes, -1)
        if exact:
            weight = scale[1] * onehot.astype(jnp.float32)
            weighted = scale[0] * image[:probes] + jnp.sum(weight[:, None, :] * blocks, axis=0)
        else:
            weight = scale[0] + scale[1] * onehot.astype(jnp.float32)
            weighted = jnp.sum(weight[:, None, :] * blocks, axis=0)
        parts = [weighted] + [
            lax.ppermute(weighted, "snp", [(k, k ^ step) for k in range(snp)]) for step in range(1, snp)
        ]
        while len(parts) > 1:
            parts = [parts[k] + parts[k + 1] for k in range(0, len(parts), 2)]
        return parts[0] + noise * current

    def per_device(genotypes, probes, env_label, variances):
        total_snps = genotypes.shape[1] * snp
        labels = jnp.arange(ENVS, dtype=jnp.int32)
        onehot = (env_label[None, :] == labels[:, None]).astype(jnp.bfloat16)
        scale = variances[:2] / total_snps
        first = apply_operator(probes.astype(jnp.float32), genotypes, onehot, scale, variances[2], True)
        second = apply_operator(first, genotypes, onehot, scale, variances[2], False)
        return (first, second)

    return per_device


def solution(mesh):
    return jax.shard_map(
        make(mesh),
        mesh=mesh,
        in_specs=(P("samp", "snp"), P(None, "samp"), P("samp"), P()),
        out_specs=(P(None, "samp"), P(None, "samp")),
        check_vma=False,
    )
```

time: 168 us -> 81.9 us (0.49)
  blocking collectives: 138 us -> 0 us
  waiting for transfers between devices: 0 us -> 29.4 us
  starting transfers between devices: 0 us -> 24.9 us
  matrix products: 22.1 us -> 20.1 us
    psum x4 -> x0, blocking collectives: 138 us -> none  [the longest x2 102 us: apply_operator(): snp_panel = lax.psum(partial_panel, 'samp').astype(jnp.bfloat16)]
    ppermute x0 -> x22, waiting for transfers between devices: none -> 29.4 us  [the longest x16 22.3 us: exchange(): lax.ppermute(block, 'samp', [(k, k ^ offset) for k in range(devices)])]
    ppermute x0 -> x22, starting transfers between devices: none -> 24.9 us  [the longest x16 15.9 us: exchange(): lax.ppermute(block, 'samp', [(k, k ^ offset) for k in range(devices)])]
    dot_general x4 -> x6, matrix products: 22.1 us -> 20.1 us  [the longest x2 10.1 us: apply_operator(): partial = jnp.dot(panel, genotypes, preferred_element_type=jnp.float32)]
    add x3 -> x5, other arithmetic: 3.74 us -> 3.47 us  [the longest x1 1.3 us: apply_operator(): weight = scale[0] + scale[1] * onehot.astype(jnp.float32)]
  transfers between devices with their start and end apart: 0 -> 22, of which waited for: 0 -> 19; matrix products, arithmetic and copies ran while one was open for 0% -> 3% of each run, Pallas kernels for 0% -> 0%
where the time goes in v1:
time: 81.9 us; the launch traced here: 81.6 us
  waiting for transfers between devices  29.4 us (36%)
  starting transfers between devices  24.9 us (30%)
  matrix products  20.1 us (25%)
  other arithmetic  4.94 us (6%)
  local copies, waits for them, and re-layouts  1.47 us (2%)
  between operations  0.87 us (1%)
    ppermute x16, waiting for transfers between devices, exchange(): lax.ppermute(block, 'samp', [(k, k ^ offset) for k in range(devices)])  22.3 us
    ppermute x16, starting transfers between devices, exchange(): lax.ppermute(block, 'samp', [(k, k ^ offset) for k in range(devices)])  15.9 us
    dot_general x2, matrix products, apply_operator(): partial = jnp.dot(panel, genotypes, preferred_element_type=jnp.float32)  10.1 us
    ppermute x6, starting transfers between devices, apply_operator(): lax.ppermute(weighted, 'snp', [(k, k ^ step) for k in range(snp)])  8.98 us
    ppermute x6, waiting for transfers between devices, apply_operator(): lax.ppermute(weighted, 'snp', [(k, k ^ step) for k in range(snp)])  7.07 us
    dot_general x2, matrix products, apply_operator(): lax.dot_general(gathered, block_of(genotypes, core, half), dims, preferre...  5.01 us
    dot_general x2, matrix products, apply_operator(): lax.dot_general(other, block_of(genotypes, 1 - core, half), dims, preferr...  4.99 us
  transfers between devices with their start and end apart: 22, of which 19 were waited for; matrix products, arithmetic and copies ran while one was open for 3% of the time, Pallas kernels for 0%

profile of v1, /device:TPU:0, one launch (start us, length us, event | category | flops | bytes accessed | tf_op | source)
XLA Modules:
  0.0 81.6 jit_solution(10709962142159537607)
XLA Ops:
  0.6 0.7 fusion.36
  1.4 5.0 %fusion.27 = f32[64,4096]{1,0:T(8,128)S(1)} fusion(bf16[1024,4096]{1,0:T(8,128)(2,1)} %param.4, bf16[8,1024]{1,0:T(8,128)(2,1)} %param.5, bf16[8,1024]{1,0:T(8,128)(2,1)S(1)} %fusion.36), kind=kOutput, calls=%fused_computation.22 | convolution fusion | flops 536936448 | bytes 9469952 | tf_op jit(solution)/shard_map/dot_general | solution.py:30
  6.3 0.0 copy-start.1
  6.4 0.6 collective-permute-start
  7.0 1.5 %collective-permute-done = f32[64,2048]{1,0:T(8,128)S(1)} collective-permute-done((f32[64,2048]{1,0:T(8,128)S(1)}, f32[64,2048]{1,0:T(8,128)S(1)}, u32[]{:S(2)}, u32[]{:S(2)}) %collective-permute-start) | collective-permute-done | bytes 524320 | tf_op jit(solution)/shard_map/ppermute | solution.py:10
  8.5 0.1 dynamic-slice_add_fusion
  8.6 2.9 %collective-permute-start.1 = (f32[64,512]{1,0:T(8,128)S(1)}, f32[64,512]{1,0:T(8,128)S(1)}, u32[]{:S(2)}, u32[]{:S(2)}) collective-permute-start(f32[64,512]{1,0:T(8,128)S(1)} %get-tuple-element.11), channel_id=1, source_target_pairs={{0,8},{4,12},{8,0},{12,4},{16,24},{20,28},{24,16},{28,20},{1,9},{5... | collective-permute-start | bytes 393224 | tf_op jit(solution)/shard_map/ppermute | solution.py:10
  11.5 1.5 %collective-permute-start.2 = (f32[64,512]{1,0:T(8,128)S(1)}, f32[64,512]{1,0:T(8,128)S(1)}, u32[]{:S(2)}, u32[]{:S(2)}) collective-permute-start(f32[64,512]{1,0:T(8,128)S(1)} %get-tuple-element.13), channel_id=1, source_target_pairs={{0,16},{4,20},{8,24},{12,28},{16,0},{20,4},{24,8},{28,12},{1,17},{... | collective-permute-start | bytes 393224 | tf_op jit(solution)/shard_map/ppermute | solution.py:10
  13.0 0.0 collective-permute-start.3
  13.1 2.4 %collective-permute-done.1 = f32[64,512]{1,0:T(8,128)S(1)} collective-permute-done((f32[64,512]{1,0:T(8,128)S(1)}, f32[64,512]{1,0:T(8,128)S(1)}, u32[]{:S(2)}, u32[]{:S(2)}) %collective-permute-start.1) | collective-permute-done | bytes 131104 | tf_op jit(solution)/shard_map/ppermute | solution.py:10
  15.5 4.1 %collective-permute-done.2 = f32[64,512]{1,0:T(8,128)S(1)} collective-permute-done((f32[64,512]{1,0:T(8,128)S(1)}, f32[64,512]{1,0:T(8,128)S(1)}, u32[]{:S(2)}, u32[]{:S(2)}) %collective-permute-start.2) | collective-permute-done | bytes 131104 | tf_op jit(solution)/shard_map/ppermute | solution.py:10
  19.6 0.0 collective-permute-done.3
  19.7 1.3 %collective-permute-start.4 = (bf16[72,512]{1,0:T(8,128)(2,1)S(1)}, bf16[72,512]{1,0:T(8,128)(2,1)S(1)}, u32[]{:S(2)}, u32[]{:S(2)}) collective-permute-start(bf16[72,512]{1,0:T(8,128)(2,1)S(1)} %get-tuple-element.14), channel_id=1, source_target_pairs={{0,8},{4,12},{8,0},{12,4},{16,24},{20,28},{24,16},{28,20},{1,9},{5... | collective-permute-start | bytes 221192 | tf_op jit(solution)/shard_map/ppermute | solution.py:10
  21.0 0.0 copy-done.3
  21.0 0.8 %collective-permute-start.5 = (bf16[72,512]{1,0:T(8,128)(2,1)S(1)}, bf16[72,512]{1,0:T(8,128)(2,1)S(1)}, u32[]{:S(2)}, u32[]{:S(2)}) collective-permute-start(bf16[72,512]{1,0:T(8,128)(2,1)S(1)} %get-tuple-element.14), channel_id=1, source_target_pairs={{0,16},{4,20},{8,24},{12,28},{16,0},{20,4},{24,8},{28,12},{1,17},{... | collective-permute-start | bytes 221192 | tf_op jit(solution)/shard_map/ppermute | solution.py:10
  21.8 1.4 %collective-permute-start.6 = (bf16[72,512]{1,0:T(8,128)(2,1)S(1)}, bf16[72,512]{1,0:T(8,128)(2,1)S(1)}, u32[]{:S(2)}, u32[]{:S(2)}) collective-permute-start(bf16[72,512]{1,0:T(8,128)(2,1)S(1)} %get-tuple-element.14), channel_id=1, source_target_pairs={{0,24},{4,28},{8,16},{12,20},{16,8},{20,12},{24,0},{28,4},{1,25},{... | collective-permute-start | bytes 221192 | tf_op jit(solution)/shard_map/ppermute | solution.py:10
  23.2 1.2 %collective-permute-done.4 = bf16[72,512]{1,0:T(8,128)(2,1)S(1)} collective-permute-done((bf16[72,512]{1,0:T(8,128)(2,1)S(1)}, bf16[72,512]{1,0:T(8,128)(2,1)S(1)}, u32[]{:S(2)}, u32[]{:S(2)}) %collective-permute-start.4) | collective-permute-done | bytes 73760 | tf_op jit(solution)/shard_map/ppermute | solution.py:10
  24.5 1.0 %collective-permute-done.5 = bf16[72,512]{1,0:T(8,128)(2,1)S(1)} collective-permute-done((bf16[72,512]{1,0:T(8,128)(2,1)S(1)}, bf16[72,512]{1,0:T(8,128)(2,1)S(1)}, u32[]{:S(2)}, u32[]{:S(2)}) %collective-permute-start.5) | collective-permute-done | bytes 73760 | tf_op jit(solution)/shard_map/ppermute | solution.py:10
  25.5 1.6 %collective-permute-done.6 = bf16[72,512]{1,0:T(8,128)(2,1)S(1)} collective-permute-done((bf16[72,512]{1,0:T(8,128)(2,1)S(1)}, bf16[72,512]{1,0:T(8,128)(2,1)S(1)}, u32[]{:S(2)}, u32[]{:S(2)}) %collective-permute-start.6) | collective-permute-done | bytes 73760 | tf_op jit(solution)/shard_map/ppermute | solution.py:10
  27.1 0.1 collective-permute-start.7
  27.2 0.6 fusion.42
  27.7 1.3 %broadcast_add_fusion = (f32[8,1024]{1,0:T(8,128)S(1)}, f32[8,1024]{1,0:T(8,128)S(1)}) fusion(f32[]{:T(128)} %bitcast, f32[]{:T(128)} %bitcast.3, s32[1024]{0:T(1024)S(1)} %copy-done.2), kind=kLoop, calls=%fused_computation.43 | loop fusion | flops 40960 | bytes 69640 | tf_op jit(solution)/shard_map/add | solution.py:53
  29.1 0.0 collective-permute-done.7
  29.1 3.6 %fusion.2 = f32[72,1024]{1,0:T(8,128)S(1)} fusion(bf16[72,2048]{1,0:T(8,128)(2,1)S(1)} %collective-permute-done.7, bf16[1024,4096]{1,0:T(8,128)(2,1)} %param.4, s32[]{:T(128)S(6)} %select_n.52), kind=kOutput, calls=%fused_computation.2 | convolution fusion | flops 301989888 | bytes 4784132 | tf_op jit(solution)/shard_map/dot_general | solution.py:47
  32.7 3.6 %fusion.8 = f32[72,1024]{1,0:T(8,128)S(1)} fusion(f32[72,1024]{1,0:T(8,128)S(1)} %fusion.2, bf16[72,2048]{1,0:T(8,128)(2,1)S(1)} %constant_dynamic-update-slice_fusion.4, bf16[1024,4096]{1,0:T(8,128)(2,1)} %param.4, s32[]{:T(128)S(6)} %select_n.27), kind=kOutput, calls=%fused_computation.8 | convolution fusion | flops 302063616 | bytes 5079044 | tf_op jit(solution)/shard_map/dot_general | solution.py:46
  36.3 0.8 fusion.35
  37.1 3.7 %collective-permute-start.10 = (f32[8,1024]{1,0:T(8,128)S(1)}, f32[8,1024]{1,0:T(8,128)S(1)}, u32[]{:S(2)}, u32[]{:S(2)}) collective-permute-start(f32[8,1024]{1,0:T(8,128)S(1)} %fusion.35), channel_id=1, source_target_pairs={{0,3},{1,2},{2,1},{3,0},{4,7},{5,6},{6,5},{7,4},{8,11},{9,10},{10,... | collective-permute-start | bytes 98312 | tf_op jit(solution)/shard_map/ppermute | solution.py:56
  40.8 0.0 collective-permute-start.8
  40.8 0.8 collective-permute-start.9
  41.6 0.6 slice.26
  42.2 1.0 %collective-permute-done.10 = f32[8,1024]{1,0:T(8,128)S(1)} collective-permute-done((f32[8,1024]{1,0:T(8,128)S(1)}, f32[8,1024]{1,0:T(8,128)S(1)}, u32[]{:S(2)}, u32[]{:S(2)}) %collective-permute-start.10) | collective-permute-done | bytes 32800 | tf_op jit(solution)/shard_map/ppermute | solution.py:56
  43.2 1.9 %collective-permute-done.8 = f32[8,1024]{1,0:T(8,128)S(1)} collective-permute-done((f32[8,1024]{1,0:T(8,128)S(1)}, f32[8,1024]{1,0:T(8,128)S(1)}, u32[]{:S(2)}, u32[]{:S(2)}) %collective-permute-start.8) | collective-permute-done | bytes 32800 | tf_op jit(solution)/shard_map/ppermute | solution.py:56
  45.1 0.6 collective-permute-done.9
  45.6 0.6 fusion.41
  46.3 0.0 copy-start
  46.3 0.0 slice-start.1
  46.3 5.1 %fusion.25 = f32[64,4096]{1,0:T(8,128)S(1)} fusion(bf16[1024,4096]{1,0:T(8,128)(2,1)} %param.4, bf16[8,1024]{1,0:T(8,128)(2,1)S(1)} %get-tuple-element.4, bf16[8,1024]{1,0:T(8,128)(2,1)S(1)} %fusion.36), kind=kOutput, calls=%fused_computation.19 | convolution fusion | flops 536936448 | bytes 9469952 | tf_op jit(solution)/shard_map/dot_general | solution.py:30
  51.4 0.1 collective-permute-start.11
  51.5 1.5 %collective-permute-done.11 = bf16[64,2048]{1,0:T(8,128)(2,1)S(1)} collective-permute-done((bf16[64,2048]{1,0:T(8,128)(2,1)S(1)}, bf16[64,2048]{1,0:T(8,128)(2,1)S(1)}, u32[]{:S(2)}, u32[]{:S(2)}) %collective-permute-start.11) | collective-permute-done | bytes 262176 | tf_op jit(solution)/shard_map/ppermute | solution.py:10
  53.0 0.1 convert_add_fusion
  53.1 1.6 %collective-permute-start.12 = (bf16[64,512]{1,0:T(8,128)(2,1)S(1)}, bf16[64,512]{1,0:T(8,128)(2,1)S(1)}, u32[]{:S(2)}, u32[]{:S(2)}) collective-permute-start(bf16[64,512]{1,0:T(8,128)(2,1)S(1)} %get-tuple-element.8), channel_id=1, source_target_pairs={{0,8},{4,12},{8,0},{12,4},{16,24},{20,28},{24,16},{28,20},{1,9},{5... | collective-permute-start | bytes 196616 | tf_op jit(solution)/shard_map/ppermute | solution.py:10
  54.7 0.5 collective-permute-start.13
  55.2 1.5 %collective-permute-start.14 = (bf16[64,512]{1,0:T(8,128)(2,1)S(1)}, bf16[64,512]{1,0:T(8,128)(2,1)S(1)}, u32[]{:S(2)}, u32[]{:S(2)}) collective-permute-start(bf16[64,512]{1,0:T(8,128)(2,1)S(1)} %get-tuple-element.9), channel_id=1, source_target_pairs={{0,24},{4,28},{8,16},{12,20},{16,8},{20,12},{24,0},{28,4},{1,25},{... | collective-permute-start | bytes 196616 | tf_op jit(solution)/shard_map/ppermute | solution.py:10
  56.7 0.8 collective-permute-done.12
  57.5 2.2 %collective-permute-done.13 = bf16[64,512]{1,0:T(8,128)(2,1)S(1)} collective-permute-done((bf16[64,512]{1,0:T(8,128)(2,1)S(1)}, bf16[64,512]{1,0:T(8,128)(2,1)S(1)}, u32[]{:S(2)}, u32[]{:S(2)}) %collective-permute-start.13) | collective-permute-done | bytes 65568 | tf_op jit(solution)/shard_map/ppermute | solution.py:10
  59.7 0.7 collective-permute-done.14
  60.4 1.3 %collective-permute-start.15 = (bf16[64,512]{1,0:T(8,128)(2,1)S(1)}, bf16[64,512]{1,0:T(8,128)(2,1)S(1)}, u32[]{:S(2)}, u32[]{:S(2)}) collective-permute-start(bf16[64,512]{1,0:T(8,128)(2,1)S(1)} %get-tuple-element.3), channel_id=1, source_target_pairs={{0,8},{4,12},{8,0},{12,4},{16,24},{20,28},{24,16},{28,20},{1,9},{5... | collective-permute-start | bytes 196616 | tf_op jit(solution)/shard_map/ppermute | solution.py:10
  61.7 0.8 %collective-permute-start.16 = (bf16[64,512]{1,0:T(8,128)(2,1)S(1)}, bf16[64,512]{1,0:T(8,128)(2,1)S(1)}, u32[]{:S(2)}, u32[]{:S(2)}) collective-permute-start(bf16[64,512]{1,0:T(8,128)(2,1)S(1)} %get-tuple-element.3), channel_id=1, source_target_pairs={{0,16},{4,20},{8,24},{12,28},{16,0},{20,4},{24,8},{28,12},{1,17},{... | collective-permute-start | bytes 196616 | tf_op jit(solution)/shard_map/ppermute | solution.py:10
  62.6 1.4 %collective-permute-start.17 = (bf16[64,512]{1,0:T(8,128)(2,1)S(1)}, bf16[64,512]{1,0:T(8,128)(2,1)S(1)}, u32[]{:S(2)}, u32[]{:S(2)}) collective-permute-start(bf16[64,512]{1,0:T(8,128)(2,1)S(1)} %get-tuple-element.3), channel_id=1, source_target_pairs={{0,24},{4,28},{8,16},{12,20},{16,8},{20,12},{24,0},{28,4},{1,25},{... | collective-permute-start | bytes 196616 | tf_op jit(solution)/shard_map/ppermute | solution.py:10
  64.0 1.1 %collective-permute-done.15 = bf16[64,512]{1,0:T(8,128)(2,1)S(1)} collective-permute-done((bf16[64,512]{1,0:T(8,128)(2,1)S(1)}, bf16[64,512]{1,0:T(8,128)(2,1)S(1)}, u32[]{:S(2)}, u32[]{:S(2)}) %collective-permute-start.15) | collective-permute-done | bytes 65568 | tf_op jit(solution)/shard_map/ppermute | solution.py:10
  65.1 0.9 %collective-permute-done.16 = bf16[64,512]{1,0:T(8,128)(2,1)S(1)} collective-permute-done((bf16[64,512]{1,0:T(8,128)(2,1)S(1)}, bf16[64,512]{1,0:T(8,128)(2,1)S(1)}, u32[]{:S(2)}, u32[]{:S(2)}) %collective-permute-start.16) | collective-permute-done | bytes 65568 | tf_op jit(solution)/shard_map/ppermute | solution.py:10
  66.0 1.7 %collective-permute-done.17 = bf16[64,512]{1,0:T(8,128)(2,1)S(1)} collective-permute-done((bf16[64,512]{1,0:T(8,128)(2,1)S(1)}, bf16[64,512]{1,0:T(8,128)(2,1)S(1)}, u32[]{:S(2)}, u32[]{:S(2)}) %collective-permute-start.17) | collective-permute-done | bytes 65568 | tf_op jit(solution)/shard_map/ppermute | solution.py:10
  67.7 0.1 collective-permute-start.18
  67.8 1.5 %collective-permute-done.18 = bf16[64,2048]{1,0:T(8,128)(2,1)S(1)} collective-permute-done((bf16[64,2048]{1,0:T(8,128)(2,1)S(1)}, bf16[64,2048]{1,0:T(8,128)(2,1)S(1)}, u32[]{:S(2)}, u32[]{:S(2)}) %collective-permute-start.18) | collective-permute-done | bytes 262176 | tf_op jit(solution)/shard_map/ppermute | solution.py:10
  69.3 0.0 slice-done.1
  69.3 1.4 %fusion = f32[64,1024]{1,0:T(8,128)S(1)} fusion(bf16[64,2048]{1,0:T(8,128)(2,1)S(1)} %collective-permute-done.18, bf16[1024,4096]{1,0:T(8,128)(2,1)S(1)} %bitcast.30, s32[]{:T(128)S(6)} %select_n.52), kind=kOutput, calls=%fused_computation | convolution fusion | flops 268435456 | bytes 4718596 | tf_op jit(solution)/shard_map/dot_general | solution.py:47
  70.7 1.4 %fusion.20 = f32[8,1024]{1,0:T(8,128)S(1)} fusion(f32[64,1024]{1,0:T(8,128)S(1)} %fusion, bf16[64,2048]{1,0:T(8,128)(2,1)S(1)} %constant_dynamic-update-slice_fusion, bf16[1024,4096]{1,0:T(8,128)(2,1)S(1)} %bitcast.30, s32[]{:T(128)S(6)} %select_n.27, f32[8,1024]{1,0:T(8,128)S(1)} %get-tuple-element.16), kind=kOutput, calls=%fused_computation.12 | convolution fusion | flops 268623872 | bytes 4784132 | tf_op jit(solution)/shard_map/dot_general | solution.py:46
  72.1 2.1 %collective-permute-start.19 = (f32[8,1024]{1,0:T(8,128)S(1)}, f32[8,1024]{1,0:T(8,128)S(1)}, u32[]{:S(2)}, u32[]{:S(2)}) collective-permute-start(f32[8,1024]{1,0:T(8,128)S(1)} %fusion.20), channel_id=1, source_target_pairs={{0,1},{1,0},{2,3},{3,2},{4,5},{5,4},{6,7},{7,6},{8,9},{9,8},{10,11... | collective-permute-start | bytes 98312 | tf_op jit(solution)/shard_map/ppermute | solution.py:56
  74.2 0.4 collective-permute-start.20
  74.6 2.1 %collective-permute-start.21 = (f32[8,1024]{1,0:T(8,128)S(1)}, f32[8,1024]{1,0:T(8,128)S(1)}, u32[]{:S(2)}, u32[]{:S(2)}) collective-permute-start(f32[8,1024]{1,0:T(8,128)S(1)} %fusion.20), channel_id=1, source_target_pairs={{0,3},{1,2},{2,1},{3,0},{4,7},{5,6},{6,5},{7,4},{8,11},{9,10},{10,... | collective-permute-start | bytes 98312 | tf_op jit(solution)/shard_map/ppermute | solution.py:56
  76.7 0.0 collective-permute-done.19
  76.7 2.8 %collective-permute-done.20 = f32[8,1024]{1,0:T(8,128)S(1)} collective-permute-done((f32[8,1024]{1,0:T(8,128)S(1)}, f32[8,1024]{1,0:T(8,128)S(1)}, u32[]{:S(2)}, u32[]{:S(2)}) %collective-permute-start.20) | collective-permute-done | bytes 32800 | tf_op jit(solution)/shard_map/ppermute | solution.py:56
  79.5 0.8 %collective-permute-done.21 = f32[8,1024]{1,0:T(8,128)S(1)} collective-permute-done((f32[8,1024]{1,0:T(8,128)S(1)}, f32[8,1024]{1,0:T(8,128)S(1)}, u32[]{:S(2)}, u32[]{:S(2)}) %collective-permute-start.21) | collective-permute-done | bytes 32800 | tf_op jit(solution)/shard_map/ppermute | solution.py:56
  80.3 1.3 %multiply_add_fusion = f32[8,1024]{1,0:T(8,128)} fusion(f32[8,1024]{1,0:T(8,128)S(1)} %get-tuple-element.5, f32[8,1024]{1,0:T(8,128)S(1)} %collective-permute-done.20, f32[8,1024]{1,0:T(8,128)S(1)} %collective-permute-done.21, f32[8,1024]{1,0:T(8,128)S(1)} %fusion.20, f32[8,1024]{1,0:T(8,128)S(1)} %collective-permute-done.19, f32[]{:T(128)} %bitcast.5), kind=kLoop, calls=%fused_computation.38 | loop fusion | flops 40960 | bytes 196612 | tf_op jit(solution)/shard_map/add | solution.py:60
  (25 shorter events, 0.4 us)
Async XLA Ops:
  1.3 19.6 %copy-start.3 = (f32[3]{0:T(128)S(1)}, f32[3]{0:T(128)}, u32[]{:S(2)}) copy-start(f32[3]{0:T(128)} %param.7) | copy-start | bytes 40
  1.3 26.4 %copy-start.2 = (s32[1024]{0:T(1024)S(1)}, s32[1024]{0:T(1024)}, u32[]{:S(2)}) copy-start(s32[1024]{0:T(1024)} %param.6) | copy-start | bytes 12292
  6.3 39.3 %copy-start.1 = (bf16[8,1024]{1,0:T(8,128)(2,1)S(1)}, bf16[8,1024]{1,0:T(8,128)(2,1)}, u32[]{:S(2)}) copy-start(bf16[8,1024]{1,0:T(8,128)(2,1)} %param.5) | copy-start | bytes 49156
  6.4 2.1 %collective-permute-start = (f32[64,2048]{1,0:T(8,128)S(1)}, f32[64,2048]{1,0:T(8,128)S(1)}, u32[]{:S(2)}, u32[]{:S(2)}) collective-permute-start(f32[64,2048]{1,0:T(8,128)S(1)} %constant_dynamic-slice_fusion.3), channel_id=1, source_target_pairs={{0,4},{4,0},{8,12},{12,8},{16,20},{20,16},{24,28},{28,24},{1,5},{5... | collective-permute-start | bytes 1572872 | tf_op jit(solution)/shard_map/ppermute | solution.py:10
  8.6 6.9 %collective-permute-start.1 = (f32[64,512]{1,0:T(8,128)S(1)}, f32[64,512]{1,0:T(8,128)S(1)}, u32[]{:S(2)}, u32[]{:S(2)}) collective-permute-start(f32[64,512]{1,0:T(8,128)S(1)} %get-tuple-element.11), channel_id=1, source_target_pairs={{0,8},{4,12},{8,0},{12,4},{16,24},{20,28},{24,16},{28,20},{1,9},{5... | collective-permute-start | bytes 393224 | tf_op jit(solution)/shard_map/ppermute | solution.py:10
  11.5 8.1 %collective-permute-start.2 = (f32[64,512]{1,0:T(8,128)S(1)}, f32[64,512]{1,0:T(8,128)S(1)}, u32[]{:S(2)}, u32[]{:S(2)}) collective-permute-start(f32[64,512]{1,0:T(8,128)S(1)} %get-tuple-element.13), channel_id=1, source_target_pairs={{0,16},{4,20},{8,24},{12,28},{16,0},{20,4},{24,8},{28,12},{1,17},{... | collective-permute-start | bytes 393224 | tf_op jit(solution)/shard_map/ppermute | solution.py:10
  13.0 6.6 %collective-permute-start.3 = (f32[64,512]{1,0:T(8,128)S(1)}, f32[64,512]{1,0:T(8,128)S(1)}, u32[]{:S(2)}, u32[]{:S(2)}) collective-permute-start(f32[64,512]{1,0:T(8,128)S(1)} %get-tuple-element.12), channel_id=1, source_target_pairs={{0,24},{4,28},{8,16},{12,20},{16,8},{20,12},{24,0},{28,4},{1,25},{... | collective-permute-start | bytes 393224 | tf_op jit(solution)/shard_map/ppermute | solution.py:10
  19.7 4.8 %collective-permute-start.4 = (bf16[72,512]{1,0:T(8,128)(2,1)S(1)}, bf16[72,512]{1,0:T(8,128)(2,1)S(1)}, u32[]{:S(2)}, u32[]{:S(2)}) collective-permute-start(bf16[72,512]{1,0:T(8,128)(2,1)S(1)} %get-tuple-element.14), channel_id=1, source_target_pairs={{0,8},{4,12},{8,0},{12,4},{16,24},{20,28},{24,16},{28,20},{1,9},{5... | collective-permute-start | bytes 221192 | tf_op jit(solution)/shard_map/ppermute | solution.py:10
  21.0 4.5 %collective-permute-start.5 = (bf16[72,512]{1,0:T(8,128)(2,1)S(1)}, bf16[72,512]{1,0:T(8,128)(2,1)S(1)}, u32[]{:S(2)}, u32[]{:S(2)}) collective-permute-start(bf16[72,512]{1,0:T(8,128)(2,1)S(1)} %get-tuple-element.14), channel_id=1, source_target_pairs={{0,16},{4,20},{8,24},{12,28},{16,0},{20,4},{24,8},{28,12},{1,17},{... | collective-permute-start | bytes 221192 | tf_op jit(solution)/shard_map/ppermute | solution.py:10
  21.8 5.3 %collective-permute-start.6 = (bf16[72,512]{1,0:T(8,128)(2,1)S(1)}, bf16[72,512]{1,0:T(8,128)(2,1)S(1)}, u32[]{:S(2)}, u32[]{:S(2)}) collective-permute-start(bf16[72,512]{1,0:T(8,128)(2,1)S(1)} %get-tuple-element.14), channel_id=1, source_target_pairs={{0,24},{4,28},{8,16},{12,20},{16,8},{20,12},{24,0},{28,4},{1,25},{... | collective-permute-start | bytes 221192 | tf_op jit(solution)/shard_map/ppermute | solution.py:10
  27.1 2.0 %collective-permute-start.7 = (bf16[72,2048]{1,0:T(8,128)(2,1)S(1)}, bf16[72,2048]{1,0:T(8,128)(2,1)S(1)}, u32[]{:S(2)}, u32[]{:S(2)}) collective-permute-start(bf16[72,2048]{1,0:T(8,128)(2,1)S(1)} %constant_dynamic-update-slice_fusion.4), channel_id=1, source_target_pairs={{0,4},{4,0},{8,12},{12,8},{16,20},{20,16},{24,28},{28,24},{1,5},{5... | collective-permute-start | bytes 884744 | tf_op jit(solution)/shard_map/ppermute | solution.py:10
  36.3 33.1 %slice-start = ((s8[8388608]{0:T(1024)(128)(4,1)}), s8[4194304]{0:T(1024)(128)(4,1)S(1)}, s32[]{:S(2)}) async-start(s8[8388608]{0:T(1024)(128)(4,1)} %bitcast.29), calls=%async_computation | async-start | bytes 8388608
  37.1 6.1 %collective-permute-start.10 = (f32[8,1024]{1,0:T(8,128)S(1)}, f32[8,1024]{1,0:T(8,128)S(1)}, u32[]{:S(2)}, u32[]{:S(2)}) collective-permute-start(f32[8,1024]{1,0:T(8,128)S(1)} %fusion.35), channel_id=1, source_target_pairs={{0,3},{1,2},{2,1},{3,0},{4,7},{5,6},{6,5},{7,4},{8,11},{9,10},{10,... | collective-permute-start | bytes 98312 | tf_op jit(solution)/shard_map/ppermute | solution.py:56
  40.8 4.3 %collective-permute-start.8 = (f32[8,1024]{1,0:T(8,128)S(1)}, f32[8,1024]{1,0:T(8,128)S(1)}, u32[]{:S(2)}, u32[]{:S(2)}) collective-permute-start(f32[8,1024]{1,0:T(8,128)S(1)} %fusion.35), channel_id=1, source_target_pairs={{0,1},{1,0},{2,3},{3,2},{4,5},{5,4},{6,7},{7,6},{8,9},{9,8},{10,11... | collective-permute-start | bytes 98312 | tf_op jit(solution)/shard_map/ppermute | solution.py:56
  40.8 4.8 %collective-permute-start.9 = (f32[8,1024]{1,0:T(8,128)S(1)}, f32[8,1024]{1,0:T(8,128)S(1)}, u32[]{:S(2)}, u32[]{:S(2)}) collective-permute-start(f32[8,1024]{1,0:T(8,128)S(1)} %fusion.35), channel_id=1, source_target_pairs={{0,2},{1,3},{2,0},{3,1},{4,6},{5,7},{6,4},{7,5},{8,10},{9,11},{10,... | collective-permute-start | bytes 98312 | tf_op jit(solution)/shard_map/ppermute | solution.py:56
  46.3 34.1 %copy-start = (f32[8,1024]{1,0:T(8,128)}, f32[8,1024]{1,0:T(8,128)S(1)}, u32[]{:S(2)}) copy-start(f32[8,1024]{1,0:T(8,128)S(1)} %get-tuple-element.5) | copy-start | bytes 98308
  46.3 23.1 %slice-start.1 = ((s8[8388608]{0:T(1024)(128)(4,1)}), s8[4194304]{0:T(1024)(128)(4,1)S(1)}, s32[]{:S(2)}) async-start(s8[8388608]{0:T(1024)(128)(4,1)} %bitcast.29), calls=%async_computation.1 | async-start | bytes 8388608
  51.4 1.6 %collective-permute-start.11 = (bf16[64,2048]{1,0:T(8,128)(2,1)S(1)}, bf16[64,2048]{1,0:T(8,128)(2,1)S(1)}, u32[]{:S(2)}, u32[]{:S(2)}) collective-permute-start(bf16[64,2048]{1,0:T(8,128)(2,1)S(1)} %dynamic-slice_convert_fusion), channel_id=1, source_target_pairs={{0,4},{4,0},{8,12},{12,8},{16,20},{20,16},{24,28},{28,24},{1,5},{5... | collective-permute-start | bytes 786440 | tf_op jit(solution)/shard_map/ppermute | solution.py:10
  53.1 4.3 %collective-permute-start.12 = (bf16[64,512]{1,0:T(8,128)(2,1)S(1)}, bf16[64,512]{1,0:T(8,128)(2,1)S(1)}, u32[]{:S(2)}, u32[]{:S(2)}) collective-permute-start(bf16[64,512]{1,0:T(8,128)(2,1)S(1)} %get-tuple-element.8), channel_id=1, source_target_pairs={{0,8},{4,12},{8,0},{12,4},{16,24},{20,28},{24,16},{28,20},{1,9},{5... | collective-permute-start | bytes 196616 | tf_op jit(solution)/shard_map/ppermute | solution.py:10
  54.7 5.0 %collective-permute-start.13 = (bf16[64,512]{1,0:T(8,128)(2,1)S(1)}, bf16[64,512]{1,0:T(8,128)(2,1)S(1)}, u32[]{:S(2)}, u32[]{:S(2)}) collective-permute-start(bf16[64,512]{1,0:T(8,128)(2,1)S(1)} %get-tuple-element.10), channel_id=1, source_target_pairs={{0,16},{4,20},{8,24},{12,28},{16,0},{20,4},{24,8},{28,12},{1,17},{... | collective-permute-start | bytes 196616 | tf_op jit(solution)/shard_map/ppermute | solution.py:10
  55.2 5.2 %collective-permute-start.14 = (bf16[64,512]{1,0:T(8,128)(2,1)S(1)}, bf16[64,512]{1,0:T(8,128)(2,1)S(1)}, u32[]{:S(2)}, u32[]{:S(2)}) collective-permute-start(bf16[64,512]{1,0:T(8,128)(2,1)S(1)} %get-tuple-element.9), channel_id=1, source_target_pairs={{0,24},{4,28},{8,16},{12,20},{16,8},{20,12},{24,0},{28,4},{1,25},{... | collective-permute-start | bytes 196616 | tf_op jit(solution)/shard_map/ppermute | solution.py:10
  60.4 4.6 %collective-permute-start.15 = (bf16[64,512]{1,0:T(8,128)(2,1)S(1)}, bf16[64,512]{1,0:T(8,128)(2,1)S(1)}, u32[]{:S(2)}, u32[]{:S(2)}) collective-permute-start(bf16[64,512]{1,0:T(8,128)(2,1)S(1)} %get-tuple-element.3), channel_id=1, source_target_pairs={{0,8},{4,12},{8,0},{12,4},{16,24},{20,28},{24,16},{28,20},{1,9},{5... | collective-permute-start | bytes 196616 | tf_op jit(solution)/shard_map/ppermute | solution.py:10
  61.7 4.3 %collective-permute-start.16 = (bf16[64,512]{1,0:T(8,128)(2,1)S(1)}, bf16[64,512]{1,0:T(8,128)(2,1)S(1)}, u32[]{:S(2)}, u32[]{:S(2)}) collective-permute-start(bf16[64,512]{1,0:T(8,128)(2,1)S(1)} %get-tuple-element.3), channel_id=1, source_target_pairs={{0,16},{4,20},{8,24},{12,28},{16,0},{20,4},{24,8},{28,12},{1,17},{... | collective-permute-start | bytes 196616 | tf_op jit(solution)/shard_map/ppermute | solution.py:10
  62.6 5.2 %collective-permute-start.17 = (bf16[64,512]{1,0:T(8,128)(2,1)S(1)}, bf16[64,512]{1,0:T(8,128)(2,1)S(1)}, u32[]{:S(2)}, u32[]{:S(2)}) collective-permute-start(bf16[64,512]{1,0:T(8,128)(2,1)S(1)} %get-tuple-element.3), channel_id=1, source_target_pairs={{0,24},{4,28},{8,16},{12,20},{16,8},{20,12},{24,0},{28,4},{1,25},{... | collective-permute-start | bytes 196616 | tf_op jit(solution)/shard_map/ppermute | solution.py:10
  67.7 1.6 %collective-permute-start.18 = (bf16[64,2048]{1,0:T(8,128)(2,1)S(1)}, bf16[64,2048]{1,0:T(8,128)(2,1)S(1)}, u32[]{:S(2)}, u32[]{:S(2)}) collective-permute-start(bf16[64,2048]{1,0:T(8,128)(2,1)S(1)} %constant_dynamic-update-slice_fusion), channel_id=1, source_target_pairs={{0,4},{4,0},{8,12},{12,8},{16,20},{20,16},{24,28},{28,24},{1,5},{5... | collective-permute-start | bytes 786440 | tf_op jit(solution)/shard_map/ppermute | solution.py:10
  72.1 4.5 %collective-permute-start.19 = (f32[8,1024]{1,0:T(8,128)S(1)}, f32[8,1024]{1,0:T(8,128)S(1)}, u32[]{:S(2)}, u32[]{:S(2)}) collective-permute-start(f32[8,1024]{1,0:T(8,128)S(1)} %fusion.20), channel_id=1, source_target_pairs={{0,1},{1,0},{2,3},{3,2},{4,5},{5,4},{6,7},{7,6},{8,9},{9,8},{10,11... | collective-permute-start | bytes 98312 | tf_op jit(solution)/shard_map/ppermute | solution.py:56
  74.2 5.3 %collective-permute-start.20 = (f32[8,1024]{1,0:T(8,128)S(1)}, f32[8,1024]{1,0:T(8,128)S(1)}, u32[]{:S(2)}, u32[]{:S(2)}) collective-permute-start(f32[8,1024]{1,0:T(8,128)S(1)} %fusion.20), channel_id=1, source_target_pairs={{0,2},{1,3},{2,0},{3,1},{4,6},{5,7},{6,4},{7,5},{8,10},{9,11},{10,... | collective-permute-start | bytes 98312 | tf_op jit(solution)/shard_map/ppermute | solution.py:56
  74.6 5.7 %collective-permute-start.21 = (f32[8,1024]{1,0:T(8,128)S(1)}, f32[8,1024]{1,0:T(8,128)S(1)}, u32[]{:S(2)}, u32[]{:S(2)}) collective-permute-start(f32[8,1024]{1,0:T(8,128)S(1)} %fusion.20), channel_id=1, source_target_pairs={{0,3},{1,2},{2,1},{3,0},{4,7},{5,6},{6,5},{7,4},{8,11},{9,10},{10,... | collective-permute-start | bytes 98312 | tf_op jit(solution)/shard_map/ppermute | solution.py:56

commit v2 on v0

v2 whole, which is shorter than its diff:
```python
import functools

import jax
import jax.numpy as jnp
from jax import lax
from jax.experimental import pallas as pl
from jax.experimental.pallas import tpu as pltpu
from jax.sharding import PartitionSpec as P

ENVS = 8
VMEM = pl.BlockSpec(memory_space=pltpu.VMEM)
SMEM = pl.BlockSpec(memory_space=pltpu.SMEM)
HBM = pl.BlockSpec(memory_space=pltpu.HBM)
LIMIT = 24 * 1024 * 1024


def build_panel(rounded, labels):
    rows = [jnp.where(labels == e, rounded, 0.0) for e in range(ENVS)]
    return jnp.concatenate(rows, axis=0).astype(jnp.bfloat16)


def load_body(place, probes, labels, genotypes, held, partial, sems, *, other):
    chips, _, width = held.shape
    core, chip = place[0], place[1]
    half = (1 - core) if other else core

    def copy(d):
        start = pl.multiple_of((half * chips + (chip ^ d)) * width, width)
        return pltpu.make_async_copy(genotypes.at[:, pl.ds(start, width)], held.at[d], sems.at[d])

    ahead = min(2, chips)
    for d in range(ahead):
        copy(d).start()
    panel = build_panel(probes[...].astype(jnp.float32), labels[...])
    for d in range(chips):
        copy(d).wait()
        if d + ahead < chips:
            copy(d + ahead).start()
        partial[:, pl.ds(d * width, width)] = jnp.dot(
            panel, held[d], preferred_element_type=jnp.float32
        ).astype(partial.dtype)


def load_half(place, probes, labels, genotypes, chips, width, other, wire):
    samples = probes.shape[1]
    rows = ENVS * probes.shape[0]
    return pl.pallas_call(
        functools.partial(load_body, other=other),
        in_specs=[SMEM, VMEM, VMEM, HBM],
        out_specs=(VMEM, VMEM),
        out_shape=(
            pltpu.VMEM((chips, samples, width), genotypes.dtype),
            jax.ShapeDtypeStruct((rows, chips * width), wire),
        ),
        scratch_shapes=[pltpu.SemaphoreType.DMA((chips,))],
        compiler_params=pltpu.CompilerParams(vmem_limit_bytes=LIMIT),
        name="load_other" if other else "load_own",
    )(place, probes, labels, genotypes)


def step_body(noise, current, labels, held, *refs, count):
    parts = [refs[k][...] for k in range(count)]
    first, panel_out, partial = refs[count:]
    while len(parts) > 1:
        parts = [parts[k] + parts[k + 1] for k in range(0, len(parts), 2)]
    value = parts[0] + noise[2] * current[...].astype(jnp.float32)
    first[...] = value
    panel = build_panel(value.astype(jnp.bfloat16).astype(jnp.float32), labels[...])
    panel_out[...] = panel
    width = held.shape[2]
    for d in range(held.shape[0]):
        partial[:, pl.ds(d * width, width)] = jnp.dot(
            panel, held[d], preferred_element_type=jnp.float32
        ).astype(partial.dtype)


def step_half(variances, current, labels, held, parts, wire):
    rows = ENVS * current.shape[0]
    chips, samples, width = held.shape
    return pl.pallas_call(
        functools.partial(step_body, count=len(parts)),
        in_specs=[SMEM] + [VMEM] * (3 + len(parts)),
        out_specs=(VMEM, VMEM, VMEM),
        out_shape=(
            jax.ShapeDtypeStruct(current.shape, jnp.float32),
            jax.ShapeDtypeStruct((rows, samples), jnp.bfloat16),
            jax.ShapeDtypeStruct((rows, chips * width), wire),
        ),
        compiler_params=pltpu.CompilerParams(vmem_limit_bytes=LIMIT),
        name="step_other",
    )(variances, current, labels, held, *parts)


def panel_body(panel, held, partial):
    width = held.shape[2]
    for d in range(held.shape[0]):
        partial[:, pl.ds(d * width, width)] = jnp.dot(panel[...], held[d], preferred_element_type=jnp.float32)


def panel_half(panel, held):
    chips, _, width = held.shape
    return pl.pallas_call(
        panel_body,
        in_specs=[VMEM, VMEM],
        out_specs=VMEM,
        out_shape=jax.ShapeDtypeStruct((panel.shape[0], chips * width), jnp.float32),
        compiler_params=pltpu.CompilerParams(vmem_limit_bytes=LIMIT),
        name="step_own",
    )(panel, held)


def dot_t(a, b):
    return lax.dot_general(a, b, (((1,), (1,)), ((), ())), preferred_element_type=jnp.float32)


def image_body(panel, held, image):
    width = held.shape[2]
    total = dot_t(panel[:, pl.ds(0, width)], held[0])
    for d in range(1, held.shape[0]):
        total += dot_t(panel[:, pl.ds(d * width, width)], held[d])
    image[...] = total


def image_half(panel, held):
    return pl.pallas_call(
        image_body,
        in_specs=[VMEM, VMEM],
        out_specs=VMEM,
        out_shape=jax.ShapeDtypeStruct((panel.shape[0], held.shape[1]), jnp.float32),
        compiler_params=pltpu.CompilerParams(vmem_limit_bytes=LIMIT),
        name="image_own",
    )(panel, held)


def finish_body(variances, labels, panel, held, image, weighted, *, snps, exact):
    width = held.shape[2]
    total = image[...]
    for d in range(held.shape[0]):
        total += dot_t(panel[:, pl.ds(d * width, width)], held[d])
    probes = weighted.shape[0]
    additive, interaction = variances[0] * (1.0 / snps), variances[1] * (1.0 / snps)
    tag = labels[...]
    skip = probes if exact else 0
    result = additive * total[:probes] if exact else None
    for e in range(ENVS):
        block = total[skip + e * probes : skip + (e + 1) * probes]
        scale = jnp.where(tag == e, interaction, 0.0) + (0.0 if exact else additive)
        term = scale * block
        result = term if result is None else result + term
    weighted[...] = result


def finish_half(variances, labels, panel, held, image, probes, snps, exact):
    return pl.pallas_call(
        functools.partial(finish_body, snps=snps, exact=exact),
        in_specs=[SMEM, VMEM, VMEM, VMEM, VMEM],
        out_specs=VMEM,
        out_shape=jax.ShapeDtypeStruct((probes, held.shape[1]), jnp.float32),
        compiler_params=pltpu.CompilerParams(vmem_limit_bytes=LIMIT),
        name="image_other",
    )(variances, labels, panel, held, image)


def make(mesh):
    samp, snp = mesh.shape["samp"], mesh.shape["snp"]
    chips = samp // 2

    def exchange(block, offset):
        return lax.ppermute(block, "samp", [(k, k ^ offset) for k in range(samp)])

    def reduce_panel(given, own, wire, probes, exact):
        width = own.shape[1] // chips
        pair = own + exchange(given, 1).astype(jnp.float32)
        total = pair[:, :width]
        for step in range(1, chips):
            block = pair[:, step * width : (step + 1) * width].astype(wire)
            total = total + exchange(block, 2 * step).astype(jnp.float32)
        if exact:
            total = jnp.concatenate([total.reshape(ENVS, probes, width).sum(0), total], axis=0)
        return total.astype(jnp.bfloat16)

    def gather_panel(mine):
        return jnp.concatenate([mine] + [exchange(mine, 2 * step) for step in range(1, chips)], axis=1)

    def per_device(genotypes, probes, env_label, variances):
        snps = genotypes.shape[1] * snp
        count = probes.shape[0]
        width = genotypes.shape[1] // samp
        index = lax.axis_index("samp")
        place = jnp.stack([index % 2, index // 2]).astype(jnp.int32)
        labels = env_label[None, :]

        def image_of(panel, exact):
            other = exchange(panel, 1)
            image = image_half(panel, held_own)
            return finish_half(variances, labels, other, held_other, image, count, snps, exact)

        def spread(weighted):
            return [weighted] + [
                lax.ppermute(weighted, "snp", [(k, k ^ step) for k in range(snp)]) for step in range(1, snp)
            ]

        held_other, given = load_half(place, probes, labels, genotypes, chips, width, True, jnp.float32)
        held_own, own = load_half(place, probes, labels, genotypes, chips, width, False, jnp.float32)
        panel = gather_panel(reduce_panel(given, own, jnp.float32, count, True))
        parts = spread(image_of(panel, True))
        first, scaled, given = step_half(variances, probes, labels, held_other, parts, jnp.bfloat16)
        own = panel_half(scaled, held_own)
        panel = gather_panel(reduce_panel(given, own, jnp.bfloat16, count, False))
        parts = spread(image_of(panel, False))
        while len(parts) > 1:
            parts = [parts[k] + parts[k + 1] for k in range(0, len(parts), 2)]
        return (first, parts[0] + variances[2] * first)

    return per_device


def solution(mesh):
    return jax.shard_map(
        make(mesh),
        mesh=mesh,
        in_specs=(P("samp", "snp"), P(None, "samp"), P("samp"), P()),
        out_specs=(P(None, "samp"), P(None, "samp")),
        check_vma=False,
    )
```

time: 168 us -> 72.8 us (0.43)
  blocking collectives: 138 us -> 0 us
  waiting for transfers between devices: 0 us -> 26.2 us
  starting transfers between devices: 0 us -> 24.4 us
  matrix products: 22.1 us -> 0 us
  Pallas kernels: 0 us -> 14.2 us
  other arithmetic: 5.97 us -> 1.53 us
  local copies, waits for them, and re-layouts: 1.44 us -> 5.42 us
    psum x4 -> x0, blocking collectives: 138 us -> none  [the longest x2 102 us: apply_operator(): snp_panel = lax.psum(partial_panel, 'samp').astype(jnp.bfloat16)]
    ppermute x0 -> x22, waiting for transfers between devices: none -> 26.2 us  [the longest x16 19.1 us: exchange(): return lax.ppermute(block, 'samp', [(k, k ^ offset) for k in range(samp)])]
    ppermute x0 -> x22, starting transfers between devices: none -> 24.4 us  [the longest x16 15.5 us: exchange(): return lax.ppermute(block, 'samp', [(k, k ^ offset) for k in range(samp)])]
    dot_general x4 -> x0, matrix products: 22.1 us -> none  [the longest x2 12.1 us: local_image(): lax.dot_general(snp_panel, genotypes, (((1,), (1,)), ((), ())), preferred...]
    pallas_call x0 -> x8, Pallas kernels: none -> 14.2 us  [the longest x2 4.94 us: load_half(): pl.pallas_call(functools.partial(load_body, other=other), in_specs=[SMEM,...]
    unnamed x4 -> x12, local copies, waits for them, and re-layouts: 0.01 us -> 4.8 us
    add x3 -> x2, other arithmetic: 3.74 us -> 1.28 us  [the longest x1 1.19 us: per_device(): return (first, parts[0] + variances[2] * first)]
  transfers between devices with their start and end apart: 0 -> 22, of which waited for: 0 -> 19; matrix products, arithmetic and copies ran while one was open for 0% -> 1% of each run, Pallas kernels for 0% -> 8%
where the time goes in v2:
time: 72.8 us; the launch traced here: 72.5 us
  waiting for transfers between devices  26.2 us (36%)
  starting transfers between devices  24.4 us (34%)
  Pallas kernels  14.2 us (20%)
  local copies, waits for them, and re-layouts  5.42 us (7%)
  other arithmetic  1.53 us (2%)
  between operations  0.8 us (1%)
    ppermute x16, waiting for transfers between devices, exchange(): return lax.ppermute(block, 'samp', [(k, k ^ offset) for k in range(samp)])  19.1 us
    ppermute x16, starting transfers between devices, exchange(): return lax.ppermute(block, 'samp', [(k, k ^ offset) for k in range(samp)])  15.5 us
    ppermute x6, starting transfers between devices, spread(): lax.ppermute(weighted, 'snp', [(k, k ^ step) for k in range(snp)])  8.9 us
    ppermute x6, waiting for transfers between devices, spread(): lax.ppermute(weighted, 'snp', [(k, k ^ step) for k in range(snp)])  7.09 us
    pallas_call x2, Pallas kernels, load_half(): pl.pallas_call(functools.partial(load_body, other=other), in_specs=[SMEM,...  4.94 us
    unnamed x12, local copies, waits for them, and re-layouts  4.8 us
    pallas_call x2, Pallas kernels, finish_half(): pl.pallas_call(functools.partial(finish_body, snps=snps, exact=exact), in...  3.84 us
    pallas_call x2, Pallas kernels, image_half(): pl.pallas_call(image_body, in_specs=[VMEM, VMEM], out_specs=VMEM, out_sha...  2.74 us
  transfers between devices with their start and end apart: 22, of which 19 were waited for; matrix products, arithmetic and copies ran while one was open for 1% of the time, Pallas kernels for 8%

profile of v2, /device:TPU:0, one launch (start us, length us, event | category | flops | bytes accessed | tf_op | source)
XLA Modules:
  0.0 72.5 jit_solution(8620260975638992436)
XLA Ops:
  0.6 0.1 pad_add_fusion.place
  0.7 3.4 %copy-done = bf16[1024,4096]{1,0:T(8,128)(2,1)S(1)} copy-done((bf16[1024,4096]{1,0:T(8,128)(2,1)S(1)}, bf16[1024,4096]{1,0:T(8,128)(2,1)}, u32[]{:S(2)}) %copy-start) | copy-done | bytes 8388632
  4.1 0.7 copy-done.1
  4.8 0.7 copy-done.3
  5.5 2.5 %load_other.1 = (bf16[4,1024,512]{2,1,0:T(8,128)(2,1)S(1)}, f32[64,2048]{1,0:T(8,128)S(1)}) custom-call(s32[2]{0:T(128)S(1)} %pad_add_fusion.place, bf16[8,1024]{1,0:T(8,128)(2,1)S(1)} %copy-done.1, s32[1,1024]{1,0:T(1,128)S(1)} %bitcast.6, bf16[1024,4096]{1,0:T(8,128)(2,1)S(1)} %copy-done), custom_call_target="tpu_custom_call" | custom-call | tf_op jit(solution)/shard_map/load_other/pallas_call | solution.py:47
  8.0 0.6 collective-permute-start
  8.5 2.5 %load_own.1 = (bf16[4,1024,512]{2,1,0:T(8,128)(2,1)S(1)}, f32[64,2048]{1,0:T(8,128)S(1)}) custom-call(s32[2]{0:T(128)S(1)} %pad_add_fusion.place, bf16[8,1024]{1,0:T(8,128)(2,1)S(1)} %copy-done.1, s32[1,1024]{1,0:T(1,128)S(1)} %bitcast.7, bf16[1024,4096]{1,0:T(8,128)(2,1)S(1)} %copy-done), custom_call_target="tpu_custom_call" | custom-call | tf_op jit(solution)/shard_map/load_own/pallas_call | solution.py:47
  11.0 0.0 collective-permute-done
  11.0 0.0 copy-start.4
  11.0 0.1 add.42
  11.2 2.6 %collective-permute-start.1 = (f32[64,512]{1,0:T(8,128)S(1)}, f32[64,512]{1,0:T(8,128)S(1)}, u32[]{:S(2)}, u32[]{:S(2)}) collective-permute-start(f32[64,512]{1,0:T(8,128)S(1)} %get-tuple-element.20), channel_id=1, source_target_pairs={{0,8},{4,12},{8,0},{12,4},{16,24},{20,28},{24,16},{28,20},{1,9},{5... | collective-permute-start | bytes 393224 | tf_op jit(solution)/shard_map/ppermute | solution.py:169
  13.7 1.5 %collective-permute-start.2 = (f32[64,512]{1,0:T(8,128)S(1)}, f32[64,512]{1,0:T(8,128)S(1)}, u32[]{:S(2)}, u32[]{:S(2)}) collective-permute-start(f32[64,512]{1,0:T(8,128)S(1)} %get-tuple-element.22), channel_id=1, source_target_pairs={{0,16},{4,20},{8,24},{12,28},{16,0},{20,4},{24,8},{28,12},{1,17},{... | collective-permute-start | bytes 393224 | tf_op jit(solution)/shard_map/ppermute | solution.py:169
  15.2 0.0 collective-permute-start.3
  15.3 2.8 %collective-permute-done.1 = f32[64,512]{1,0:T(8,128)S(1)} collective-permute-done((f32[64,512]{1,0:T(8,128)S(1)}, f32[64,512]{1,0:T(8,128)S(1)}, u32[]{:S(2)}, u32[]{:S(2)}) %collective-permute-start.1) | collective-permute-done | bytes 131104 | tf_op jit(solution)/shard_map/ppermute | solution.py:169
  18.0 4.1 %collective-permute-done.2 = f32[64,512]{1,0:T(8,128)S(1)} collective-permute-done((f32[64,512]{1,0:T(8,128)S(1)}, f32[64,512]{1,0:T(8,128)S(1)}, u32[]{:S(2)}, u32[]{:S(2)}) %collective-permute-start.2) | collective-permute-done | bytes 131104 | tf_op jit(solution)/shard_map/ppermute | solution.py:169
  22.2 0.0 collective-permute-done.3
  22.2 1.3 %collective-permute-start.4 = (bf16[72,512]{1,0:T(8,128)(2,1)S(1)}, bf16[72,512]{1,0:T(8,128)(2,1)S(1)}, u32[]{:S(2)}, u32[]{:S(2)}) collective-permute-start(bf16[72,512]{1,0:T(8,128)(2,1)S(1)} %pad_maximum_fusion.2), channel_id=1, source_target_pairs={{0,8},{4,12},{8,0},{12,4},{16,24},{20,28},{24,16},{28,20},{1,9},{5... | collective-permute-start | bytes 221192 | tf_op jit(solution)/shard_map/ppermute | solution.py:169
  23.5 0.8 %collective-permute-start.5 = (bf16[72,512]{1,0:T(8,128)(2,1)S(1)}, bf16[72,512]{1,0:T(8,128)(2,1)S(1)}, u32[]{:S(2)}, u32[]{:S(2)}) collective-permute-start(bf16[72,512]{1,0:T(8,128)(2,1)S(1)} %pad_maximum_fusion.2), channel_id=1, source_target_pairs={{0,16},{4,20},{8,24},{12,28},{16,0},{20,4},{24,8},{28,12},{1,17},{... | collective-permute-start | bytes 221192 | tf_op jit(solution)/shard_map/ppermute | solution.py:169
  24.3 1.4 %collective-permute-start.6 = (bf16[72,512]{1,0:T(8,128)(2,1)S(1)}, bf16[72,512]{1,0:T(8,128)(2,1)S(1)}, u32[]{:S(2)}, u32[]{:S(2)}) collective-permute-start(bf16[72,512]{1,0:T(8,128)(2,1)S(1)} %pad_maximum_fusion.2), channel_id=1, source_target_pairs={{0,24},{4,28},{8,16},{12,20},{16,8},{20,12},{24,0},{28,4},{1,25},{... | collective-permute-start | bytes 221192 | tf_op jit(solution)/shard_map/ppermute | solution.py:169
  25.8 0.9 %collective-permute-done.4 = bf16[72,512]{1,0:T(8,128)(2,1)S(1)} collective-permute-done((bf16[72,512]{1,0:T(8,128)(2,1)S(1)}, bf16[72,512]{1,0:T(8,128)(2,1)S(1)}, u32[]{:S(2)}, u32[]{:S(2)}) %collective-permute-start.4) | collective-permute-done | bytes 73760 | tf_op jit(solution)/shard_map/ppermute | solution.py:169
  26.6 1.7 %collective-permute-done.5 = bf16[72,512]{1,0:T(8,128)(2,1)S(1)} collective-permute-done((bf16[72,512]{1,0:T(8,128)(2,1)S(1)}, bf16[72,512]{1,0:T(8,128)(2,1)S(1)}, u32[]{:S(2)}, u32[]{:S(2)}) %collective-permute-start.5) | collective-permute-done | bytes 73760 | tf_op jit(solution)/shard_map/ppermute | solution.py:169
  28.4 1.2 %collective-permute-done.6 = bf16[72,512]{1,0:T(8,128)(2,1)S(1)} collective-permute-done((bf16[72,512]{1,0:T(8,128)(2,1)S(1)}, bf16[72,512]{1,0:T(8,128)(2,1)S(1)}, u32[]{:S(2)}, u32[]{:S(2)}) %collective-permute-start.6) | collective-permute-done | bytes 73760 | tf_op jit(solution)/shard_map/ppermute | solution.py:169
  29.6 0.1 collective-permute-start.7
  29.7 0.0 copy-start.2
  29.7 1.4 %image_own.2.image = f32[72,1024]{1,0:T(8,128)S(1)} custom-call(bf16[72,2048]{1,0:T(8,128)(2,1)S(1)} %pad_maximum_fusion.panel, bf16[4,1024,512]{2,1,0:T(8,128)(2,1)S(1)} %get-tuple-element.12.held), custom_call_target="tpu_custom_call" | custom-call | tf_op jit(solution)/shard_map/image_own/pallas_call | solution.py:125
  31.1 0.2 collective-permute-done.7.panel
  31.3 0.0 copy-done.4
  31.3 1.9 %image_other.2.refs_0_ = f32[8,1024]{1,0:T(8,128)S(1)} custom-call(f32[3]{0:T(128)S(1)} %copy-done.4, s32[1,1024]{1,0:T(1,128)S(1)} %bitcast.8, bf16[72,2048]{1,0:T(8,128)(2,1)S(1)} %collective-permute-done.7.panel, bf16[4,1024,512]{2,1,0:T(8,128)(2,1)S(1)} %get-tuple-element.9.held, f32[72,1024]{1,0:T(8,128)S(1)} %image_own.2.image), custom_call_target="tpu_custom_call" | custom-call | tf_op jit(solution)/shard_map/image_other/pallas_call | solution.py:154
  33.2 3.7 %collective-permute-start.10 = (f32[8,1024]{1,0:T(8,128)S(1)}, f32[8,1024]{1,0:T(8,128)S(1)}, u32[]{:S(2)}, u32[]{:S(2)}) collective-permute-start(f32[8,1024]{1,0:T(8,128)S(1)} %image_other.2.refs_0_), channel_id=1, source_target_pairs={{0,3},{1,2},{2,1},{3,0},{4,7},{5,6},{6,5},{7,4},{8,11},{9,10},{10,... | collective-permute-start | bytes 98312 | tf_op jit(solution)/shard_map/ppermute | solution.py:200
  36.9 0.0 collective-permute-start.8
  36.9 0.8 %collective-permute-start.9 = (f32[8,1024]{1,0:T(8,128)S(1)}, f32[8,1024]{1,0:T(8,128)S(1)}, u32[]{:S(2)}, u32[]{:S(2)}) collective-permute-start(f32[8,1024]{1,0:T(8,128)S(1)} %image_other.2.refs_0_), channel_id=1, source_target_pairs={{0,2},{1,3},{2,0},{3,1},{4,6},{5,7},{6,4},{7,5},{8,10},{9,11},{10,... | collective-permute-start | bytes 98312 | tf_op jit(solution)/shard_map/ppermute | solution.py:200
  37.6 1.4 %collective-permute-done.10.refs_3_ = f32[8,1024]{1,0:T(8,128)S(1)} collective-permute-done((f32[8,1024]{1,0:T(8,128)S(1)}, f32[8,1024]{1,0:T(8,128)S(1)}, u32[]{:S(2)}, u32[]{:S(2)}) %collective-permute-start.10) | collective-permute-done | bytes 32800 | tf_op jit(solution)/shard_map/ppermute | solution.py:200
  39.1 2.0 %collective-permute-done.8.refs_1_ = f32[8,1024]{1,0:T(8,128)S(1)} collective-permute-done((f32[8,1024]{1,0:T(8,128)S(1)}, f32[8,1024]{1,0:T(8,128)S(1)}, u32[]{:S(2)}, u32[]{:S(2)}) %collective-permute-start.8) | collective-permute-done | bytes 32800 | tf_op jit(solution)/shard_map/ppermute | solution.py:200
  41.1 0.9 %collective-permute-done.9.refs_2_ = f32[8,1024]{1,0:T(8,128)S(1)} collective-permute-done((f32[8,1024]{1,0:T(8,128)S(1)}, f32[8,1024]{1,0:T(8,128)S(1)}, u32[]{:S(2)}, u32[]{:S(2)}) %collective-permute-start.9) | collective-permute-done | bytes 32800 | tf_op jit(solution)/shard_map/ppermute | solution.py:200
  42.0 1.9 %step_other.1 = (f32[8,1024]{1,0:T(8,128)}, bf16[64,1024]{1,0:T(8,128)(2,1)S(1)}, bf16[64,2048]{1,0:T(8,128)(2,1)S(1)}) custom-call(f32[3]{0:T(128)S(1)} %copy-done.4, bf16[8,1024]{1,0:T(8,128)(2,1)S(1)} %copy-done.2, s32[1,1024]{1,0:T(1,128)S(1)} %bitcast.9, bf16[4,1024,512]{2,1,0:T(8,128)(2,1)S(1)} %get-tuple-element.9.held, ...), custom_call_target="tpu_custom_call" | custom-call | tf_op jit(solution)/shard_map/step_other/pallas_call | solution.py:80
  43.9 0.0 collective-permute-start.11
  43.9 0.8 %step_own.1 = f32[64,2048]{1,0:T(8,128)S(1)} custom-call(bf16[64,1024]{1,0:T(8,128)(2,1)S(1)} %get-tuple-element.14.panel, bf16[4,1024,512]{2,1,0:T(8,128)(2,1)S(1)} %get-tuple-element.12.held), custom_call_target="tpu_custom_call" | custom-call | tf_op jit(solution)/shard_map/step_own/pallas_call | solution.py:102
  44.7 0.7 collective-permute-done.11
  45.4 0.1 fusion.5
  45.5 1.2 %collective-permute-start.12 = (bf16[64,512]{1,0:T(8,128)(2,1)S(1)}, bf16[64,512]{1,0:T(8,128)(2,1)S(1)}, u32[]{:S(2)}, u32[]{:S(2)}) collective-permute-start(bf16[64,512]{1,0:T(8,128)(2,1)S(1)} %get-tuple-element.23), channel_id=1, source_target_pairs={{0,8},{4,12},{8,0},{12,4},{16,24},{20,28},{24,16},{28,20},{1,9},{5... | collective-permute-start | bytes 196616 | tf_op jit(solution)/shard_map/ppermute | solution.py:169
  46.7 0.5 collective-permute-start.13
  47.2 1.8 %collective-permute-start.14 = (bf16[64,512]{1,0:T(8,128)(2,1)S(1)}, bf16[64,512]{1,0:T(8,128)(2,1)S(1)}, u32[]{:S(2)}, u32[]{:S(2)}) collective-permute-start(bf16[64,512]{1,0:T(8,128)(2,1)S(1)} %get-tuple-element.24), channel_id=1, source_target_pairs={{0,24},{4,28},{8,16},{12,20},{16,8},{20,12},{24,0},{28,4},{1,25},{... | collective-permute-start | bytes 196616 | tf_op jit(solution)/shard_map/ppermute | solution.py:169
  49.1 0.8 %collective-permute-done.12 = bf16[64,512]{1,0:T(8,128)(2,1)S(1)} collective-permute-done((bf16[64,512]{1,0:T(8,128)(2,1)S(1)}, bf16[64,512]{1,0:T(8,128)(2,1)S(1)}, u32[]{:S(2)}, u32[]{:S(2)}) %collective-permute-start.12) | collective-permute-done | bytes 65568 | tf_op jit(solution)/shard_map/ppermute | solution.py:169
  49.8 1.8 %collective-permute-done.13 = bf16[64,512]{1,0:T(8,128)(2,1)S(1)} collective-permute-done((bf16[64,512]{1,0:T(8,128)(2,1)S(1)}, bf16[64,512]{1,0:T(8,128)(2,1)S(1)}, u32[]{:S(2)}, u32[]{:S(2)}) %collective-permute-start.13) | collective-permute-done | bytes 65568 | tf_op jit(solution)/shard_map/ppermute | solution.py:169
  51.7 0.7 collective-permute-done.14
  52.4 1.3 %collective-permute-start.15 = (bf16[64,512]{1,0:T(8,128)(2,1)S(1)}, bf16[64,512]{1,0:T(8,128)(2,1)S(1)}, u32[]{:S(2)}, u32[]{:S(2)}) collective-permute-start(bf16[64,512]{1,0:T(8,128)(2,1)S(1)} %fusion.2), channel_id=1, source_target_pairs={{0,8},{4,12},{8,0},{12,4},{16,24},{20,28},{24,16},{28,20},{1,9},{5... | collective-permute-start | bytes 196616 | tf_op jit(solution)/shard_map/ppermute | solution.py:169
  53.7 1.2 %collective-permute-start.16 = (bf16[64,512]{1,0:T(8,128)(2,1)S(1)}, bf16[64,512]{1,0:T(8,128)(2,1)S(1)}, u32[]{:S(2)}, u32[]{:S(2)}) collective-permute-start(bf16[64,512]{1,0:T(8,128)(2,1)S(1)} %fusion.2), channel_id=1, source_target_pairs={{0,16},{4,20},{8,24},{12,28},{16,0},{20,4},{24,8},{28,12},{1,17},{... | collective-permute-start | bytes 196616 | tf_op jit(solution)/shard_map/ppermute | solution.py:169
  54.9 1.1 %collective-permute-start.17 = (bf16[64,512]{1,0:T(8,128)(2,1)S(1)}, bf16[64,512]{1,0:T(8,128)(2,1)S(1)}, u32[]{:S(2)}, u32[]{:S(2)}) collective-permute-start(bf16[64,512]{1,0:T(8,128)(2,1)S(1)} %fusion.2), channel_id=1, source_target_pairs={{0,24},{4,28},{8,16},{12,20},{16,8},{20,12},{24,0},{28,4},{1,25},{... | collective-permute-start | bytes 196616 | tf_op jit(solution)/shard_map/ppermute | solution.py:169
  56.0 1.2 %collective-permute-done.15 = bf16[64,512]{1,0:T(8,128)(2,1)S(1)} collective-permute-done((bf16[64,512]{1,0:T(8,128)(2,1)S(1)}, bf16[64,512]{1,0:T(8,128)(2,1)S(1)}, u32[]{:S(2)}, u32[]{:S(2)}) %collective-permute-start.15) | collective-permute-done | bytes 65568 | tf_op jit(solution)/shard_map/ppermute | solution.py:169
  57.2 0.8 %collective-permute-done.16 = bf16[64,512]{1,0:T(8,128)(2,1)S(1)} collective-permute-done((bf16[64,512]{1,0:T(8,128)(2,1)S(1)}, bf16[64,512]{1,0:T(8,128)(2,1)S(1)}, u32[]{:S(2)}, u32[]{:S(2)}) %collective-permute-start.16) | collective-permute-done | bytes 65568 | tf_op jit(solution)/shard_map/ppermute | solution.py:169
  58.0 2.1 %collective-permute-done.17 = bf16[64,512]{1,0:T(8,128)(2,1)S(1)} collective-permute-done((bf16[64,512]{1,0:T(8,128)(2,1)S(1)}, bf16[64,512]{1,0:T(8,128)(2,1)S(1)}, u32[]{:S(2)}, u32[]{:S(2)}) %collective-permute-start.17) | collective-permute-done | bytes 65568 | tf_op jit(solution)/shard_map/ppermute | solution.py:169
  60.1 0.0 copy-start.5
  60.1 0.1 collective-permute-start.18
  60.2 1.4 %image_own.3.image = f32[64,1024]{1,0:T(8,128)S(1)} custom-call(bf16[64,2048]{1,0:T(8,128)(2,1)S(1)} %pad_maximum_fusion.1.panel, bf16[4,1024,512]{2,1,0:T(8,128)(2,1)S(1)} %get-tuple-element.12.held), custom_call_target="tpu_custom_call" | custom-call | tf_op jit(solution)/shard_map/image_own/pallas_call | solution.py:125
  61.5 0.2 collective-permute-done.18.panel
  61.7 1.9 %image_other.3 = f32[8,1024]{1,0:T(8,128)S(1)} custom-call(f32[3]{0:T(128)S(1)} %copy-done.4, s32[1,1024]{1,0:T(1,128)S(1)} %bitcast.10, bf16[64,2048]{1,0:T(8,128)(2,1)S(1)} %collective-permute-done.18.panel, bf16[4,1024,512]{2,1,0:T(8,128)(2,1)S(1)} %get-tuple-element.9.held, f32[64,1024]{1,0:T(8,128)S(1)} %image_own.3.image), custom_call_target="tpu_custom_call" | custom-call | tf_op jit(solution)/shard_map/image_other/pallas_call | solution.py:154
  63.6 1.7 %collective-permute-start.19 = (f32[8,1024]{1,0:T(8,128)S(1)}, f32[8,1024]{1,0:T(8,128)S(1)}, u32[]{:S(2)}, u32[]{:S(2)}) collective-permute-start(f32[8,1024]{1,0:T(8,128)S(1)} %image_other.3), channel_id=1, source_target_pairs={{0,1},{1,0},{2,3},{3,2},{4,5},{5,4},{6,7},{7,6},{8,9},{9,8},{10,11... | collective-permute-start | bytes 98312 | tf_op jit(solution)/shard_map/ppermute | solution.py:200
  65.3 0.2 collective-permute-start.20
  65.5 2.5 %collective-permute-start.21 = (f32[8,1024]{1,0:T(8,128)S(1)}, f32[8,1024]{1,0:T(8,128)S(1)}, u32[]{:S(2)}, u32[]{:S(2)}) collective-permute-start(f32[8,1024]{1,0:T(8,128)S(1)} %image_other.3), channel_id=1, source_target_pairs={{0,3},{1,2},{2,1},{3,0},{4,7},{5,6},{6,5},{7,4},{8,11},{9,10},{10,... | collective-permute-start | bytes 98312 | tf_op jit(solution)/shard_map/ppermute | solution.py:200
  68.1 0.6 slice.38
  68.6 0.0 collective-permute-done.19
  68.6 2.2 %collective-permute-done.20 = f32[8,1024]{1,0:T(8,128)S(1)} collective-permute-done((f32[8,1024]{1,0:T(8,128)S(1)}, f32[8,1024]{1,0:T(8,128)S(1)}, u32[]{:S(2)}, u32[]{:S(2)}) %collective-permute-start.20) | collective-permute-done | bytes 32800 | tf_op jit(solution)/shard_map/ppermute | solution.py:200
  70.8 0.5 collective-permute-done.21
  71.3 1.2 %multiply_add_fusion = f32[8,1024]{1,0:T(8,128)} fusion(f32[8,1024]{1,0:T(8,128)S(1)} %copy-done.5, f32[8,1024]{1,0:T(8,128)S(1)} %collective-permute-done.20, f32[8,1024]{1,0:T(8,128)S(1)} %collective-permute-done.21, f32[8,1024]{1,0:T(8,128)S(1)} %image_other.3, f32[8,1024]{1,0:T(8,128)S(1)} %collective-permute-done.19, f32[]{:T(128)} %bitcast.4), kind=kLoop, calls=%fused_computation.12 | loop fusion | flops 40960 | bytes 196612 | tf_op jit(solution)/shard_map/add | solution.py:213
  (12 shorter events, 0.2 us)
Async XLA Ops:
  0.7 3.4 %copy-start = (bf16[1024,4096]{1,0:T(8,128)(2,1)S(1)}, bf16[1024,4096]{1,0:T(8,128)(2,1)}, u32[]{:S(2)}) copy-start(bf16[1024,4096]{1,0:T(8,128)(2,1)} %genotypes.3) | copy-start | bytes 25165828
  4.1 0.7 copy-start.1
  4.8 0.7 copy-start.3
  8.0 3.0 %collective-permute-start = (f32[64,2048]{1,0:T(8,128)S(1)}, f32[64,2048]{1,0:T(8,128)S(1)}, u32[]{:S(2)}, u32[]{:S(2)}) collective-permute-start(f32[64,2048]{1,0:T(8,128)S(1)} %get-tuple-element.11), channel_id=1, source_target_pairs={{0,4},{4,0},{8,12},{12,8},{16,20},{20,16},{24,28},{28,24},{1,5},{5... | collective-permute-start | bytes 1572872 | tf_op jit(solution)/shard_map/ppermute | solution.py:169
  11.0 20.2 %copy-start.4 = (f32[3]{0:T(128)S(1)}, f32[3]{0:T(128)}, u32[]{:S(2)}) copy-start(f32[3]{0:T(128)} %variances.3) | copy-start | bytes 40
  11.2 6.9 %collective-permute-start.1 = (f32[64,512]{1,0:T(8,128)S(1)}, f32[64,512]{1,0:T(8,128)S(1)}, u32[]{:S(2)}, u32[]{:S(2)}) collective-permute-start(f32[64,512]{1,0:T(8,128)S(1)} %get-tuple-element.20), channel_id=1, source_target_pairs={{0,8},{4,12},{8,0},{12,4},{16,24},{20,28},{24,16},{28,20},{1,9},{5... | collective-permute-start | bytes 393224 | tf_op jit(solution)/shard_map/ppermute | solution.py:169
  13.7 8.4 %collective-permute-start.2 = (f32[64,512]{1,0:T(8,128)S(1)}, f32[64,512]{1,0:T(8,128)S(1)}, u32[]{:S(2)}, u32[]{:S(2)}) collective-permute-start(f32[64,512]{1,0:T(8,128)S(1)} %get-tuple-element.22), channel_id=1, source_target_pairs={{0,16},{4,20},{8,24},{12,28},{16,0},{20,4},{24,8},{28,12},{1,17},{... | collective-permute-start | bytes 393224 | tf_op jit(solution)/shard_map/ppermute | solution.py:169
  15.2 6.9 %collective-permute-start.3 = (f32[64,512]{1,0:T(8,128)S(1)}, f32[64,512]{1,0:T(8,128)S(1)}, u32[]{:S(2)}, u32[]{:S(2)}) collective-permute-start(f32[64,512]{1,0:T(8,128)S(1)} %get-tuple-element.21), channel_id=1, source_target_pairs={{0,24},{4,28},{8,16},{12,20},{16,8},{20,12},{24,0},{28,4},{1,25},{... | collective-permute-start | bytes 393224 | tf_op jit(solution)/shard_map/ppermute | solution.py:169
  22.2 4.4 %collective-permute-start.4 = (bf16[72,512]{1,0:T(8,128)(2,1)S(1)}, bf16[72,512]{1,0:T(8,128)(2,1)S(1)}, u32[]{:S(2)}, u32[]{:S(2)}) collective-permute-start(bf16[72,512]{1,0:T(8,128)(2,1)S(1)} %pad_maximum_fusion.2), channel_id=1, source_target_pairs={{0,8},{4,12},{8,0},{12,4},{16,24},{20,28},{24,16},{28,20},{1,9},{5... | collective-permute-start | bytes 221192 | tf_op jit(solution)/shard_map/ppermute | solution.py:169
  23.5 4.8 %collective-permute-start.5 = (bf16[72,512]{1,0:T(8,128)(2,1)S(1)}, bf16[72,512]{1,0:T(8,128)(2,1)S(1)}, u32[]{:S(2)}, u32[]{:S(2)}) collective-permute-start(bf16[72,512]{1,0:T(8,128)(2,1)S(1)} %pad_maximum_fusion.2), channel_id=1, source_target_pairs={{0,16},{4,20},{8,24},{12,28},{16,0},{20,4},{24,8},{28,12},{1,17},{... | collective-permute-start | bytes 221192 | tf_op jit(solution)/shard_map/ppermute | solution.py:169
  24.3 5.3 %collective-permute-start.6 = (bf16[72,512]{1,0:T(8,128)(2,1)S(1)}, bf16[72,512]{1,0:T(8,128)(2,1)S(1)}, u32[]{:S(2)}, u32[]{:S(2)}) collective-permute-start(bf16[72,512]{1,0:T(8,128)(2,1)S(1)} %pad_maximum_fusion.2), channel_id=1, source_target_pairs={{0,24},{4,28},{8,16},{12,20},{16,8},{20,12},{24,0},{28,4},{1,25},{... | collective-permute-start | bytes 221192 | tf_op jit(solution)/shard_map/ppermute | solution.py:169
  29.6 1.6 %collective-permute-start.7 = (bf16[72,2048]{1,0:T(8,128)(2,1)S(1)}, bf16[72,2048]{1,0:T(8,128)(2,1)S(1)}, u32[]{:S(2)}, u32[]{:S(2)}) collective-permute-start(bf16[72,2048]{1,0:T(8,128)(2,1)S(1)} %pad_maximum_fusion.panel), channel_id=1, source_target_pairs={{0,4},{4,0},{8,12},{12,8},{16,20},{20,16},{24,28},{28,24},{1,5},{5... | collective-permute-start | bytes 884744 | tf_op jit(solution)/shard_map/ppermute | solution.py:169
  29.7 12.3 %copy-start.2 = (bf16[8,1024]{1,0:T(8,128)(2,1)S(1)}, bf16[8,1024]{1,0:T(8,128)(2,1)}, u32[]{:S(2)}) copy-start(bf16[8,1024]{1,0:T(8,128)(2,1)} %current.1) | copy-start | bytes 49156
  33.2 5.9 %collective-permute-start.10 = (f32[8,1024]{1,0:T(8,128)S(1)}, f32[8,1024]{1,0:T(8,128)S(1)}, u32[]{:S(2)}, u32[]{:S(2)}) collective-permute-start(f32[8,1024]{1,0:T(8,128)S(1)} %image_other.2.refs_0_), channel_id=1, source_target_pairs={{0,3},{1,2},{2,1},{3,0},{4,7},{5,6},{6,5},{7,4},{8,11},{9,10},{10,... | collective-permute-start | bytes 98312 | tf_op jit(solution)/shard_map/ppermute | solution.py:200
  36.9 4.2 %collective-permute-start.8 = (f32[8,1024]{1,0:T(8,128)S(1)}, f32[8,1024]{1,0:T(8,128)S(1)}, u32[]{:S(2)}, u32[]{:S(2)}) collective-permute-start(f32[8,1024]{1,0:T(8,128)S(1)} %image_other.2.refs_0_), channel_id=1, source_target_pairs={{0,1},{1,0},{2,3},{3,2},{4,5},{5,4},{6,7},{7,6},{8,9},{9,8},{10,11... | collective-permute-start | bytes 98312 | tf_op jit(solution)/shard_map/ppermute | solution.py:200
  36.9 5.2 %collective-permute-start.9 = (f32[8,1024]{1,0:T(8,128)S(1)}, f32[8,1024]{1,0:T(8,128)S(1)}, u32[]{:S(2)}, u32[]{:S(2)}) collective-permute-start(f32[8,1024]{1,0:T(8,128)S(1)} %image_other.2.refs_0_), channel_id=1, source_target_pairs={{0,2},{1,3},{2,0},{3,1},{4,6},{5,7},{6,4},{7,5},{8,10},{9,11},{10,... | collective-permute-start | bytes 98312 | tf_op jit(solution)/shard_map/ppermute | solution.py:200
  43.9 1.5 %collective-permute-start.11 = (bf16[64,2048]{1,0:T(8,128)(2,1)S(1)}, bf16[64,2048]{1,0:T(8,128)(2,1)S(1)}, u32[]{:S(2)}, u32[]{:S(2)}) collective-permute-start(bf16[64,2048]{1,0:T(8,128)(2,1)S(1)} %get-tuple-element.15), channel_id=1, source_target_pairs={{0,4},{4,0},{8,12},{12,8},{16,20},{20,16},{24,28},{28,24},{1,5},{5... | collective-permute-start | bytes 786440 | tf_op jit(solution)/shard_map/ppermute | solution.py:169
  45.5 4.3 %collective-permute-start.12 = (bf16[64,512]{1,0:T(8,128)(2,1)S(1)}, bf16[64,512]{1,0:T(8,128)(2,1)S(1)}, u32[]{:S(2)}, u32[]{:S(2)}) collective-permute-start(bf16[64,512]{1,0:T(8,128)(2,1)S(1)} %get-tuple-element.23), channel_id=1, source_target_pairs={{0,8},{4,12},{8,0},{12,4},{16,24},{20,28},{24,16},{28,20},{1,9},{5... | collective-permute-start | bytes 196616 | tf_op jit(solution)/shard_map/ppermute | solution.py:169
  46.7 5.0 %collective-permute-start.13 = (bf16[64,512]{1,0:T(8,128)(2,1)S(1)}, bf16[64,512]{1,0:T(8,128)(2,1)S(1)}, u32[]{:S(2)}, u32[]{:S(2)}) collective-permute-start(bf16[64,512]{1,0:T(8,128)(2,1)S(1)} %get-tuple-element.25), channel_id=1, source_target_pairs={{0,16},{4,20},{8,24},{12,28},{16,0},{20,4},{24,8},{28,12},{1,17},{... | collective-permute-start | bytes 196616 | tf_op jit(solution)/shard_map/ppermute | solution.py:169
  47.2 5.2 %collective-permute-start.14 = (bf16[64,512]{1,0:T(8,128)(2,1)S(1)}, bf16[64,512]{1,0:T(8,128)(2,1)S(1)}, u32[]{:S(2)}, u32[]{:S(2)}) collective-permute-start(bf16[64,512]{1,0:T(8,128)(2,1)S(1)} %get-tuple-element.24), channel_id=1, source_target_pairs={{0,24},{4,28},{8,16},{12,20},{16,8},{20,12},{24,0},{28,4},{1,25},{... | collective-permute-start | bytes 196616 | tf_op jit(solution)/shard_map/ppermute | solution.py:169
  52.4 4.7 %collective-permute-start.15 = (bf16[64,512]{1,0:T(8,128)(2,1)S(1)}, bf16[64,512]{1,0:T(8,128)(2,1)S(1)}, u32[]{:S(2)}, u32[]{:S(2)}) collective-permute-start(bf16[64,512]{1,0:T(8,128)(2,1)S(1)} %fusion.2), channel_id=1, source_target_pairs={{0,8},{4,12},{8,0},{12,4},{16,24},{20,28},{24,16},{28,20},{1,9},{5... | collective-permute-start | bytes 196616 | tf_op jit(solution)/shard_map/ppermute | solution.py:169
  53.7 4.3 %collective-permute-start.16 = (bf16[64,512]{1,0:T(8,128)(2,1)S(1)}, bf16[64,512]{1,0:T(8,128)(2,1)S(1)}, u32[]{:S(2)}, u32[]{:S(2)}) collective-permute-start(bf16[64,512]{1,0:T(8,128)(2,1)S(1)} %fusion.2), channel_id=1, source_target_pairs={{0,16},{4,20},{8,24},{12,28},{16,0},{20,4},{24,8},{28,12},{1,17},{... | collective-permute-start | bytes 196616 | tf_op jit(solution)/shard_map/ppermute | solution.py:169
  54.9 5.2 %collective-permute-start.17 = (bf16[64,512]{1,0:T(8,128)(2,1)S(1)}, bf16[64,512]{1,0:T(8,128)(2,1)S(1)}, u32[]{:S(2)}, u32[]{:S(2)}) collective-permute-start(bf16[64,512]{1,0:T(8,128)(2,1)S(1)} %fusion.2), channel_id=1, source_target_pairs={{0,24},{4,28},{8,16},{12,20},{16,8},{20,12},{24,0},{28,4},{1,25},{... | collective-permute-start | bytes 196616 | tf_op jit(solution)/shard_map/ppermute | solution.py:169
  60.1 11.3 %copy-start.5 = (f32[8,1024]{1,0:T(8,128)S(1)}, f32[8,1024]{1,0:T(8,128)}, u32[]{:S(2)}) copy-start(f32[8,1024]{1,0:T(8,128)} %get-tuple-element.7) | copy-start | bytes 98308
  60.1 1.6 %collective-permute-start.18 = (bf16[64,2048]{1,0:T(8,128)(2,1)S(1)}, bf16[64,2048]{1,0:T(8,128)(2,1)S(1)}, u32[]{:S(2)}, u32[]{:S(2)}) collective-permute-start(bf16[64,2048]{1,0:T(8,128)(2,1)S(1)} %pad_maximum_fusion.1.panel), channel_id=1, source_target_pairs={{0,4},{4,0},{8,12},{12,8},{16,20},{20,16},{24,28},{28,24},{1,5},{5... | collective-permute-start | bytes 786440 | tf_op jit(solution)/shard_map/ppermute | solution.py:169
  63.6 5.0 %collective-permute-start.19 = (f32[8,1024]{1,0:T(8,128)S(1)}, f32[8,1024]{1,0:T(8,128)S(1)}, u32[]{:S(2)}, u32[]{:S(2)}) collective-permute-start(f32[8,1024]{1,0:T(8,128)S(1)} %image_other.3), channel_id=1, source_target_pairs={{0,1},{1,0},{2,3},{3,2},{4,5},{5,4},{6,7},{7,6},{8,9},{9,8},{10,11... | collective-permute-start | bytes 98312 | tf_op jit(solution)/shard_map/ppermute | solution.py:200
  65.3 5.5 %collective-permute-start.20 = (f32[8,1024]{1,0:T(8,128)S(1)}, f32[8,1024]{1,0:T(8,128)S(1)}, u32[]{:S(2)}, u32[]{:S(2)}) collective-permute-start(f32[8,1024]{1,0:T(8,128)S(1)} %image_other.3), channel_id=1, source_target_pairs={{0,2},{1,3},{2,0},{3,1},{4,6},{5,7},{6,4},{7,5},{8,10},{9,11},{10,... | collective-permute-start | bytes 98312 | tf_op jit(solution)/shard_map/ppermute | solution.py:200
  65.5 5.8 %collective-permute-start.21 = (f32[8,1024]{1,0:T(8,128)S(1)}, f32[8,1024]{1,0:T(8,128)S(1)}, u32[]{:S(2)}, u32[]{:S(2)}) collective-permute-start(f32[8,1024]{1,0:T(8,128)S(1)} %image_other.3), channel_id=1, source_target_pairs={{0,3},{1,2},{2,1},{3,0},{4,7},{5,6},{6,5},{7,4},{8,11},{9,10},{10,... | collective-permute-start | bytes 98312 | tf_op jit(solution)/shard_map/ppermute | solution.py:200

commit v3 on v2

--- a/solution.py
+++ b/solution.py
@@ -19,52 +19,85 @@
     return jnp.concatenate(rows, axis=0).astype(jnp.bfloat16)
 
 
-def load_body(place, probes, labels, genotypes, held, partial, sems, *, other):
+def load_body(place, probes, labels, genotypes, *refs, first):
+    if first:
+        held, partial, panel, probes_in, labels_in, sems, small = refs
+    else:
+        held, partial, sems = refs
     chips, _, width = held.shape
-    core, chip = place[0], place[1]
-    half = (1 - core) if other else core
+    half = (1 - place[0]) if first else place[0]
 
     def copy(d):
-        start = pl.multiple_of((half * chips + (chip ^ d)) * width, width)
+        start = pl.multiple_of((half * chips + (place[1] ^ d)) * width, width)
         return pltpu.make_async_copy(genotypes.at[:, pl.ds(start, width)], held.at[d], sems.at[d])
 
+    if first:
+        inputs = (
+            pltpu.make_async_copy(probes, probes_in, small.at[0]),
+            pltpu.make_async_copy(labels, labels_in, small.at[1]),
+        )
+        for move in inputs:
+            move.start()
     ahead = min(2, chips)
     for d in range(ahead):
         copy(d).start()
-    panel = build_panel(probes[...].astype(jnp.float32), labels[...])
+    if first:
+        for move in inputs:
+            move.wait()
+        panel[...] = build_panel(probes_in[...].astype(jnp.float32), labels_in[...])
+    else:
+        panel = probes
     for d in range(chips):
         copy(d).wait()
         if d + ahead < chips:
             copy(d + ahead).start()
-        partial[:, pl.ds(d * width, width)] = jnp.dot(
-            panel, held[d], preferred_element_type=jnp.float32
-        ).astype(partial.dtype)
-
-
-def load_half(place, probes, labels, genotypes, chips, width, other, wire):
-    samples = probes.shape[1]
-    rows = ENVS * probes.shape[0]
-    return pl.pallas_call(
-        functools.partial(load_body, other=other),
+        partial[:, pl.ds(d * width, width)] = jnp.dot(panel[...], held[d], preferred_element_type=jnp.float32)
+
+
+def load_first(place, probes, labels, genotypes, chips, width):
+    count, samples = probes.shape
+    rows = ENVS * count
+    return pl.pallas_call(
+        functools.partial(load_body, first=True),
+        in_specs=[SMEM, HBM, HBM, HBM],
+        out_specs=(VMEM,) * 5,
+        out_shape=(
+            pltpu.VMEM((chips, samples, width), genotypes.dtype),
+            jax.ShapeDtypeStruct((rows, chips * width), jnp.float32),
+            jax.ShapeDtypeStruct((rows, samples), jnp.bfloat16),
+            pltpu.VMEM(probes.shape, probes.dtype),
+            pltpu.VMEM(labels.shape, labels.dtype),
+        ),
+        scratch_shapes=[pltpu.SemaphoreType.DMA((chips,)), pltpu.SemaphoreType.DMA((2,))],
+        compiler_params=pltpu.CompilerParams(vmem_limit_bytes=LIMIT),
+        name="load_other",
+    )(place, probes, labels, genotypes)
+
+
+def load_second(place, panel, labels, genotypes, chips, width):
+    rows, samples = panel.shape
+    return pl.pallas_call(
+        functools.partial(load_body, first=False),
         in_specs=[SMEM, VMEM, VMEM, HBM],
         out_specs=(VMEM, VMEM),
         out_shape=(
             pltpu.VMEM((chips, samples, width), genotypes.dtype),
-            jax.ShapeDtypeStruct((rows, chips * width), wire),
+            jax.ShapeDtypeStruct((rows, chips * width), jnp.float32),
         ),
         scratch_shapes=[pltpu.SemaphoreType.DMA((chips,))],
         compiler_params=pltpu.CompilerParams(vmem_limit_bytes=LIMIT),
-        name="load_other" if other else "load_own",
-    )(place, probes, labels, genotypes)
+        name="load_own",
+    )(place, panel, labels, genotypes)
 
 
 def step_body(noise, current, labels, held, *refs, count):
     parts = [refs[k][...] for k in range(count)]
-    first, panel_out, partial = refs[count:]
+    first, noise_term, panel_out, partial = refs[count:]
     while len(parts) > 1:
         parts = [parts[k] + parts[k + 1] for k in range(0, len(parts), 2)]
     value = parts[0] + noise[2] * current[...].astype(jnp.float32)
     first[...] = value
+    noise_term[...] = noise[2] * value
     panel = build_panel(value.astype(jnp.bfloat16).astype(jnp.float32), labels[...])
     panel_out[...] = panel
     width = held.shape[2]
@@ -80,9 +113,10 @@
     return pl.pallas_call(
         functools.partial(step_body, count=len(parts)),
         in_specs=[SMEM] + [VMEM] * (3 + len(parts)),
-        out_specs=(VMEM, VMEM, VMEM),
+        out_specs=(VMEM,) * 4,
         out_shape=(
-            jax.ShapeDtypeStruct(current.shape, jnp.float32),
+            pltpu.VMEM(current.shape, jnp.float32),
+            pltpu.VMEM(current.shape, jnp.float32),
             jax.ShapeDtypeStruct((rows, samples), jnp.bfloat16),
             jax.ShapeDtypeStruct((rows, chips * width), wire),
         ),
@@ -165,6 +199,8 @@
     samp, snp = mesh.shape["samp"], mesh.shape["snp"]
     chips = samp // 2
 
+    far = sorted(range(1, chips), key=lambda step: -bin(step).count("1"))
+
     def exchange(block, offset):
         return lax.ppermute(block, "samp", [(k, k ^ offset) for k in range(samp)])
 
@@ -172,23 +208,26 @@
         width = own.shape[1] // chips
         pair = own + exchange(given, 1).astype(jnp.float32)
         total = pair[:, :width]
-        for step in range(1, chips):
+        for step in far:
             block = pair[:, step * width : (step + 1) * width].astype(wire)
-            total = total + exchange(block, 2 * step).astype(jnp.float32)
+            total = total + exchange(block, 2 * step + step % 2).astype(jnp.float32)
         if exact:
             total = jnp.concatenate([total.reshape(ENVS, probes, width).sum(0), total], axis=0)
         return total.astype(jnp.bfloat16)
 
     def gather_panel(mine):
-        return jnp.concatenate([mine] + [exchange(mine, 2 * step) for step in range(1, chips)], axis=1)
+        pieces = {step: exchange(mine, 2 * step + step % 2) for step in far}
+        return jnp.concatenate([mine] + [pieces[step] for step in range(1, chips)], axis=1)
 
     def per_device(genotypes, probes, env_label, variances):
         snps = genotypes.shape[1] * snp
         count = probes.shape[0]
         width = genotypes.shape[1] // samp
         index = lax.axis_index("samp")
-        place = jnp.stack([index % 2, index // 2]).astype(jnp.int32)
+        core, chip = index & 1, index >> 1
+        place = jnp.stack([core ^ (chip & 1), chip]).astype(jnp.int32)
         labels = env_label[None, :]
+        genotypes, probes, labels = (pltpu.with_memory_space_constraint(a, pltpu.HBM) for a in (genotypes, probes, labels))
 
         def image_of(panel, exact):
             other = exchange(panel, 1)
@@ -196,21 +235,23 @@
             return finish_half(variances, labels, other, held_other, image, count, snps, exact)
 
         def spread(weighted):
-            return [weighted] + [
-                lax.ppermute(weighted, "snp", [(k, k ^ step) for k in range(snp)]) for step in range(1, snp)
-            ]
-
-        held_other, given = load_half(place, probes, labels, genotypes, chips, width, True, jnp.float32)
-        held_own, own = load_half(place, probes, labels, genotypes, chips, width, False, jnp.float32)
+            pieces = {
+                step: lax.ppermute(weighted, "snp", [(k, k ^ step) for k in range(snp)])
+                for step in range(snp - 1, 0, -1)
+            }
+            return [weighted] + [pieces[step] for step in range(1, snp)]
+
+        held_other, given, scaled, current, labels = load_first(place, probes, labels, genotypes, chips, width)
+        held_own, own = load_second(place, scaled, labels, genotypes, chips, width)
         panel = gather_panel(reduce_panel(given, own, jnp.float32, count, True))
         parts = spread(image_of(panel, True))
-        first, scaled, given = step_half(variances, probes, labels, held_other, parts, jnp.bfloat16)
+        first, noise, scaled, given = step_half(variances, current, labels, held_other, parts, jnp.bfloat16)
         own = panel_half(scaled, held_own)
         panel = gather_panel(reduce_panel(given, own, jnp.bfloat16, count, False))
         parts = spread(image_of(panel, False))
         while len(parts) > 1:
             parts = [parts[k] + parts[k + 1] for k in range(0, len(parts), 2)]
-        return (first, parts[0] + variances[2] * first)
+        return (first, parts[0] + noise)
 
     return per_device
 

time: 72.8 us -> 66.8 us (0.918)
  local copies, waits for them, and re-layouts: 5.42 us -> 0.66 us
  Pallas kernels: 14.2 us -> 16.2 us
  starting transfers between devices: 24.4 us -> 23 us
  waiting for transfers between devices: 26.2 us -> 24.9 us
    unnamed x12 -> x3, local copies, waits for them, and re-layouts: 4.8 us -> 0.62 us
    pallas_call x2, Pallas kernels: 4.94 us -> 7.47 us  [the longest x1 3.76 us: load_first(): pl.pallas_call(functools.partial(load_body, first=True), in_specs=[SMEM,...]
    ppermute x16, starting transfers between devices: 15.5 us -> 14.1 us  [exchange(): return lax.ppermute(block, 'samp', [(k, k ^ offset) for k in range(samp)])]
    ppermute x6, waiting for transfers between devices: 7.09 us -> 5.97 us  [spread(): lax.ppermute(weighted, 'snp', [(k, k ^ step) for k in range(snp)])]
  transfers between devices with their start and end apart: 22 -> 22, of which waited for: 19 -> 17; matrix products, arithmetic and copies ran while one was open for 1% -> 1% of each run, Pallas kernels for 8% -> 11%
where the time goes in v3:
time: 66.8 us; the launch traced here: 66.6 us
  waiting for transfers between devices  24.9 us (37%)
  starting transfers between devices  23 us (34%)
  Pallas kernels  16.2 us (24%)
  other arithmetic  0.95 us (1%)
  between operations  0.78 us (1%)
    ppermute x16, waiting for transfers between devices, exchange(): return lax.ppermute(block, 'samp', [(k, k ^ offset) for k in range(samp)])  19 us
    ppermute x16, starting transfers between devices, exchange(): return lax.ppermute(block, 'samp', [(k, k ^ offset) for k in range(samp)])  14.1 us
    ppermute x6, starting transfers between devices, spread(): lax.ppermute(weighted, 'snp', [(k, k ^ step) for k in range(snp)])  8.9 us
    ppermute x6, waiting for transfers between devices, spread(): lax.ppermute(weighted, 'snp', [(k, k ^ step) for k in range(snp)])  5.97 us
    pallas_call x2, Pallas kernels, finish_half(): pl.pallas_call(functools.partial(finish_body, snps=snps, exact=exact), in...  3.84 us
    pallas_call x1, Pallas kernels, load_first(): pl.pallas_call(functools.partial(load_body, first=True), in_specs=[SMEM,...  3.76 us
    pallas_call x1, Pallas kernels, load_second(): pl.pallas_call(functools.partial(load_body, first=False), in_specs=[SMEM,...  3.71 us
    pallas_call x2, Pallas kernels, image_half(): pl.pallas_call(image_body, in_specs=[VMEM, VMEM], out_specs=VMEM, out_sha...  2.73 us
  transfers between devices with their start and end apart: 22, of which 17 were waited for; matrix products, arithmetic and copies ran while one was open for 1% of the time, Pallas kernels for 11%

profile of v3, /device:TPU:0, one launch (start us, length us, event | category | flops | bytes accessed | tf_op | source)
XLA Modules:
  0.0 66.6 jit_solution(2681873266900520979)
XLA Ops:
  0.6 0.1 pad_add_fusion.place
  0.7 3.8 %load_other.1 = (bf16[4,1024,512]{2,1,0:T(8,128)(2,1)S(1)}, f32[64,2048]{1,0:T(8,128)S(1)}, bf16[64,1024]{1,0:T(8,128)(2,1)S(1)}, bf16[8,1024]{1,0:T(8,128)(2,1)S(1)}, s32[1,1024]{1,0:T(1,128)S(1)}) custom-call(s32[2]{0:T(128)S(1)} %pad_add_fusion.place, bf16[8,1024]{1,0:T(8,128)(2,1)} %probes.1, s32[1,1024]{1,0:T(1,128)} %bitcast.5, ...), custom_call_target="tpu_custom_call" | custom-call | tf_op jit(solution)/shard_map/load_other/pallas_call | solution.py:60
  4.5 0.6 collective-permute-start
  5.0 3.7 %load_own.1 = (bf16[4,1024,512]{2,1,0:T(8,128)(2,1)S(1)}, f32[64,2048]{1,0:T(8,128)S(1)}) custom-call(s32[2]{0:T(128)S(1)} %pad_add_fusion.place, bf16[64,1024]{1,0:T(8,128)(2,1)S(1)} %get-tuple-element.16.probes, s32[1,1024]{1,0:T(1,128)S(1)} %get-tuple-element.14.labels, bf16[1024,4096]{1,0:T(8,128)(2,1)} %genotypes.3), custom_call_target="tpu_custom_call" | custom-call | tf_op jit(solution)/shard_map/load_own/pallas_call | solution.py:79
  8.8 0.0 collective-permute-done
  8.8 0.0 copy-start
  8.8 0.1 add.36
  8.9 3.6 %collective-permute-start.1 = (f32[64,512]{1,0:T(8,128)S(1)}, f32[64,512]{1,0:T(8,128)S(1)}, u32[]{:S(2)}, u32[]{:S(2)}) collective-permute-start(f32[64,512]{1,0:T(8,128)S(1)} %get-tuple-element.28), channel_id=1, source_target_pairs={{0,28},{4,24},{8,20},{12,16},{16,12},{20,8},{24,4},{28,0},{1,29},{... | collective-permute-start | bytes 393224 | tf_op jit(solution)/shard_map/ppermute | solution.py:205
  12.5 0.5 collective-permute-start.3
  13.0 0.0 collective-permute-start.2
  13.0 3.4 %collective-permute-done.1 = f32[64,512]{1,0:T(8,128)S(1)} collective-permute-done((f32[64,512]{1,0:T(8,128)S(1)}, f32[64,512]{1,0:T(8,128)S(1)}, u32[]{:S(2)}, u32[]{:S(2)}) %collective-permute-start.1) | collective-permute-done | bytes 131104 | tf_op jit(solution)/shard_map/ppermute | solution.py:205
  16.5 2.9 %collective-permute-done.3 = f32[64,512]{1,0:T(8,128)S(1)} collective-permute-done((f32[64,512]{1,0:T(8,128)S(1)}, f32[64,512]{1,0:T(8,128)S(1)}, u32[]{:S(2)}, u32[]{:S(2)}) %collective-permute-start.3) | collective-permute-done | bytes 131104 | tf_op jit(solution)/shard_map/ppermute | solution.py:205
  19.4 0.0 collective-permute-done.2
  19.4 1.4 %collective-permute-start.6 = (bf16[72,512]{1,0:T(8,128)(2,1)S(1)}, bf16[72,512]{1,0:T(8,128)(2,1)S(1)}, u32[]{:S(2)}, u32[]{:S(2)}) collective-permute-start(bf16[72,512]{1,0:T(8,128)(2,1)S(1)} %pad_maximum_fusion.2), channel_id=1, source_target_pairs={{0,28},{4,24},{8,20},{12,16},{16,12},{20,8},{24,4},{28,0},{1,29},{... | collective-permute-start | bytes 221192 | tf_op jit(solution)/shard_map/ppermute | solution.py:205
  20.8 1.4 %collective-permute-start.5 = (bf16[72,512]{1,0:T(8,128)(2,1)S(1)}, bf16[72,512]{1,0:T(8,128)(2,1)S(1)}, u32[]{:S(2)}, u32[]{:S(2)}) collective-permute-start(bf16[72,512]{1,0:T(8,128)(2,1)S(1)} %pad_maximum_fusion.2), channel_id=1, source_target_pairs={{0,16},{4,20},{8,24},{12,28},{16,0},{20,4},{24,8},{28,12},{1,17},{... | collective-permute-start | bytes 221192 | tf_op jit(solution)/shard_map/ppermute | solution.py:205
  22.3 0.2 collective-permute-start.4
  22.4 2.3 %collective-permute-done.6 = bf16[72,512]{1,0:T(8,128)(2,1)S(1)} collective-permute-done((bf16[72,512]{1,0:T(8,128)(2,1)S(1)}, bf16[72,512]{1,0:T(8,128)(2,1)S(1)}, u32[]{:S(2)}, u32[]{:S(2)}) %collective-permute-start.6) | collective-permute-done | bytes 73760 | tf_op jit(solution)/shard_map/ppermute | solution.py:205
  24.7 1.8 %collective-permute-done.5 = bf16[72,512]{1,0:T(8,128)(2,1)S(1)} collective-permute-done((bf16[72,512]{1,0:T(8,128)(2,1)S(1)}, bf16[72,512]{1,0:T(8,128)(2,1)S(1)}, u32[]{:S(2)}, u32[]{:S(2)}) %collective-permute-start.5) | collective-permute-done | bytes 73760 | tf_op jit(solution)/shard_map/ppermute | solution.py:205
  26.5 0.0 collective-permute-done.4
  26.6 0.2 collective-permute-start.7
  26.7 1.4 %image_own.2.image = f32[72,1024]{1,0:T(8,128)S(1)} custom-call(bf16[72,2048]{1,0:T(8,128)(2,1)S(1)} %pad_maximum_fusion.panel, bf16[4,1024,512]{2,1,0:T(8,128)(2,1)S(1)} %get-tuple-element.19.held), custom_call_target="tpu_custom_call" | custom-call | tf_op jit(solution)/shard_map/image_own/pallas_call | solution.py:159
  28.1 0.1 collective-permute-done.7.panel
  28.2 0.0 copy-done
  28.2 1.9 %image_other.2.refs_0_ = f32[8,1024]{1,0:T(8,128)S(1)} custom-call(f32[3]{0:T(128)S(1)} %copy-done, s32[1,1024]{1,0:T(1,128)S(1)} %get-tuple-element.14.labels, bf16[72,2048]{1,0:T(8,128)(2,1)S(1)} %collective-permute-done.7.panel, bf16[4,1024,512]{2,1,0:T(8,128)(2,1)S(1)} %get-tuple-element.15.held, f32[72,1024]{1,0:T(8,128)S(1)} %image_own.2.image), custom_call_target="tpu_custom_call" | custom-call | tf_op jit(solution)/shard_map/image_other/pallas_call | solution.py:188
  30.1 3.8 %collective-permute-start.10 = (f32[8,1024]{1,0:T(8,128)S(1)}, f32[8,1024]{1,0:T(8,128)S(1)}, u32[]{:S(2)}, u32[]{:S(2)}) collective-permute-start(f32[8,1024]{1,0:T(8,128)S(1)} %image_other.2.refs_0_), channel_id=1, source_target_pairs={{0,3},{1,2},{2,1},{3,0},{4,7},{5,6},{6,5},{7,4},{8,11},{9,10},{10,... | collective-permute-start | bytes 98312 | tf_op jit(solution)/shard_map/ppermute | solution.py:239
  33.9 0.0 collective-permute-start.9
  33.9 0.7 %collective-permute-start.8 = (f32[8,1024]{1,0:T(8,128)S(1)}, f32[8,1024]{1,0:T(8,128)S(1)}, u32[]{:S(2)}, u32[]{:S(2)}) collective-permute-start(f32[8,1024]{1,0:T(8,128)S(1)} %image_other.2.refs_0_), channel_id=1, source_target_pairs={{0,1},{1,0},{2,3},{3,2},{4,5},{5,4},{6,7},{7,6},{8,9},{9,8},{10,11... | collective-permute-start | bytes 98312 | tf_op jit(solution)/shard_map/ppermute | solution.py:239
  34.6 1.3 %collective-permute-done.10.refs_3_ = f32[8,1024]{1,0:T(8,128)S(1)} collective-permute-done((f32[8,1024]{1,0:T(8,128)S(1)}, f32[8,1024]{1,0:T(8,128)S(1)}, u32[]{:S(2)}, u32[]{:S(2)}) %collective-permute-start.10) | collective-permute-done | bytes 32800 | tf_op jit(solution)/shard_map/ppermute | solution.py:239
  35.9 2.8 %collective-permute-done.9.refs_2_ = f32[8,1024]{1,0:T(8,128)S(1)} collective-permute-done((f32[8,1024]{1,0:T(8,128)S(1)}, f32[8,1024]{1,0:T(8,128)S(1)}, u32[]{:S(2)}, u32[]{:S(2)}) %collective-permute-start.9) | collective-permute-done | bytes 32800 | tf_op jit(solution)/shard_map/ppermute | solution.py:239
  38.7 0.0 collective-permute-done.8.refs_1_
  38.7 1.4 %step_other.1 = (f32[8,1024]{1,0:T(8,128)S(1)}, f32[8,1024]{1,0:T(8,128)S(1)}, bf16[64,1024]{1,0:T(8,128)(2,1)S(1)}, bf16[64,2048]{1,0:T(8,128)(2,1)S(1)}) custom-call(f32[3]{0:T(128)S(1)} %copy-done, bf16[8,1024]{1,0:T(8,128)(2,1)S(1)} %get-tuple-element.13.current, s32[1,1024]{1,0:T(1,128)S(1)} %get-tuple-element.14.labels, ...), custom_call_target="tpu_custom_call" | custom-call | tf_op jit(solution)/shard_map/step_other/pallas_call | solution.py:113
  40.1 0.1 collective-permute-start.11
  40.2 0.8 %step_own.1 = f32[64,2048]{1,0:T(8,128)S(1)} custom-call(bf16[64,1024]{1,0:T(8,128)(2,1)S(1)} %get-tuple-element.21.panel, bf16[4,1024,512]{2,1,0:T(8,128)(2,1)S(1)} %get-tuple-element.19.held), custom_call_target="tpu_custom_call" | custom-call | tf_op jit(solution)/shard_map/step_own/pallas_call | solution.py:136
  41.0 0.7 %collective-permute-done.11 = bf16[64,2048]{1,0:T(8,128)(2,1)S(1)} collective-permute-done((bf16[64,2048]{1,0:T(8,128)(2,1)S(1)}, bf16[64,2048]{1,0:T(8,128)(2,1)S(1)}, u32[]{:S(2)}, u32[]{:S(2)}) %collective-permute-start.11) | collective-permute-done | bytes 262176 | tf_op jit(solution)/shard_map/ppermute | solution.py:205
  41.7 0.1 fusion.5
  41.8 1.6 %collective-permute-start.12 = (bf16[64,512]{1,0:T(8,128)(2,1)S(1)}, bf16[64,512]{1,0:T(8,128)(2,1)S(1)}, u32[]{:S(2)}, u32[]{:S(2)}) collective-permute-start(bf16[64,512]{1,0:T(8,128)(2,1)S(1)} %get-tuple-element.31), channel_id=1, source_target_pairs={{0,28},{4,24},{8,20},{12,16},{16,12},{20,8},{24,4},{28,0},{1,29},{... | collective-permute-start | bytes 196616 | tf_op jit(solution)/shard_map/ppermute | solution.py:205
  43.4 1.2 %collective-permute-start.14 = (bf16[64,512]{1,0:T(8,128)(2,1)S(1)}, bf16[64,512]{1,0:T(8,128)(2,1)S(1)}, u32[]{:S(2)}, u32[]{:S(2)}) collective-permute-start(bf16[64,512]{1,0:T(8,128)(2,1)S(1)} %get-tuple-element.32), channel_id=1, source_target_pairs={{0,16},{4,20},{8,24},{12,28},{16,0},{20,4},{24,8},{28,12},{1,17},{... | collective-permute-start | bytes 196616 | tf_op jit(solution)/shard_map/ppermute | solution.py:205
  44.6 0.2 collective-permute-start.13
  44.8 2.1 %collective-permute-done.12 = bf16[64,512]{1,0:T(8,128)(2,1)S(1)} collective-permute-done((bf16[64,512]{1,0:T(8,128)(2,1)S(1)}, bf16[64,512]{1,0:T(8,128)(2,1)S(1)}, u32[]{:S(2)}, u32[]{:S(2)}) %collective-permute-start.12) | collective-permute-done | bytes 65568 | tf_op jit(solution)/shard_map/ppermute | solution.py:205
  46.9 1.7 %collective-permute-done.14 = bf16[64,512]{1,0:T(8,128)(2,1)S(1)} collective-permute-done((bf16[64,512]{1,0:T(8,128)(2,1)S(1)}, bf16[64,512]{1,0:T(8,128)(2,1)S(1)}, u32[]{:S(2)}, u32[]{:S(2)}) %collective-permute-start.14) | collective-permute-done | bytes 65568 | tf_op jit(solution)/shard_map/ppermute | solution.py:205
  48.6 0.1 collective-permute-done.13
  48.7 1.4 %collective-permute-start.17 = (bf16[64,512]{1,0:T(8,128)(2,1)S(1)}, bf16[64,512]{1,0:T(8,128)(2,1)S(1)}, u32[]{:S(2)}, u32[]{:S(2)}) collective-permute-start(bf16[64,512]{1,0:T(8,128)(2,1)S(1)} %fusion.2), channel_id=1, source_target_pairs={{0,28},{4,24},{8,20},{12,16},{16,12},{20,8},{24,4},{28,0},{1,29},{... | collective-permute-start | bytes 196616 | tf_op jit(solution)/shard_map/ppermute | solution.py:205
  50.1 1.2 %collective-permute-start.16 = (bf16[64,512]{1,0:T(8,128)(2,1)S(1)}, bf16[64,512]{1,0:T(8,128)(2,1)S(1)}, u32[]{:S(2)}, u32[]{:S(2)}) collective-permute-start(bf16[64,512]{1,0:T(8,128)(2,1)S(1)} %fusion.2), channel_id=1, source_target_pairs={{0,16},{4,20},{8,24},{12,28},{16,0},{20,4},{24,8},{28,12},{1,17},{... | collective-permute-start | bytes 196616 | tf_op jit(solution)/shard_map/ppermute | solution.py:205
  51.3 0.4 collective-permute-start.15
  51.7 2.1 %collective-permute-done.17 = bf16[64,512]{1,0:T(8,128)(2,1)S(1)} collective-permute-done((bf16[64,512]{1,0:T(8,128)(2,1)S(1)}, bf16[64,512]{1,0:T(8,128)(2,1)S(1)}, u32[]{:S(2)}, u32[]{:S(2)}) %collective-permute-start.17) | collective-permute-done | bytes 65568 | tf_op jit(solution)/shard_map/ppermute | solution.py:205
  53.9 1.6 %collective-permute-done.16 = bf16[64,512]{1,0:T(8,128)(2,1)S(1)} collective-permute-done((bf16[64,512]{1,0:T(8,128)(2,1)S(1)}, bf16[64,512]{1,0:T(8,128)(2,1)S(1)}, u32[]{:S(2)}, u32[]{:S(2)}) %collective-permute-start.16) | collective-permute-done | bytes 65568 | tf_op jit(solution)/shard_map/ppermute | solution.py:205
  55.5 0.0 collective-permute-done.15
  55.5 0.2 collective-permute-start.18
  55.7 1.4 %image_own.3.image = f32[64,1024]{1,0:T(8,128)S(1)} custom-call(bf16[64,2048]{1,0:T(8,128)(2,1)S(1)} %pad_maximum_fusion.1.panel, bf16[4,1024,512]{2,1,0:T(8,128)(2,1)S(1)} %get-tuple-element.19.held), custom_call_target="tpu_custom_call" | custom-call | tf_op jit(solution)/shard_map/image_own/pallas_call | solution.py:159
  57.1 0.1 collective-permute-done.18.panel
  57.1 1.9 %image_other.3 = f32[8,1024]{1,0:T(8,128)S(1)} custom-call(f32[3]{0:T(128)S(1)} %copy-done, s32[1,1024]{1,0:T(1,128)S(1)} %get-tuple-element.14.labels, bf16[64,2048]{1,0:T(8,128)(2,1)S(1)} %collective-permute-done.18.panel, bf16[4,1024,512]{2,1,0:T(8,128)(2,1)S(1)} %get-tuple-element.15.held, f32[64,1024]{1,0:T(8,128)S(1)} %image_own.3.image), custom_call_target="tpu_custom_call" | custom-call | tf_op jit(solution)/shard_map/image_other/pallas_call | solution.py:188
  59.0 1.7 %collective-permute-start.21 = (f32[8,1024]{1,0:T(8,128)S(1)}, f32[8,1024]{1,0:T(8,128)S(1)}, u32[]{:S(2)}, u32[]{:S(2)}) collective-permute-start(f32[8,1024]{1,0:T(8,128)S(1)} %image_other.3), channel_id=1, source_target_pairs={{0,3},{1,2},{2,1},{3,0},{4,7},{5,6},{6,5},{7,4},{8,11},{9,10},{10,... | collective-permute-start | bytes 98312 | tf_op jit(solution)/shard_map/ppermute | solution.py:239
  60.7 0.5 collective-permute-start.20
  61.2 2.3 %collective-permute-start.19 = (f32[8,1024]{1,0:T(8,128)S(1)}, f32[8,1024]{1,0:T(8,128)S(1)}, u32[]{:S(2)}, u32[]{:S(2)}) collective-permute-start(f32[8,1024]{1,0:T(8,128)S(1)} %image_other.3), channel_id=1, source_target_pairs={{0,1},{1,0},{2,3},{3,2},{4,5},{5,4},{6,7},{7,6},{8,9},{9,8},{10,11... | collective-permute-start | bytes 98312 | tf_op jit(solution)/shard_map/ppermute | solution.py:239
  63.5 0.6 copy.6
  64.1 0.9 %collective-permute-done.21 = f32[8,1024]{1,0:T(8,128)S(1)} collective-permute-done((f32[8,1024]{1,0:T(8,128)S(1)}, f32[8,1024]{1,0:T(8,128)S(1)}, u32[]{:S(2)}, u32[]{:S(2)}) %collective-permute-start.21) | collective-permute-done | bytes 32800 | tf_op jit(solution)/shard_map/ppermute | solution.py:239
  65.0 0.8 %collective-permute-done.20 = f32[8,1024]{1,0:T(8,128)S(1)} collective-permute-done((f32[8,1024]{1,0:T(8,128)S(1)}, f32[8,1024]{1,0:T(8,128)S(1)}, u32[]{:S(2)}, u32[]{:S(2)}) %collective-permute-start.20) | collective-permute-done | bytes 32800 | tf_op jit(solution)/shard_map/ppermute | solution.py:239
  65.8 0.2 collective-permute-done.19
  65.9 0.6 add_add_fusion
  (7 shorter events, 0.2 us)
Async XLA Ops:
  4.5 4.3 %collective-permute-start = (f32[64,2048]{1,0:T(8,128)S(1)}, f32[64,2048]{1,0:T(8,128)S(1)}, u32[]{:S(2)}, u32[]{:S(2)}) collective-permute-start(f32[64,2048]{1,0:T(8,128)S(1)} %get-tuple-element.18), channel_id=1, source_target_pairs={{0,4},{4,0},{8,12},{12,8},{16,20},{20,16},{24,28},{28,24},{1,5},{5... | collective-permute-start | bytes 1572872 | tf_op jit(solution)/shard_map/ppermute | solution.py:205
  8.8 19.5 %copy-start = (f32[3]{0:T(128)S(1)}, f32[3]{0:T(128)}, u32[]{:S(2)}) copy-start(f32[3]{0:T(128)} %variances.3) | copy-start | bytes 40
  8.9 7.6 %collective-permute-start.1 = (f32[64,512]{1,0:T(8,128)S(1)}, f32[64,512]{1,0:T(8,128)S(1)}, u32[]{:S(2)}, u32[]{:S(2)}) collective-permute-start(f32[64,512]{1,0:T(8,128)S(1)} %get-tuple-element.28), channel_id=1, source_target_pairs={{0,28},{4,24},{8,20},{12,16},{16,12},{20,8},{24,4},{28,0},{1,29},{... | collective-permute-start | bytes 393224 | tf_op jit(solution)/shard_map/ppermute | solution.py:205
  12.5 6.9 %collective-permute-start.3 = (f32[64,512]{1,0:T(8,128)S(1)}, f32[64,512]{1,0:T(8,128)S(1)}, u32[]{:S(2)}, u32[]{:S(2)}) collective-permute-start(f32[64,512]{1,0:T(8,128)S(1)} %get-tuple-element.29), channel_id=1, source_target_pairs={{0,16},{4,20},{8,24},{12,28},{16,0},{20,4},{24,8},{28,12},{1,17},{... | collective-permute-start | bytes 393224 | tf_op jit(solution)/shard_map/ppermute | solution.py:205
  13.0 6.4 %collective-permute-start.2 = (f32[64,512]{1,0:T(8,128)S(1)}, f32[64,512]{1,0:T(8,128)S(1)}, u32[]{:S(2)}, u32[]{:S(2)}) collective-permute-start(f32[64,512]{1,0:T(8,128)S(1)} %get-tuple-element.30), channel_id=1, source_target_pairs={{0,12},{4,8},{8,4},{12,0},{16,28},{20,24},{24,20},{28,16},{1,13},{... | collective-permute-start | bytes 393224 | tf_op jit(solution)/shard_map/ppermute | solution.py:205
  19.4 5.3 %collective-permute-start.6 = (bf16[72,512]{1,0:T(8,128)(2,1)S(1)}, bf16[72,512]{1,0:T(8,128)(2,1)S(1)}, u32[]{:S(2)}, u32[]{:S(2)}) collective-permute-start(bf16[72,512]{1,0:T(8,128)(2,1)S(1)} %pad_maximum_fusion.2), channel_id=1, source_target_pairs={{0,28},{4,24},{8,20},{12,16},{16,12},{20,8},{24,4},{28,0},{1,29},{... | collective-permute-start | bytes 221192 | tf_op jit(solution)/shard_map/ppermute | solution.py:205
  20.8 5.7 %collective-permute-start.5 = (bf16[72,512]{1,0:T(8,128)(2,1)S(1)}, bf16[72,512]{1,0:T(8,128)(2,1)S(1)}, u32[]{:S(2)}, u32[]{:S(2)}) collective-permute-start(bf16[72,512]{1,0:T(8,128)(2,1)S(1)} %pad_maximum_fusion.2), channel_id=1, source_target_pairs={{0,16},{4,20},{8,24},{12,28},{16,0},{20,4},{24,8},{28,12},{1,17},{... | collective-permute-start | bytes 221192 | tf_op jit(solution)/shard_map/ppermute | solution.py:205
  22.3 4.3 %collective-permute-start.4 = (bf16[72,512]{1,0:T(8,128)(2,1)S(1)}, bf16[72,512]{1,0:T(8,128)(2,1)S(1)}, u32[]{:S(2)}, u32[]{:S(2)}) collective-permute-start(bf16[72,512]{1,0:T(8,128)(2,1)S(1)} %pad_maximum_fusion.2), channel_id=1, source_target_pairs={{0,12},{4,8},{8,4},{12,0},{16,28},{20,24},{24,20},{28,16},{1,13},{... | collective-permute-start | bytes 221192 | tf_op jit(solution)/shard_map/ppermute | solution.py:205
  26.6 1.6 %collective-permute-start.7 = (bf16[72,2048]{1,0:T(8,128)(2,1)S(1)}, bf16[72,2048]{1,0:T(8,128)(2,1)S(1)}, u32[]{:S(2)}, u32[]{:S(2)}) collective-permute-start(bf16[72,2048]{1,0:T(8,128)(2,1)S(1)} %pad_maximum_fusion.panel), channel_id=1, source_target_pairs={{0,4},{4,0},{8,12},{12,8},{16,20},{20,16},{24,28},{28,24},{1,5},{5... | collective-permute-start | bytes 884744 | tf_op jit(solution)/shard_map/ppermute | solution.py:205
  30.1 5.8 %collective-permute-start.10 = (f32[8,1024]{1,0:T(8,128)S(1)}, f32[8,1024]{1,0:T(8,128)S(1)}, u32[]{:S(2)}, u32[]{:S(2)}) collective-permute-start(f32[8,1024]{1,0:T(8,128)S(1)} %image_other.2.refs_0_), channel_id=1, source_target_pairs={{0,3},{1,2},{2,1},{3,0},{4,7},{5,6},{6,5},{7,4},{8,11},{9,10},{10,... | collective-permute-start | bytes 98312 | tf_op jit(solution)/shard_map/ppermute | solution.py:239
  33.9 4.8 %collective-permute-start.9 = (f32[8,1024]{1,0:T(8,128)S(1)}, f32[8,1024]{1,0:T(8,128)S(1)}, u32[]{:S(2)}, u32[]{:S(2)}) collective-permute-start(f32[8,1024]{1,0:T(8,128)S(1)} %image_other.2.refs_0_), channel_id=1, source_target_pairs={{0,2},{1,3},{2,0},{3,1},{4,6},{5,7},{6,4},{7,5},{8,10},{9,11},{10,... | collective-permute-start | bytes 98312 | tf_op jit(solution)/shard_map/ppermute | solution.py:239
  33.9 4.8 %collective-permute-start.8 = (f32[8,1024]{1,0:T(8,128)S(1)}, f32[8,1024]{1,0:T(8,128)S(1)}, u32[]{:S(2)}, u32[]{:S(2)}) collective-permute-start(f32[8,1024]{1,0:T(8,128)S(1)} %image_other.2.refs_0_), channel_id=1, source_target_pairs={{0,1},{1,0},{2,3},{3,2},{4,5},{5,4},{6,7},{7,6},{8,9},{9,8},{10,11... | collective-permute-start | bytes 98312 | tf_op jit(solution)/shard_map/ppermute | solution.py:239
  40.1 1.6 %collective-permute-start.11 = (bf16[64,2048]{1,0:T(8,128)(2,1)S(1)}, bf16[64,2048]{1,0:T(8,128)(2,1)S(1)}, u32[]{:S(2)}, u32[]{:S(2)}) collective-permute-start(bf16[64,2048]{1,0:T(8,128)(2,1)S(1)} %get-tuple-element.22), channel_id=1, source_target_pairs={{0,4},{4,0},{8,12},{12,8},{16,20},{20,16},{24,28},{28,24},{1,5},{5... | collective-permute-start | bytes 786440 | tf_op jit(solution)/shard_map/ppermute | solution.py:205
  41.8 5.1 %collective-permute-start.12 = (bf16[64,512]{1,0:T(8,128)(2,1)S(1)}, bf16[64,512]{1,0:T(8,128)(2,1)S(1)}, u32[]{:S(2)}, u32[]{:S(2)}) collective-permute-start(bf16[64,512]{1,0:T(8,128)(2,1)S(1)} %get-tuple-element.31), channel_id=1, source_target_pairs={{0,28},{4,24},{8,20},{12,16},{16,12},{20,8},{24,4},{28,0},{1,29},{... | collective-permute-start | bytes 196616 | tf_op jit(solution)/shard_map/ppermute | solution.py:205
  43.4 5.2 %collective-permute-start.14 = (bf16[64,512]{1,0:T(8,128)(2,1)S(1)}, bf16[64,512]{1,0:T(8,128)(2,1)S(1)}, u32[]{:S(2)}, u32[]{:S(2)}) collective-permute-start(bf16[64,512]{1,0:T(8,128)(2,1)S(1)} %get-tuple-element.32), channel_id=1, source_target_pairs={{0,16},{4,20},{8,24},{12,28},{16,0},{20,4},{24,8},{28,12},{1,17},{... | collective-permute-start | bytes 196616 | tf_op jit(solution)/shard_map/ppermute | solution.py:205
  44.6 4.1 %collective-permute-start.13 = (bf16[64,512]{1,0:T(8,128)(2,1)S(1)}, bf16[64,512]{1,0:T(8,128)(2,1)S(1)}, u32[]{:S(2)}, u32[]{:S(2)}) collective-permute-start(bf16[64,512]{1,0:T(8,128)(2,1)S(1)} %get-tuple-element.33), channel_id=1, source_target_pairs={{0,12},{4,8},{8,4},{12,0},{16,28},{20,24},{24,20},{28,16},{1,13},{... | collective-permute-start | bytes 196616 | tf_op jit(solution)/shard_map/ppermute | solution.py:205
  48.7 5.1 %collective-permute-start.17 = (bf16[64,512]{1,0:T(8,128)(2,1)S(1)}, bf16[64,512]{1,0:T(8,128)(2,1)S(1)}, u32[]{:S(2)}, u32[]{:S(2)}) collective-permute-start(bf16[64,512]{1,0:T(8,128)(2,1)S(1)} %fusion.2), channel_id=1, source_target_pairs={{0,28},{4,24},{8,20},{12,16},{16,12},{20,8},{24,4},{28,0},{1,29},{... | collective-permute-start | bytes 196616 | tf_op jit(solution)/shard_map/ppermute | solution.py:205
  50.1 5.4 %collective-permute-start.16 = (bf16[64,512]{1,0:T(8,128)(2,1)S(1)}, bf16[64,512]{1,0:T(8,128)(2,1)S(1)}, u32[]{:S(2)}, u32[]{:S(2)}) collective-permute-start(bf16[64,512]{1,0:T(8,128)(2,1)S(1)} %fusion.2), channel_id=1, source_target_pairs={{0,16},{4,20},{8,24},{12,28},{16,0},{20,4},{24,8},{28,12},{1,17},{... | collective-permute-start | bytes 196616 | tf_op jit(solution)/shard_map/ppermute | solution.py:205
  51.3 4.2 %collective-permute-start.15 = (bf16[64,512]{1,0:T(8,128)(2,1)S(1)}, bf16[64,512]{1,0:T(8,128)(2,1)S(1)}, u32[]{:S(2)}, u32[]{:S(2)}) collective-permute-start(bf16[64,512]{1,0:T(8,128)(2,1)S(1)} %fusion.2), channel_id=1, source_target_pairs={{0,12},{4,8},{8,4},{12,0},{16,28},{20,24},{24,20},{28,16},{1,13},{... | collective-permute-start | bytes 196616 | tf_op jit(solution)/shard_map/ppermute | solution.py:205
  55.5 1.6 %collective-permute-start.18 = (bf16[64,2048]{1,0:T(8,128)(2,1)S(1)}, bf16[64,2048]{1,0:T(8,128)(2,1)S(1)}, u32[]{:S(2)}, u32[]{:S(2)}) collective-permute-start(bf16[64,2048]{1,0:T(8,128)(2,1)S(1)} %pad_maximum_fusion.1.panel), channel_id=1, source_target_pairs={{0,4},{4,0},{8,12},{12,8},{16,20},{20,16},{24,28},{28,24},{1,5},{5... | collective-permute-start | bytes 786440 | tf_op jit(solution)/shard_map/ppermute | solution.py:205
  59.0 6.0 %collective-permute-start.21 = (f32[8,1024]{1,0:T(8,128)S(1)}, f32[8,1024]{1,0:T(8,128)S(1)}, u32[]{:S(2)}, u32[]{:S(2)}) collective-permute-start(f32[8,1024]{1,0:T(8,128)S(1)} %image_other.3), channel_id=1, source_target_pairs={{0,3},{1,2},{2,1},{3,0},{4,7},{5,6},{6,5},{7,4},{8,11},{9,10},{10,... | collective-permute-start | bytes 98312 | tf_op jit(solution)/shard_map/ppermute | solution.py:239
  60.7 5.1 %collective-permute-start.20 = (f32[8,1024]{1,0:T(8,128)S(1)}, f32[8,1024]{1,0:T(8,128)S(1)}, u32[]{:S(2)}, u32[]{:S(2)}) collective-permute-start(f32[8,1024]{1,0:T(8,128)S(1)} %image_other.3), channel_id=1, source_target_pairs={{0,2},{1,3},{2,0},{3,1},{4,6},{5,7},{6,4},{7,5},{8,10},{9,11},{10,... | collective-permute-start | bytes 98312 | tf_op jit(solution)/shard_map/ppermute | solution.py:239
  61.2 4.8 %collective-permute-start.19 = (f32[8,1024]{1,0:T(8,128)S(1)}, f32[8,1024]{1,0:T(8,128)S(1)}, u32[]{:S(2)}, u32[]{:S(2)}) collective-permute-start(f32[8,1024]{1,0:T(8,128)S(1)} %image_other.3), channel_id=1, source_target_pairs={{0,1},{1,0},{2,3},{3,2},{4,5},{5,4},{6,7},{7,6},{8,9},{9,8},{10,11... | collective-permute-start | bytes 98312 | tf_op jit(solution)/shard_map/ppermute | solution.py:239

commit v4 on v0

v4 whole, which is shorter than its diff:
```python
import functools

import jax
import jax.numpy as jnp
from jax import lax
from jax.experimental import pallas as pl
from jax.experimental.pallas import tpu as pltpu
from jax.sharding import PartitionSpec as P


ENVS = 8
VMEM = pl.BlockSpec(memory_space=pltpu.VMEM)
HBM = pl.BlockSpec(memory_space=pltpu.HBM)
PARAMS = pltpu.CompilerParams(vmem_limit_bytes=24 * 1024 * 1024)
f32 = jnp.float32


def build_panel(rounded, tags):
    rows = [jnp.where(tags == e, rounded, 0.0) for e in range(ENVS)]
    return jnp.concatenate(rows, axis=0).astype(jnp.bfloat16)


def dot_t(a, b):
    return lax.dot_general(a, b, (((1,), (1,)), ((), ())), preferred_element_type=f32)


def copies(genotypes, held, sems, other):
    chips, _, width = held.shape
    index = lax.axis_index("samp")
    core, chip = index & 1, index >> 1
    half = core ^ (chip & 1)
    if other:
        half = 1 - half

    def copy(d):
        start = pl.multiple_of((half * chips + (chip ^ d)) * width, width)
        return pltpu.make_async_copy(genotypes.at[:, pl.ds(start, width)], held.at[d], sems.at[d])

    return [copy(d) for d in range(chips)]


def products(panel, held, partial):
    width = held.shape[2]
    for d in range(held.shape[0]):
        partial[:, pl.ds(d * width, width)] = jnp.dot(panel, held[d], preferred_element_type=f32).astype(partial.dtype)


def first_body(probes, labels, variances, genotypes, held, partial, panel, current, tags, scales, labels_in, numbers, sems, small, *, snps):
    moves = copies(genotypes, held, sems, True)
    inputs = (
        pltpu.make_async_copy(probes, current, small.at[0]),
        pltpu.make_async_copy(labels, labels_in, small.at[1]),
        pltpu.make_async_copy(variances, numbers, small.at[2]),
    )
    for move in inputs:
        move.start()
    for move in moves:
        move.start()
    for move in inputs:
        move.wait()
    tag = jnp.broadcast_to(labels_in[...], tags.shape)
    tags[...] = tag
    built = build_panel(current[...].astype(f32), tag)
    panel[...] = built
    shape = scales.shape[1:]
    scales[0] = jnp.full(shape, numbers[0] * (1.0 / snps), f32)
    scales[1] = jnp.full(shape, numbers[1] * (1.0 / snps), f32)
    scales[2] = jnp.full(shape, numbers[2], f32)
    width = held.shape[2]
    for d, move in enumerate(moves):
        move.wait()
        partial[:, pl.ds(d * width, width)] = jnp.dot(built, held[d], preferred_element_type=f32)


def load_first(probes, labels, variances, genotypes, chips, width, snps):
    count, samples = probes.shape
    rows = ENVS * count
    return pl.pallas_call(
        functools.partial(first_body, snps=snps),
        in_specs=[HBM] * 4,
        out_specs=(VMEM,) * 6,
        out_shape=(
            pltpu.VMEM((chips, samples, width), genotypes.dtype),
            pltpu.VMEM((rows, chips * width), f32),
            pltpu.VMEM((rows, samples), jnp.bfloat16),
            pltpu.VMEM(probes.shape, probes.dtype),
            pltpu.VMEM(probes.shape, jnp.int32),
            pltpu.VMEM((3,) + probes.shape, f32),
        ),
        scratch_shapes=[
            pltpu.VMEM(labels.shape, labels.dtype),
            pltpu.SMEM(variances.shape, variances.dtype),
            pltpu.SemaphoreType.DMA((chips,)),
            pltpu.SemaphoreType.DMA((3,)),
        ],
        compiler_params=PARAMS,
        name="load_other",
    )(probes, labels, variances, genotypes)


def second_body(panel, genotypes, held, partial, sems):
    moves = copies(genotypes, held, sems, False)
    for move in moves:
        move.start()
    width = held.shape[2]
    for d, move in enumerate(moves):
        move.wait()
        partial[:, pl.ds(d * width, width)] = jnp.dot(panel[...], held[d], preferred_element_type=f32)


def load_second(panel, genotypes, chips, width):
    rows, samples = panel.shape
    return pl.pallas_call(
        second_body,
        in_specs=[VMEM, HBM],
        out_specs=(VMEM, VMEM),
        out_shape=(
            pltpu.VMEM((chips, samples, width), genotypes.dtype),
            pltpu.VMEM((rows, chips * width), f32),
        ),
        scratch_shapes=[pltpu.SemaphoreType.DMA((chips,))],
        compiler_params=PARAMS,
        name="load_own",
    )(panel, genotypes)


def tree_sum(parts):
    while len(parts) > 1:
        parts = [parts[k] + parts[k + 1] for k in range(0, len(parts), 2)]
    return parts[0]


def step_body(current, tags, scales, held, *refs, count):
    first, noise, panel, partial = refs[count:]
    value = tree_sum([refs[k][...] for k in range(count)]) + scales[2] * current[...].astype(f32)
    first[...] = value
    noise[...] = scales[2] * value
    built = build_panel(value.astype(jnp.bfloat16).astype(f32), tags[...])
    panel[...] = built
    products(built, held, partial)


def step_half(current, tags, scales, held, parts, wire):
    rows = ENVS * current.shape[0]
    chips, samples, width = held.shape
    return pl.pallas_call(
        functools.partial(step_body, count=len(parts)),
        in_specs=[VMEM] * (4 + len(parts)),
        out_specs=(VMEM,) * 4,
        out_shape=(
            pltpu.VMEM(current.shape, f32),
            pltpu.VMEM(current.shape, f32),
            pltpu.VMEM((rows, samples), jnp.bfloat16),
            pltpu.VMEM((rows, chips * width), wire),
        ),
        compiler_params=PARAMS,
        name="step_other",
    )(current, tags, scales, held, *parts)


def panel_body(panel, held, partial):
    products(panel[...], held, partial)


def panel_half(panel, held):
    chips, _, width = held.shape
    return pl.pallas_call(
        panel_body,
        in_specs=[VMEM, VMEM],
        out_specs=VMEM,
        out_shape=pltpu.VMEM((panel.shape[0], chips * width), f32),
        compiler_params=PARAMS,
        name="step_own",
    )(panel, held)


def image_body(*refs, blocks, pieces, more, probes):
    panels, refs = refs[:pieces], refs[pieces:]
    held, refs = refs[0], refs[1:]
    width = held.shape[2]
    total = None
    if more:
        total, refs = refs[0][...], refs[1:]
    for k, d in enumerate(blocks):
        per = panels[0].shape[1] // width
        part = panels[k // per][:, pl.ds((k % per) * width, width)]
        term = dot_t(part, held[d])
        total = term if total is None else total + term
    if probes is None:
        refs[0][...] = total
        return
    tags, scales, weighted = refs
    exact = total.shape[0] > ENVS * probes
    tag, additive, interaction = tags[...], scales[0], scales[1]
    skip = probes if exact else 0
    low = jnp.zeros_like(additive) if exact else additive
    high = interaction if exact else additive + interaction
    result = additive * total[:probes] if exact else None
    for e in range(ENVS):
        term = jnp.where(tag == e, high, low) * total[skip + e * probes : skip + (e + 1) * probes]
        result = term if result is None else result + term
    weighted[...] = result


def image(panels, held, blocks, before=None, finish=None):
    rows, samples = panels[0].shape[0], held.shape[1]
    operands = list(panels) + [held] + ([before] if before is not None else [])
    probes = None
    out = pltpu.VMEM((rows, samples), f32)
    if finish is not None:
        operands += list(finish)
        probes = finish[0].shape[0]
        out = pltpu.VMEM(finish[0].shape, f32)
    return pl.pallas_call(
        functools.partial(image_body, blocks=tuple(blocks), pieces=len(panels), more=before is not None, probes=probes),
        in_specs=[VMEM] * len(operands),
        out_specs=VMEM,
        out_shape=out,
        compiler_params=PARAMS,
        name="image",
    )(*operands)


def make(mesh):
    samp, snp = mesh.shape["samp"], mesh.shape["snp"]
    chips = samp // 2
    far = sorted(range(1, chips), key=lambda step: -bin(step).count("1"))
    early = [0] + far[: chips // 2 - 1]
    late = far[chips // 2 - 1 :]

    def exchange(block, offset):
        return lax.ppermute(block, "samp", [(k, k ^ offset) for k in range(samp)])

    def between(block, step):
        return exchange(block, 2 * step + step % 2)

    def reduce_panel(given, own, wire, probes, exact):
        width = own.shape[1] // chips
        pair = own + exchange(given, 1).astype(f32)
        total = pair[:, :width]
        for step in far:
            total = total + between(pair[:, step * width : (step + 1) * width].astype(wire), step).astype(f32)
        if exact:
            total = jnp.concatenate([total.reshape(ENVS, probes, width).sum(0), total], axis=0)
        return total.astype(jnp.bfloat16)

    def spread_image(mine, held_own, held_other, finish):
        pieces = {0: mine}
        for step in far:
            pieces[step] = between(mine, step)
        early_pieces = [pieces[d] for d in early]
        late_pieces = [pieces[d] for d in late]
        early_other = exchange(jnp.concatenate(early_pieces, axis=1), 1)
        late_other = exchange(jnp.concatenate(late_pieces, axis=1), 1)
        total = image([mine], held_own, [0])
        total = image(early_pieces[1:], held_own, early[1:], total)
        total = image([early_other], held_other, early, total)
        total = image(late_pieces, held_own, late, total)
        return image([late_other], held_other, late, total, finish)

    def per_device(genotypes, probes, env_label, variances):
        snps = genotypes.shape[1] * snp
        count = probes.shape[0]
        width = genotypes.shape[1] // samp
        inputs = (genotypes, probes, env_label[None, :], variances)
        genotypes, probes, labels, variances = (pltpu.with_memory_space_constraint(a, pltpu.HBM) for a in inputs)

        def spread(weighted):
            pieces = {
                step: lax.ppermute(weighted, "snp", [(k, k ^ step) for k in range(snp)])
                for step in range(snp - 1, 0, -1)
            }
            return [weighted] + [pieces[step] for step in range(1, snp)]

        held_other, given, panel, current, tags, scales = load_first(probes, labels, variances, genotypes, chips, width, snps)
        held_own, own = load_second(panel, genotypes, chips, width)
        mine = reduce_panel(given, own, f32, count, True)
        parts = spread(spread_image(mine, held_own, held_other, (tags, scales)))
        first, noise, panel, given = step_half(current, tags, scales, held_other, parts, jnp.bfloat16)
        own = panel_half(panel, held_own)
        mine = reduce_panel(given, own, jnp.bfloat16, count, False)
        parts = spread(spread_image(mine, held_own, held_other, (tags, scales)))
        return (first, tree_sum(parts) + noise)

    return per_device


def solution(mesh):
    return jax.shard_map(
        make(mesh),
        mesh=mesh,
        in_specs=(P("samp", "snp"), P(None, "samp"), P("samp"), P()),
        out_specs=(P(None, "samp"), P(None, "samp")),
        check_vma=False,
    )
```

time: 168 us -> 63.4 us (0.38)
  blocking collectives: 138 us -> 0 us
  waiting for transfers between devices: 0 us -> 24.4 us
  starting transfers between devices: 0 us -> 23.4 us
  matrix products: 22.1 us -> 0 us
  Pallas kernels: 0 us -> 13.1 us
  other arithmetic: 5.97 us -> 0.87 us
    psum x4 -> x0, blocking collectives: 138 us -> none  [the longest x2 102 us: apply_operator(): snp_panel = lax.psum(partial_panel, 'samp').astype(jnp.bfloat16)]
    ppermute x0 -> x24, waiting for transfers between devices: none -> 24.4 us  [the longest x18 18.3 us: exchange(): return lax.ppermute(block, 'samp', [(k, k ^ offset) for k in range(samp)])]
    ppermute x0 -> x24, starting transfers between devices: none -> 23.4 us  [the longest x18 14.5 us: exchange(): return lax.ppermute(block, 'samp', [(k, k ^ offset) for k in range(samp)])]
    dot_general x4 -> x0, matrix products: 22.1 us -> none  [the longest x2 12.1 us: local_image(): lax.dot_general(snp_panel, genotypes, (((1,), (1,)), ((), ())), preferred...]
    pallas_call x0 -> x14, Pallas kernels: none -> 13.1 us  [the longest x10 6.3 us: image(): pl.pallas_call(functools.partial(image_body, blocks=tuple(blocks), pieces...]
    add x3 -> x2, other arithmetic: 3.74 us -> 0.68 us  [the longest x1 0.63 us: per_device(): return (first, tree_sum(parts) + noise)]
  transfers between devices with their start and end apart: 0 -> 24, of which waited for: 0 -> 15; matrix products, arithmetic and copies ran while one was open for 0% -> 1% of each run, Pallas kernels for 0% -> 13%
where the time goes in v4:
time: 63.4 us; the launch traced here: 63.2 us
  waiting for transfers between devices  24.4 us (38%)
  starting transfers between devices  23.4 us (37%)
  Pallas kernels  13.1 us (21%)
  other arithmetic  0.87 us (1%)
  between operations  0.8 us (1%)
  local copies, waits for them, and re-layouts  0.66 us (1%)
    ppermute x18, waiting for transfers between devices, exchange(): return lax.ppermute(block, 'samp', [(k, k ^ offset) for k in range(samp)])  18.3 us
    ppermute x18, starting transfers between devices, exchange(): return lax.ppermute(block, 'samp', [(k, k ^ offset) for k in range(samp)])  14.5 us
    ppermute x6, starting transfers between devices, spread(): lax.ppermute(weighted, 'snp', [(k, k ^ step) for k in range(snp)])  8.9 us
    pallas_call x10, Pallas kernels, image(): pl.pallas_call(functools.partial(image_body, blocks=tuple(blocks), pieces...  6.3 us
    ppermute x6, waiting for transfers between devices, spread(): lax.ppermute(weighted, 'snp', [(k, k ^ step) for k in range(snp)])  6.02 us
    pallas_call x1, Pallas kernels, load_first(): pl.pallas_call(functools.partial(first_body, snps=snps), in_specs=[HBM] *...  2.59 us
    pallas_call x1, Pallas kernels, load_second(): pl.pallas_call(second_body, in_specs=[VMEM, HBM], out_specs=(VMEM, VMEM),...  2.53 us
  transfers between devices with their start and end apart: 24, of which 15 were waited for; matrix products, arithmetic and copies ran while one was open for 1% of the time, Pallas kernels for 13%

profile of v4, /device:TPU:0, one launch (start us, length us, event | category | flops | bytes accessed | tf_op | source)
XLA Modules:
  0.0 63.2 jit_solution(1930910698366475365)
XLA Ops:
  0.6 2.6 %load_other.1 = (bf16[4,1024,512]{2,1,0:T(8,128)(2,1)S(1)}, f32[64,2048]{1,0:T(8,128)S(1)}, bf16[64,1024]{1,0:T(8,128)(2,1)S(1)}, bf16[8,1024]{1,0:T(8,128)(2,1)...) custom-call(bf16[8,1024]{1,0:T(8,128)(2,1)} %probes.1, s32[1,1024]{1,0:T(1,128)} %bitcast.3, f32[3]{0:T(128)} %variances.1, ...), custom_call_target="tpu_custom_call" | custom-call | tf_op jit(solution)/shard_map/load_other/pallas_call | solution.py:78
  3.2 0.6 collective-permute-start
  3.8 2.5 %load_own.1 = (bf16[4,1024,512]{2,1,0:T(8,128)(2,1)S(1)}, f32[64,2048]{1,0:T(8,128)S(1)}) custom-call(bf16[64,1024]{1,0:T(8,128)(2,1)S(1)} %get-tuple-element.18.panel, bf16[1024,4096]{1,0:T(8,128)(2,1)} %genotypes.3), custom_call_target="tpu_custom_call" | custom-call | tf_op jit(solution)/shard_map/load_own/pallas_call | solution.py:113
  6.3 0.0 collective-permute-done
  6.3 0.1 add.36
  6.4 3.6 %collective-permute-start.1 = (f32[64,512]{1,0:T(8,128)S(1)}, f32[64,512]{1,0:T(8,128)S(1)}, u32[]{:S(2)}, u32[]{:S(2)}) collective-permute-start(f32[64,512]{1,0:T(8,128)S(1)} %get-tuple-element.30), channel_id=1, source_target_pairs={{0,28},{4,24},{8,20},{12,16},{16,12},{20,8},{24,4},{28,0},{1,29},{... | collective-permute-start | bytes 393224 | tf_op jit(solution)/shard_map/ppermute | solution.py:232
  10.0 0.5 collective-permute-start.3
  10.6 0.0 collective-permute-start.2
  10.6 3.4 %collective-permute-done.1 = f32[64,512]{1,0:T(8,128)S(1)} collective-permute-done((f32[64,512]{1,0:T(8,128)S(1)}, f32[64,512]{1,0:T(8,128)S(1)}, u32[]{:S(2)}, u32[]{:S(2)}) %collective-permute-start.1) | collective-permute-done | bytes 131104 | tf_op jit(solution)/shard_map/ppermute | solution.py:232
  14.0 2.9 %collective-permute-done.3 = f32[64,512]{1,0:T(8,128)S(1)} collective-permute-done((f32[64,512]{1,0:T(8,128)S(1)}, f32[64,512]{1,0:T(8,128)S(1)}, u32[]{:S(2)}, u32[]{:S(2)}) %collective-permute-start.3) | collective-permute-done | bytes 131104 | tf_op jit(solution)/shard_map/ppermute | solution.py:232
  16.9 0.0 collective-permute-done.2
  17.0 1.4 %collective-permute-start.7 = (bf16[72,512]{1,0:T(8,128)(2,1)S(1)}, bf16[72,512]{1,0:T(8,128)(2,1)S(1)}, u32[]{:S(2)}, u32[]{:S(2)}) collective-permute-start(bf16[72,512]{1,0:T(8,128)(2,1)S(1)} %pad_maximum_fusion.4.refs_0_), channel_id=1, source_target_pairs={{0,28},{4,24},{8,20},{12,16},{16,12},{20,8},{24,4},{28,0},{1,29},{... | collective-permute-start | bytes 221192 | tf_op jit(solution)/shard_map/ppermute | solution.py:232
  18.4 1.4 %collective-permute-start.5 = (bf16[72,512]{1,0:T(8,128)(2,1)S(1)}, bf16[72,512]{1,0:T(8,128)(2,1)S(1)}, u32[]{:S(2)}, u32[]{:S(2)}) collective-permute-start(bf16[72,512]{1,0:T(8,128)(2,1)S(1)} %pad_maximum_fusion.4.refs_0_), channel_id=1, source_target_pairs={{0,16},{4,20},{8,24},{12,28},{16,0},{20,4},{24,8},{28,12},{1,17},{... | collective-permute-start | bytes 221192 | tf_op jit(solution)/shard_map/ppermute | solution.py:232
  19.8 0.2 collective-permute-start.4
  20.0 2.3 %collective-permute-done.7.refs_0_ = bf16[72,512]{1,0:T(8,128)(2,1)S(1)} collective-permute-done((bf16[72,512]{1,0:T(8,128)(2,1)S(1)}, bf16[72,512]{1,0:T(8,128)(2,1)S(1)}, u32[]{:S(2)}, u32[]{:S(2)}) %collective-permute-start.7) | collective-permute-done | bytes 73760 | tf_op jit(solution)/shard_map/ppermute | solution.py:232
  22.3 0.2 collective-permute-start.8
  22.5 1.6 %collective-permute-done.5.refs_1_ = bf16[72,512]{1,0:T(8,128)(2,1)S(1)} collective-permute-done((bf16[72,512]{1,0:T(8,128)(2,1)S(1)}, bf16[72,512]{1,0:T(8,128)(2,1)S(1)}, u32[]{:S(2)}, u32[]{:S(2)}) %collective-permute-start.5) | collective-permute-done | bytes 73760 | tf_op jit(solution)/shard_map/ppermute | solution.py:232
  24.1 0.0 collective-permute-done.4.refs_0_
  24.1 0.2 collective-permute-start.6
  24.3 0.4 image.10.refs_2_
  24.7 0.5 image.11.refs_2_
  25.2 0.0 collective-permute-done.8.refs_0_
  25.2 0.8 %image.12.refs_3_ = f32[72,1024]{1,0:T(8,128)S(1)} custom-call(bf16[72,1024]{1,0:T(8,128)(2,1)S(1)} %collective-permute-done.8.refs_0_, bf16[4,1024,512]{2,1,0:T(8,128)(2,1)S(1)} %get-tuple-element.17.refs_1_.held, f32[72,1024]{1,0:T(8,128)S(1)} %image.11.refs_2_), custom_call_target="tpu_custom_call" | custom-call | tf_op jit(solution)/shard_map/image/pallas_call | solution.py:214
  25.9 0.8 %image.13.refs_2_ = f32[72,1024]{1,0:T(8,128)S(1)} custom-call(bf16[72,512]{1,0:T(8,128)(2,1)S(1)} %collective-permute-done.4.refs_0_, bf16[72,512]{1,0:T(8,128)(2,1)S(1)} %collective-permute-done.5.refs_1_, bf16[4,1024,512]{2,1,0:T(8,128)(2,1)S(1)} %get-tuple-element.21.refs_1_.refs_2_.held, f32[72,1024]{1,0:T(8,128)S(1)} %image.12.refs_3_), custom_call_target="tpu_custom_call" | custom-call | tf_op jit(solution)/shard_map/image/pallas_call | solution.py:214
  26.7 0.0 collective-permute-done.6.refs_0_
  26.7 0.8 %image.14.refs_0_ = f32[8,1024]{1,0:T(8,128)S(1)} custom-call(bf16[72,1024]{1,0:T(8,128)(2,1)S(1)} %collective-permute-done.6.refs_0_, bf16[4,1024,512]{2,1,0:T(8,128)(2,1)S(1)} %get-tuple-element.17.refs_1_.held, f32[72,1024]{1,0:T(8,128)S(1)} %image.13.refs_2_, s32[8,1024]{1,0:T(8,128)S(1)} %get-tuple-element.15.refs_3_.tags, ...), custom_call_target="tpu_custom_call" | custom-call | tf_op jit(solution)/shard_map/image/pallas_call | solution.py:214
  27.5 3.8 %collective-permute-start.11 = (f32[8,1024]{1,0:T(8,128)S(1)}, f32[8,1024]{1,0:T(8,128)S(1)}, u32[]{:S(2)}, u32[]{:S(2)}) collective-permute-start(f32[8,1024]{1,0:T(8,128)S(1)} %image.14.refs_0_), channel_id=1, source_target_pairs={{0,3},{1,2},{2,1},{3,0},{4,7},{5,6},{6,5},{7,4},{8,11},{9,10},{10,... | collective-permute-start | bytes 98312 | tf_op jit(solution)/shard_map/ppermute | solution.py:270
  31.2 0.0 collective-permute-start.10
  31.2 0.7 %collective-permute-start.9 = (f32[8,1024]{1,0:T(8,128)S(1)}, f32[8,1024]{1,0:T(8,128)S(1)}, u32[]{:S(2)}, u32[]{:S(2)}) collective-permute-start(f32[8,1024]{1,0:T(8,128)S(1)} %image.14.refs_0_), channel_id=1, source_target_pairs={{0,1},{1,0},{2,3},{3,2},{4,5},{5,4},{6,7},{7,6},{8,9},{9,8},{10,11... | collective-permute-start | bytes 98312 | tf_op jit(solution)/shard_map/ppermute | solution.py:270
  31.9 1.3 %collective-permute-done.11.refs_3_ = f32[8,1024]{1,0:T(8,128)S(1)} collective-permute-done((f32[8,1024]{1,0:T(8,128)S(1)}, f32[8,1024]{1,0:T(8,128)S(1)}, u32[]{:S(2)}, u32[]{:S(2)}) %collective-permute-start.11) | collective-permute-done | bytes 32800 | tf_op jit(solution)/shard_map/ppermute | solution.py:270
  33.3 2.8 %collective-permute-done.10.refs_2_ = f32[8,1024]{1,0:T(8,128)S(1)} collective-permute-done((f32[8,1024]{1,0:T(8,128)S(1)}, f32[8,1024]{1,0:T(8,128)S(1)}, u32[]{:S(2)}, u32[]{:S(2)}) %collective-permute-start.10) | collective-permute-done | bytes 32800 | tf_op jit(solution)/shard_map/ppermute | solution.py:270
  36.1 0.0 collective-permute-done.9.refs_1_
  36.1 0.8 %step_other.1 = (f32[8,1024]{1,0:T(8,128)S(1)}, f32[8,1024]{1,0:T(8,128)S(1)}, bf16[64,1024]{1,0:T(8,128)(2,1)S(1)}, bf16[64,2048]{1,0:T(8,128)(2,1)S(1)}) custom-call(bf16[8,1024]{1,0:T(8,128)(2,1)S(1)} %get-tuple-element.14.current, s32[8,1024]{1,0:T(8,128)S(1)} %get-tuple-element.15.refs_3_.tags, f32[3,8,1024]{2,1,0:T(8,128)S(1)} %get-tuple-element.16.refs_4_.scales, ...), custom_call_target="tpu_custom_call" | custom-call | tf_op jit(solution)/shard_map/step_other/pallas_call | solution.py:146
  36.9 0.1 collective-permute-start.12
  37.0 0.8 %step_own.1 = f32[64,2048]{1,0:T(8,128)S(1)} custom-call(bf16[64,1024]{1,0:T(8,128)(2,1)S(1)} %get-tuple-element.23.panel, bf16[4,1024,512]{2,1,0:T(8,128)(2,1)S(1)} %get-tuple-element.21.refs_1_.refs_2_.held), custom_call_target="tpu_custom_call" | custom-call | tf_op jit(solution)/shard_map/step_own/pallas_call | solution.py:167
  37.8 0.7 %collective-permute-done.12 = bf16[64,2048]{1,0:T(8,128)(2,1)S(1)} collective-permute-done((bf16[64,2048]{1,0:T(8,128)(2,1)S(1)}, bf16[64,2048]{1,0:T(8,128)(2,1)S(1)}, u32[]{:S(2)}, u32[]{:S(2)}) %collective-permute-start.12) | collective-permute-done | bytes 262176 | tf_op jit(solution)/shard_map/ppermute | solution.py:232
  38.5 0.1 fusion.5
  38.6 1.5 %collective-permute-start.13 = (bf16[64,512]{1,0:T(8,128)(2,1)S(1)}, bf16[64,512]{1,0:T(8,128)(2,1)S(1)}, u32[]{:S(2)}, u32[]{:S(2)}) collective-permute-start(bf16[64,512]{1,0:T(8,128)(2,1)S(1)} %get-tuple-element.33), channel_id=1, source_target_pairs={{0,28},{4,24},{8,20},{12,16},{16,12},{20,8},{24,4},{28,0},{1,29},{... | collective-permute-start | bytes 196616 | tf_op jit(solution)/shard_map/ppermute | solution.py:232
  40.1 1.2 %collective-permute-start.15 = (bf16[64,512]{1,0:T(8,128)(2,1)S(1)}, bf16[64,512]{1,0:T(8,128)(2,1)S(1)}, u32[]{:S(2)}, u32[]{:S(2)}) collective-permute-start(bf16[64,512]{1,0:T(8,128)(2,1)S(1)} %get-tuple-element.34), channel_id=1, source_target_pairs={{0,16},{4,20},{8,24},{12,28},{16,0},{20,4},{24,8},{28,12},{1,17},{... | collective-permute-start | bytes 196616 | tf_op jit(solution)/shard_map/ppermute | solution.py:232
  41.3 0.3 collective-permute-start.14
  41.6 2.1 %collective-permute-done.13 = bf16[64,512]{1,0:T(8,128)(2,1)S(1)} collective-permute-done((bf16[64,512]{1,0:T(8,128)(2,1)S(1)}, bf16[64,512]{1,0:T(8,128)(2,1)S(1)}, u32[]{:S(2)}, u32[]{:S(2)}) %collective-permute-start.13) | collective-permute-done | bytes 65568 | tf_op jit(solution)/shard_map/ppermute | solution.py:232
  43.7 1.7 %collective-permute-done.15 = bf16[64,512]{1,0:T(8,128)(2,1)S(1)} collective-permute-done((bf16[64,512]{1,0:T(8,128)(2,1)S(1)}, bf16[64,512]{1,0:T(8,128)(2,1)S(1)}, u32[]{:S(2)}, u32[]{:S(2)}) %collective-permute-start.15) | collective-permute-done | bytes 65568 | tf_op jit(solution)/shard_map/ppermute | solution.py:232
  45.4 0.1 collective-permute-done.14
  45.5 1.4 %collective-permute-start.19 = (bf16[64,512]{1,0:T(8,128)(2,1)S(1)}, bf16[64,512]{1,0:T(8,128)(2,1)S(1)}, u32[]{:S(2)}, u32[]{:S(2)}) collective-permute-start(bf16[64,512]{1,0:T(8,128)(2,1)S(1)} %fusion.2.refs_0_), channel_id=1, source_target_pairs={{0,28},{4,24},{8,20},{12,16},{16,12},{20,8},{24,4},{28,0},{1,29},{... | collective-permute-start | bytes 196616 | tf_op jit(solution)/shard_map/ppermute | solution.py:232
  46.9 1.2 %collective-permute-start.17 = (bf16[64,512]{1,0:T(8,128)(2,1)S(1)}, bf16[64,512]{1,0:T(8,128)(2,1)S(1)}, u32[]{:S(2)}, u32[]{:S(2)}) collective-permute-start(bf16[64,512]{1,0:T(8,128)(2,1)S(1)} %fusion.2.refs_0_), channel_id=1, source_target_pairs={{0,16},{4,20},{8,24},{12,28},{16,0},{20,4},{24,8},{28,12},{1,17},{... | collective-permute-start | bytes 196616 | tf_op jit(solution)/shard_map/ppermute | solution.py:232
  48.0 0.4 collective-permute-start.16
  48.5 2.1 %collective-permute-done.19.refs_0_ = bf16[64,512]{1,0:T(8,128)(2,1)S(1)} collective-permute-done((bf16[64,512]{1,0:T(8,128)(2,1)S(1)}, bf16[64,512]{1,0:T(8,128)(2,1)S(1)}, u32[]{:S(2)}, u32[]{:S(2)}) %collective-permute-start.19) | collective-permute-done | bytes 65568 | tf_op jit(solution)/shard_map/ppermute | solution.py:232
  50.6 0.2 collective-permute-start.20
  50.8 1.4 %collective-permute-done.17.refs_1_ = bf16[64,512]{1,0:T(8,128)(2,1)S(1)} collective-permute-done((bf16[64,512]{1,0:T(8,128)(2,1)S(1)}, bf16[64,512]{1,0:T(8,128)(2,1)S(1)}, u32[]{:S(2)}, u32[]{:S(2)}) %collective-permute-start.17) | collective-permute-done | bytes 65568 | tf_op jit(solution)/shard_map/ppermute | solution.py:232
  52.2 0.0 collective-permute-done.16.refs_0_
  52.2 0.2 collective-permute-start.18
  52.4 0.4 image.15.refs_2_
  52.9 0.4 image.16.refs_2_
  53.3 0.8 %image.17.refs_3_ = f32[64,1024]{1,0:T(8,128)S(1)} custom-call(bf16[64,1024]{1,0:T(8,128)(2,1)S(1)} %collective-permute-done.20.refs_0_, bf16[4,1024,512]{2,1,0:T(8,128)(2,1)S(1)} %get-tuple-element.17.refs_1_.held, f32[64,1024]{1,0:T(8,128)S(1)} %image.16.refs_2_), custom_call_target="tpu_custom_call" | custom-call | tf_op jit(solution)/shard_map/image/pallas_call | solution.py:214
  54.1 0.8 %image.18.refs_2_ = f32[64,1024]{1,0:T(8,128)S(1)} custom-call(bf16[64,512]{1,0:T(8,128)(2,1)S(1)} %collective-permute-done.16.refs_0_, bf16[64,512]{1,0:T(8,128)(2,1)S(1)} %collective-permute-done.17.refs_1_, bf16[4,1024,512]{2,1,0:T(8,128)(2,1)S(1)} %get-tuple-element.21.refs_1_.refs_2_.held, f32[64,1024]{1,0:T(8,128)S(1)} %image.17.refs_3_), custom_call_target="tpu_custom_call" | custom-call | tf_op jit(solution)/shard_map/image/pallas_call | solution.py:214
  54.8 0.8 %image.19 = f32[8,1024]{1,0:T(8,128)S(1)} custom-call(bf16[64,1024]{1,0:T(8,128)(2,1)S(1)} %collective-permute-done.18.refs_0_, bf16[4,1024,512]{2,1,0:T(8,128)(2,1)S(1)} %get-tuple-element.17.refs_1_.held, f32[64,1024]{1,0:T(8,128)S(1)} %image.18.refs_2_, s32[8,1024]{1,0:T(8,128)S(1)} %get-tuple-element.15.refs_3_.tags, ...), custom_call_target="tpu_custom_call" | custom-call | tf_op jit(solution)/shard_map/image/pallas_call | solution.py:214
  55.6 1.7 %collective-permute-start.23 = (f32[8,1024]{1,0:T(8,128)S(1)}, f32[8,1024]{1,0:T(8,128)S(1)}, u32[]{:S(2)}, u32[]{:S(2)}) collective-permute-start(f32[8,1024]{1,0:T(8,128)S(1)} %image.19), channel_id=1, source_target_pairs={{0,3},{1,2},{2,1},{3,0},{4,7},{5,6},{6,5},{7,4},{8,11},{9,10},{10,... | collective-permute-start | bytes 98312 | tf_op jit(solution)/shard_map/ppermute | solution.py:270
  57.3 0.5 collective-permute-start.22
  57.7 2.3 %collective-permute-start.21 = (f32[8,1024]{1,0:T(8,128)S(1)}, f32[8,1024]{1,0:T(8,128)S(1)}, u32[]{:S(2)}, u32[]{:S(2)}) collective-permute-start(f32[8,1024]{1,0:T(8,128)S(1)} %image.19), channel_id=1, source_target_pairs={{0,1},{1,0},{2,3},{3,2},{4,5},{5,4},{6,7},{7,6},{8,9},{9,8},{10,11... | collective-permute-start | bytes 98312 | tf_op jit(solution)/shard_map/ppermute | solution.py:270
  60.0 0.6 copy.6
  60.6 0.9 %collective-permute-done.23 = f32[8,1024]{1,0:T(8,128)S(1)} collective-permute-done((f32[8,1024]{1,0:T(8,128)S(1)}, f32[8,1024]{1,0:T(8,128)S(1)}, u32[]{:S(2)}, u32[]{:S(2)}) %collective-permute-start.23) | collective-permute-done | bytes 32800 | tf_op jit(solution)/shard_map/ppermute | solution.py:270
  61.5 0.9 %collective-permute-done.22 = f32[8,1024]{1,0:T(8,128)S(1)} collective-permute-done((f32[8,1024]{1,0:T(8,128)S(1)}, f32[8,1024]{1,0:T(8,128)S(1)}, u32[]{:S(2)}, u32[]{:S(2)}) %collective-permute-start.22) | collective-permute-done | bytes 32800 | tf_op jit(solution)/shard_map/ppermute | solution.py:270
  62.4 0.1 collective-permute-done.21
  62.5 0.6 add_add_fusion
  (11 shorter events, 0.2 us)
Async XLA Ops:
  3.2 3.1 %collective-permute-start = (f32[64,2048]{1,0:T(8,128)S(1)}, f32[64,2048]{1,0:T(8,128)S(1)}, u32[]{:S(2)}, u32[]{:S(2)}) collective-permute-start(f32[64,2048]{1,0:T(8,128)S(1)} %get-tuple-element.20), channel_id=1, source_target_pairs={{0,4},{4,0},{8,12},{12,8},{16,20},{20,16},{24,28},{28,24},{1,5},{5... | collective-permute-start | bytes 1572872 | tf_op jit(solution)/shard_map/ppermute | solution.py:232
  6.4 7.6 %collective-permute-start.1 = (f32[64,512]{1,0:T(8,128)S(1)}, f32[64,512]{1,0:T(8,128)S(1)}, u32[]{:S(2)}, u32[]{:S(2)}) collective-permute-start(f32[64,512]{1,0:T(8,128)S(1)} %get-tuple-element.30), channel_id=1, source_target_pairs={{0,28},{4,24},{8,20},{12,16},{16,12},{20,8},{24,4},{28,0},{1,29},{... | collective-permute-start | bytes 393224 | tf_op jit(solution)/shard_map/ppermute | solution.py:232
  10.0 6.9 %collective-permute-start.3 = (f32[64,512]{1,0:T(8,128)S(1)}, f32[64,512]{1,0:T(8,128)S(1)}, u32[]{:S(2)}, u32[]{:S(2)}) collective-permute-start(f32[64,512]{1,0:T(8,128)S(1)} %get-tuple-element.31), channel_id=1, source_target_pairs={{0,16},{4,20},{8,24},{12,28},{16,0},{20,4},{24,8},{28,12},{1,17},{... | collective-permute-start | bytes 393224 | tf_op jit(solution)/shard_map/ppermute | solution.py:232
  10.6 6.4 %collective-permute-start.2 = (f32[64,512]{1,0:T(8,128)S(1)}, f32[64,512]{1,0:T(8,128)S(1)}, u32[]{:S(2)}, u32[]{:S(2)}) collective-permute-start(f32[64,512]{1,0:T(8,128)S(1)} %get-tuple-element.32), channel_id=1, source_target_pairs={{0,12},{4,8},{8,4},{12,0},{16,28},{20,24},{24,20},{28,16},{1,13},{... | collective-permute-start | bytes 393224 | tf_op jit(solution)/shard_map/ppermute | solution.py:232
  17.0 5.3 %collective-permute-start.7 = (bf16[72,512]{1,0:T(8,128)(2,1)S(1)}, bf16[72,512]{1,0:T(8,128)(2,1)S(1)}, u32[]{:S(2)}, u32[]{:S(2)}) collective-permute-start(bf16[72,512]{1,0:T(8,128)(2,1)S(1)} %pad_maximum_fusion.4.refs_0_), channel_id=1, source_target_pairs={{0,28},{4,24},{8,20},{12,16},{16,12},{20,8},{24,4},{28,0},{1,29},{... | collective-permute-start | bytes 221192 | tf_op jit(solution)/shard_map/ppermute | solution.py:232
  18.4 5.7 %collective-permute-start.5 = (bf16[72,512]{1,0:T(8,128)(2,1)S(1)}, bf16[72,512]{1,0:T(8,128)(2,1)S(1)}, u32[]{:S(2)}, u32[]{:S(2)}) collective-permute-start(bf16[72,512]{1,0:T(8,128)(2,1)S(1)} %pad_maximum_fusion.4.refs_0_), channel_id=1, source_target_pairs={{0,16},{4,20},{8,24},{12,28},{16,0},{20,4},{24,8},{28,12},{1,17},{... | collective-permute-start | bytes 221192 | tf_op jit(solution)/shard_map/ppermute | solution.py:232
  19.8 4.3 %collective-permute-start.4 = (bf16[72,512]{1,0:T(8,128)(2,1)S(1)}, bf16[72,512]{1,0:T(8,128)(2,1)S(1)}, u32[]{:S(2)}, u32[]{:S(2)}) collective-permute-start(bf16[72,512]{1,0:T(8,128)(2,1)S(1)} %pad_maximum_fusion.4.refs_0_), channel_id=1, source_target_pairs={{0,12},{4,8},{8,4},{12,0},{16,28},{20,24},{24,20},{28,16},{1,13},{... | collective-permute-start | bytes 221192 | tf_op jit(solution)/shard_map/ppermute | solution.py:232
  22.3 2.9 %collective-permute-start.8 = (bf16[72,1024]{1,0:T(8,128)(2,1)S(1)}, bf16[72,1024]{1,0:T(8,128)(2,1)S(1)}, u32[]{:S(2)}, u32[]{:S(2)}) collective-permute-start(bf16[72,1024]{1,0:T(8,128)(2,1)S(1)} %pad_maximum_fusion.1), channel_id=1, source_target_pairs={{0,4},{4,0},{8,12},{12,8},{16,20},{20,16},{24,28},{28,24},{1,5},{5... | collective-permute-start | bytes 442376 | tf_op jit(solution)/shard_map/ppermute | solution.py:232
  24.1 2.6 %collective-permute-start.6 = (bf16[72,1024]{1,0:T(8,128)(2,1)S(1)}, bf16[72,1024]{1,0:T(8,128)(2,1)S(1)}, u32[]{:S(2)}, u32[]{:S(2)}) collective-permute-start(bf16[72,1024]{1,0:T(8,128)(2,1)S(1)} %pad_maximum_fusion), channel_id=1, source_target_pairs={{0,4},{4,0},{8,12},{12,8},{16,20},{20,16},{24,28},{28,24},{1,5},{5... | collective-permute-start | bytes 442376 | tf_op jit(solution)/shard_map/ppermute | solution.py:232
  27.5 5.8 %collective-permute-start.11 = (f32[8,1024]{1,0:T(8,128)S(1)}, f32[8,1024]{1,0:T(8,128)S(1)}, u32[]{:S(2)}, u32[]{:S(2)}) collective-permute-start(f32[8,1024]{1,0:T(8,128)S(1)} %image.14.refs_0_), channel_id=1, source_target_pairs={{0,3},{1,2},{2,1},{3,0},{4,7},{5,6},{6,5},{7,4},{8,11},{9,10},{10,... | collective-permute-start | bytes 98312 | tf_op jit(solution)/shard_map/ppermute | solution.py:270
  31.2 4.8 %collective-permute-start.10 = (f32[8,1024]{1,0:T(8,128)S(1)}, f32[8,1024]{1,0:T(8,128)S(1)}, u32[]{:S(2)}, u32[]{:S(2)}) collective-permute-start(f32[8,1024]{1,0:T(8,128)S(1)} %image.14.refs_0_), channel_id=1, source_target_pairs={{0,2},{1,3},{2,0},{3,1},{4,6},{5,7},{6,4},{7,5},{8,10},{9,11},{10,... | collective-permute-start | bytes 98312 | tf_op jit(solution)/shard_map/ppermute | solution.py:270
  31.2 4.8 %collective-permute-start.9 = (f32[8,1024]{1,0:T(8,128)S(1)}, f32[8,1024]{1,0:T(8,128)S(1)}, u32[]{:S(2)}, u32[]{:S(2)}) collective-permute-start(f32[8,1024]{1,0:T(8,128)S(1)} %image.14.refs_0_), channel_id=1, source_target_pairs={{0,1},{1,0},{2,3},{3,2},{4,5},{5,4},{6,7},{7,6},{8,9},{9,8},{10,11... | collective-permute-start | bytes 98312 | tf_op jit(solution)/shard_map/ppermute | solution.py:270
  36.9 1.6 %collective-permute-start.12 = (bf16[64,2048]{1,0:T(8,128)(2,1)S(1)}, bf16[64,2048]{1,0:T(8,128)(2,1)S(1)}, u32[]{:S(2)}, u32[]{:S(2)}) collective-permute-start(bf16[64,2048]{1,0:T(8,128)(2,1)S(1)} %get-tuple-element.24), channel_id=1, source_target_pairs={{0,4},{4,0},{8,12},{12,8},{16,20},{20,16},{24,28},{28,24},{1,5},{5... | collective-permute-start | bytes 786440 | tf_op jit(solution)/shard_map/ppermute | solution.py:232
  38.6 5.1 %collective-permute-start.13 = (bf16[64,512]{1,0:T(8,128)(2,1)S(1)}, bf16[64,512]{1,0:T(8,128)(2,1)S(1)}, u32[]{:S(2)}, u32[]{:S(2)}) collective-permute-start(bf16[64,512]{1,0:T(8,128)(2,1)S(1)} %get-tuple-element.33), channel_id=1, source_target_pairs={{0,28},{4,24},{8,20},{12,16},{16,12},{20,8},{24,4},{28,0},{1,29},{... | collective-permute-start | bytes 196616 | tf_op jit(solution)/shard_map/ppermute | solution.py:232
  40.1 5.3 %collective-permute-start.15 = (bf16[64,512]{1,0:T(8,128)(2,1)S(1)}, bf16[64,512]{1,0:T(8,128)(2,1)S(1)}, u32[]{:S(2)}, u32[]{:S(2)}) collective-permute-start(bf16[64,512]{1,0:T(8,128)(2,1)S(1)} %get-tuple-element.34), channel_id=1, source_target_pairs={{0,16},{4,20},{8,24},{12,28},{16,0},{20,4},{24,8},{28,12},{1,17},{... | collective-permute-start | bytes 196616 | tf_op jit(solution)/shard_map/ppermute | solution.py:232
  41.3 4.1 %collective-permute-start.14 = (bf16[64,512]{1,0:T(8,128)(2,1)S(1)}, bf16[64,512]{1,0:T(8,128)(2,1)S(1)}, u32[]{:S(2)}, u32[]{:S(2)}) collective-permute-start(bf16[64,512]{1,0:T(8,128)(2,1)S(1)} %get-tuple-element.35), channel_id=1, source_target_pairs={{0,12},{4,8},{8,4},{12,0},{16,28},{20,24},{24,20},{28,16},{1,13},{... | collective-permute-start | bytes 196616 | tf_op jit(solution)/shard_map/ppermute | solution.py:232
  45.5 5.1 %collective-permute-start.19 = (bf16[64,512]{1,0:T(8,128)(2,1)S(1)}, bf16[64,512]{1,0:T(8,128)(2,1)S(1)}, u32[]{:S(2)}, u32[]{:S(2)}) collective-permute-start(bf16[64,512]{1,0:T(8,128)(2,1)S(1)} %fusion.2.refs_0_), channel_id=1, source_target_pairs={{0,28},{4,24},{8,20},{12,16},{16,12},{20,8},{24,4},{28,0},{1,29},{... | collective-permute-start | bytes 196616 | tf_op jit(solution)/shard_map/ppermute | solution.py:232
  46.9 5.4 %collective-permute-start.17 = (bf16[64,512]{1,0:T(8,128)(2,1)S(1)}, bf16[64,512]{1,0:T(8,128)(2,1)S(1)}, u32[]{:S(2)}, u32[]{:S(2)}) collective-permute-start(bf16[64,512]{1,0:T(8,128)(2,1)S(1)} %fusion.2.refs_0_), channel_id=1, source_target_pairs={{0,16},{4,20},{8,24},{12,28},{16,0},{20,4},{24,8},{28,12},{1,17},{... | collective-permute-start | bytes 196616 | tf_op jit(solution)/shard_map/ppermute | solution.py:232
  48.0 4.2 %collective-permute-start.16 = (bf16[64,512]{1,0:T(8,128)(2,1)S(1)}, bf16[64,512]{1,0:T(8,128)(2,1)S(1)}, u32[]{:S(2)}, u32[]{:S(2)}) collective-permute-start(bf16[64,512]{1,0:T(8,128)(2,1)S(1)} %fusion.2.refs_0_), channel_id=1, source_target_pairs={{0,12},{4,8},{8,4},{12,0},{16,28},{20,24},{24,20},{28,16},{1,13},{... | collective-permute-start | bytes 196616 | tf_op jit(solution)/shard_map/ppermute | solution.py:232
  50.6 2.7 %collective-permute-start.20 = (bf16[64,1024]{1,0:T(8,128)(2,1)S(1)}, bf16[64,1024]{1,0:T(8,128)(2,1)S(1)}, u32[]{:S(2)}, u32[]{:S(2)}) collective-permute-start(bf16[64,1024]{1,0:T(8,128)(2,1)S(1)} %pad_maximum_fusion.3), channel_id=1, source_target_pairs={{0,4},{4,0},{8,12},{12,8},{16,20},{20,16},{24,28},{28,24},{1,5},{5... | collective-permute-start | bytes 393224 | tf_op jit(solution)/shard_map/ppermute | solution.py:232
  52.2 2.6 %collective-permute-start.18 = (bf16[64,1024]{1,0:T(8,128)(2,1)S(1)}, bf16[64,1024]{1,0:T(8,128)(2,1)S(1)}, u32[]{:S(2)}, u32[]{:S(2)}) collective-permute-start(bf16[64,1024]{1,0:T(8,128)(2,1)S(1)} %pad_maximum_fusion.2), channel_id=1, source_target_pairs={{0,4},{4,0},{8,12},{12,8},{16,20},{20,16},{24,28},{28,24},{1,5},{5... | collective-permute-start | bytes 393224 | tf_op jit(solution)/shard_map/ppermute | solution.py:232
  55.6 6.0 %collective-permute-start.23 = (f32[8,1024]{1,0:T(8,128)S(1)}, f32[8,1024]{1,0:T(8,128)S(1)}, u32[]{:S(2)}, u32[]{:S(2)}) collective-permute-start(f32[8,1024]{1,0:T(8,128)S(1)} %image.19), channel_id=1, source_target_pairs={{0,3},{1,2},{2,1},{3,0},{4,7},{5,6},{6,5},{7,4},{8,11},{9,10},{10,... | collective-permute-start | bytes 98312 | tf_op jit(solution)/shard_map/ppermute | solution.py:270
  57.3 5.2 %collective-permute-start.22 = (f32[8,1024]{1,0:T(8,128)S(1)}, f32[8,1024]{1,0:T(8,128)S(1)}, u32[]{:S(2)}, u32[]{:S(2)}) collective-permute-start(f32[8,1024]{1,0:T(8,128)S(1)} %image.19), channel_id=1, source_target_pairs={{0,2},{1,3},{2,0},{3,1},{4,6},{5,7},{6,4},{7,5},{8,10},{9,11},{10,... | collective-permute-start | bytes 98312 | tf_op jit(solution)/shard_map/ppermute | solution.py:270
  57.7 4.8 %collective-permute-start.21 = (f32[8,1024]{1,0:T(8,128)S(1)}, f32[8,1024]{1,0:T(8,128)S(1)}, u32[]{:S(2)}, u32[]{:S(2)}) collective-permute-start(f32[8,1024]{1,0:T(8,128)S(1)} %image.19), channel_id=1, source_target_pairs={{0,1},{1,0},{2,3},{3,2},{4,5},{5,4},{6,7},{7,6},{8,9},{9,8},{10,11... | collective-permute-start | bytes 98312 | tf_op jit(solution)/shard_map/ppermute | solution.py:270

commit v5 on v4

--- a/solution.py
+++ b/solution.py
@@ -225,7 +225,7 @@
     samp, snp = mesh.shape["samp"], mesh.shape["snp"]
     chips = samp // 2
     far = sorted(range(1, chips), key=lambda step: -bin(step).count("1"))
-    early = [0] + far[: chips // 2 - 1]
+    early = far[: chips // 2 - 1]
     late = far[chips // 2 - 1 :]
 
     def exchange(block, offset):
@@ -245,18 +245,20 @@
         return total.astype(jnp.bfloat16)
 
     def spread_image(mine, held_own, held_other, finish):
-        pieces = {0: mine}
+        pieces = {}
         for step in far:
             pieces[step] = between(mine, step)
-        early_pieces = [pieces[d] for d in early]
-        late_pieces = [pieces[d] for d in late]
-        early_other = exchange(jnp.concatenate(early_pieces, axis=1), 1)
-        late_other = exchange(jnp.concatenate(late_pieces, axis=1), 1)
+        other = exchange(mine, 1)
         total = image([mine], held_own, [0])
-        total = image(early_pieces[1:], held_own, early[1:], total)
-        total = image([early_other], held_other, early, total)
+        total = image([other], held_other, [0], total)
+        for step in early:
+            other = exchange(pieces[step], 1)
+            total = image([pieces[step]], held_own, [step], total)
+            total = image([other], held_other, [step], total)
+        late_pieces = [pieces[step] for step in late]
+        other = exchange(jnp.concatenate(late_pieces, axis=1), 1)
         total = image(late_pieces, held_own, late, total)
-        return image([late_other], held_other, late, total, finish)
+        return image([other], held_other, late, total, finish)
 
     def per_device(genotypes, probes, env_label, variances):
         snps = genotypes.shape[1] * snp

time: 63.4 us -> 64.1 us (1.011)
  starting transfers between devices: 23.4 us -> 24.9 us
  waiting for transfers between devices: 24.4 us -> 23.2 us
    ppermute x18 -> x20, starting transfers between devices: 14.5 us -> 16 us  [exchange(): return lax.ppermute(block, 'samp', [(k, k ^ offset) for k in range(samp)])]
    ppermute x18 -> x20, waiting for transfers between devices: 18.3 us -> 17.3 us  [exchange(): return lax.ppermute(block, 'samp', [(k, k ^ offset) for k in range(samp)])]
    pallas_call x10 -> x12, Pallas kernels: 6.3 us -> 6.55 us  [image(): pl.pallas_call(functools.partial(image_body, blocks=tuple(blocks), pieces...]
  transfers between devices with their start and end apart: 24 -> 26, of which waited for: 15 -> 17; matrix products, arithmetic and copies ran while one was open for 1% -> 1% of each run, Pallas kernels for 13% -> 13%
where the time goes in v5:
time: 64.1 us; the launch traced here: 63.8 us
  starting transfers between devices  24.9 us (39%)
  waiting for transfers between devices  23.2 us (36%)
  Pallas kernels  13.3 us (21%)
  other arithmetic  0.84 us (1%)
  between operations  0.8 us (1%)
  local copies, waits for them, and re-layouts  0.66 us (1%)
    ppermute x20, waiting for transfers between devices, exchange(): return lax.ppermute(block, 'samp', [(k, k ^ offset) for k in range(samp)])  17.3 us
    ppermute x20, starting transfers between devices, exchange(): return lax.ppermute(block, 'samp', [(k, k ^ offset) for k in range(samp)])  16 us
    ppermute x6, starting transfers between devices, spread(): lax.ppermute(weighted, 'snp', [(k, k ^ step) for k in range(snp)])  8.9 us
    pallas_call x12, Pallas kernels, image(): pl.pallas_call(functools.partial(image_body, blocks=tuple(blocks), pieces...  6.55 us
    ppermute x6, waiting for transfers between devices, spread(): lax.ppermute(weighted, 'snp', [(k, k ^ step) for k in range(snp)])  5.89 us
    pallas_call x1, Pallas kernels, load_first(): pl.pallas_call(functools.partial(first_body, snps=snps), in_specs=[HBM] *...  2.59 us
    pallas_call x1, Pallas kernels, load_second(): pl.pallas_call(second_body, in_specs=[VMEM, HBM], out_specs=(VMEM, VMEM),...  2.53 us
  transfers between devices with their start and end apart: 26, of which 17 were waited for; matrix products, arithmetic and copies ran while one was open for 1% of the time, Pallas kernels for 13%

profile of v5, /device:TPU:0, one launch (start us, length us, event | category | flops | bytes accessed | tf_op | source)
XLA Modules:
  0.0 63.8 jit_solution(17688519317793003832)
XLA Ops:
  0.6 2.6 %load_other.1 = (bf16[4,1024,512]{2,1,0:T(8,128)(2,1)S(1)}, f32[64,2048]{1,0:T(8,128)S(1)}, bf16[64,1024]{1,0:T(8,128)(2,1)S(1)}, bf16[8,1024]{1,0:T(8,128)(2,1)...) custom-call(bf16[8,1024]{1,0:T(8,128)(2,1)} %probes.1, s32[1,1024]{1,0:T(1,128)} %bitcast.3, f32[3]{0:T(128)} %variances.1, ...), custom_call_target="tpu_custom_call" | custom-call | tf_op jit(solution)/shard_map/load_other/pallas_call | solution.py:78
  3.2 0.6 collective-permute-start
  3.8 2.5 %load_own.1 = (bf16[4,1024,512]{2,1,0:T(8,128)(2,1)S(1)}, f32[64,2048]{1,0:T(8,128)S(1)}) custom-call(bf16[64,1024]{1,0:T(8,128)(2,1)S(1)} %get-tuple-element.18.panel, bf16[1024,4096]{1,0:T(8,128)(2,1)} %genotypes.3), custom_call_target="tpu_custom_call" | custom-call | tf_op jit(solution)/shard_map/load_own/pallas_call | solution.py:113
  6.3 0.1 add.36
  6.4 3.6 %collective-permute-start.1 = (f32[64,512]{1,0:T(8,128)S(1)}, f32[64,512]{1,0:T(8,128)S(1)}, u32[]{:S(2)}, u32[]{:S(2)}) collective-permute-start(f32[64,512]{1,0:T(8,128)S(1)} %get-tuple-element.30), channel_id=1, source_target_pairs={{0,28},{4,24},{8,20},{12,16},{16,12},{20,8},{24,4},{28,0},{1,29},{... | collective-permute-start | bytes 393224 | tf_op jit(solution)/shard_map/ppermute | solution.py:232
  10.0 0.5 collective-permute-start.3
  10.6 0.0 collective-permute-start.2
  10.6 3.4 %collective-permute-done.1 = f32[64,512]{1,0:T(8,128)S(1)} collective-permute-done((f32[64,512]{1,0:T(8,128)S(1)}, f32[64,512]{1,0:T(8,128)S(1)}, u32[]{:S(2)}, u32[]{:S(2)}) %collective-permute-start.1) | collective-permute-done | bytes 131104 | tf_op jit(solution)/shard_map/ppermute | solution.py:232
  14.0 2.9 %collective-permute-done.3 = f32[64,512]{1,0:T(8,128)S(1)} collective-permute-done((f32[64,512]{1,0:T(8,128)S(1)}, f32[64,512]{1,0:T(8,128)S(1)}, u32[]{:S(2)}, u32[]{:S(2)}) %collective-permute-start.3) | collective-permute-done | bytes 131104 | tf_op jit(solution)/shard_map/ppermute | solution.py:232
  17.0 1.7 %collective-permute-start.5 = (bf16[72,512]{1,0:T(8,128)(2,1)S(1)}, bf16[72,512]{1,0:T(8,128)(2,1)S(1)}, u32[]{:S(2)}, u32[]{:S(2)}) collective-permute-start(bf16[72,512]{1,0:T(8,128)(2,1)S(1)} %pad_maximum_fusion.2.refs_0_), channel_id=1, source_target_pairs={{0,16},{4,20},{8,24},{12,28},{16,0},{20,4},{24,8},{28,12},{1,17},{... | collective-permute-start | bytes 221192 | tf_op jit(solution)/shard_map/ppermute | solution.py:232
  18.7 0.0 collective-permute-start.4
  18.7 1.6 %collective-permute-start.7 = (bf16[72,512]{1,0:T(8,128)(2,1)S(1)}, bf16[72,512]{1,0:T(8,128)(2,1)S(1)}, u32[]{:S(2)}, u32[]{:S(2)}) collective-permute-start(bf16[72,512]{1,0:T(8,128)(2,1)S(1)} %pad_maximum_fusion.2.refs_0_), channel_id=1, source_target_pairs={{0,28},{4,24},{8,20},{12,16},{16,12},{20,8},{24,4},{28,0},{1,29},{... | collective-permute-start | bytes 221192 | tf_op jit(solution)/shard_map/ppermute | solution.py:232
  20.2 1.1 %collective-permute-done.5.refs_1_ = bf16[72,512]{1,0:T(8,128)(2,1)S(1)} collective-permute-done((bf16[72,512]{1,0:T(8,128)(2,1)S(1)}, bf16[72,512]{1,0:T(8,128)(2,1)S(1)}, u32[]{:S(2)}, u32[]{:S(2)}) %collective-permute-start.5) | collective-permute-done | bytes 73760 | tf_op jit(solution)/shard_map/ppermute | solution.py:232
  21.4 1.8 %collective-permute-done.4.refs_0_ = bf16[72,512]{1,0:T(8,128)(2,1)S(1)} collective-permute-done((bf16[72,512]{1,0:T(8,128)(2,1)S(1)}, bf16[72,512]{1,0:T(8,128)(2,1)S(1)}, u32[]{:S(2)}, u32[]{:S(2)}) %collective-permute-start.4) | collective-permute-done | bytes 73760 | tf_op jit(solution)/shard_map/ppermute | solution.py:232
  23.2 0.1 collective-permute-start.6
  23.3 0.5 collective-permute-start.9
  23.7 0.4 collective-permute-done.7.refs_0_
  24.1 0.4 collective-permute-start.8
  24.5 0.4 image.12.refs_2_
  24.9 0.4 image.13.refs_2_
  25.4 0.4 image.14.refs_2_
  25.8 0.0 collective-permute-done.8.refs_0_
  25.8 0.4 image.15.refs_3_
  26.3 0.8 %image.16.refs_2_ = f32[72,1024]{1,0:T(8,128)S(1)} custom-call(bf16[72,512]{1,0:T(8,128)(2,1)S(1)} %collective-permute-done.4.refs_0_, bf16[72,512]{1,0:T(8,128)(2,1)S(1)} %collective-permute-done.5.refs_1_, bf16[4,1024,512]{2,1,0:T(8,128)(2,1)S(1)} %get-tuple-element.21.refs_1_.refs_2_.held, f32[72,1024]{1,0:T(8,128)S(1)} %image.15.refs_3_), custom_call_target="tpu_custom_call" | custom-call | tf_op jit(solution)/shard_map/image/pallas_call | solution.py:214
  27.0 0.0 collective-permute-done.6.refs_0_
  27.0 0.8 %image.17.refs_0_ = f32[8,1024]{1,0:T(8,128)S(1)} custom-call(bf16[72,1024]{1,0:T(8,128)(2,1)S(1)} %collective-permute-done.6.refs_0_, bf16[4,1024,512]{2,1,0:T(8,128)(2,1)S(1)} %get-tuple-element.17.refs_1_.held, f32[72,1024]{1,0:T(8,128)S(1)} %image.16.refs_2_, s32[8,1024]{1,0:T(8,128)S(1)} %get-tuple-element.15.refs_3_.tags, ...), custom_call_target="tpu_custom_call" | custom-call | tf_op jit(solution)/shard_map/image/pallas_call | solution.py:214
  27.8 3.8 %collective-permute-start.12 = (f32[8,1024]{1,0:T(8,128)S(1)}, f32[8,1024]{1,0:T(8,128)S(1)}, u32[]{:S(2)}, u32[]{:S(2)}) collective-permute-start(f32[8,1024]{1,0:T(8,128)S(1)} %image.17.refs_0_), channel_id=1, source_target_pairs={{0,3},{1,2},{2,1},{3,0},{4,7},{5,6},{6,5},{7,4},{8,11},{9,10},{10,... | collective-permute-start | bytes 98312 | tf_op jit(solution)/shard_map/ppermute | solution.py:272
  31.6 0.7 %collective-permute-start.10 = (f32[8,1024]{1,0:T(8,128)S(1)}, f32[8,1024]{1,0:T(8,128)S(1)}, u32[]{:S(2)}, u32[]{:S(2)}) collective-permute-start(f32[8,1024]{1,0:T(8,128)S(1)} %image.17.refs_0_), channel_id=1, source_target_pairs={{0,1},{1,0},{2,3},{3,2},{4,5},{5,4},{6,7},{7,6},{8,9},{9,8},{10,11... | collective-permute-start | bytes 98312 | tf_op jit(solution)/shard_map/ppermute | solution.py:272
  32.2 1.3 %collective-permute-done.12.refs_3_ = f32[8,1024]{1,0:T(8,128)S(1)} collective-permute-done((f32[8,1024]{1,0:T(8,128)S(1)}, f32[8,1024]{1,0:T(8,128)S(1)}, u32[]{:S(2)}, u32[]{:S(2)}) %collective-permute-start.12) | collective-permute-done | bytes 32800 | tf_op jit(solution)/shard_map/ppermute | solution.py:272
  33.6 2.8 %collective-permute-done.11.refs_2_ = f32[8,1024]{1,0:T(8,128)S(1)} collective-permute-done((f32[8,1024]{1,0:T(8,128)S(1)}, f32[8,1024]{1,0:T(8,128)S(1)}, u32[]{:S(2)}, u32[]{:S(2)}) %collective-permute-start.11) | collective-permute-done | bytes 32800 | tf_op jit(solution)/shard_map/ppermute | solution.py:272
  36.4 0.8 %step_other.1 = (f32[8,1024]{1,0:T(8,128)S(1)}, f32[8,1024]{1,0:T(8,128)S(1)}, bf16[64,1024]{1,0:T(8,128)(2,1)S(1)}, bf16[64,2048]{1,0:T(8,128)(2,1)S(1)}) custom-call(bf16[8,1024]{1,0:T(8,128)(2,1)S(1)} %get-tuple-element.14.current, s32[8,1024]{1,0:T(8,128)S(1)} %get-tuple-element.15.refs_3_.tags, f32[3,8,1024]{2,1,0:T(8,128)S(1)} %get-tuple-element.16.refs_4_.scales, ...), custom_call_target="tpu_custom_call" | custom-call | tf_op jit(solution)/shard_map/step_other/pallas_call | solution.py:146
  37.2 0.1 collective-permute-start.13
  37.3 0.8 %step_own.1 = f32[64,2048]{1,0:T(8,128)S(1)} custom-call(bf16[64,1024]{1,0:T(8,128)(2,1)S(1)} %get-tuple-element.23.panel, bf16[4,1024,512]{2,1,0:T(8,128)(2,1)S(1)} %get-tuple-element.21.refs_1_.refs_2_.held), custom_call_target="tpu_custom_call" | custom-call | tf_op jit(solution)/shard_map/step_own/pallas_call | solution.py:167
  38.1 0.7 %collective-permute-done.13 = bf16[64,2048]{1,0:T(8,128)(2,1)S(1)} collective-permute-done((bf16[64,2048]{1,0:T(8,128)(2,1)S(1)}, bf16[64,2048]{1,0:T(8,128)(2,1)S(1)}, u32[]{:S(2)}, u32[]{:S(2)}) %collective-permute-start.13) | collective-permute-done | bytes 262176 | tf_op jit(solution)/shard_map/ppermute | solution.py:232
  38.8 0.1 fusion.5
  38.9 1.5 %collective-permute-start.14 = (bf16[64,512]{1,0:T(8,128)(2,1)S(1)}, bf16[64,512]{1,0:T(8,128)(2,1)S(1)}, u32[]{:S(2)}, u32[]{:S(2)}) collective-permute-start(bf16[64,512]{1,0:T(8,128)(2,1)S(1)} %get-tuple-element.33), channel_id=1, source_target_pairs={{0,28},{4,24},{8,20},{12,16},{16,12},{20,8},{24,4},{28,0},{1,29},{... | collective-permute-start | bytes 196616 | tf_op jit(solution)/shard_map/ppermute | solution.py:232
  40.5 1.3 %collective-permute-start.16 = (bf16[64,512]{1,0:T(8,128)(2,1)S(1)}, bf16[64,512]{1,0:T(8,128)(2,1)S(1)}, u32[]{:S(2)}, u32[]{:S(2)}) collective-permute-start(bf16[64,512]{1,0:T(8,128)(2,1)S(1)} %get-tuple-element.34), channel_id=1, source_target_pairs={{0,16},{4,20},{8,24},{12,28},{16,0},{20,4},{24,8},{28,12},{1,17},{... | collective-permute-start | bytes 196616 | tf_op jit(solution)/shard_map/ppermute | solution.py:232
  41.8 0.1 collective-permute-start.15
  41.9 2.1 %collective-permute-done.14 = bf16[64,512]{1,0:T(8,128)(2,1)S(1)} collective-permute-done((bf16[64,512]{1,0:T(8,128)(2,1)S(1)}, bf16[64,512]{1,0:T(8,128)(2,1)S(1)}, u32[]{:S(2)}, u32[]{:S(2)}) %collective-permute-start.14) | collective-permute-done | bytes 65568 | tf_op jit(solution)/shard_map/ppermute | solution.py:232
  44.0 1.7 %collective-permute-done.16 = bf16[64,512]{1,0:T(8,128)(2,1)S(1)} collective-permute-done((bf16[64,512]{1,0:T(8,128)(2,1)S(1)}, bf16[64,512]{1,0:T(8,128)(2,1)S(1)}, u32[]{:S(2)}, u32[]{:S(2)}) %collective-permute-start.16) | collective-permute-done | bytes 65568 | tf_op jit(solution)/shard_map/ppermute | solution.py:232
  45.7 0.2 collective-permute-done.15
  45.9 1.4 %collective-permute-start.18 = (bf16[64,512]{1,0:T(8,128)(2,1)S(1)}, bf16[64,512]{1,0:T(8,128)(2,1)S(1)}, u32[]{:S(2)}, u32[]{:S(2)}) collective-permute-start(bf16[64,512]{1,0:T(8,128)(2,1)S(1)} %fusion.2.refs_0_), channel_id=1, source_target_pairs={{0,16},{4,20},{8,24},{12,28},{16,0},{20,4},{24,8},{28,12},{1,17},{... | collective-permute-start | bytes 196616 | tf_op jit(solution)/shard_map/ppermute | solution.py:232
  47.3 0.2 collective-permute-start.17
  47.5 1.7 %collective-permute-start.20 = (bf16[64,512]{1,0:T(8,128)(2,1)S(1)}, bf16[64,512]{1,0:T(8,128)(2,1)S(1)}, u32[]{:S(2)}, u32[]{:S(2)}) collective-permute-start(bf16[64,512]{1,0:T(8,128)(2,1)S(1)} %fusion.2.refs_0_), channel_id=1, source_target_pairs={{0,28},{4,24},{8,20},{12,16},{16,12},{20,8},{24,4},{28,0},{1,29},{... | collective-permute-start | bytes 196616 | tf_op jit(solution)/shard_map/ppermute | solution.py:232
  49.2 1.1 %collective-permute-done.18.refs_1_ = bf16[64,512]{1,0:T(8,128)(2,1)S(1)} collective-permute-done((bf16[64,512]{1,0:T(8,128)(2,1)S(1)}, bf16[64,512]{1,0:T(8,128)(2,1)S(1)}, u32[]{:S(2)}, u32[]{:S(2)}) %collective-permute-start.18) | collective-permute-done | bytes 65568 | tf_op jit(solution)/shard_map/ppermute | solution.py:232
  50.2 1.4 %collective-permute-done.17.refs_0_ = bf16[64,512]{1,0:T(8,128)(2,1)S(1)} collective-permute-done((bf16[64,512]{1,0:T(8,128)(2,1)S(1)}, bf16[64,512]{1,0:T(8,128)(2,1)S(1)}, u32[]{:S(2)}, u32[]{:S(2)}) %collective-permute-start.17) | collective-permute-done | bytes 65568 | tf_op jit(solution)/shard_map/ppermute | solution.py:232
  51.7 0.1 collective-permute-start.19
  51.8 0.4 collective-permute-start.22
  52.2 0.6 collective-permute-done.20.refs_0_
  52.8 0.2 collective-permute-start.21
  53.1 0.4 image.18.refs_2_
  53.5 0.4 image.19.refs_2_
  53.9 0.4 image.20.refs_2_
  54.4 0.4 image.21.refs_3_
  54.8 0.8 %image.22.refs_2_ = f32[64,1024]{1,0:T(8,128)S(1)} custom-call(bf16[64,512]{1,0:T(8,128)(2,1)S(1)} %collective-permute-done.17.refs_0_, bf16[64,512]{1,0:T(8,128)(2,1)S(1)} %collective-permute-done.18.refs_1_, bf16[4,1024,512]{2,1,0:T(8,128)(2,1)S(1)} %get-tuple-element.21.refs_1_.refs_2_.held, f32[64,1024]{1,0:T(8,128)S(1)} %image.21.refs_3_), custom_call_target="tpu_custom_call" | custom-call | tf_op jit(solution)/shard_map/image/pallas_call | solution.py:214
  55.6 0.8 %image.23 = f32[8,1024]{1,0:T(8,128)S(1)} custom-call(bf16[64,1024]{1,0:T(8,128)(2,1)S(1)} %collective-permute-done.19.refs_0_, bf16[4,1024,512]{2,1,0:T(8,128)(2,1)S(1)} %get-tuple-element.17.refs_1_.held, f32[64,1024]{1,0:T(8,128)S(1)} %image.22.refs_2_, s32[8,1024]{1,0:T(8,128)S(1)} %get-tuple-element.15.refs_3_.tags, ...), custom_call_target="tpu_custom_call" | custom-call | tf_op jit(solution)/shard_map/image/pallas_call | solution.py:214
  56.4 1.7 %collective-permute-start.25 = (f32[8,1024]{1,0:T(8,128)S(1)}, f32[8,1024]{1,0:T(8,128)S(1)}, u32[]{:S(2)}, u32[]{:S(2)}) collective-permute-start(f32[8,1024]{1,0:T(8,128)S(1)} %image.23), channel_id=1, source_target_pairs={{0,3},{1,2},{2,1},{3,0},{4,7},{5,6},{6,5},{7,4},{8,11},{9,10},{10,... | collective-permute-start | bytes 98312 | tf_op jit(solution)/shard_map/ppermute | solution.py:272
  58.0 0.5 collective-permute-start.24
  58.5 2.3 %collective-permute-start.23 = (f32[8,1024]{1,0:T(8,128)S(1)}, f32[8,1024]{1,0:T(8,128)S(1)}, u32[]{:S(2)}, u32[]{:S(2)}) collective-permute-start(f32[8,1024]{1,0:T(8,128)S(1)} %image.23), channel_id=1, source_target_pairs={{0,1},{1,0},{2,3},{3,2},{4,5},{5,4},{6,7},{7,6},{8,9},{9,8},{10,11... | collective-permute-start | bytes 98312 | tf_op jit(solution)/shard_map/ppermute | solution.py:272
  60.8 0.6 copy.6
  61.4 1.0 %collective-permute-done.25 = f32[8,1024]{1,0:T(8,128)S(1)} collective-permute-done((f32[8,1024]{1,0:T(8,128)S(1)}, f32[8,1024]{1,0:T(8,128)S(1)}, u32[]{:S(2)}, u32[]{:S(2)}) %collective-permute-start.25) | collective-permute-done | bytes 32800 | tf_op jit(solution)/shard_map/ppermute | solution.py:272
  62.5 0.6 %collective-permute-done.24 = f32[8,1024]{1,0:T(8,128)S(1)} collective-permute-done((f32[8,1024]{1,0:T(8,128)S(1)}, f32[8,1024]{1,0:T(8,128)S(1)}, u32[]{:S(2)}, u32[]{:S(2)}) %collective-permute-start.24) | collective-permute-done | bytes 32800 | tf_op jit(solution)/shard_map/ppermute | solution.py:272
  63.1 0.1 collective-permute-done.23
  63.2 0.6 add_add_fusion
  (15 shorter events, 0.2 us)
Async XLA Ops:
  3.2 3.1 %collective-permute-start = (f32[64,2048]{1,0:T(8,128)S(1)}, f32[64,2048]{1,0:T(8,128)S(1)}, u32[]{:S(2)}, u32[]{:S(2)}) collective-permute-start(f32[64,2048]{1,0:T(8,128)S(1)} %get-tuple-element.20), channel_id=1, source_target_pairs={{0,4},{4,0},{8,12},{12,8},{16,20},{20,16},{24,28},{28,24},{1,5},{5... | collective-permute-start | bytes 1572872 | tf_op jit(solution)/shard_map/ppermute | solution.py:232
  6.4 7.6 %collective-permute-start.1 = (f32[64,512]{1,0:T(8,128)S(1)}, f32[64,512]{1,0:T(8,128)S(1)}, u32[]{:S(2)}, u32[]{:S(2)}) collective-permute-start(f32[64,512]{1,0:T(8,128)S(1)} %get-tuple-element.30), channel_id=1, source_target_pairs={{0,28},{4,24},{8,20},{12,16},{16,12},{20,8},{24,4},{28,0},{1,29},{... | collective-permute-start | bytes 393224 | tf_op jit(solution)/shard_map/ppermute | solution.py:232
  10.0 6.9 %collective-permute-start.3 = (f32[64,512]{1,0:T(8,128)S(1)}, f32[64,512]{1,0:T(8,128)S(1)}, u32[]{:S(2)}, u32[]{:S(2)}) collective-permute-start(f32[64,512]{1,0:T(8,128)S(1)} %get-tuple-element.31), channel_id=1, source_target_pairs={{0,16},{4,20},{8,24},{12,28},{16,0},{20,4},{24,8},{28,12},{1,17},{... | collective-permute-start | bytes 393224 | tf_op jit(solution)/shard_map/ppermute | solution.py:232
  10.6 6.4 %collective-permute-start.2 = (f32[64,512]{1,0:T(8,128)S(1)}, f32[64,512]{1,0:T(8,128)S(1)}, u32[]{:S(2)}, u32[]{:S(2)}) collective-permute-start(f32[64,512]{1,0:T(8,128)S(1)} %get-tuple-element.32), channel_id=1, source_target_pairs={{0,12},{4,8},{8,4},{12,0},{16,28},{20,24},{24,20},{28,16},{1,13},{... | collective-permute-start | bytes 393224 | tf_op jit(solution)/shard_map/ppermute | solution.py:232
  17.0 4.4 %collective-permute-start.5 = (bf16[72,512]{1,0:T(8,128)(2,1)S(1)}, bf16[72,512]{1,0:T(8,128)(2,1)S(1)}, u32[]{:S(2)}, u32[]{:S(2)}) collective-permute-start(bf16[72,512]{1,0:T(8,128)(2,1)S(1)} %pad_maximum_fusion.2.refs_0_), channel_id=1, source_target_pairs={{0,16},{4,20},{8,24},{12,28},{16,0},{20,4},{24,8},{28,12},{1,17},{... | collective-permute-start | bytes 221192 | tf_op jit(solution)/shard_map/ppermute | solution.py:232
  18.7 4.5 %collective-permute-start.4 = (bf16[72,512]{1,0:T(8,128)(2,1)S(1)}, bf16[72,512]{1,0:T(8,128)(2,1)S(1)}, u32[]{:S(2)}, u32[]{:S(2)}) collective-permute-start(bf16[72,512]{1,0:T(8,128)(2,1)S(1)} %pad_maximum_fusion.2.refs_0_), channel_id=1, source_target_pairs={{0,12},{4,8},{8,4},{12,0},{16,28},{20,24},{24,20},{28,16},{1,13},{... | collective-permute-start | bytes 221192 | tf_op jit(solution)/shard_map/ppermute | solution.py:232
  18.7 5.4 %collective-permute-start.7 = (bf16[72,512]{1,0:T(8,128)(2,1)S(1)}, bf16[72,512]{1,0:T(8,128)(2,1)S(1)}, u32[]{:S(2)}, u32[]{:S(2)}) collective-permute-start(bf16[72,512]{1,0:T(8,128)(2,1)S(1)} %pad_maximum_fusion.2.refs_0_), channel_id=1, source_target_pairs={{0,28},{4,24},{8,20},{12,16},{16,12},{20,8},{24,4},{28,0},{1,29},{... | collective-permute-start | bytes 221192 | tf_op jit(solution)/shard_map/ppermute | solution.py:232
  23.2 3.9 %collective-permute-start.6 = (bf16[72,1024]{1,0:T(8,128)(2,1)S(1)}, bf16[72,1024]{1,0:T(8,128)(2,1)S(1)}, u32[]{:S(2)}, u32[]{:S(2)}) collective-permute-start(bf16[72,1024]{1,0:T(8,128)(2,1)S(1)} %pad_maximum_fusion), channel_id=1, source_target_pairs={{0,4},{4,0},{8,12},{12,8},{16,20},{20,16},{24,28},{28,24},{1,5},{5... | collective-permute-start | bytes 442376 | tf_op jit(solution)/shard_map/ppermute | solution.py:232
  23.3 1.6 %collective-permute-start.9 = (bf16[72,512]{1,0:T(8,128)(2,1)S(1)}, bf16[72,512]{1,0:T(8,128)(2,1)S(1)}, u32[]{:S(2)}, u32[]{:S(2)}) collective-permute-start(bf16[72,512]{1,0:T(8,128)(2,1)S(1)} %pad_maximum_fusion.2.refs_0_), channel_id=1, source_target_pairs={{0,4},{4,0},{8,12},{12,8},{16,20},{20,16},{24,28},{28,24},{1,5},{5... | collective-permute-start | bytes 221192 | tf_op jit(solution)/shard_map/ppermute | solution.py:232
  24.1 1.7 %collective-permute-start.8 = (bf16[72,512]{1,0:T(8,128)(2,1)S(1)}, bf16[72,512]{1,0:T(8,128)(2,1)S(1)}, u32[]{:S(2)}, u32[]{:S(2)}) collective-permute-start(bf16[72,512]{1,0:T(8,128)(2,1)S(1)} %collective-permute-done.7.refs_0_), channel_id=1, source_target_pairs={{0,4},{4,0},{8,12},{12,8},{16,20},{20,16},{24,28},{28,24},{1,5},{5... | collective-permute-start | bytes 221192 | tf_op jit(solution)/shard_map/ppermute | solution.py:232
  27.8 5.8 %collective-permute-start.12 = (f32[8,1024]{1,0:T(8,128)S(1)}, f32[8,1024]{1,0:T(8,128)S(1)}, u32[]{:S(2)}, u32[]{:S(2)}) collective-permute-start(f32[8,1024]{1,0:T(8,128)S(1)} %image.17.refs_0_), channel_id=1, source_target_pairs={{0,3},{1,2},{2,1},{3,0},{4,7},{5,6},{6,5},{7,4},{8,11},{9,10},{10,... | collective-permute-start | bytes 98312 | tf_op jit(solution)/shard_map/ppermute | solution.py:272
  31.6 4.8 %collective-permute-start.11 = (f32[8,1024]{1,0:T(8,128)S(1)}, f32[8,1024]{1,0:T(8,128)S(1)}, u32[]{:S(2)}, u32[]{:S(2)}) collective-permute-start(f32[8,1024]{1,0:T(8,128)S(1)} %image.17.refs_0_), channel_id=1, source_target_pairs={{0,2},{1,3},{2,0},{3,1},{4,6},{5,7},{6,4},{7,5},{8,10},{9,11},{10,... | collective-permute-start | bytes 98312 | tf_op jit(solution)/shard_map/ppermute | solution.py:272
  31.6 4.8 %collective-permute-start.10 = (f32[8,1024]{1,0:T(8,128)S(1)}, f32[8,1024]{1,0:T(8,128)S(1)}, u32[]{:S(2)}, u32[]{:S(2)}) collective-permute-start(f32[8,1024]{1,0:T(8,128)S(1)} %image.17.refs_0_), channel_id=1, source_target_pairs={{0,1},{1,0},{2,3},{3,2},{4,5},{5,4},{6,7},{7,6},{8,9},{9,8},{10,11... | collective-permute-start | bytes 98312 | tf_op jit(solution)/shard_map/ppermute | solution.py:272
  37.2 1.6 %collective-permute-start.13 = (bf16[64,2048]{1,0:T(8,128)(2,1)S(1)}, bf16[64,2048]{1,0:T(8,128)(2,1)S(1)}, u32[]{:S(2)}, u32[]{:S(2)}) collective-permute-start(bf16[64,2048]{1,0:T(8,128)(2,1)S(1)} %get-tuple-element.24), channel_id=1, source_target_pairs={{0,4},{4,0},{8,12},{12,8},{16,20},{20,16},{24,28},{28,24},{1,5},{5... | collective-permute-start | bytes 786440 | tf_op jit(solution)/shard_map/ppermute | solution.py:232
  38.9 5.1 %collective-permute-start.14 = (bf16[64,512]{1,0:T(8,128)(2,1)S(1)}, bf16[64,512]{1,0:T(8,128)(2,1)S(1)}, u32[]{:S(2)}, u32[]{:S(2)}) collective-permute-start(bf16[64,512]{1,0:T(8,128)(2,1)S(1)} %get-tuple-element.33), channel_id=1, source_target_pairs={{0,28},{4,24},{8,20},{12,16},{16,12},{20,8},{24,4},{28,0},{1,29},{... | collective-permute-start | bytes 196616 | tf_op jit(solution)/shard_map/ppermute | solution.py:232
  40.5 5.2 %collective-permute-start.16 = (bf16[64,512]{1,0:T(8,128)(2,1)S(1)}, bf16[64,512]{1,0:T(8,128)(2,1)S(1)}, u32[]{:S(2)}, u32[]{:S(2)}) collective-permute-start(bf16[64,512]{1,0:T(8,128)(2,1)S(1)} %get-tuple-element.34), channel_id=1, source_target_pairs={{0,16},{4,20},{8,24},{12,28},{16,0},{20,4},{24,8},{28,12},{1,17},{... | collective-permute-start | bytes 196616 | tf_op jit(solution)/shard_map/ppermute | solution.py:232
  41.8 4.1 %collective-permute-start.15 = (bf16[64,512]{1,0:T(8,128)(2,1)S(1)}, bf16[64,512]{1,0:T(8,128)(2,1)S(1)}, u32[]{:S(2)}, u32[]{:S(2)}) collective-permute-start(bf16[64,512]{1,0:T(8,128)(2,1)S(1)} %get-tuple-element.35), channel_id=1, source_target_pairs={{0,12},{4,8},{8,4},{12,0},{16,28},{20,24},{24,20},{28,16},{1,13},{... | collective-permute-start | bytes 196616 | tf_op jit(solution)/shard_map/ppermute | solution.py:232
  45.9 4.3 %collective-permute-start.18 = (bf16[64,512]{1,0:T(8,128)(2,1)S(1)}, bf16[64,512]{1,0:T(8,128)(2,1)S(1)}, u32[]{:S(2)}, u32[]{:S(2)}) collective-permute-start(bf16[64,512]{1,0:T(8,128)(2,1)S(1)} %fusion.2.refs_0_), channel_id=1, source_target_pairs={{0,16},{4,20},{8,24},{12,28},{16,0},{20,4},{24,8},{28,12},{1,17},{... | collective-permute-start | bytes 196616 | tf_op jit(solution)/shard_map/ppermute | solution.py:232
  47.3 4.4 %collective-permute-start.17 = (bf16[64,512]{1,0:T(8,128)(2,1)S(1)}, bf16[64,512]{1,0:T(8,128)(2,1)S(1)}, u32[]{:S(2)}, u32[]{:S(2)}) collective-permute-start(bf16[64,512]{1,0:T(8,128)(2,1)S(1)} %fusion.2.refs_0_), channel_id=1, source_target_pairs={{0,12},{4,8},{8,4},{12,0},{16,28},{20,24},{24,20},{28,16},{1,13},{... | collective-permute-start | bytes 196616 | tf_op jit(solution)/shard_map/ppermute | solution.py:232
  47.5 5.3 %collective-permute-start.20 = (bf16[64,512]{1,0:T(8,128)(2,1)S(1)}, bf16[64,512]{1,0:T(8,128)(2,1)S(1)}, u32[]{:S(2)}, u32[]{:S(2)}) collective-permute-start(bf16[64,512]{1,0:T(8,128)(2,1)S(1)} %fusion.2.refs_0_), channel_id=1, source_target_pairs={{0,28},{4,24},{8,20},{12,16},{16,12},{20,8},{24,4},{28,0},{1,29},{... | collective-permute-start | bytes 196616 | tf_op jit(solution)/shard_map/ppermute | solution.py:232
  51.7 3.9 %collective-permute-start.19 = (bf16[64,1024]{1,0:T(8,128)(2,1)S(1)}, bf16[64,1024]{1,0:T(8,128)(2,1)S(1)}, u32[]{:S(2)}, u32[]{:S(2)}) collective-permute-start(bf16[64,1024]{1,0:T(8,128)(2,1)S(1)} %pad_maximum_fusion.1), channel_id=1, source_target_pairs={{0,4},{4,0},{8,12},{12,8},{16,20},{20,16},{24,28},{28,24},{1,5},{5... | collective-permute-start | bytes 393224 | tf_op jit(solution)/shard_map/ppermute | solution.py:232
  51.8 1.7 %collective-permute-start.22 = (bf16[64,512]{1,0:T(8,128)(2,1)S(1)}, bf16[64,512]{1,0:T(8,128)(2,1)S(1)}, u32[]{:S(2)}, u32[]{:S(2)}) collective-permute-start(bf16[64,512]{1,0:T(8,128)(2,1)S(1)} %fusion.2.refs_0_), channel_id=1, source_target_pairs={{0,4},{4,0},{8,12},{12,8},{16,20},{20,16},{24,28},{28,24},{1,5},{5... | collective-permute-start | bytes 196616 | tf_op jit(solution)/shard_map/ppermute | solution.py:232
  52.8 1.6 %collective-permute-start.21 = (bf16[64,512]{1,0:T(8,128)(2,1)S(1)}, bf16[64,512]{1,0:T(8,128)(2,1)S(1)}, u32[]{:S(2)}, u32[]{:S(2)}) collective-permute-start(bf16[64,512]{1,0:T(8,128)(2,1)S(1)} %collective-permute-done.20.refs_0_), channel_id=1, source_target_pairs={{0,4},{4,0},{8,12},{12,8},{16,20},{20,16},{24,28},{28,24},{1,5},{5... | collective-permute-start | bytes 196616 | tf_op jit(solution)/shard_map/ppermute | solution.py:232
  56.4 6.1 %collective-permute-start.25 = (f32[8,1024]{1,0:T(8,128)S(1)}, f32[8,1024]{1,0:T(8,128)S(1)}, u32[]{:S(2)}, u32[]{:S(2)}) collective-permute-start(f32[8,1024]{1,0:T(8,128)S(1)} %image.23), channel_id=1, source_target_pairs={{0,3},{1,2},{2,1},{3,0},{4,7},{5,6},{6,5},{7,4},{8,11},{9,10},{10,... | collective-permute-start | bytes 98312 | tf_op jit(solution)/shard_map/ppermute | solution.py:272
  58.0 5.1 %collective-permute-start.24 = (f32[8,1024]{1,0:T(8,128)S(1)}, f32[8,1024]{1,0:T(8,128)S(1)}, u32[]{:S(2)}, u32[]{:S(2)}) collective-permute-start(f32[8,1024]{1,0:T(8,128)S(1)} %image.23), channel_id=1, source_target_pairs={{0,2},{1,3},{2,0},{3,1},{4,6},{5,7},{6,4},{7,5},{8,10},{9,11},{10,... | collective-permute-start | bytes 98312 | tf_op jit(solution)/shard_map/ppermute | solution.py:272
  58.5 4.7 %collective-permute-start.23 = (f32[8,1024]{1,0:T(8,128)S(1)}, f32[8,1024]{1,0:T(8,128)S(1)}, u32[]{:S(2)}, u32[]{:S(2)}) collective-permute-start(f32[8,1024]{1,0:T(8,128)S(1)} %image.23), channel_id=1, source_target_pairs={{0,1},{1,0},{2,3},{3,2},{4,5},{5,4},{6,7},{7,6},{8,9},{9,8},{10,11... | collective-permute-start | bytes 98312 | tf_op jit(solution)/shard_map/ppermute | solution.py:272

commit v6 on v5

--- a/solution.py
+++ b/solution.py
@@ -9,6 +9,7 @@
 
 
 ENVS = 8
+SCALE_ROWS = 8
 VMEM = pl.BlockSpec(memory_space=pltpu.VMEM)
 HBM = pl.BlockSpec(memory_space=pltpu.HBM)
 PARAMS = pltpu.CompilerParams(vmem_limit_bytes=24 * 1024 * 1024)
@@ -37,6 +38,13 @@
         return pltpu.make_async_copy(genotypes.at[:, pl.ds(start, width)], held.at[d], sems.at[d])
 
     return [copy(d) for d in range(chips)]
+
+
+def store_bounded(partial, d, block):
+    rows, width = block.shape
+    partial[pl.ds(0, rows), pl.ds(d * width, width)] = block
+    top = jnp.max(jnp.abs(block), axis=0, keepdims=True)
+    partial[pl.ds(rows, SCALE_ROWS), pl.ds(d * width, width)] = jnp.broadcast_to(top, (SCALE_ROWS, width))
 
 
 def products(panel, held, partial):
@@ -66,10 +74,9 @@
     scales[0] = jnp.full(shape, numbers[0] * (1.0 / snps), f32)
     scales[1] = jnp.full(shape, numbers[1] * (1.0 / snps), f32)
     scales[2] = jnp.full(shape, numbers[2], f32)
-    width = held.shape[2]
     for d, move in enumerate(moves):
         move.wait()
-        partial[:, pl.ds(d * width, width)] = jnp.dot(built, held[d], preferred_element_type=f32)
+        store_bounded(partial, d, jnp.dot(built, held[d], preferred_element_type=f32))
 
 
 def load_first(probes, labels, variances, genotypes, chips, width, snps):
@@ -81,7 +88,7 @@
         out_specs=(VMEM,) * 6,
         out_shape=(
             pltpu.VMEM((chips, samples, width), genotypes.dtype),
-            pltpu.VMEM((rows, chips * width), f32),
+            pltpu.VMEM((rows + SCALE_ROWS, chips * width), f32),
             pltpu.VMEM((rows, samples), jnp.bfloat16),
             pltpu.VMEM(probes.shape, probes.dtype),
             pltpu.VMEM(probes.shape, jnp.int32),
@@ -102,10 +109,9 @@
     moves = copies(genotypes, held, sems, False)
     for move in moves:
         move.start()
-    width = held.shape[2]
     for d, move in enumerate(moves):
         move.wait()
-        partial[:, pl.ds(d * width, width)] = jnp.dot(panel[...], held[d], preferred_element_type=f32)
+        store_bounded(partial, d, jnp.dot(panel[...], held[d], preferred_element_type=f32))
 
 
 def load_second(panel, genotypes, chips, width):
@@ -116,7 +122,7 @@
         out_specs=(VMEM, VMEM),
         out_shape=(
             pltpu.VMEM((chips, samples, width), genotypes.dtype),
-            pltpu.VMEM((rows, chips * width), f32),
+            pltpu.VMEM((rows + SCALE_ROWS, chips * width), f32),
         ),
         scratch_shapes=[pltpu.SemaphoreType.DMA((chips,))],
         compiler_params=PARAMS,
@@ -234,12 +240,27 @@
     def between(block, step):
         return exchange(block, 2 * step + step % 2)
 
-    def reduce_panel(given, own, wire, probes, exact):
+    def pack(pair):
+        rows, columns = pair.shape[0] - SCALE_ROWS, pair.shape[1]
+        exponent = jnp.ceil(jnp.log2(jnp.maximum(pair[rows:], 1e-30)))
+        scaled = pair[:rows].reshape(-1, SCALE_ROWS, columns) * jnp.exp2(15.0 - exponent)
+        return jnp.concatenate([scaled.reshape(rows, columns), exponent], axis=0).astype(jnp.float16)
+
+    def unpack(block):
+        rows, columns = block.shape[0] - SCALE_ROWS, block.shape[1]
+        block = block.astype(f32)
+        scaled = block[:rows].reshape(-1, SCALE_ROWS, columns) * jnp.exp2(block[rows:] - 15.0)
+        return scaled.reshape(rows, columns)
+
+    def reduce_panel(given, own, probes, exact):
         width = own.shape[1] // chips
+        rows = ENVS * probes
         pair = own + exchange(given, 1).astype(f32)
-        total = pair[:, :width]
+        sent = pack(pair) if exact else pair.astype(jnp.bfloat16)
+        total = pair[:rows, :width]
         for step in far:
-            total = total + between(pair[:, step * width : (step + 1) * width].astype(wire), step).astype(f32)
+            taken = between(sent[:, step * width : (step + 1) * width], step)
+            total = total + (unpack(taken) if exact else taken.astype(f32))
         if exact:
             total = jnp.concatenate([total.reshape(ENVS, probes, width).sum(0), total], axis=0)
         return total.astype(jnp.bfloat16)
@@ -276,11 +297,11 @@
 
         held_other, given, panel, current, tags, scales = load_first(probes, labels, variances, genotypes, chips, width, snps)
         held_own, own = load_second(panel, genotypes, chips, width)
-        mine = reduce_panel(given, own, f32, count, True)
+        mine = reduce_panel(given, own, count, True)
         parts = spread(spread_image(mine, held_own, held_other, (tags, scales)))
         first, noise, panel, given = step_half(current, tags, scales, held_other, parts, jnp.bfloat16)
         own = panel_half(panel, held_own)
-        mine = reduce_panel(given, own, jnp.bfloat16, count, False)
+        mine = reduce_panel(given, own, count, False)
         parts = spread(spread_image(mine, held_own, held_other, (tags, scales)))
         return (first, tree_sum(parts) + noise)
 

time: 64.1 us -> 62.2 us (0.970)
  waiting for transfers between devices: 23.2 us -> 20.7 us
    ppermute x20, waiting for transfers between devices: 17.3 us -> 14.8 us  [exchange(): return lax.ppermute(block, 'samp', [(k, k ^ offset) for k in range(samp)])]
  transfers between devices with their start and end apart: 26 -> 26, of which waited for: 17 -> 17; matrix products, arithmetic and copies ran while one was open for 1% -> 1% of each run, Pallas kernels for 13% -> 14%
where the time goes in v6:
time: 62.2 us; the launch traced here: 62 us
  starting transfers between devices  25.4 us (41%)
  waiting for transfers between devices  20.7 us (33%)
  Pallas kernels  13.3 us (21%)
  other arithmetic  1.07 us (2%)
  between operations  0.85 us (1%)
  local copies, waits for them, and re-layouts  0.63 us (1%)
    ppermute x20, starting transfers between devices, exchange(): return lax.ppermute(block, 'samp', [(k, k ^ offset) for k in range(samp)])  16.5 us
    ppermute x20, waiting for transfers between devices, exchange(): return lax.ppermute(block, 'samp', [(k, k ^ offset) for k in range(samp)])  14.8 us
    ppermute x6, starting transfers between devices, spread(): lax.ppermute(weighted, 'snp', [(k, k ^ step) for k in range(snp)])  8.9 us
    pallas_call x12, Pallas kernels, image(): pl.pallas_call(functools.partial(image_body, blocks=tuple(blocks), pieces...  6.55 us
    ppermute x6, waiting for transfers between devices, spread(): lax.ppermute(weighted, 'snp', [(k, k ^ step) for k in range(snp)])  5.86 us
    pallas_call x1, Pallas kernels, load_first(): pl.pallas_call(functools.partial(first_body, snps=snps), in_specs=[HBM] *...  2.6 us
    pallas_call x1, Pallas kernels, load_second(): pl.pallas_call(second_body, in_specs=[VMEM, HBM], out_specs=(VMEM, VMEM),...  2.53 us
  transfers between devices with their start and end apart: 26, of which 17 were waited for; matrix products, arithmetic and copies ran while one was open for 1% of the time, Pallas kernels for 14%

profile of v6, /device:TPU:0, one launch (start us, length us, event | category | flops | bytes accessed | tf_op | source)
XLA Modules:
  0.0 62.0 jit_solution(17647191791826909390)
XLA Ops:
  0.6 2.6 %load_other.1 = (bf16[4,1024,512]{2,1,0:T(8,128)(2,1)S(1)}, f32[72,2048]{1,0:T(8,128)S(1)}, bf16[64,1024]{1,0:T(8,128)(2,1)S(1)}, bf16[8,1024]{1,0:T(8,128)(2,1)...) custom-call(bf16[8,1024]{1,0:T(8,128)(2,1)} %probes.1, s32[1,1024]{1,0:T(1,128)} %bitcast.14, f32[3]{0:T(128)} %variances.1, ...), custom_call_target="tpu_custom_call" | custom-call | tf_op jit(solution)/shard_map/load_other/pallas_call | solution.py:85
  3.2 0.6 collective-permute-start
  3.8 2.5 %load_own.1 = (bf16[4,1024,512]{2,1,0:T(8,128)(2,1)S(1)}, f32[72,2048]{1,0:T(8,128)S(1)}) custom-call(bf16[64,1024]{1,0:T(8,128)(2,1)S(1)} %get-tuple-element.18.panel, bf16[1024,4096]{1,0:T(8,128)(2,1)} %genotypes.3), custom_call_target="tpu_custom_call" | custom-call | tf_op jit(solution)/shard_map/load_own/pallas_call | solution.py:119
  6.3 0.1 add.39
  6.5 0.1 pad_maximum_fusion.4
  6.6 3.6 %collective-permute-start.1 = (f16[72,512]{1,0:T(8,128)(2,1)S(1)}, f16[72,512]{1,0:T(8,128)(2,1)S(1)}, u32[]{:S(2)}, u32[]{:S(2)}) collective-permute-start(f16[72,512]{1,0:T(8,128)(2,1)S(1)} %get-tuple-element.32), channel_id=1, source_target_pairs={{0,28},{4,24},{8,20},{12,16},{16,12},{20,8},{24,4},{28,0},{1,29},{... | collective-permute-start | bytes 221192 | tf_op jit(solution)/shard_map/ppermute | solution.py:238
  10.2 0.2 collective-permute-start.2
  10.4 0.5 collective-permute-start.3
  10.8 2.0 %collective-permute-done.1 = f16[72,512]{1,0:T(8,128)(2,1)S(1)} collective-permute-done((f16[72,512]{1,0:T(8,128)(2,1)S(1)}, f16[72,512]{1,0:T(8,128)(2,1)S(1)}, u32[]{:S(2)}, u32[]{:S(2)}) %collective-permute-start.1) | collective-permute-done | bytes 73760 | tf_op jit(solution)/shard_map/ppermute | solution.py:238
  12.9 1.7 %collective-permute-done.2 = f16[72,512]{1,0:T(8,128)(2,1)S(1)} collective-permute-done((f16[72,512]{1,0:T(8,128)(2,1)S(1)}, f16[72,512]{1,0:T(8,128)(2,1)S(1)}, u32[]{:S(2)}, u32[]{:S(2)}) %collective-permute-start.2) | collective-permute-done | bytes 73760 | tf_op jit(solution)/shard_map/ppermute | solution.py:238
  14.6 0.4 collective-permute-done.3
  15.1 0.1 bitcast_reduce_fusion
  15.1 1.3 %collective-permute-start.5 = (bf16[72,512]{1,0:T(8,128)(2,1)S(1)}, bf16[72,512]{1,0:T(8,128)(2,1)S(1)}, u32[]{:S(2)}, u32[]{:S(2)}) collective-permute-start(bf16[72,512]{1,0:T(8,128)(2,1)S(1)} %pad_maximum_fusion.5.refs_0_), channel_id=1, source_target_pairs={{0,16},{4,20},{8,24},{12,28},{16,0},{20,4},{24,8},{28,12},{1,17},{... | collective-permute-start | bytes 221192 | tf_op jit(solution)/shard_map/ppermute | solution.py:238
  16.4 0.7 %collective-permute-start.4 = (bf16[72,512]{1,0:T(8,128)(2,1)S(1)}, bf16[72,512]{1,0:T(8,128)(2,1)S(1)}, u32[]{:S(2)}, u32[]{:S(2)}) collective-permute-start(bf16[72,512]{1,0:T(8,128)(2,1)S(1)} %pad_maximum_fusion.5.refs_0_), channel_id=1, source_target_pairs={{0,12},{4,8},{8,4},{12,0},{16,28},{20,24},{24,20},{28,16},{1,13},{... | collective-permute-start | bytes 221192 | tf_op jit(solution)/shard_map/ppermute | solution.py:238
  17.1 1.3 %collective-permute-start.7 = (bf16[72,512]{1,0:T(8,128)(2,1)S(1)}, bf16[72,512]{1,0:T(8,128)(2,1)S(1)}, u32[]{:S(2)}, u32[]{:S(2)}) collective-permute-start(bf16[72,512]{1,0:T(8,128)(2,1)S(1)} %pad_maximum_fusion.5.refs_0_), channel_id=1, source_target_pairs={{0,28},{4,24},{8,20},{12,16},{16,12},{20,8},{24,4},{28,0},{1,29},{... | collective-permute-start | bytes 221192 | tf_op jit(solution)/shard_map/ppermute | solution.py:238
  18.4 1.1 %collective-permute-done.5.refs_1_ = bf16[72,512]{1,0:T(8,128)(2,1)S(1)} collective-permute-done((bf16[72,512]{1,0:T(8,128)(2,1)S(1)}, bf16[72,512]{1,0:T(8,128)(2,1)S(1)}, u32[]{:S(2)}, u32[]{:S(2)}) %collective-permute-start.5) | collective-permute-done | bytes 73760 | tf_op jit(solution)/shard_map/ppermute | solution.py:238
  19.5 1.4 %collective-permute-done.4.refs_0_ = bf16[72,512]{1,0:T(8,128)(2,1)S(1)} collective-permute-done((bf16[72,512]{1,0:T(8,128)(2,1)S(1)}, bf16[72,512]{1,0:T(8,128)(2,1)S(1)}, u32[]{:S(2)}, u32[]{:S(2)}) %collective-permute-start.4) | collective-permute-done | bytes 73760 | tf_op jit(solution)/shard_map/ppermute | solution.py:238
  20.9 0.2 collective-permute-start.6
  21.1 0.4 collective-permute-start.9
  21.5 0.5 collective-permute-done.7.refs_0_
  22.0 0.7 %collective-permute-start.8 = (bf16[72,512]{1,0:T(8,128)(2,1)S(1)}, bf16[72,512]{1,0:T(8,128)(2,1)S(1)}, u32[]{:S(2)}, u32[]{:S(2)}) collective-permute-start(bf16[72,512]{1,0:T(8,128)(2,1)S(1)} %collective-permute-done.7.refs_0_), channel_id=1, source_target_pairs={{0,4},{4,0},{8,12},{12,8},{16,20},{20,16},{24,28},{28,24},{1,5},{5... | collective-permute-start | bytes 221192 | tf_op jit(solution)/shard_map/ppermute | solution.py:238
  22.7 0.4 image.12.refs_2_
  23.1 0.4 image.13.refs_2_
  23.6 0.4 image.14.refs_2_
  24.0 0.4 image.15.refs_3_
  24.5 0.8 %image.16.refs_2_ = f32[72,1024]{1,0:T(8,128)S(1)} custom-call(bf16[72,512]{1,0:T(8,128)(2,1)S(1)} %collective-permute-done.4.refs_0_, bf16[72,512]{1,0:T(8,128)(2,1)S(1)} %collective-permute-done.5.refs_1_, bf16[4,1024,512]{2,1,0:T(8,128)(2,1)S(1)} %get-tuple-element.21.refs_1_.refs_2_.held, f32[72,1024]{1,0:T(8,128)S(1)} %image.15.refs_3_), custom_call_target="tpu_custom_call" | custom-call | tf_op jit(solution)/shard_map/image/pallas_call | solution.py:220
  25.2 0.8 %image.17.refs_0_ = f32[8,1024]{1,0:T(8,128)S(1)} custom-call(bf16[72,1024]{1,0:T(8,128)(2,1)S(1)} %collective-permute-done.6.refs_0_, bf16[4,1024,512]{2,1,0:T(8,128)(2,1)S(1)} %get-tuple-element.17.refs_1_.held, f32[72,1024]{1,0:T(8,128)S(1)} %image.16.refs_2_, s32[8,1024]{1,0:T(8,128)S(1)} %get-tuple-element.15.refs_3_.tags, ...), custom_call_target="tpu_custom_call" | custom-call | tf_op jit(solution)/shard_map/image/pallas_call | solution.py:220
  26.0 3.7 %collective-permute-start.12 = (f32[8,1024]{1,0:T(8,128)S(1)}, f32[8,1024]{1,0:T(8,128)S(1)}, u32[]{:S(2)}, u32[]{:S(2)}) collective-permute-start(f32[8,1024]{1,0:T(8,128)S(1)} %image.17.refs_0_), channel_id=1, source_target_pairs={{0,3},{1,2},{2,1},{3,0},{4,7},{5,6},{6,5},{7,4},{8,11},{9,10},{10,... | collective-permute-start | bytes 98312 | tf_op jit(solution)/shard_map/ppermute | solution.py:293
  29.7 0.8 %collective-permute-start.10 = (f32[8,1024]{1,0:T(8,128)S(1)}, f32[8,1024]{1,0:T(8,128)S(1)}, u32[]{:S(2)}, u32[]{:S(2)}) collective-permute-start(f32[8,1024]{1,0:T(8,128)S(1)} %image.17.refs_0_), channel_id=1, source_target_pairs={{0,1},{1,0},{2,3},{3,2},{4,5},{5,4},{6,7},{7,6},{8,9},{9,8},{10,11... | collective-permute-start | bytes 98312 | tf_op jit(solution)/shard_map/ppermute | solution.py:293
  30.5 1.3 %collective-permute-done.12.refs_3_ = f32[8,1024]{1,0:T(8,128)S(1)} collective-permute-done((f32[8,1024]{1,0:T(8,128)S(1)}, f32[8,1024]{1,0:T(8,128)S(1)}, u32[]{:S(2)}, u32[]{:S(2)}) %collective-permute-start.12) | collective-permute-done | bytes 32800 | tf_op jit(solution)/shard_map/ppermute | solution.py:293
  31.8 2.7 %collective-permute-done.11.refs_2_ = f32[8,1024]{1,0:T(8,128)S(1)} collective-permute-done((f32[8,1024]{1,0:T(8,128)S(1)}, f32[8,1024]{1,0:T(8,128)S(1)}, u32[]{:S(2)}, u32[]{:S(2)}) %collective-permute-start.11) | collective-permute-done | bytes 32800 | tf_op jit(solution)/shard_map/ppermute | solution.py:293
  34.5 0.8 %step_other.1 = (f32[8,1024]{1,0:T(8,128)S(1)}, f32[8,1024]{1,0:T(8,128)S(1)}, bf16[64,1024]{1,0:T(8,128)(2,1)S(1)}, bf16[64,2048]{1,0:T(8,128)(2,1)S(1)}) custom-call(bf16[8,1024]{1,0:T(8,128)(2,1)S(1)} %get-tuple-element.14.current, s32[8,1024]{1,0:T(8,128)S(1)} %get-tuple-element.15.refs_3_.tags, f32[3,8,1024]{2,1,0:T(8,128)S(1)} %get-tuple-element.16.refs_4_.scales, ...), custom_call_target="tpu_custom_call" | custom-call | tf_op jit(solution)/shard_map/step_other/pallas_call | solution.py:152
  35.3 0.1 collective-permute-start.13
  35.4 0.8 %step_own.1 = f32[64,2048]{1,0:T(8,128)S(1)} custom-call(bf16[64,1024]{1,0:T(8,128)(2,1)S(1)} %get-tuple-element.23.panel, bf16[4,1024,512]{2,1,0:T(8,128)(2,1)S(1)} %get-tuple-element.21.refs_1_.refs_2_.held), custom_call_target="tpu_custom_call" | custom-call | tf_op jit(solution)/shard_map/step_own/pallas_call | solution.py:173
  36.2 0.7 %collective-permute-done.13 = bf16[64,2048]{1,0:T(8,128)(2,1)S(1)} collective-permute-done((bf16[64,2048]{1,0:T(8,128)(2,1)S(1)}, bf16[64,2048]{1,0:T(8,128)(2,1)S(1)}, u32[]{:S(2)}, u32[]{:S(2)}) %collective-permute-start.13) | collective-permute-done | bytes 262176 | tf_op jit(solution)/shard_map/ppermute | solution.py:238
  36.9 0.1 fusion.17
  37.0 1.9 %collective-permute-start.14 = (bf16[64,512]{1,0:T(8,128)(2,1)S(1)}, bf16[64,512]{1,0:T(8,128)(2,1)S(1)}, u32[]{:S(2)}, u32[]{:S(2)}) collective-permute-start(bf16[64,512]{1,0:T(8,128)(2,1)S(1)} %get-tuple-element.35), channel_id=1, source_target_pairs={{0,28},{4,24},{8,20},{12,16},{16,12},{20,8},{24,4},{28,0},{1,29},{... | collective-permute-start | bytes 196616 | tf_op jit(solution)/shard_map/ppermute | solution.py:238
  38.9 1.0 %collective-permute-start.16 = (bf16[64,512]{1,0:T(8,128)(2,1)S(1)}, bf16[64,512]{1,0:T(8,128)(2,1)S(1)}, u32[]{:S(2)}, u32[]{:S(2)}) collective-permute-start(bf16[64,512]{1,0:T(8,128)(2,1)S(1)} %get-tuple-element.36), channel_id=1, source_target_pairs={{0,16},{4,20},{8,24},{12,28},{16,0},{20,4},{24,8},{28,12},{1,17},{... | collective-permute-start | bytes 196616 | tf_op jit(solution)/shard_map/ppermute | solution.py:238
  39.9 0.2 collective-permute-start.15
  40.0 2.1 %collective-permute-done.14 = bf16[64,512]{1,0:T(8,128)(2,1)S(1)} collective-permute-done((bf16[64,512]{1,0:T(8,128)(2,1)S(1)}, bf16[64,512]{1,0:T(8,128)(2,1)S(1)}, u32[]{:S(2)}, u32[]{:S(2)}) %collective-permute-start.14) | collective-permute-done | bytes 65568 | tf_op jit(solution)/shard_map/ppermute | solution.py:238
  42.1 1.7 %collective-permute-done.16 = bf16[64,512]{1,0:T(8,128)(2,1)S(1)} collective-permute-done((bf16[64,512]{1,0:T(8,128)(2,1)S(1)}, bf16[64,512]{1,0:T(8,128)(2,1)S(1)}, u32[]{:S(2)}, u32[]{:S(2)}) %collective-permute-start.16) | collective-permute-done | bytes 65568 | tf_op jit(solution)/shard_map/ppermute | solution.py:238
  43.8 0.2 collective-permute-done.15
  44.0 1.1 %collective-permute-start.18 = (bf16[64,512]{1,0:T(8,128)(2,1)S(1)}, bf16[64,512]{1,0:T(8,128)(2,1)S(1)}, u32[]{:S(2)}, u32[]{:S(2)}) collective-permute-start(bf16[64,512]{1,0:T(8,128)(2,1)S(1)} %fusion.3.refs_0_), channel_id=1, source_target_pairs={{0,16},{4,20},{8,24},{12,28},{16,0},{20,4},{24,8},{28,12},{1,17},{... | collective-permute-start | bytes 196616 | tf_op jit(solution)/shard_map/ppermute | solution.py:238
  45.1 0.4 collective-permute-start.17
  45.5 1.8 %collective-permute-start.20 = (bf16[64,512]{1,0:T(8,128)(2,1)S(1)}, bf16[64,512]{1,0:T(8,128)(2,1)S(1)}, u32[]{:S(2)}, u32[]{:S(2)}) collective-permute-start(bf16[64,512]{1,0:T(8,128)(2,1)S(1)} %fusion.3.refs_0_), channel_id=1, source_target_pairs={{0,28},{4,24},{8,20},{12,16},{16,12},{20,8},{24,4},{28,0},{1,29},{... | collective-permute-start | bytes 196616 | tf_op jit(solution)/shard_map/ppermute | solution.py:238
  47.3 1.1 %collective-permute-done.18.refs_1_ = bf16[64,512]{1,0:T(8,128)(2,1)S(1)} collective-permute-done((bf16[64,512]{1,0:T(8,128)(2,1)S(1)}, bf16[64,512]{1,0:T(8,128)(2,1)S(1)}, u32[]{:S(2)}, u32[]{:S(2)}) %collective-permute-start.18) | collective-permute-done | bytes 65568 | tf_op jit(solution)/shard_map/ppermute | solution.py:238
  48.3 1.2 %collective-permute-done.17.refs_0_ = bf16[64,512]{1,0:T(8,128)(2,1)S(1)} collective-permute-done((bf16[64,512]{1,0:T(8,128)(2,1)S(1)}, bf16[64,512]{1,0:T(8,128)(2,1)S(1)}, u32[]{:S(2)}, u32[]{:S(2)}) %collective-permute-start.17) | collective-permute-done | bytes 65568 | tf_op jit(solution)/shard_map/ppermute | solution.py:238
  49.5 0.2 collective-permute-start.19
  49.7 0.4 collective-permute-start.22
  50.1 0.8 %collective-permute-done.20.refs_0_ = bf16[64,512]{1,0:T(8,128)(2,1)S(1)} collective-permute-done((bf16[64,512]{1,0:T(8,128)(2,1)S(1)}, bf16[64,512]{1,0:T(8,128)(2,1)S(1)}, u32[]{:S(2)}, u32[]{:S(2)}) %collective-permute-start.20) | collective-permute-done | bytes 65568 | tf_op jit(solution)/shard_map/ppermute | solution.py:238
  50.9 0.3 collective-permute-start.21
  51.2 0.4 image.18.refs_2_
  51.6 0.4 image.19.refs_2_
  52.0 0.4 image.20.refs_2_
  52.5 0.4 image.21.refs_3_
  52.9 0.8 %image.22.refs_2_ = f32[64,1024]{1,0:T(8,128)S(1)} custom-call(bf16[64,512]{1,0:T(8,128)(2,1)S(1)} %collective-permute-done.17.refs_0_, bf16[64,512]{1,0:T(8,128)(2,1)S(1)} %collective-permute-done.18.refs_1_, bf16[4,1024,512]{2,1,0:T(8,128)(2,1)S(1)} %get-tuple-element.21.refs_1_.refs_2_.held, f32[64,1024]{1,0:T(8,128)S(1)} %image.21.refs_3_), custom_call_target="tpu_custom_call" | custom-call | tf_op jit(solution)/shard_map/image/pallas_call | solution.py:220
  53.7 0.8 %image.23 = f32[8,1024]{1,0:T(8,128)S(1)} custom-call(bf16[64,1024]{1,0:T(8,128)(2,1)S(1)} %collective-permute-done.19.refs_0_, bf16[4,1024,512]{2,1,0:T(8,128)(2,1)S(1)} %get-tuple-element.17.refs_1_.held, f32[64,1024]{1,0:T(8,128)S(1)} %image.22.refs_2_, s32[8,1024]{1,0:T(8,128)S(1)} %get-tuple-element.15.refs_3_.tags, ...), custom_call_target="tpu_custom_call" | custom-call | tf_op jit(solution)/shard_map/image/pallas_call | solution.py:220
  54.5 1.7 %collective-permute-start.25 = (f32[8,1024]{1,0:T(8,128)S(1)}, f32[8,1024]{1,0:T(8,128)S(1)}, u32[]{:S(2)}, u32[]{:S(2)}) collective-permute-start(f32[8,1024]{1,0:T(8,128)S(1)} %image.23), channel_id=1, source_target_pairs={{0,3},{1,2},{2,1},{3,0},{4,7},{5,6},{6,5},{7,4},{8,11},{9,10},{10,... | collective-permute-start | bytes 98312 | tf_op jit(solution)/shard_map/ppermute | solution.py:293
  56.2 0.5 collective-permute-start.24
  56.6 2.3 %collective-permute-start.23 = (f32[8,1024]{1,0:T(8,128)S(1)}, f32[8,1024]{1,0:T(8,128)S(1)}, u32[]{:S(2)}, u32[]{:S(2)}) collective-permute-start(f32[8,1024]{1,0:T(8,128)S(1)} %image.23), channel_id=1, source_target_pairs={{0,1},{1,0},{2,3},{3,2},{4,5},{5,4},{6,7},{7,6},{8,9},{9,8},{10,11... | collective-permute-start | bytes 98312 | tf_op jit(solution)/shard_map/ppermute | solution.py:293
  58.9 0.6 copy.6
  59.5 1.1 %collective-permute-done.25 = f32[8,1024]{1,0:T(8,128)S(1)} collective-permute-done((f32[8,1024]{1,0:T(8,128)S(1)}, f32[8,1024]{1,0:T(8,128)S(1)}, u32[]{:S(2)}, u32[]{:S(2)}) %collective-permute-start.25) | collective-permute-done | bytes 32800 | tf_op jit(solution)/shard_map/ppermute | solution.py:293
  60.6 0.8 %collective-permute-done.24 = f32[8,1024]{1,0:T(8,128)S(1)} collective-permute-done((f32[8,1024]{1,0:T(8,128)S(1)}, f32[8,1024]{1,0:T(8,128)S(1)}, u32[]{:S(2)}, u32[]{:S(2)}) %collective-permute-start.24) | collective-permute-done | bytes 32800 | tf_op jit(solution)/shard_map/ppermute | solution.py:293
  61.3 0.6 %add_add_fusion = f32[8,1024]{1,0:T(8,128)} fusion(f32[8,1024]{1,0:T(8,128)S(1)} %get-tuple-element.25, f32[8,1024]{1,0:T(8,128)S(1)} %collective-permute-done.24, f32[8,1024]{1,0:T(8,128)S(1)} %collective-permute-done.25, f32[8,1024]{1,0:T(8,128)S(1)} %image.23, f32[8,1024]{1,0:T(8,128)S(1)} %collective-permute-done.23), kind=kLoop, calls=%fused_computation.26 | loop fusion | flops 32768 | bytes 196608 | tf_op jit(solution)/shard_map/add | solution.py:306
  (23 shorter events, 0.3 us)
Async XLA Ops:
  3.2 3.1 %collective-permute-start = (f32[72,2048]{1,0:T(8,128)S(1)}, f32[72,2048]{1,0:T(8,128)S(1)}, u32[]{:S(2)}, u32[]{:S(2)}) collective-permute-start(f32[72,2048]{1,0:T(8,128)S(1)} %get-tuple-element.20), channel_id=1, source_target_pairs={{0,4},{4,0},{8,12},{12,8},{16,20},{20,16},{24,28},{28,24},{1,5},{5... | collective-permute-start | bytes 1769480 | tf_op jit(solution)/shard_map/ppermute | solution.py:238
  6.6 6.3 %collective-permute-start.1 = (f16[72,512]{1,0:T(8,128)(2,1)S(1)}, f16[72,512]{1,0:T(8,128)(2,1)S(1)}, u32[]{:S(2)}, u32[]{:S(2)}) collective-permute-start(f16[72,512]{1,0:T(8,128)(2,1)S(1)} %get-tuple-element.32), channel_id=1, source_target_pairs={{0,28},{4,24},{8,20},{12,16},{16,12},{20,8},{24,4},{28,0},{1,29},{... | collective-permute-start | bytes 221192 | tf_op jit(solution)/shard_map/ppermute | solution.py:238
  10.2 4.4 %collective-permute-start.2 = (f16[72,512]{1,0:T(8,128)(2,1)S(1)}, f16[72,512]{1,0:T(8,128)(2,1)S(1)}, u32[]{:S(2)}, u32[]{:S(2)}) collective-permute-start(f16[72,512]{1,0:T(8,128)(2,1)S(1)} %get-tuple-element.33), channel_id=1, source_target_pairs={{0,12},{4,8},{8,4},{12,0},{16,28},{20,24},{24,20},{28,16},{1,13},{... | collective-permute-start | bytes 221192 | tf_op jit(solution)/shard_map/ppermute | solution.py:238
  10.4 4.7 %collective-permute-start.3 = (f16[72,512]{1,0:T(8,128)(2,1)S(1)}, f16[72,512]{1,0:T(8,128)(2,1)S(1)}, u32[]{:S(2)}, u32[]{:S(2)}) collective-permute-start(f16[72,512]{1,0:T(8,128)(2,1)S(1)} %get-tuple-element.34), channel_id=1, source_target_pairs={{0,16},{4,20},{8,24},{12,28},{16,0},{20,4},{24,8},{28,12},{1,17},{... | collective-permute-start | bytes 221192 | tf_op jit(solution)/shard_map/ppermute | solution.py:238
  15.1 4.4 %collective-permute-start.5 = (bf16[72,512]{1,0:T(8,128)(2,1)S(1)}, bf16[72,512]{1,0:T(8,128)(2,1)S(1)}, u32[]{:S(2)}, u32[]{:S(2)}) collective-permute-start(bf16[72,512]{1,0:T(8,128)(2,1)S(1)} %pad_maximum_fusion.5.refs_0_), channel_id=1, source_target_pairs={{0,16},{4,20},{8,24},{12,28},{16,0},{20,4},{24,8},{28,12},{1,17},{... | collective-permute-start | bytes 221192 | tf_op jit(solution)/shard_map/ppermute | solution.py:238
  16.4 4.5 %collective-permute-start.4 = (bf16[72,512]{1,0:T(8,128)(2,1)S(1)}, bf16[72,512]{1,0:T(8,128)(2,1)S(1)}, u32[]{:S(2)}, u32[]{:S(2)}) collective-permute-start(bf16[72,512]{1,0:T(8,128)(2,1)S(1)} %pad_maximum_fusion.5.refs_0_), channel_id=1, source_target_pairs={{0,12},{4,8},{8,4},{12,0},{16,28},{20,24},{24,20},{28,16},{1,13},{... | collective-permute-start | bytes 221192 | tf_op jit(solution)/shard_map/ppermute | solution.py:238
  17.1 4.9 %collective-permute-start.7 = (bf16[72,512]{1,0:T(8,128)(2,1)S(1)}, bf16[72,512]{1,0:T(8,128)(2,1)S(1)}, u32[]{:S(2)}, u32[]{:S(2)}) collective-permute-start(bf16[72,512]{1,0:T(8,128)(2,1)S(1)} %pad_maximum_fusion.5.refs_0_), channel_id=1, source_target_pairs={{0,28},{4,24},{8,20},{12,16},{16,12},{20,8},{24,4},{28,0},{1,29},{... | collective-permute-start | bytes 221192 | tf_op jit(solution)/shard_map/ppermute | solution.py:238
  20.9 4.3 %collective-permute-start.6 = (bf16[72,1024]{1,0:T(8,128)(2,1)S(1)}, bf16[72,1024]{1,0:T(8,128)(2,1)S(1)}, u32[]{:S(2)}, u32[]{:S(2)}) collective-permute-start(bf16[72,1024]{1,0:T(8,128)(2,1)S(1)} %pad_maximum_fusion), channel_id=1, source_target_pairs={{0,4},{4,0},{8,12},{12,8},{16,20},{20,16},{24,28},{28,24},{1,5},{5... | collective-permute-start | bytes 442376 | tf_op jit(solution)/shard_map/ppermute | solution.py:238
  21.1 2.0 %collective-permute-start.9 = (bf16[72,512]{1,0:T(8,128)(2,1)S(1)}, bf16[72,512]{1,0:T(8,128)(2,1)S(1)}, u32[]{:S(2)}, u32[]{:S(2)}) collective-permute-start(bf16[72,512]{1,0:T(8,128)(2,1)S(1)} %pad_maximum_fusion.5.refs_0_), channel_id=1, source_target_pairs={{0,4},{4,0},{8,12},{12,8},{16,20},{20,16},{24,28},{28,24},{1,5},{5... | collective-permute-start | bytes 221192 | tf_op jit(solution)/shard_map/ppermute | solution.py:238
  22.0 2.0 %collective-permute-start.8 = (bf16[72,512]{1,0:T(8,128)(2,1)S(1)}, bf16[72,512]{1,0:T(8,128)(2,1)S(1)}, u32[]{:S(2)}, u32[]{:S(2)}) collective-permute-start(bf16[72,512]{1,0:T(8,128)(2,1)S(1)} %collective-permute-done.7.refs_0_), channel_id=1, source_target_pairs={{0,4},{4,0},{8,12},{12,8},{16,20},{20,16},{24,28},{28,24},{1,5},{5... | collective-permute-start | bytes 221192 | tf_op jit(solution)/shard_map/ppermute | solution.py:238
  26.0 5.8 %collective-permute-start.12 = (f32[8,1024]{1,0:T(8,128)S(1)}, f32[8,1024]{1,0:T(8,128)S(1)}, u32[]{:S(2)}, u32[]{:S(2)}) collective-permute-start(f32[8,1024]{1,0:T(8,128)S(1)} %image.17.refs_0_), channel_id=1, source_target_pairs={{0,3},{1,2},{2,1},{3,0},{4,7},{5,6},{6,5},{7,4},{8,11},{9,10},{10,... | collective-permute-start | bytes 98312 | tf_op jit(solution)/shard_map/ppermute | solution.py:293
  29.7 4.8 %collective-permute-start.11 = (f32[8,1024]{1,0:T(8,128)S(1)}, f32[8,1024]{1,0:T(8,128)S(1)}, u32[]{:S(2)}, u32[]{:S(2)}) collective-permute-start(f32[8,1024]{1,0:T(8,128)S(1)} %image.17.refs_0_), channel_id=1, source_target_pairs={{0,2},{1,3},{2,0},{3,1},{4,6},{5,7},{6,4},{7,5},{8,10},{9,11},{10,... | collective-permute-start | bytes 98312 | tf_op jit(solution)/shard_map/ppermute | solution.py:293
  29.7 4.8 %collective-permute-start.10 = (f32[8,1024]{1,0:T(8,128)S(1)}, f32[8,1024]{1,0:T(8,128)S(1)}, u32[]{:S(2)}, u32[]{:S(2)}) collective-permute-start(f32[8,1024]{1,0:T(8,128)S(1)} %image.17.refs_0_), channel_id=1, source_target_pairs={{0,1},{1,0},{2,3},{3,2},{4,5},{5,4},{6,7},{7,6},{8,9},{9,8},{10,11... | collective-permute-start | bytes 98312 | tf_op jit(solution)/shard_map/ppermute | solution.py:293
  35.3 1.6 %collective-permute-start.13 = (bf16[64,2048]{1,0:T(8,128)(2,1)S(1)}, bf16[64,2048]{1,0:T(8,128)(2,1)S(1)}, u32[]{:S(2)}, u32[]{:S(2)}) collective-permute-start(bf16[64,2048]{1,0:T(8,128)(2,1)S(1)} %get-tuple-element.24), channel_id=1, source_target_pairs={{0,4},{4,0},{8,12},{12,8},{16,20},{20,16},{24,28},{28,24},{1,5},{5... | collective-permute-start | bytes 786440 | tf_op jit(solution)/shard_map/ppermute | solution.py:238
  37.0 5.1 %collective-permute-start.14 = (bf16[64,512]{1,0:T(8,128)(2,1)S(1)}, bf16[64,512]{1,0:T(8,128)(2,1)S(1)}, u32[]{:S(2)}, u32[]{:S(2)}) collective-permute-start(bf16[64,512]{1,0:T(8,128)(2,1)S(1)} %get-tuple-element.35), channel_id=1, source_target_pairs={{0,28},{4,24},{8,20},{12,16},{16,12},{20,8},{24,4},{28,0},{1,29},{... | collective-permute-start | bytes 196616 | tf_op jit(solution)/shard_map/ppermute | solution.py:238
  38.9 4.9 %collective-permute-start.16 = (bf16[64,512]{1,0:T(8,128)(2,1)S(1)}, bf16[64,512]{1,0:T(8,128)(2,1)S(1)}, u32[]{:S(2)}, u32[]{:S(2)}) collective-permute-start(bf16[64,512]{1,0:T(8,128)(2,1)S(1)} %get-tuple-element.36), channel_id=1, source_target_pairs={{0,16},{4,20},{8,24},{12,28},{16,0},{20,4},{24,8},{28,12},{1,17},{... | collective-permute-start | bytes 196616 | tf_op jit(solution)/shard_map/ppermute | solution.py:238
  39.9 4.1 %collective-permute-start.15 = (bf16[64,512]{1,0:T(8,128)(2,1)S(1)}, bf16[64,512]{1,0:T(8,128)(2,1)S(1)}, u32[]{:S(2)}, u32[]{:S(2)}) collective-permute-start(bf16[64,512]{1,0:T(8,128)(2,1)S(1)} %get-tuple-element.37), channel_id=1, source_target_pairs={{0,12},{4,8},{8,4},{12,0},{16,28},{20,24},{24,20},{28,16},{1,13},{... | collective-permute-start | bytes 196616 | tf_op jit(solution)/shard_map/ppermute | solution.py:238
  44.0 4.3 %collective-permute-start.18 = (bf16[64,512]{1,0:T(8,128)(2,1)S(1)}, bf16[64,512]{1,0:T(8,128)(2,1)S(1)}, u32[]{:S(2)}, u32[]{:S(2)}) collective-permute-start(bf16[64,512]{1,0:T(8,128)(2,1)S(1)} %fusion.3.refs_0_), channel_id=1, source_target_pairs={{0,16},{4,20},{8,24},{12,28},{16,0},{20,4},{24,8},{28,12},{1,17},{... | collective-permute-start | bytes 196616 | tf_op jit(solution)/shard_map/ppermute | solution.py:238
  45.1 4.4 %collective-permute-start.17 = (bf16[64,512]{1,0:T(8,128)(2,1)S(1)}, bf16[64,512]{1,0:T(8,128)(2,1)S(1)}, u32[]{:S(2)}, u32[]{:S(2)}) collective-permute-start(bf16[64,512]{1,0:T(8,128)(2,1)S(1)} %fusion.3.refs_0_), channel_id=1, source_target_pairs={{0,12},{4,8},{8,4},{12,0},{16,28},{20,24},{24,20},{28,16},{1,13},{... | collective-permute-start | bytes 196616 | tf_op jit(solution)/shard_map/ppermute | solution.py:238
  45.5 5.4 %collective-permute-start.20 = (bf16[64,512]{1,0:T(8,128)(2,1)S(1)}, bf16[64,512]{1,0:T(8,128)(2,1)S(1)}, u32[]{:S(2)}, u32[]{:S(2)}) collective-permute-start(bf16[64,512]{1,0:T(8,128)(2,1)S(1)} %fusion.3.refs_0_), channel_id=1, source_target_pairs={{0,28},{4,24},{8,20},{12,16},{16,12},{20,8},{24,4},{28,0},{1,29},{... | collective-permute-start | bytes 196616 | tf_op jit(solution)/shard_map/ppermute | solution.py:238
  49.5 4.2 %collective-permute-start.19 = (bf16[64,1024]{1,0:T(8,128)(2,1)S(1)}, bf16[64,1024]{1,0:T(8,128)(2,1)S(1)}, u32[]{:S(2)}, u32[]{:S(2)}) collective-permute-start(bf16[64,1024]{1,0:T(8,128)(2,1)S(1)} %pad_maximum_fusion.1), channel_id=1, source_target_pairs={{0,4},{4,0},{8,12},{12,8},{16,20},{20,16},{24,28},{28,24},{1,5},{5... | collective-permute-start | bytes 393224 | tf_op jit(solution)/shard_map/ppermute | solution.py:238
  49.7 1.9 %collective-permute-start.22 = (bf16[64,512]{1,0:T(8,128)(2,1)S(1)}, bf16[64,512]{1,0:T(8,128)(2,1)S(1)}, u32[]{:S(2)}, u32[]{:S(2)}) collective-permute-start(bf16[64,512]{1,0:T(8,128)(2,1)S(1)} %fusion.3.refs_0_), channel_id=1, source_target_pairs={{0,4},{4,0},{8,12},{12,8},{16,20},{20,16},{24,28},{28,24},{1,5},{5... | collective-permute-start | bytes 196616 | tf_op jit(solution)/shard_map/ppermute | solution.py:238
  50.9 1.6 %collective-permute-start.21 = (bf16[64,512]{1,0:T(8,128)(2,1)S(1)}, bf16[64,512]{1,0:T(8,128)(2,1)S(1)}, u32[]{:S(2)}, u32[]{:S(2)}) collective-permute-start(bf16[64,512]{1,0:T(8,128)(2,1)S(1)} %collective-permute-done.20.refs_0_), channel_id=1, source_target_pairs={{0,4},{4,0},{8,12},{12,8},{16,20},{20,16},{24,28},{28,24},{1,5},{5... | collective-permute-start | bytes 196616 | tf_op jit(solution)/shard_map/ppermute | solution.py:238
  54.5 6.1 %collective-permute-start.25 = (f32[8,1024]{1,0:T(8,128)S(1)}, f32[8,1024]{1,0:T(8,128)S(1)}, u32[]{:S(2)}, u32[]{:S(2)}) collective-permute-start(f32[8,1024]{1,0:T(8,128)S(1)} %image.23), channel_id=1, source_target_pairs={{0,3},{1,2},{2,1},{3,0},{4,7},{5,6},{6,5},{7,4},{8,11},{9,10},{10,... | collective-permute-start | bytes 98312 | tf_op jit(solution)/shard_map/ppermute | solution.py:293
  56.2 5.2 %collective-permute-start.24 = (f32[8,1024]{1,0:T(8,128)S(1)}, f32[8,1024]{1,0:T(8,128)S(1)}, u32[]{:S(2)}, u32[]{:S(2)}) collective-permute-start(f32[8,1024]{1,0:T(8,128)S(1)} %image.23), channel_id=1, source_target_pairs={{0,2},{1,3},{2,0},{3,1},{4,6},{5,7},{6,4},{7,5},{8,10},{9,11},{10,... | collective-permute-start | bytes 98312 | tf_op jit(solution)/shard_map/ppermute | solution.py:293
  56.6 4.7 %collective-permute-start.23 = (f32[8,1024]{1,0:T(8,128)S(1)}, f32[8,1024]{1,0:T(8,128)S(1)}, u32[]{:S(2)}, u32[]{:S(2)}) collective-permute-start(f32[8,1024]{1,0:T(8,128)S(1)} %image.23), channel_id=1, source_target_pairs={{0,1},{1,0},{2,3},{3,2},{4,5},{5,4},{6,7},{7,6},{8,9},{9,8},{10,11... | collective-permute-start | bytes 98312 | tf_op jit(solution)/shard_map/ppermute | solution.py:293

commit v7 on v6

--- a/solution.py
+++ b/solution.py
@@ -231,8 +231,9 @@
     samp, snp = mesh.shape["samp"], mesh.shape["snp"]
     chips = samp // 2
     far = sorted(range(1, chips), key=lambda step: -bin(step).count("1"))
-    early = far[: chips // 2 - 1]
-    late = far[chips // 2 - 1 :]
+    near = [1] + [step for step in far if step != 1]
+    early = near[: chips // 2 - 1]
+    late = near[chips // 2 - 1 :]
 
     def exchange(block, offset):
         return lax.ppermute(block, "samp", [(k, k ^ offset) for k in range(samp)])
@@ -267,7 +268,7 @@
 
     def spread_image(mine, held_own, held_other, finish):
         pieces = {}
-        for step in far:
+        for step in near:
             pieces[step] = between(mine, step)
         other = exchange(mine, 1)
         total = image([mine], held_own, [0])

time: 62.2 us -> 62.8 us (level)
  waiting for transfers between devices: 20.7 us -> 22 us
  starting transfers between devices: 25.4 us -> 24.7 us
    ppermute x20, waiting for transfers between devices: 14.8 us -> 16 us  [exchange(): return lax.ppermute(block, 'samp', [(k, k ^ offset) for k in range(samp)])]
    ppermute x20, starting transfers between devices: 16.5 us -> 15.8 us  [exchange(): return lax.ppermute(block, 'samp', [(k, k ^ offset) for k in range(samp)])]
  transfers between devices with their start and end apart: 26 -> 26, of which waited for: 17 -> 18; matrix products, arithmetic and copies ran while one was open for 1% -> 1% of each run, Pallas kernels for 14% -> 13%
where the time goes in v7:
time: 62.8 us; the launch traced here: 62.5 us
  starting transfers between devices  24.7 us (39%)
  waiting for transfers between devices  22 us (35%)
  Pallas kernels  13.3 us (21%)
  other arithmetic  1.07 us (2%)
  between operations  0.85 us (1%)
  local copies, waits for them, and re-layouts  0.63 us (1%)
    ppermute x20, waiting for transfers between devices, exchange(): return lax.ppermute(block, 'samp', [(k, k ^ offset) for k in range(samp)])  16 us
    ppermute x20, starting transfers between devices, exchange(): return lax.ppermute(block, 'samp', [(k, k ^ offset) for k in range(samp)])  15.8 us
    ppermute x6, starting transfers between devices, spread(): lax.ppermute(weighted, 'snp', [(k, k ^ step) for k in range(snp)])  8.9 us
    pallas_call x12, Pallas kernels, image(): pl.pallas_call(functools.partial(image_body, blocks=tuple(blocks), pieces...  6.55 us
    ppermute x6, waiting for transfers between devices, spread(): lax.ppermute(weighted, 'snp', [(k, k ^ step) for k in range(snp)])  5.94 us
    pallas_call x1, Pallas kernels, load_first(): pl.pallas_call(functools.partial(first_body, snps=snps), in_specs=[HBM] *...  2.6 us
    pallas_call x1, Pallas kernels, load_second(): pl.pallas_call(second_body, in_specs=[VMEM, HBM], out_specs=(VMEM, VMEM),...  2.53 us
  transfers between devices with their start and end apart: 26, of which 18 were waited for; matrix products, arithmetic and copies ran while one was open for 1% of the time, Pallas kernels for 13%

profile of v7, /device:TPU:0, one launch (start us, length us, event | category | flops | bytes accessed | tf_op | source)
XLA Modules:
  0.0 62.5 jit_solution(2336595584478237000)
XLA Ops:
  0.6 2.6 %load_other.1 = (bf16[4,1024,512]{2,1,0:T(8,128)(2,1)S(1)}, f32[72,2048]{1,0:T(8,128)S(1)}, bf16[64,1024]{1,0:T(8,128)(2,1)S(1)}, bf16[8,1024]{1,0:T(8,128)(2,1)...) custom-call(bf16[8,1024]{1,0:T(8,128)(2,1)} %probes.1, s32[1,1024]{1,0:T(1,128)} %bitcast.14, f32[3]{0:T(128)} %variances.1, ...), custom_call_target="tpu_custom_call" | custom-call | tf_op jit(solution)/shard_map/load_other/pallas_call | solution.py:85
  3.2 0.6 collective-permute-start
  3.8 2.5 %load_own.1 = (bf16[4,1024,512]{2,1,0:T(8,128)(2,1)S(1)}, f32[72,2048]{1,0:T(8,128)S(1)}) custom-call(bf16[64,1024]{1,0:T(8,128)(2,1)S(1)} %get-tuple-element.18.panel, bf16[1024,4096]{1,0:T(8,128)(2,1)} %genotypes.3), custom_call_target="tpu_custom_call" | custom-call | tf_op jit(solution)/shard_map/load_own/pallas_call | solution.py:119
  6.3 0.1 add.39
  6.5 0.1 pad_maximum_fusion.4
  6.6 3.6 %collective-permute-start.1 = (f16[72,512]{1,0:T(8,128)(2,1)S(1)}, f16[72,512]{1,0:T(8,128)(2,1)S(1)}, u32[]{:S(2)}, u32[]{:S(2)}) collective-permute-start(f16[72,512]{1,0:T(8,128)(2,1)S(1)} %get-tuple-element.32), channel_id=1, source_target_pairs={{0,28},{4,24},{8,20},{12,16},{16,12},{20,8},{24,4},{28,0},{1,29},{... | collective-permute-start | bytes 221192 | tf_op jit(solution)/shard_map/ppermute | solution.py:239
  10.2 0.2 collective-permute-start.2
  10.4 0.5 collective-permute-start.3
  10.8 2.0 %collective-permute-done.1 = f16[72,512]{1,0:T(8,128)(2,1)S(1)} collective-permute-done((f16[72,512]{1,0:T(8,128)(2,1)S(1)}, f16[72,512]{1,0:T(8,128)(2,1)S(1)}, u32[]{:S(2)}, u32[]{:S(2)}) %collective-permute-start.1) | collective-permute-done | bytes 73760 | tf_op jit(solution)/shard_map/ppermute | solution.py:239
  12.9 1.7 %collective-permute-done.2 = f16[72,512]{1,0:T(8,128)(2,1)S(1)} collective-permute-done((f16[72,512]{1,0:T(8,128)(2,1)S(1)}, f16[72,512]{1,0:T(8,128)(2,1)S(1)}, u32[]{:S(2)}, u32[]{:S(2)}) %collective-permute-start.2) | collective-permute-done | bytes 73760 | tf_op jit(solution)/shard_map/ppermute | solution.py:239
  14.6 0.4 collective-permute-done.3
  15.1 1.3 %collective-permute-start.5 = (bf16[72,512]{1,0:T(8,128)(2,1)S(1)}, bf16[72,512]{1,0:T(8,128)(2,1)S(1)}, u32[]{:S(2)}, u32[]{:S(2)}) collective-permute-start(bf16[72,512]{1,0:T(8,128)(2,1)S(1)} %pad_maximum_fusion.5.refs_0_), channel_id=1, source_target_pairs={{0,16},{4,20},{8,24},{12,28},{16,0},{20,4},{24,8},{28,12},{1,17},{... | collective-permute-start | bytes 221192 | tf_op jit(solution)/shard_map/ppermute | solution.py:239
  16.4 1.0 %collective-permute-start.4 = (bf16[72,512]{1,0:T(8,128)(2,1)S(1)}, bf16[72,512]{1,0:T(8,128)(2,1)S(1)}, u32[]{:S(2)}, u32[]{:S(2)}) collective-permute-start(bf16[72,512]{1,0:T(8,128)(2,1)S(1)} %pad_maximum_fusion.5.refs_0_), channel_id=1, source_target_pairs={{0,28},{4,24},{8,20},{12,16},{16,12},{20,8},{24,4},{28,0},{1,29},{... | collective-permute-start | bytes 221192 | tf_op jit(solution)/shard_map/ppermute | solution.py:239
  17.4 1.0 %collective-permute-start.7 = (bf16[72,512]{1,0:T(8,128)(2,1)S(1)}, bf16[72,512]{1,0:T(8,128)(2,1)S(1)}, u32[]{:S(2)}, u32[]{:S(2)}) collective-permute-start(bf16[72,512]{1,0:T(8,128)(2,1)S(1)} %pad_maximum_fusion.5.refs_0_), channel_id=1, source_target_pairs={{0,12},{4,8},{8,4},{12,0},{16,28},{20,24},{24,20},{28,16},{1,13},{... | collective-permute-start | bytes 221192 | tf_op jit(solution)/shard_map/ppermute | solution.py:239
  18.4 1.1 %collective-permute-done.5.refs_1_ = bf16[72,512]{1,0:T(8,128)(2,1)S(1)} collective-permute-done((bf16[72,512]{1,0:T(8,128)(2,1)S(1)}, bf16[72,512]{1,0:T(8,128)(2,1)S(1)}, u32[]{:S(2)}, u32[]{:S(2)}) %collective-permute-start.5) | collective-permute-done | bytes 73760 | tf_op jit(solution)/shard_map/ppermute | solution.py:239
  19.5 2.3 %collective-permute-done.4.refs_0_ = bf16[72,512]{1,0:T(8,128)(2,1)S(1)} collective-permute-done((bf16[72,512]{1,0:T(8,128)(2,1)S(1)}, bf16[72,512]{1,0:T(8,128)(2,1)S(1)}, u32[]{:S(2)}, u32[]{:S(2)}) %collective-permute-start.4) | collective-permute-done | bytes 73760 | tf_op jit(solution)/shard_map/ppermute | solution.py:239
  21.8 0.1 collective-permute-start.6
  22.0 0.4 collective-permute-start.9
  22.4 0.1 collective-permute-start.8
  22.5 0.4 image.12.refs_2_
  22.9 0.4 collective-permute-done.9.refs_0_
  23.4 0.4 image.13.refs_2_
  23.8 0.4 image.14.refs_2_
  24.3 0.4 image.15.refs_3_
  24.7 0.8 %image.16.refs_2_ = f32[72,1024]{1,0:T(8,128)S(1)} custom-call(bf16[72,512]{1,0:T(8,128)(2,1)S(1)} %collective-permute-done.4.refs_0_, bf16[72,512]{1,0:T(8,128)(2,1)S(1)} %collective-permute-done.5.refs_1_, bf16[4,1024,512]{2,1,0:T(8,128)(2,1)S(1)} %get-tuple-element.21.refs_1_.refs_2_.held, f32[72,1024]{1,0:T(8,128)S(1)} %image.15.refs_3_), custom_call_target="tpu_custom_call" | custom-call | tf_op jit(solution)/shard_map/image/pallas_call | solution.py:220
  25.5 0.8 %image.17.refs_0_ = f32[8,1024]{1,0:T(8,128)S(1)} custom-call(bf16[72,1024]{1,0:T(8,128)(2,1)S(1)} %collective-permute-done.6.refs_0_, bf16[4,1024,512]{2,1,0:T(8,128)(2,1)S(1)} %get-tuple-element.17.refs_1_.held, f32[72,1024]{1,0:T(8,128)S(1)} %image.16.refs_2_, s32[8,1024]{1,0:T(8,128)S(1)} %get-tuple-element.15.refs_3_.tags, ...), custom_call_target="tpu_custom_call" | custom-call | tf_op jit(solution)/shard_map/image/pallas_call | solution.py:220
  26.2 3.7 %collective-permute-start.12 = (f32[8,1024]{1,0:T(8,128)S(1)}, f32[8,1024]{1,0:T(8,128)S(1)}, u32[]{:S(2)}, u32[]{:S(2)}) collective-permute-start(f32[8,1024]{1,0:T(8,128)S(1)} %image.17.refs_0_), channel_id=1, source_target_pairs={{0,3},{1,2},{2,1},{3,0},{4,7},{5,6},{6,5},{7,4},{8,11},{9,10},{10,... | collective-permute-start | bytes 98312 | tf_op jit(solution)/shard_map/ppermute | solution.py:294
  29.9 0.8 %collective-permute-start.10 = (f32[8,1024]{1,0:T(8,128)S(1)}, f32[8,1024]{1,0:T(8,128)S(1)}, u32[]{:S(2)}, u32[]{:S(2)}) collective-permute-start(f32[8,1024]{1,0:T(8,128)S(1)} %image.17.refs_0_), channel_id=1, source_target_pairs={{0,1},{1,0},{2,3},{3,2},{4,5},{5,4},{6,7},{7,6},{8,9},{9,8},{10,11... | collective-permute-start | bytes 98312 | tf_op jit(solution)/shard_map/ppermute | solution.py:294
  30.7 1.3 %collective-permute-done.12.refs_3_ = f32[8,1024]{1,0:T(8,128)S(1)} collective-permute-done((f32[8,1024]{1,0:T(8,128)S(1)}, f32[8,1024]{1,0:T(8,128)S(1)}, u32[]{:S(2)}, u32[]{:S(2)}) %collective-permute-start.12) | collective-permute-done | bytes 32800 | tf_op jit(solution)/shard_map/ppermute | solution.py:294
  32.0 2.7 %collective-permute-done.11.refs_2_ = f32[8,1024]{1,0:T(8,128)S(1)} collective-permute-done((f32[8,1024]{1,0:T(8,128)S(1)}, f32[8,1024]{1,0:T(8,128)S(1)}, u32[]{:S(2)}, u32[]{:S(2)}) %collective-permute-start.11) | collective-permute-done | bytes 32800 | tf_op jit(solution)/shard_map/ppermute | solution.py:294
  34.8 0.8 %step_other.1 = (f32[8,1024]{1,0:T(8,128)S(1)}, f32[8,1024]{1,0:T(8,128)S(1)}, bf16[64,1024]{1,0:T(8,128)(2,1)S(1)}, bf16[64,2048]{1,0:T(8,128)(2,1)S(1)}) custom-call(bf16[8,1024]{1,0:T(8,128)(2,1)S(1)} %get-tuple-element.14.current, s32[8,1024]{1,0:T(8,128)S(1)} %get-tuple-element.15.refs_3_.tags, f32[3,8,1024]{2,1,0:T(8,128)S(1)} %get-tuple-element.16.refs_4_.scales, ...), custom_call_target="tpu_custom_call" | custom-call | tf_op jit(solution)/shard_map/step_other/pallas_call | solution.py:152
  35.6 0.1 collective-permute-start.13
  35.7 0.8 %step_own.1 = f32[64,2048]{1,0:T(8,128)S(1)} custom-call(bf16[64,1024]{1,0:T(8,128)(2,1)S(1)} %get-tuple-element.23.panel, bf16[4,1024,512]{2,1,0:T(8,128)(2,1)S(1)} %get-tuple-element.21.refs_1_.refs_2_.held), custom_call_target="tpu_custom_call" | custom-call | tf_op jit(solution)/shard_map/step_own/pallas_call | solution.py:173
  36.5 0.7 %collective-permute-done.13 = bf16[64,2048]{1,0:T(8,128)(2,1)S(1)} collective-permute-done((bf16[64,2048]{1,0:T(8,128)(2,1)S(1)}, bf16[64,2048]{1,0:T(8,128)(2,1)S(1)}, u32[]{:S(2)}, u32[]{:S(2)}) %collective-permute-start.13) | collective-permute-done | bytes 262176 | tf_op jit(solution)/shard_map/ppermute | solution.py:239
  37.2 0.1 fusion.17
  37.3 1.8 %collective-permute-start.14 = (bf16[64,512]{1,0:T(8,128)(2,1)S(1)}, bf16[64,512]{1,0:T(8,128)(2,1)S(1)}, u32[]{:S(2)}, u32[]{:S(2)}) collective-permute-start(bf16[64,512]{1,0:T(8,128)(2,1)S(1)} %get-tuple-element.35), channel_id=1, source_target_pairs={{0,28},{4,24},{8,20},{12,16},{16,12},{20,8},{24,4},{28,0},{1,29},{... | collective-permute-start | bytes 196616 | tf_op jit(solution)/shard_map/ppermute | solution.py:239
  39.0 1.0 %collective-permute-start.16 = (bf16[64,512]{1,0:T(8,128)(2,1)S(1)}, bf16[64,512]{1,0:T(8,128)(2,1)S(1)}, u32[]{:S(2)}, u32[]{:S(2)}) collective-permute-start(bf16[64,512]{1,0:T(8,128)(2,1)S(1)} %get-tuple-element.36), channel_id=1, source_target_pairs={{0,16},{4,20},{8,24},{12,28},{16,0},{20,4},{24,8},{28,12},{1,17},{... | collective-permute-start | bytes 196616 | tf_op jit(solution)/shard_map/ppermute | solution.py:239
  40.1 0.2 collective-permute-start.15
  40.3 2.1 %collective-permute-done.14 = bf16[64,512]{1,0:T(8,128)(2,1)S(1)} collective-permute-done((bf16[64,512]{1,0:T(8,128)(2,1)S(1)}, bf16[64,512]{1,0:T(8,128)(2,1)S(1)}, u32[]{:S(2)}, u32[]{:S(2)}) %collective-permute-start.14) | collective-permute-done | bytes 65568 | tf_op jit(solution)/shard_map/ppermute | solution.py:239
  42.4 1.7 %collective-permute-done.16 = bf16[64,512]{1,0:T(8,128)(2,1)S(1)} collective-permute-done((bf16[64,512]{1,0:T(8,128)(2,1)S(1)}, bf16[64,512]{1,0:T(8,128)(2,1)S(1)}, u32[]{:S(2)}, u32[]{:S(2)}) %collective-permute-start.16) | collective-permute-done | bytes 65568 | tf_op jit(solution)/shard_map/ppermute | solution.py:239
  44.0 0.1 collective-permute-done.15
  44.2 1.1 %collective-permute-start.18 = (bf16[64,512]{1,0:T(8,128)(2,1)S(1)}, bf16[64,512]{1,0:T(8,128)(2,1)S(1)}, u32[]{:S(2)}, u32[]{:S(2)}) collective-permute-start(bf16[64,512]{1,0:T(8,128)(2,1)S(1)} %fusion.3.refs_0_), channel_id=1, source_target_pairs={{0,16},{4,20},{8,24},{12,28},{16,0},{20,4},{24,8},{28,12},{1,17},{... | collective-permute-start | bytes 196616 | tf_op jit(solution)/shard_map/ppermute | solution.py:239
  45.3 0.9 %collective-permute-start.17 = (bf16[64,512]{1,0:T(8,128)(2,1)S(1)}, bf16[64,512]{1,0:T(8,128)(2,1)S(1)}, u32[]{:S(2)}, u32[]{:S(2)}) collective-permute-start(bf16[64,512]{1,0:T(8,128)(2,1)S(1)} %fusion.3.refs_0_), channel_id=1, source_target_pairs={{0,28},{4,24},{8,20},{12,16},{16,12},{20,8},{24,4},{28,0},{1,29},{... | collective-permute-start | bytes 196616 | tf_op jit(solution)/shard_map/ppermute | solution.py:239
  46.1 1.4 %collective-permute-start.20 = (bf16[64,512]{1,0:T(8,128)(2,1)S(1)}, bf16[64,512]{1,0:T(8,128)(2,1)S(1)}, u32[]{:S(2)}, u32[]{:S(2)}) collective-permute-start(bf16[64,512]{1,0:T(8,128)(2,1)S(1)} %fusion.3.refs_0_), channel_id=1, source_target_pairs={{0,12},{4,8},{8,4},{12,0},{16,28},{20,24},{24,20},{28,16},{1,13},{... | collective-permute-start | bytes 196616 | tf_op jit(solution)/shard_map/ppermute | solution.py:239
  47.5 1.1 %collective-permute-done.18.refs_1_ = bf16[64,512]{1,0:T(8,128)(2,1)S(1)} collective-permute-done((bf16[64,512]{1,0:T(8,128)(2,1)S(1)}, bf16[64,512]{1,0:T(8,128)(2,1)S(1)}, u32[]{:S(2)}, u32[]{:S(2)}) %collective-permute-start.18) | collective-permute-done | bytes 65568 | tf_op jit(solution)/shard_map/ppermute | solution.py:239
  48.6 2.0 %collective-permute-done.17.refs_0_ = bf16[64,512]{1,0:T(8,128)(2,1)S(1)} collective-permute-done((bf16[64,512]{1,0:T(8,128)(2,1)S(1)}, bf16[64,512]{1,0:T(8,128)(2,1)S(1)}, u32[]{:S(2)}, u32[]{:S(2)}) %collective-permute-start.17) | collective-permute-done | bytes 65568 | tf_op jit(solution)/shard_map/ppermute | solution.py:239
  50.6 0.2 collective-permute-start.19
  50.8 0.4 collective-permute-start.22
  51.2 0.4 collective-permute-done.20.refs_0_
  51.5 0.1 collective-permute-start.21
  51.7 0.4 image.18.refs_2_
  52.1 0.4 image.19.refs_2_
  52.5 0.4 image.20.refs_2_
  53.0 0.4 image.21.refs_3_
  53.4 0.8 %image.22.refs_2_ = f32[64,1024]{1,0:T(8,128)S(1)} custom-call(bf16[64,512]{1,0:T(8,128)(2,1)S(1)} %collective-permute-done.17.refs_0_, bf16[64,512]{1,0:T(8,128)(2,1)S(1)} %collective-permute-done.18.refs_1_, bf16[4,1024,512]{2,1,0:T(8,128)(2,1)S(1)} %get-tuple-element.21.refs_1_.refs_2_.held, f32[64,1024]{1,0:T(8,128)S(1)} %image.21.refs_3_), custom_call_target="tpu_custom_call" | custom-call | tf_op jit(solution)/shard_map/image/pallas_call | solution.py:220
  54.2 0.8 %image.23 = f32[8,1024]{1,0:T(8,128)S(1)} custom-call(bf16[64,1024]{1,0:T(8,128)(2,1)S(1)} %collective-permute-done.19.refs_0_, bf16[4,1024,512]{2,1,0:T(8,128)(2,1)S(1)} %get-tuple-element.17.refs_1_.held, f32[64,1024]{1,0:T(8,128)S(1)} %image.22.refs_2_, s32[8,1024]{1,0:T(8,128)S(1)} %get-tuple-element.15.refs_3_.tags, ...), custom_call_target="tpu_custom_call" | custom-call | tf_op jit(solution)/shard_map/image/pallas_call | solution.py:220
  55.0 1.7 %collective-permute-start.25 = (f32[8,1024]{1,0:T(8,128)S(1)}, f32[8,1024]{1,0:T(8,128)S(1)}, u32[]{:S(2)}, u32[]{:S(2)}) collective-permute-start(f32[8,1024]{1,0:T(8,128)S(1)} %image.23), channel_id=1, source_target_pairs={{0,3},{1,2},{2,1},{3,0},{4,7},{5,6},{6,5},{7,4},{8,11},{9,10},{10,... | collective-permute-start | bytes 98312 | tf_op jit(solution)/shard_map/ppermute | solution.py:294
  56.6 0.5 collective-permute-start.24
  57.1 2.3 %collective-permute-start.23 = (f32[8,1024]{1,0:T(8,128)S(1)}, f32[8,1024]{1,0:T(8,128)S(1)}, u32[]{:S(2)}, u32[]{:S(2)}) collective-permute-start(f32[8,1024]{1,0:T(8,128)S(1)} %image.23), channel_id=1, source_target_pairs={{0,1},{1,0},{2,3},{3,2},{4,5},{5,4},{6,7},{7,6},{8,9},{9,8},{10,11... | collective-permute-start | bytes 98312 | tf_op jit(solution)/shard_map/ppermute | solution.py:294
  59.4 0.6 copy.6
  60.0 0.9 %collective-permute-done.25 = f32[8,1024]{1,0:T(8,128)S(1)} collective-permute-done((f32[8,1024]{1,0:T(8,128)S(1)}, f32[8,1024]{1,0:T(8,128)S(1)}, u32[]{:S(2)}, u32[]{:S(2)}) %collective-permute-start.25) | collective-permute-done | bytes 32800 | tf_op jit(solution)/shard_map/ppermute | solution.py:294
  60.9 0.9 %collective-permute-done.24 = f32[8,1024]{1,0:T(8,128)S(1)} collective-permute-done((f32[8,1024]{1,0:T(8,128)S(1)}, f32[8,1024]{1,0:T(8,128)S(1)}, u32[]{:S(2)}, u32[]{:S(2)}) %collective-permute-start.24) | collective-permute-done | bytes 32800 | tf_op jit(solution)/shard_map/ppermute | solution.py:294
  61.8 0.1 collective-permute-done.23
  61.9 0.6 %add_add_fusion = f32[8,1024]{1,0:T(8,128)} fusion(f32[8,1024]{1,0:T(8,128)S(1)} %get-tuple-element.25, f32[8,1024]{1,0:T(8,128)S(1)} %collective-permute-done.24, f32[8,1024]{1,0:T(8,128)S(1)} %collective-permute-done.25, f32[8,1024]{1,0:T(8,128)S(1)} %image.23, f32[8,1024]{1,0:T(8,128)S(1)} %collective-permute-done.23), kind=kLoop, calls=%fused_computation.26 | loop fusion | flops 32768 | bytes 196608 | tf_op jit(solution)/shard_map/add | solution.py:307
  (23 shorter events, 0.3 us)
Async XLA Ops:
  3.2 3.1 %collective-permute-start = (f32[72,2048]{1,0:T(8,128)S(1)}, f32[72,2048]{1,0:T(8,128)S(1)}, u32[]{:S(2)}, u32[]{:S(2)}) collective-permute-start(f32[72,2048]{1,0:T(8,128)S(1)} %get-tuple-element.20), channel_id=1, source_target_pairs={{0,4},{4,0},{8,12},{12,8},{16,20},{20,16},{24,28},{28,24},{1,5},{5... | collective-permute-start | bytes 1769480 | tf_op jit(solution)/shard_map/ppermute | solution.py:239
  6.6 6.3 %collective-permute-start.1 = (f16[72,512]{1,0:T(8,128)(2,1)S(1)}, f16[72,512]{1,0:T(8,128)(2,1)S(1)}, u32[]{:S(2)}, u32[]{:S(2)}) collective-permute-start(f16[72,512]{1,0:T(8,128)(2,1)S(1)} %get-tuple-element.32), channel_id=1, source_target_pairs={{0,28},{4,24},{8,20},{12,16},{16,12},{20,8},{24,4},{28,0},{1,29},{... | collective-permute-start | bytes 221192 | tf_op jit(solution)/shard_map/ppermute | solution.py:239
  10.2 4.4 %collective-permute-start.2 = (f16[72,512]{1,0:T(8,128)(2,1)S(1)}, f16[72,512]{1,0:T(8,128)(2,1)S(1)}, u32[]{:S(2)}, u32[]{:S(2)}) collective-permute-start(f16[72,512]{1,0:T(8,128)(2,1)S(1)} %get-tuple-element.33), channel_id=1, source_target_pairs={{0,12},{4,8},{8,4},{12,0},{16,28},{20,24},{24,20},{28,16},{1,13},{... | collective-permute-start | bytes 221192 | tf_op jit(solution)/shard_map/ppermute | solution.py:239
  10.4 4.7 %collective-permute-start.3 = (f16[72,512]{1,0:T(8,128)(2,1)S(1)}, f16[72,512]{1,0:T(8,128)(2,1)S(1)}, u32[]{:S(2)}, u32[]{:S(2)}) collective-permute-start(f16[72,512]{1,0:T(8,128)(2,1)S(1)} %get-tuple-element.34), channel_id=1, source_target_pairs={{0,16},{4,20},{8,24},{12,28},{16,0},{20,4},{24,8},{28,12},{1,17},{... | collective-permute-start | bytes 221192 | tf_op jit(solution)/shard_map/ppermute | solution.py:239
  15.1 4.4 %collective-permute-start.5 = (bf16[72,512]{1,0:T(8,128)(2,1)S(1)}, bf16[72,512]{1,0:T(8,128)(2,1)S(1)}, u32[]{:S(2)}, u32[]{:S(2)}) collective-permute-start(bf16[72,512]{1,0:T(8,128)(2,1)S(1)} %pad_maximum_fusion.5.refs_0_), channel_id=1, source_target_pairs={{0,16},{4,20},{8,24},{12,28},{16,0},{20,4},{24,8},{28,12},{1,17},{... | collective-permute-start | bytes 221192 | tf_op jit(solution)/shard_map/ppermute | solution.py:239
  16.4 5.4 %collective-permute-start.4 = (bf16[72,512]{1,0:T(8,128)(2,1)S(1)}, bf16[72,512]{1,0:T(8,128)(2,1)S(1)}, u32[]{:S(2)}, u32[]{:S(2)}) collective-permute-start(bf16[72,512]{1,0:T(8,128)(2,1)S(1)} %pad_maximum_fusion.5.refs_0_), channel_id=1, source_target_pairs={{0,28},{4,24},{8,20},{12,16},{16,12},{20,8},{24,4},{28,0},{1,29},{... | collective-permute-start | bytes 221192 | tf_op jit(solution)/shard_map/ppermute | solution.py:239
  17.4 5.0 %collective-permute-start.7 = (bf16[72,512]{1,0:T(8,128)(2,1)S(1)}, bf16[72,512]{1,0:T(8,128)(2,1)S(1)}, u32[]{:S(2)}, u32[]{:S(2)}) collective-permute-start(bf16[72,512]{1,0:T(8,128)(2,1)S(1)} %pad_maximum_fusion.5.refs_0_), channel_id=1, source_target_pairs={{0,12},{4,8},{8,4},{12,0},{16,28},{20,24},{24,20},{28,16},{1,13},{... | collective-permute-start | bytes 221192 | tf_op jit(solution)/shard_map/ppermute | solution.py:239
  21.8 3.6 %collective-permute-start.6 = (bf16[72,1024]{1,0:T(8,128)(2,1)S(1)}, bf16[72,1024]{1,0:T(8,128)(2,1)S(1)}, u32[]{:S(2)}, u32[]{:S(2)}) collective-permute-start(bf16[72,1024]{1,0:T(8,128)(2,1)S(1)} %pad_maximum_fusion), channel_id=1, source_target_pairs={{0,4},{4,0},{8,12},{12,8},{16,20},{20,16},{24,28},{28,24},{1,5},{5... | collective-permute-start | bytes 442376 | tf_op jit(solution)/shard_map/ppermute | solution.py:239
  22.0 1.4 %collective-permute-start.9 = (bf16[72,512]{1,0:T(8,128)(2,1)S(1)}, bf16[72,512]{1,0:T(8,128)(2,1)S(1)}, u32[]{:S(2)}, u32[]{:S(2)}) collective-permute-start(bf16[72,512]{1,0:T(8,128)(2,1)S(1)} %pad_maximum_fusion.5.refs_0_), channel_id=1, source_target_pairs={{0,4},{4,0},{8,12},{12,8},{16,20},{20,16},{24,28},{28,24},{1,5},{5... | collective-permute-start | bytes 221192 | tf_op jit(solution)/shard_map/ppermute | solution.py:239
  22.4 1.9 %collective-permute-start.8 = (bf16[72,512]{1,0:T(8,128)(2,1)S(1)}, bf16[72,512]{1,0:T(8,128)(2,1)S(1)}, u32[]{:S(2)}, u32[]{:S(2)}) collective-permute-start(bf16[72,512]{1,0:T(8,128)(2,1)S(1)} %collective-permute-done.7.refs_0_), channel_id=1, source_target_pairs={{0,4},{4,0},{8,12},{12,8},{16,20},{20,16},{24,28},{28,24},{1,5},{5... | collective-permute-start | bytes 221192 | tf_op jit(solution)/shard_map/ppermute | solution.py:239
  26.2 5.8 %collective-permute-start.12 = (f32[8,1024]{1,0:T(8,128)S(1)}, f32[8,1024]{1,0:T(8,128)S(1)}, u32[]{:S(2)}, u32[]{:S(2)}) collective-permute-start(f32[8,1024]{1,0:T(8,128)S(1)} %image.17.refs_0_), channel_id=1, source_target_pairs={{0,3},{1,2},{2,1},{3,0},{4,7},{5,6},{6,5},{7,4},{8,11},{9,10},{10,... | collective-permute-start | bytes 98312 | tf_op jit(solution)/shard_map/ppermute | solution.py:294
  29.9 4.8 %collective-permute-start.11 = (f32[8,1024]{1,0:T(8,128)S(1)}, f32[8,1024]{1,0:T(8,128)S(1)}, u32[]{:S(2)}, u32[]{:S(2)}) collective-permute-start(f32[8,1024]{1,0:T(8,128)S(1)} %image.17.refs_0_), channel_id=1, source_target_pairs={{0,2},{1,3},{2,0},{3,1},{4,6},{5,7},{6,4},{7,5},{8,10},{9,11},{10,... | collective-permute-start | bytes 98312 | tf_op jit(solution)/shard_map/ppermute | solution.py:294
  29.9 4.8 %collective-permute-start.10 = (f32[8,1024]{1,0:T(8,128)S(1)}, f32[8,1024]{1,0:T(8,128)S(1)}, u32[]{:S(2)}, u32[]{:S(2)}) collective-permute-start(f32[8,1024]{1,0:T(8,128)S(1)} %image.17.refs_0_), channel_id=1, source_target_pairs={{0,1},{1,0},{2,3},{3,2},{4,5},{5,4},{6,7},{7,6},{8,9},{9,8},{10,11... | collective-permute-start | bytes 98312 | tf_op jit(solution)/shard_map/ppermute | solution.py:294
  35.6 1.6 %collective-permute-start.13 = (bf16[64,2048]{1,0:T(8,128)(2,1)S(1)}, bf16[64,2048]{1,0:T(8,128)(2,1)S(1)}, u32[]{:S(2)}, u32[]{:S(2)}) collective-permute-start(bf16[64,2048]{1,0:T(8,128)(2,1)S(1)} %get-tuple-element.24), channel_id=1, source_target_pairs={{0,4},{4,0},{8,12},{12,8},{16,20},{20,16},{24,28},{28,24},{1,5},{5... | collective-permute-start | bytes 786440 | tf_op jit(solution)/shard_map/ppermute | solution.py:239
  37.3 5.1 %collective-permute-start.14 = (bf16[64,512]{1,0:T(8,128)(2,1)S(1)}, bf16[64,512]{1,0:T(8,128)(2,1)S(1)}, u32[]{:S(2)}, u32[]{:S(2)}) collective-permute-start(bf16[64,512]{1,0:T(8,128)(2,1)S(1)} %get-tuple-element.35), channel_id=1, source_target_pairs={{0,28},{4,24},{8,20},{12,16},{16,12},{20,8},{24,4},{28,0},{1,29},{... | collective-permute-start | bytes 196616 | tf_op jit(solution)/shard_map/ppermute | solution.py:239
  39.0 5.0 %collective-permute-start.16 = (bf16[64,512]{1,0:T(8,128)(2,1)S(1)}, bf16[64,512]{1,0:T(8,128)(2,1)S(1)}, u32[]{:S(2)}, u32[]{:S(2)}) collective-permute-start(bf16[64,512]{1,0:T(8,128)(2,1)S(1)} %get-tuple-element.36), channel_id=1, source_target_pairs={{0,16},{4,20},{8,24},{12,28},{16,0},{20,4},{24,8},{28,12},{1,17},{... | collective-permute-start | bytes 196616 | tf_op jit(solution)/shard_map/ppermute | solution.py:239
  40.1 4.1 %collective-permute-start.15 = (bf16[64,512]{1,0:T(8,128)(2,1)S(1)}, bf16[64,512]{1,0:T(8,128)(2,1)S(1)}, u32[]{:S(2)}, u32[]{:S(2)}) collective-permute-start(bf16[64,512]{1,0:T(8,128)(2,1)S(1)} %get-tuple-element.37), channel_id=1, source_target_pairs={{0,12},{4,8},{8,4},{12,0},{16,28},{20,24},{24,20},{28,16},{1,13},{... | collective-permute-start | bytes 196616 | tf_op jit(solution)/shard_map/ppermute | solution.py:239
  44.2 4.3 %collective-permute-start.18 = (bf16[64,512]{1,0:T(8,128)(2,1)S(1)}, bf16[64,512]{1,0:T(8,128)(2,1)S(1)}, u32[]{:S(2)}, u32[]{:S(2)}) collective-permute-start(bf16[64,512]{1,0:T(8,128)(2,1)S(1)} %fusion.3.refs_0_), channel_id=1, source_target_pairs={{0,16},{4,20},{8,24},{12,28},{16,0},{20,4},{24,8},{28,12},{1,17},{... | collective-permute-start | bytes 196616 | tf_op jit(solution)/shard_map/ppermute | solution.py:239
  45.3 5.3 %collective-permute-start.17 = (bf16[64,512]{1,0:T(8,128)(2,1)S(1)}, bf16[64,512]{1,0:T(8,128)(2,1)S(1)}, u32[]{:S(2)}, u32[]{:S(2)}) collective-permute-start(bf16[64,512]{1,0:T(8,128)(2,1)S(1)} %fusion.3.refs_0_), channel_id=1, source_target_pairs={{0,28},{4,24},{8,20},{12,16},{16,12},{20,8},{24,4},{28,0},{1,29},{... | collective-permute-start | bytes 196616 | tf_op jit(solution)/shard_map/ppermute | solution.py:239
  46.1 5.4 %collective-permute-start.20 = (bf16[64,512]{1,0:T(8,128)(2,1)S(1)}, bf16[64,512]{1,0:T(8,128)(2,1)S(1)}, u32[]{:S(2)}, u32[]{:S(2)}) collective-permute-start(bf16[64,512]{1,0:T(8,128)(2,1)S(1)} %fusion.3.refs_0_), channel_id=1, source_target_pairs={{0,12},{4,8},{8,4},{12,0},{16,28},{20,24},{24,20},{28,16},{1,13},{... | collective-permute-start | bytes 196616 | tf_op jit(solution)/shard_map/ppermute | solution.py:239
  50.6 3.6 %collective-permute-start.19 = (bf16[64,1024]{1,0:T(8,128)(2,1)S(1)}, bf16[64,1024]{1,0:T(8,128)(2,1)S(1)}, u32[]{:S(2)}, u32[]{:S(2)}) collective-permute-start(bf16[64,1024]{1,0:T(8,128)(2,1)S(1)} %pad_maximum_fusion.1), channel_id=1, source_target_pairs={{0,4},{4,0},{8,12},{12,8},{16,20},{20,16},{24,28},{28,24},{1,5},{5... | collective-permute-start | bytes 393224 | tf_op jit(solution)/shard_map/ppermute | solution.py:239
  50.8 1.3 %collective-permute-start.22 = (bf16[64,512]{1,0:T(8,128)(2,1)S(1)}, bf16[64,512]{1,0:T(8,128)(2,1)S(1)}, u32[]{:S(2)}, u32[]{:S(2)}) collective-permute-start(bf16[64,512]{1,0:T(8,128)(2,1)S(1)} %fusion.3.refs_0_), channel_id=1, source_target_pairs={{0,4},{4,0},{8,12},{12,8},{16,20},{20,16},{24,28},{28,24},{1,5},{5... | collective-permute-start | bytes 196616 | tf_op jit(solution)/shard_map/ppermute | solution.py:239
  51.5 1.4 %collective-permute-start.21 = (bf16[64,512]{1,0:T(8,128)(2,1)S(1)}, bf16[64,512]{1,0:T(8,128)(2,1)S(1)}, u32[]{:S(2)}, u32[]{:S(2)}) collective-permute-start(bf16[64,512]{1,0:T(8,128)(2,1)S(1)} %collective-permute-done.20.refs_0_), channel_id=1, source_target_pairs={{0,4},{4,0},{8,12},{12,8},{16,20},{20,16},{24,28},{28,24},{1,5},{5... | collective-permute-start | bytes 196616 | tf_op jit(solution)/shard_map/ppermute | solution.py:239
  55.0 6.0 %collective-permute-start.25 = (f32[8,1024]{1,0:T(8,128)S(1)}, f32[8,1024]{1,0:T(8,128)S(1)}, u32[]{:S(2)}, u32[]{:S(2)}) collective-permute-start(f32[8,1024]{1,0:T(8,128)S(1)} %image.23), channel_id=1, source_target_pairs={{0,3},{1,2},{2,1},{3,0},{4,7},{5,6},{6,5},{7,4},{8,11},{9,10},{10,... | collective-permute-start | bytes 98312 | tf_op jit(solution)/shard_map/ppermute | solution.py:294
  56.6 5.2 %collective-permute-start.24 = (f32[8,1024]{1,0:T(8,128)S(1)}, f32[8,1024]{1,0:T(8,128)S(1)}, u32[]{:S(2)}, u32[]{:S(2)}) collective-permute-start(f32[8,1024]{1,0:T(8,128)S(1)} %image.23), channel_id=1, source_target_pairs={{0,2},{1,3},{2,0},{3,1},{4,6},{5,7},{6,4},{7,5},{8,10},{9,11},{10,... | collective-permute-start | bytes 98312 | tf_op jit(solution)/shard_map/ppermute | solution.py:294
  57.1 4.8 %collective-permute-start.23 = (f32[8,1024]{1,0:T(8,128)S(1)}, f32[8,1024]{1,0:T(8,128)S(1)}, u32[]{:S(2)}, u32[]{:S(2)}) collective-permute-start(f32[8,1024]{1,0:T(8,128)S(1)} %image.23), channel_id=1, source_target_pairs={{0,1},{1,0},{2,3},{3,2},{4,5},{5,4},{6,7},{7,6},{8,9},{9,8},{10,11... | collective-permute-start | bytes 98312 | tf_op jit(solution)/shard_map/ppermute | solution.py:294

commit v8 on v7

--- a/solution.py
+++ b/solution.py
@@ -10,6 +10,7 @@
 
 ENVS = 8
 SCALE_ROWS = 8
+BEGUN = 1
 VMEM = pl.BlockSpec(memory_space=pltpu.VMEM)
 HBM = pl.BlockSpec(memory_space=pltpu.HBM)
 PARAMS = pltpu.CompilerParams(vmem_limit_bytes=24 * 1024 * 1024)
@@ -25,7 +26,7 @@
     return lax.dot_general(a, b, (((1,), (1,)), ((), ())), preferred_element_type=f32)
 
 
-def copies(genotypes, held, sems, other):
+def copies(genotypes, held, sems, other, blocks, base=0):
     chips, _, width = held.shape
     index = lax.axis_index("samp")
     core, chip = index & 1, index >> 1
@@ -35,9 +36,9 @@
 
     def copy(d):
         start = pl.multiple_of((half * chips + (chip ^ d)) * width, width)
-        return pltpu.make_async_copy(genotypes.at[:, pl.ds(start, width)], held.at[d], sems.at[d])
-
-    return [copy(d) for d in range(chips)]
+        return pltpu.make_async_copy(genotypes.at[:, pl.ds(start, width)], held.at[d], sems.at[base + d])
+
+    return [copy(d) for d in blocks]
 
 
 def store_bounded(partial, d, block):
@@ -53,8 +54,13 @@
         partial[:, pl.ds(d * width, width)] = jnp.dot(panel, held[d], preferred_element_type=f32).astype(partial.dtype)
 
 
-def first_body(probes, labels, variances, genotypes, held, partial, panel, current, tags, scales, labels_in, numbers, sems, small, *, snps):
-    moves = copies(genotypes, held, sems, True)
+def first_body(
+    probes, labels, variances, genotypes,
+    held, held_own, partial, panel, current, tags, scales,
+    labels_in, numbers, sems, small, *, snps
+):
+    moves = copies(genotypes, held, sems, True, range(held.shape[0]))
+    begun = copies(genotypes, held_own, sems, False, range(BEGUN), held.shape[0])
     inputs = (
         pltpu.make_async_copy(probes, current, small.at[0]),
         pltpu.make_async_copy(labels, labels_in, small.at[1]),
@@ -63,6 +69,8 @@
     for move in inputs:
         move.start()
     for move in moves:
+        move.start()
+    for move in begun:
         move.start()
     for move in inputs:
         move.wait()
@@ -77,6 +85,8 @@
     for d, move in enumerate(moves):
         move.wait()
         store_bounded(partial, d, jnp.dot(built, held[d], preferred_element_type=f32))
+    for move in begun:
+        move.wait()
 
 
 def load_first(probes, labels, variances, genotypes, chips, width, snps):
@@ -85,8 +95,9 @@
     return pl.pallas_call(
         functools.partial(first_body, snps=snps),
         in_specs=[HBM] * 4,
-        out_specs=(VMEM,) * 6,
+        out_specs=(VMEM,) * 7,
         out_shape=(
+            pltpu.VMEM((chips, samples, width), genotypes.dtype),
             pltpu.VMEM((chips, samples, width), genotypes.dtype),
             pltpu.VMEM((rows + SCALE_ROWS, chips * width), f32),
             pltpu.VMEM((rows, samples), jnp.bfloat16),
@@ -97,7 +108,7 @@
         scratch_shapes=[
             pltpu.VMEM(labels.shape, labels.dtype),
             pltpu.SMEM(variances.shape, variances.dtype),
-            pltpu.SemaphoreType.DMA((chips,)),
+            pltpu.SemaphoreType.DMA((chips + BEGUN,)),
             pltpu.SemaphoreType.DMA((3,)),
         ],
         compiler_params=PARAMS,
@@ -105,29 +116,34 @@
     )(probes, labels, variances, genotypes)
 
 
-def second_body(panel, genotypes, held, partial, sems):
-    moves = copies(genotypes, held, sems, False)
+def second_body(panel, genotypes, begun, held, partial, sems):
+    chips = held.shape[0]
+    moves = copies(genotypes, held, sems, False, range(BEGUN, chips))
     for move in moves:
         move.start()
-    for d, move in enumerate(moves):
-        move.wait()
-        store_bounded(partial, d, jnp.dot(panel[...], held[d], preferred_element_type=f32))
-
-
-def load_second(panel, genotypes, chips, width):
-    rows, samples = panel.shape
+    for d in range(chips):
+        if d >= BEGUN:
+            moves[d - BEGUN].wait()
+        block = begun[d] if d < BEGUN else held[d]
+        store_bounded(partial, d, jnp.dot(panel[...], block, preferred_element_type=f32))
+
+
+def load_second(panel, genotypes, begun):
+    rows = panel.shape[0]
+    chips, _, width = begun.shape
     return pl.pallas_call(
         second_body,
-        in_specs=[VMEM, HBM],
+        in_specs=[VMEM, HBM, VMEM],
         out_specs=(VMEM, VMEM),
         out_shape=(
-            pltpu.VMEM((chips, samples, width), genotypes.dtype),
+            pltpu.VMEM(begun.shape, begun.dtype),
             pltpu.VMEM((rows + SCALE_ROWS, chips * width), f32),
         ),
+        input_output_aliases={2: 0},
         scratch_shapes=[pltpu.SemaphoreType.DMA((chips,))],
         compiler_params=PARAMS,
         name="load_own",
-    )(panel, genotypes)
+    )(panel, genotypes, begun)
 
 
 def tree_sum(parts):
@@ -296,8 +312,10 @@
             }
             return [weighted] + [pieces[step] for step in range(1, snp)]
 
-        held_other, given, panel, current, tags, scales = load_first(probes, labels, variances, genotypes, chips, width, snps)
-        held_own, own = load_second(panel, genotypes, chips, width)
+        held_other, begun, given, panel, current, tags, scales = load_first(
+            probes, labels, variances, genotypes, chips, width, snps
+        )
+        held_own, own = load_second(panel, genotypes, begun)
         mine = reduce_panel(given, own, count, True)
         parts = spread(spread_image(mine, held_own, held_other, (tags, scales)))
         first, noise, panel, given = step_half(current, tags, scales, held_other, parts, jnp.bfloat16)

time: 62.8 us -> 62.5 us (level)
  no operation moved by 1% of the time
where the time goes in v8:
time: 62.5 us; the launch traced here: 62.2 us
  starting transfers between devices  24.7 us (40%)
  waiting for transfers between devices  22 us (35%)
  Pallas kernels  13.1 us (21%)
  other arithmetic  1.07 us (2%)
  between operations  0.84 us (1%)
  local copies, waits for them, and re-layouts  0.63 us (1%)
    ppermute x20, waiting for transfers between devices, exchange(): return lax.ppermute(block, 'samp', [(k, k ^ offset) for k in range(samp)])  16 us
    ppermute x20, starting transfers between devices, exchange(): return lax.ppermute(block, 'samp', [(k, k ^ offset) for k in range(samp)])  15.8 us
    ppermute x6, starting transfers between devices, spread(): lax.ppermute(weighted, 'snp', [(k, k ^ step) for k in range(snp)])  8.9 us
    pallas_call x12, Pallas kernels, image(): pl.pallas_call(functools.partial(image_body, blocks=tuple(blocks), pieces...  6.55 us
    ppermute x6, waiting for transfers between devices, spread(): lax.ppermute(weighted, 'snp', [(k, k ^ step) for k in range(snp)])  5.95 us
    pallas_call x1, Pallas kernels, load_first(): pl.pallas_call(functools.partial(first_body, snps=snps), in_specs=[HBM] *...  2.63 us
    pallas_call x1, Pallas kernels, load_second(): pl.pallas_call(second_body, in_specs=[VMEM, HBM, VMEM], out_specs=(VMEM,...  2.21 us
  transfers between devices with their start and end apart: 26, of which 18 were waited for; matrix products, arithmetic and copies ran while one was open for 1% of the time, Pallas kernels for 13%

profile of v8, /device:TPU:0, one launch (start us, length us, event | category | flops | bytes accessed | tf_op | source)
XLA Modules:
  0.0 62.2 jit_solution(6101539317302803259)
XLA Ops:
  0.6 2.6 %load_other.1 = (bf16[4,1024,512]{2,1,0:T(8,128)(2,1)S(1)}, bf16[4,1024,512]{2,1,0:T(8,128)(2,1)S(1)}, f32[72,2048]{1,0:T(8,128)S(1)}, bf16[64,1024]{1,0:T(8,128...) custom-call(bf16[8,1024]{1,0:T(8,128)(2,1)} %probes.1, ...), custom_call_target="tpu_custom_call" | custom-call | tf_op jit(solution)/shard_map/load_other/pallas_call | solution.py:95
  3.3 0.6 collective-permute-start
  3.8 2.2 %load_own.1 = (bf16[4,1024,512]{2,1,0:T(8,128)(2,1)S(1)}, f32[72,2048]{1,0:T(8,128)S(1)}) custom-call(bf16[64,1024]{1,0:T(8,128)(2,1)S(1)} %get-tuple-element.19.panel, bf16[1024,4096]{1,0:T(8,128)(2,1)} %genotypes.3, bf16[4,1024,512]{2,1,0:T(8,128)(2,1)S(1)} %get-tuple-element.20.begun), custom_call_target="tpu_custom_call", output_to_operand_aliasing={{0}: (2, {})} | custom-call | tf_op jit(solution)/shard_map/load_own/pallas_call | solution.py:134
  6.1 0.1 add.39
  6.2 0.1 pad_maximum_fusion.4
  6.3 3.6 %collective-permute-start.1 = (f16[72,512]{1,0:T(8,128)(2,1)S(1)}, f16[72,512]{1,0:T(8,128)(2,1)S(1)}, u32[]{:S(2)}, u32[]{:S(2)}) collective-permute-start(f16[72,512]{1,0:T(8,128)(2,1)S(1)} %get-tuple-element.34), channel_id=1, source_target_pairs={{0,28},{4,24},{8,20},{12,16},{16,12},{20,8},{24,4},{28,0},{1,29},{... | collective-permute-start | bytes 221192 | tf_op jit(solution)/shard_map/ppermute | solution.py:255
  9.9 0.2 collective-permute-start.2
  10.1 0.5 collective-permute-start.3
  10.5 2.0 %collective-permute-done.1 = f16[72,512]{1,0:T(8,128)(2,1)S(1)} collective-permute-done((f16[72,512]{1,0:T(8,128)(2,1)S(1)}, f16[72,512]{1,0:T(8,128)(2,1)S(1)}, u32[]{:S(2)}, u32[]{:S(2)}) %collective-permute-start.1) | collective-permute-done | bytes 73760 | tf_op jit(solution)/shard_map/ppermute | solution.py:255
  12.6 1.7 %collective-permute-done.2 = f16[72,512]{1,0:T(8,128)(2,1)S(1)} collective-permute-done((f16[72,512]{1,0:T(8,128)(2,1)S(1)}, f16[72,512]{1,0:T(8,128)(2,1)S(1)}, u32[]{:S(2)}, u32[]{:S(2)}) %collective-permute-start.2) | collective-permute-done | bytes 73760 | tf_op jit(solution)/shard_map/ppermute | solution.py:255
  14.3 0.4 collective-permute-done.3
  14.8 1.3 %collective-permute-start.5 = (bf16[72,512]{1,0:T(8,128)(2,1)S(1)}, bf16[72,512]{1,0:T(8,128)(2,1)S(1)}, u32[]{:S(2)}, u32[]{:S(2)}) collective-permute-start(bf16[72,512]{1,0:T(8,128)(2,1)S(1)} %pad_maximum_fusion.5.refs_0_), channel_id=1, source_target_pairs={{0,16},{4,20},{8,24},{12,28},{16,0},{20,4},{24,8},{28,12},{1,17},{... | collective-permute-start | bytes 221192 | tf_op jit(solution)/shard_map/ppermute | solution.py:255
  16.1 1.0 %collective-permute-start.4 = (bf16[72,512]{1,0:T(8,128)(2,1)S(1)}, bf16[72,512]{1,0:T(8,128)(2,1)S(1)}, u32[]{:S(2)}, u32[]{:S(2)}) collective-permute-start(bf16[72,512]{1,0:T(8,128)(2,1)S(1)} %pad_maximum_fusion.5.refs_0_), channel_id=1, source_target_pairs={{0,28},{4,24},{8,20},{12,16},{16,12},{20,8},{24,4},{28,0},{1,29},{... | collective-permute-start | bytes 221192 | tf_op jit(solution)/shard_map/ppermute | solution.py:255
  17.2 1.0 %collective-permute-start.7 = (bf16[72,512]{1,0:T(8,128)(2,1)S(1)}, bf16[72,512]{1,0:T(8,128)(2,1)S(1)}, u32[]{:S(2)}, u32[]{:S(2)}) collective-permute-start(bf16[72,512]{1,0:T(8,128)(2,1)S(1)} %pad_maximum_fusion.5.refs_0_), channel_id=1, source_target_pairs={{0,12},{4,8},{8,4},{12,0},{16,28},{20,24},{24,20},{28,16},{1,13},{... | collective-permute-start | bytes 221192 | tf_op jit(solution)/shard_map/ppermute | solution.py:255
  18.1 1.1 %collective-permute-done.5.refs_1_ = bf16[72,512]{1,0:T(8,128)(2,1)S(1)} collective-permute-done((bf16[72,512]{1,0:T(8,128)(2,1)S(1)}, bf16[72,512]{1,0:T(8,128)(2,1)S(1)}, u32[]{:S(2)}, u32[]{:S(2)}) %collective-permute-start.5) | collective-permute-done | bytes 73760 | tf_op jit(solution)/shard_map/ppermute | solution.py:255
  19.3 2.3 %collective-permute-done.4.refs_0_ = bf16[72,512]{1,0:T(8,128)(2,1)S(1)} collective-permute-done((bf16[72,512]{1,0:T(8,128)(2,1)S(1)}, bf16[72,512]{1,0:T(8,128)(2,1)S(1)}, u32[]{:S(2)}, u32[]{:S(2)}) %collective-permute-start.4) | collective-permute-done | bytes 73760 | tf_op jit(solution)/shard_map/ppermute | solution.py:255
  21.5 0.1 collective-permute-start.6
  21.7 0.4 collective-permute-start.9
  22.1 0.1 collective-permute-start.8
  22.2 0.4 image.12.refs_2_
  22.6 0.4 collective-permute-done.9.refs_0_
  23.1 0.4 image.13.refs_2_
  23.5 0.4 image.14.refs_2_
  24.0 0.4 image.15.refs_3_
  24.4 0.8 %image.16.refs_2_ = f32[72,1024]{1,0:T(8,128)S(1)} custom-call(bf16[72,512]{1,0:T(8,128)(2,1)S(1)} %collective-permute-done.4.refs_0_, bf16[72,512]{1,0:T(8,128)(2,1)S(1)} %collective-permute-done.5.refs_1_, bf16[4,1024,512]{2,1,0:T(8,128)(2,1)S(1)} %get-tuple-element.23.refs_1_.refs_2_.held, f32[72,1024]{1,0:T(8,128)S(1)} %image.15.refs_3_), custom_call_target="tpu_custom_call" | custom-call | tf_op jit(solution)/shard_map/image/pallas_call | solution.py:236
  25.2 0.8 %image.17.refs_0_ = f32[8,1024]{1,0:T(8,128)S(1)} custom-call(bf16[72,1024]{1,0:T(8,128)(2,1)S(1)} %collective-permute-done.6.refs_0_, bf16[4,1024,512]{2,1,0:T(8,128)(2,1)S(1)} %get-tuple-element.18.refs_1_.held, f32[72,1024]{1,0:T(8,128)S(1)} %image.16.refs_2_, s32[8,1024]{1,0:T(8,128)S(1)} %get-tuple-element.16.refs_3_.tags, ...), custom_call_target="tpu_custom_call" | custom-call | tf_op jit(solution)/shard_map/image/pallas_call | solution.py:236
  26.0 3.7 %collective-permute-start.12 = (f32[8,1024]{1,0:T(8,128)S(1)}, f32[8,1024]{1,0:T(8,128)S(1)}, u32[]{:S(2)}, u32[]{:S(2)}) collective-permute-start(f32[8,1024]{1,0:T(8,128)S(1)} %image.17.refs_0_), channel_id=1, source_target_pairs={{0,3},{1,2},{2,1},{3,0},{4,7},{5,6},{6,5},{7,4},{8,11},{9,10},{10,... | collective-permute-start | bytes 98312 | tf_op jit(solution)/shard_map/ppermute | solution.py:310
  29.6 0.8 %collective-permute-start.10 = (f32[8,1024]{1,0:T(8,128)S(1)}, f32[8,1024]{1,0:T(8,128)S(1)}, u32[]{:S(2)}, u32[]{:S(2)}) collective-permute-start(f32[8,1024]{1,0:T(8,128)S(1)} %image.17.refs_0_), channel_id=1, source_target_pairs={{0,1},{1,0},{2,3},{3,2},{4,5},{5,4},{6,7},{7,6},{8,9},{9,8},{10,11... | collective-permute-start | bytes 98312 | tf_op jit(solution)/shard_map/ppermute | solution.py:310
  30.4 1.3 %collective-permute-done.12.refs_3_ = f32[8,1024]{1,0:T(8,128)S(1)} collective-permute-done((f32[8,1024]{1,0:T(8,128)S(1)}, f32[8,1024]{1,0:T(8,128)S(1)}, u32[]{:S(2)}, u32[]{:S(2)}) %collective-permute-start.12) | collective-permute-done | bytes 32800 | tf_op jit(solution)/shard_map/ppermute | solution.py:310
  31.7 2.7 %collective-permute-done.11.refs_2_ = f32[8,1024]{1,0:T(8,128)S(1)} collective-permute-done((f32[8,1024]{1,0:T(8,128)S(1)}, f32[8,1024]{1,0:T(8,128)S(1)}, u32[]{:S(2)}, u32[]{:S(2)}) %collective-permute-start.11) | collective-permute-done | bytes 32800 | tf_op jit(solution)/shard_map/ppermute | solution.py:310
  34.5 0.8 %step_other.1 = (f32[8,1024]{1,0:T(8,128)S(1)}, f32[8,1024]{1,0:T(8,128)S(1)}, bf16[64,1024]{1,0:T(8,128)(2,1)S(1)}, bf16[64,2048]{1,0:T(8,128)(2,1)S(1)}) custom-call(bf16[8,1024]{1,0:T(8,128)(2,1)S(1)} %get-tuple-element.15.current, s32[8,1024]{1,0:T(8,128)S(1)} %get-tuple-element.16.refs_3_.tags, f32[3,8,1024]{2,1,0:T(8,128)S(1)} %get-tuple-element.17.refs_4_.scales, ...), custom_call_target="tpu_custom_call" | custom-call | tf_op jit(solution)/shard_map/step_other/pallas_call | solution.py:168
  35.3 0.1 collective-permute-start.13
  35.4 0.8 %step_own.1 = f32[64,2048]{1,0:T(8,128)S(1)} custom-call(bf16[64,1024]{1,0:T(8,128)(2,1)S(1)} %get-tuple-element.25.panel, bf16[4,1024,512]{2,1,0:T(8,128)(2,1)S(1)} %get-tuple-element.23.refs_1_.refs_2_.held), custom_call_target="tpu_custom_call" | custom-call | tf_op jit(solution)/shard_map/step_own/pallas_call | solution.py:189
  36.2 0.7 %collective-permute-done.13 = bf16[64,2048]{1,0:T(8,128)(2,1)S(1)} collective-permute-done((bf16[64,2048]{1,0:T(8,128)(2,1)S(1)}, bf16[64,2048]{1,0:T(8,128)(2,1)S(1)}, u32[]{:S(2)}, u32[]{:S(2)}) %collective-permute-start.13) | collective-permute-done | bytes 262176 | tf_op jit(solution)/shard_map/ppermute | solution.py:255
  36.9 0.1 fusion.17
  37.0 1.8 %collective-permute-start.14 = (bf16[64,512]{1,0:T(8,128)(2,1)S(1)}, bf16[64,512]{1,0:T(8,128)(2,1)S(1)}, u32[]{:S(2)}, u32[]{:S(2)}) collective-permute-start(bf16[64,512]{1,0:T(8,128)(2,1)S(1)} %get-tuple-element.37), channel_id=1, source_target_pairs={{0,28},{4,24},{8,20},{12,16},{16,12},{20,8},{24,4},{28,0},{1,29},{... | collective-permute-start | bytes 196616 | tf_op jit(solution)/shard_map/ppermute | solution.py:255
  38.7 1.0 %collective-permute-start.16 = (bf16[64,512]{1,0:T(8,128)(2,1)S(1)}, bf16[64,512]{1,0:T(8,128)(2,1)S(1)}, u32[]{:S(2)}, u32[]{:S(2)}) collective-permute-start(bf16[64,512]{1,0:T(8,128)(2,1)S(1)} %get-tuple-element.38), channel_id=1, source_target_pairs={{0,16},{4,20},{8,24},{12,28},{16,0},{20,4},{24,8},{28,12},{1,17},{... | collective-permute-start | bytes 196616 | tf_op jit(solution)/shard_map/ppermute | solution.py:255
  39.8 0.2 collective-permute-start.15
  40.0 2.1 %collective-permute-done.14 = bf16[64,512]{1,0:T(8,128)(2,1)S(1)} collective-permute-done((bf16[64,512]{1,0:T(8,128)(2,1)S(1)}, bf16[64,512]{1,0:T(8,128)(2,1)S(1)}, u32[]{:S(2)}, u32[]{:S(2)}) %collective-permute-start.14) | collective-permute-done | bytes 65568 | tf_op jit(solution)/shard_map/ppermute | solution.py:255
  42.1 1.7 %collective-permute-done.16 = bf16[64,512]{1,0:T(8,128)(2,1)S(1)} collective-permute-done((bf16[64,512]{1,0:T(8,128)(2,1)S(1)}, bf16[64,512]{1,0:T(8,128)(2,1)S(1)}, u32[]{:S(2)}, u32[]{:S(2)}) %collective-permute-start.16) | collective-permute-done | bytes 65568 | tf_op jit(solution)/shard_map/ppermute | solution.py:255
  43.8 0.1 collective-permute-done.15
  43.9 1.1 %collective-permute-start.18 = (bf16[64,512]{1,0:T(8,128)(2,1)S(1)}, bf16[64,512]{1,0:T(8,128)(2,1)S(1)}, u32[]{:S(2)}, u32[]{:S(2)}) collective-permute-start(bf16[64,512]{1,0:T(8,128)(2,1)S(1)} %fusion.3.refs_0_), channel_id=1, source_target_pairs={{0,16},{4,20},{8,24},{12,28},{16,0},{20,4},{24,8},{28,12},{1,17},{... | collective-permute-start | bytes 196616 | tf_op jit(solution)/shard_map/ppermute | solution.py:255
  45.0 0.9 %collective-permute-start.17 = (bf16[64,512]{1,0:T(8,128)(2,1)S(1)}, bf16[64,512]{1,0:T(8,128)(2,1)S(1)}, u32[]{:S(2)}, u32[]{:S(2)}) collective-permute-start(bf16[64,512]{1,0:T(8,128)(2,1)S(1)} %fusion.3.refs_0_), channel_id=1, source_target_pairs={{0,28},{4,24},{8,20},{12,16},{16,12},{20,8},{24,4},{28,0},{1,29},{... | collective-permute-start | bytes 196616 | tf_op jit(solution)/shard_map/ppermute | solution.py:255
  45.9 1.4 %collective-permute-start.20 = (bf16[64,512]{1,0:T(8,128)(2,1)S(1)}, bf16[64,512]{1,0:T(8,128)(2,1)S(1)}, u32[]{:S(2)}, u32[]{:S(2)}) collective-permute-start(bf16[64,512]{1,0:T(8,128)(2,1)S(1)} %fusion.3.refs_0_), channel_id=1, source_target_pairs={{0,12},{4,8},{8,4},{12,0},{16,28},{20,24},{24,20},{28,16},{1,13},{... | collective-permute-start | bytes 196616 | tf_op jit(solution)/shard_map/ppermute | solution.py:255
  47.2 1.1 %collective-permute-done.18.refs_1_ = bf16[64,512]{1,0:T(8,128)(2,1)S(1)} collective-permute-done((bf16[64,512]{1,0:T(8,128)(2,1)S(1)}, bf16[64,512]{1,0:T(8,128)(2,1)S(1)}, u32[]{:S(2)}, u32[]{:S(2)}) %collective-permute-start.18) | collective-permute-done | bytes 65568 | tf_op jit(solution)/shard_map/ppermute | solution.py:255
  48.3 2.0 %collective-permute-done.17.refs_0_ = bf16[64,512]{1,0:T(8,128)(2,1)S(1)} collective-permute-done((bf16[64,512]{1,0:T(8,128)(2,1)S(1)}, bf16[64,512]{1,0:T(8,128)(2,1)S(1)}, u32[]{:S(2)}, u32[]{:S(2)}) %collective-permute-start.17) | collective-permute-done | bytes 65568 | tf_op jit(solution)/shard_map/ppermute | solution.py:255
  50.3 0.2 collective-permute-start.19
  50.5 0.4 collective-permute-start.22
  50.9 0.4 collective-permute-done.20.refs_0_
  51.2 0.1 collective-permute-start.21
  51.4 0.4 image.18.refs_2_
  51.8 0.4 image.19.refs_2_
  52.2 0.4 image.20.refs_2_
  52.7 0.4 image.21.refs_3_
  53.1 0.8 %image.22.refs_2_ = f32[64,1024]{1,0:T(8,128)S(1)} custom-call(bf16[64,512]{1,0:T(8,128)(2,1)S(1)} %collective-permute-done.17.refs_0_, bf16[64,512]{1,0:T(8,128)(2,1)S(1)} %collective-permute-done.18.refs_1_, bf16[4,1024,512]{2,1,0:T(8,128)(2,1)S(1)} %get-tuple-element.23.refs_1_.refs_2_.held, f32[64,1024]{1,0:T(8,128)S(1)} %image.21.refs_3_), custom_call_target="tpu_custom_call" | custom-call | tf_op jit(solution)/shard_map/image/pallas_call | solution.py:236
  53.9 0.8 %image.23 = f32[8,1024]{1,0:T(8,128)S(1)} custom-call(bf16[64,1024]{1,0:T(8,128)(2,1)S(1)} %collective-permute-done.19.refs_0_, bf16[4,1024,512]{2,1,0:T(8,128)(2,1)S(1)} %get-tuple-element.18.refs_1_.held, f32[64,1024]{1,0:T(8,128)S(1)} %image.22.refs_2_, s32[8,1024]{1,0:T(8,128)S(1)} %get-tuple-element.16.refs_3_.tags, ...), custom_call_target="tpu_custom_call" | custom-call | tf_op jit(solution)/shard_map/image/pallas_call | solution.py:236
  54.7 1.7 %collective-permute-start.25 = (f32[8,1024]{1,0:T(8,128)S(1)}, f32[8,1024]{1,0:T(8,128)S(1)}, u32[]{:S(2)}, u32[]{:S(2)}) collective-permute-start(f32[8,1024]{1,0:T(8,128)S(1)} %image.23), channel_id=1, source_target_pairs={{0,3},{1,2},{2,1},{3,0},{4,7},{5,6},{6,5},{7,4},{8,11},{9,10},{10,... | collective-permute-start | bytes 98312 | tf_op jit(solution)/shard_map/ppermute | solution.py:310
  56.3 0.5 collective-permute-start.24
  56.8 2.3 %collective-permute-start.23 = (f32[8,1024]{1,0:T(8,128)S(1)}, f32[8,1024]{1,0:T(8,128)S(1)}, u32[]{:S(2)}, u32[]{:S(2)}) collective-permute-start(f32[8,1024]{1,0:T(8,128)S(1)} %image.23), channel_id=1, source_target_pairs={{0,1},{1,0},{2,3},{3,2},{4,5},{5,4},{6,7},{7,6},{8,9},{9,8},{10,11... | collective-permute-start | bytes 98312 | tf_op jit(solution)/shard_map/ppermute | solution.py:310
  59.1 0.6 copy.8
  59.7 0.9 %collective-permute-done.25 = f32[8,1024]{1,0:T(8,128)S(1)} collective-permute-done((f32[8,1024]{1,0:T(8,128)S(1)}, f32[8,1024]{1,0:T(8,128)S(1)}, u32[]{:S(2)}, u32[]{:S(2)}) %collective-permute-start.25) | collective-permute-done | bytes 32800 | tf_op jit(solution)/shard_map/ppermute | solution.py:310
  60.6 0.9 %collective-permute-done.24 = f32[8,1024]{1,0:T(8,128)S(1)} collective-permute-done((f32[8,1024]{1,0:T(8,128)S(1)}, f32[8,1024]{1,0:T(8,128)S(1)}, u32[]{:S(2)}, u32[]{:S(2)}) %collective-permute-start.24) | collective-permute-done | bytes 32800 | tf_op jit(solution)/shard_map/ppermute | solution.py:310
  61.5 0.1 collective-permute-done.23
  61.6 0.6 %add_add_fusion = f32[8,1024]{1,0:T(8,128)} fusion(f32[8,1024]{1,0:T(8,128)S(1)} %get-tuple-element.27, f32[8,1024]{1,0:T(8,128)S(1)} %collective-permute-done.24, f32[8,1024]{1,0:T(8,128)S(1)} %collective-permute-done.25, f32[8,1024]{1,0:T(8,128)S(1)} %image.23, f32[8,1024]{1,0:T(8,128)S(1)} %collective-permute-done.23), kind=kLoop, calls=%fused_computation.26 | loop fusion | flops 32768 | bytes 196608 | tf_op jit(solution)/shard_map/add | solution.py:325
  (23 shorter events, 0.3 us)
Async XLA Ops:
  3.3 2.8 %collective-permute-start = (f32[72,2048]{1,0:T(8,128)S(1)}, f32[72,2048]{1,0:T(8,128)S(1)}, u32[]{:S(2)}, u32[]{:S(2)}) collective-permute-start(f32[72,2048]{1,0:T(8,128)S(1)} %get-tuple-element.22), channel_id=1, source_target_pairs={{0,4},{4,0},{8,12},{12,8},{16,20},{20,16},{24,28},{28,24},{1,5},{5... | collective-permute-start | bytes 1769480 | tf_op jit(solution)/shard_map/ppermute | solution.py:255
  6.3 6.3 %collective-permute-start.1 = (f16[72,512]{1,0:T(8,128)(2,1)S(1)}, f16[72,512]{1,0:T(8,128)(2,1)S(1)}, u32[]{:S(2)}, u32[]{:S(2)}) collective-permute-start(f16[72,512]{1,0:T(8,128)(2,1)S(1)} %get-tuple-element.34), channel_id=1, source_target_pairs={{0,28},{4,24},{8,20},{12,16},{16,12},{20,8},{24,4},{28,0},{1,29},{... | collective-permute-start | bytes 221192 | tf_op jit(solution)/shard_map/ppermute | solution.py:255
  9.9 4.4 %collective-permute-start.2 = (f16[72,512]{1,0:T(8,128)(2,1)S(1)}, f16[72,512]{1,0:T(8,128)(2,1)S(1)}, u32[]{:S(2)}, u32[]{:S(2)}) collective-permute-start(f16[72,512]{1,0:T(8,128)(2,1)S(1)} %get-tuple-element.35), channel_id=1, source_target_pairs={{0,12},{4,8},{8,4},{12,0},{16,28},{20,24},{24,20},{28,16},{1,13},{... | collective-permute-start | bytes 221192 | tf_op jit(solution)/shard_map/ppermute | solution.py:255
  10.1 4.7 %collective-permute-start.3 = (f16[72,512]{1,0:T(8,128)(2,1)S(1)}, f16[72,512]{1,0:T(8,128)(2,1)S(1)}, u32[]{:S(2)}, u32[]{:S(2)}) collective-permute-start(f16[72,512]{1,0:T(8,128)(2,1)S(1)} %get-tuple-element.36), channel_id=1, source_target_pairs={{0,16},{4,20},{8,24},{12,28},{16,0},{20,4},{24,8},{28,12},{1,17},{... | collective-permute-start | bytes 221192 | tf_op jit(solution)/shard_map/ppermute | solution.py:255
  14.8 4.4 %collective-permute-start.5 = (bf16[72,512]{1,0:T(8,128)(2,1)S(1)}, bf16[72,512]{1,0:T(8,128)(2,1)S(1)}, u32[]{:S(2)}, u32[]{:S(2)}) collective-permute-start(bf16[72,512]{1,0:T(8,128)(2,1)S(1)} %pad_maximum_fusion.5.refs_0_), channel_id=1, source_target_pairs={{0,16},{4,20},{8,24},{12,28},{16,0},{20,4},{24,8},{28,12},{1,17},{... | collective-permute-start | bytes 221192 | tf_op jit(solution)/shard_map/ppermute | solution.py:255
  16.1 5.4 %collective-permute-start.4 = (bf16[72,512]{1,0:T(8,128)(2,1)S(1)}, bf16[72,512]{1,0:T(8,128)(2,1)S(1)}, u32[]{:S(2)}, u32[]{:S(2)}) collective-permute-start(bf16[72,512]{1,0:T(8,128)(2,1)S(1)} %pad_maximum_fusion.5.refs_0_), channel_id=1, source_target_pairs={{0,28},{4,24},{8,20},{12,16},{16,12},{20,8},{24,4},{28,0},{1,29},{... | collective-permute-start | bytes 221192 | tf_op jit(solution)/shard_map/ppermute | solution.py:255
  17.2 5.0 %collective-permute-start.7 = (bf16[72,512]{1,0:T(8,128)(2,1)S(1)}, bf16[72,512]{1,0:T(8,128)(2,1)S(1)}, u32[]{:S(2)}, u32[]{:S(2)}) collective-permute-start(bf16[72,512]{1,0:T(8,128)(2,1)S(1)} %pad_maximum_fusion.5.refs_0_), channel_id=1, source_target_pairs={{0,12},{4,8},{8,4},{12,0},{16,28},{20,24},{24,20},{28,16},{1,13},{... | collective-permute-start | bytes 221192 | tf_op jit(solution)/shard_map/ppermute | solution.py:255
  21.5 3.6 %collective-permute-start.6 = (bf16[72,1024]{1,0:T(8,128)(2,1)S(1)}, bf16[72,1024]{1,0:T(8,128)(2,1)S(1)}, u32[]{:S(2)}, u32[]{:S(2)}) collective-permute-start(bf16[72,1024]{1,0:T(8,128)(2,1)S(1)} %pad_maximum_fusion), channel_id=1, source_target_pairs={{0,4},{4,0},{8,12},{12,8},{16,20},{20,16},{24,28},{28,24},{1,5},{5... | collective-permute-start | bytes 442376 | tf_op jit(solution)/shard_map/ppermute | solution.py:255
  21.7 1.4 %collective-permute-start.9 = (bf16[72,512]{1,0:T(8,128)(2,1)S(1)}, bf16[72,512]{1,0:T(8,128)(2,1)S(1)}, u32[]{:S(2)}, u32[]{:S(2)}) collective-permute-start(bf16[72,512]{1,0:T(8,128)(2,1)S(1)} %pad_maximum_fusion.5.refs_0_), channel_id=1, source_target_pairs={{0,4},{4,0},{8,12},{12,8},{16,20},{20,16},{24,28},{28,24},{1,5},{5... | collective-permute-start | bytes 221192 | tf_op jit(solution)/shard_map/ppermute | solution.py:255
  22.1 1.9 %collective-permute-start.8 = (bf16[72,512]{1,0:T(8,128)(2,1)S(1)}, bf16[72,512]{1,0:T(8,128)(2,1)S(1)}, u32[]{:S(2)}, u32[]{:S(2)}) collective-permute-start(bf16[72,512]{1,0:T(8,128)(2,1)S(1)} %collective-permute-done.7.refs_0_), channel_id=1, source_target_pairs={{0,4},{4,0},{8,12},{12,8},{16,20},{20,16},{24,28},{28,24},{1,5},{5... | collective-permute-start | bytes 221192 | tf_op jit(solution)/shard_map/ppermute | solution.py:255
  26.0 5.8 %collective-permute-start.12 = (f32[8,1024]{1,0:T(8,128)S(1)}, f32[8,1024]{1,0:T(8,128)S(1)}, u32[]{:S(2)}, u32[]{:S(2)}) collective-permute-start(f32[8,1024]{1,0:T(8,128)S(1)} %image.17.refs_0_), channel_id=1, source_target_pairs={{0,3},{1,2},{2,1},{3,0},{4,7},{5,6},{6,5},{7,4},{8,11},{9,10},{10,... | collective-permute-start | bytes 98312 | tf_op jit(solution)/shard_map/ppermute | solution.py:310
  29.6 4.8 %collective-permute-start.11 = (f32[8,1024]{1,0:T(8,128)S(1)}, f32[8,1024]{1,0:T(8,128)S(1)}, u32[]{:S(2)}, u32[]{:S(2)}) collective-permute-start(f32[8,1024]{1,0:T(8,128)S(1)} %image.17.refs_0_), channel_id=1, source_target_pairs={{0,2},{1,3},{2,0},{3,1},{4,6},{5,7},{6,4},{7,5},{8,10},{9,11},{10,... | collective-permute-start | bytes 98312 | tf_op jit(solution)/shard_map/ppermute | solution.py:310
  29.6 4.8 %collective-permute-start.10 = (f32[8,1024]{1,0:T(8,128)S(1)}, f32[8,1024]{1,0:T(8,128)S(1)}, u32[]{:S(2)}, u32[]{:S(2)}) collective-permute-start(f32[8,1024]{1,0:T(8,128)S(1)} %image.17.refs_0_), channel_id=1, source_target_pairs={{0,1},{1,0},{2,3},{3,2},{4,5},{5,4},{6,7},{7,6},{8,9},{9,8},{10,11... | collective-permute-start | bytes 98312 | tf_op jit(solution)/shard_map/ppermute | solution.py:310
  35.3 1.6 %collective-permute-start.13 = (bf16[64,2048]{1,0:T(8,128)(2,1)S(1)}, bf16[64,2048]{1,0:T(8,128)(2,1)S(1)}, u32[]{:S(2)}, u32[]{:S(2)}) collective-permute-start(bf16[64,2048]{1,0:T(8,128)(2,1)S(1)} %get-tuple-element.26), channel_id=1, source_target_pairs={{0,4},{4,0},{8,12},{12,8},{16,20},{20,16},{24,28},{28,24},{1,5},{5... | collective-permute-start | bytes 786440 | tf_op jit(solution)/shard_map/ppermute | solution.py:255
  37.0 5.1 %collective-permute-start.14 = (bf16[64,512]{1,0:T(8,128)(2,1)S(1)}, bf16[64,512]{1,0:T(8,128)(2,1)S(1)}, u32[]{:S(2)}, u32[]{:S(2)}) collective-permute-start(bf16[64,512]{1,0:T(8,128)(2,1)S(1)} %get-tuple-element.37), channel_id=1, source_target_pairs={{0,28},{4,24},{8,20},{12,16},{16,12},{20,8},{24,4},{28,0},{1,29},{... | collective-permute-start | bytes 196616 | tf_op jit(solution)/shard_map/ppermute | solution.py:255
  38.7 5.0 %collective-permute-start.16 = (bf16[64,512]{1,0:T(8,128)(2,1)S(1)}, bf16[64,512]{1,0:T(8,128)(2,1)S(1)}, u32[]{:S(2)}, u32[]{:S(2)}) collective-permute-start(bf16[64,512]{1,0:T(8,128)(2,1)S(1)} %get-tuple-element.38), channel_id=1, source_target_pairs={{0,16},{4,20},{8,24},{12,28},{16,0},{20,4},{24,8},{28,12},{1,17},{... | collective-permute-start | bytes 196616 | tf_op jit(solution)/shard_map/ppermute | solution.py:255
  39.8 4.1 %collective-permute-start.15 = (bf16[64,512]{1,0:T(8,128)(2,1)S(1)}, bf16[64,512]{1,0:T(8,128)(2,1)S(1)}, u32[]{:S(2)}, u32[]{:S(2)}) collective-permute-start(bf16[64,512]{1,0:T(8,128)(2,1)S(1)} %get-tuple-element.39), channel_id=1, source_target_pairs={{0,12},{4,8},{8,4},{12,0},{16,28},{20,24},{24,20},{28,16},{1,13},{... | collective-permute-start | bytes 196616 | tf_op jit(solution)/shard_map/ppermute | solution.py:255
  43.9 4.3 %collective-permute-start.18 = (bf16[64,512]{1,0:T(8,128)(2,1)S(1)}, bf16[64,512]{1,0:T(8,128)(2,1)S(1)}, u32[]{:S(2)}, u32[]{:S(2)}) collective-permute-start(bf16[64,512]{1,0:T(8,128)(2,1)S(1)} %fusion.3.refs_0_), channel_id=1, source_target_pairs={{0,16},{4,20},{8,24},{12,28},{16,0},{20,4},{24,8},{28,12},{1,17},{... | collective-permute-start | bytes 196616 | tf_op jit(solution)/shard_map/ppermute | solution.py:255
  45.0 5.3 %collective-permute-start.17 = (bf16[64,512]{1,0:T(8,128)(2,1)S(1)}, bf16[64,512]{1,0:T(8,128)(2,1)S(1)}, u32[]{:S(2)}, u32[]{:S(2)}) collective-permute-start(bf16[64,512]{1,0:T(8,128)(2,1)S(1)} %fusion.3.refs_0_), channel_id=1, source_target_pairs={{0,28},{4,24},{8,20},{12,16},{16,12},{20,8},{24,4},{28,0},{1,29},{... | collective-permute-start | bytes 196616 | tf_op jit(solution)/shard_map/ppermute | solution.py:255
  45.9 5.4 %collective-permute-start.20 = (bf16[64,512]{1,0:T(8,128)(2,1)S(1)}, bf16[64,512]{1,0:T(8,128)(2,1)S(1)}, u32[]{:S(2)}, u32[]{:S(2)}) collective-permute-start(bf16[64,512]{1,0:T(8,128)(2,1)S(1)} %fusion.3.refs_0_), channel_id=1, source_target_pairs={{0,12},{4,8},{8,4},{12,0},{16,28},{20,24},{24,20},{28,16},{1,13},{... | collective-permute-start | bytes 196616 | tf_op jit(solution)/shard_map/ppermute | solution.py:255
  50.3 3.6 %collective-permute-start.19 = (bf16[64,1024]{1,0:T(8,128)(2,1)S(1)}, bf16[64,1024]{1,0:T(8,128)(2,1)S(1)}, u32[]{:S(2)}, u32[]{:S(2)}) collective-permute-start(bf16[64,1024]{1,0:T(8,128)(2,1)S(1)} %pad_maximum_fusion.1), channel_id=1, source_target_pairs={{0,4},{4,0},{8,12},{12,8},{16,20},{20,16},{24,28},{28,24},{1,5},{5... | collective-permute-start | bytes 393224 | tf_op jit(solution)/shard_map/ppermute | solution.py:255
  50.5 1.3 %collective-permute-start.22 = (bf16[64,512]{1,0:T(8,128)(2,1)S(1)}, bf16[64,512]{1,0:T(8,128)(2,1)S(1)}, u32[]{:S(2)}, u32[]{:S(2)}) collective-permute-start(bf16[64,512]{1,0:T(8,128)(2,1)S(1)} %fusion.3.refs_0_), channel_id=1, source_target_pairs={{0,4},{4,0},{8,12},{12,8},{16,20},{20,16},{24,28},{28,24},{1,5},{5... | collective-permute-start | bytes 196616 | tf_op jit(solution)/shard_map/ppermute | solution.py:255
  51.2 1.4 %collective-permute-start.21 = (bf16[64,512]{1,0:T(8,128)(2,1)S(1)}, bf16[64,512]{1,0:T(8,128)(2,1)S(1)}, u32[]{:S(2)}, u32[]{:S(2)}) collective-permute-start(bf16[64,512]{1,0:T(8,128)(2,1)S(1)} %collective-permute-done.20.refs_0_), channel_id=1, source_target_pairs={{0,4},{4,0},{8,12},{12,8},{16,20},{20,16},{24,28},{28,24},{1,5},{5... | collective-permute-start | bytes 196616 | tf_op jit(solution)/shard_map/ppermute | solution.py:255
  54.7 6.0 %collective-permute-start.25 = (f32[8,1024]{1,0:T(8,128)S(1)}, f32[8,1024]{1,0:T(8,128)S(1)}, u32[]{:S(2)}, u32[]{:S(2)}) collective-permute-start(f32[8,1024]{1,0:T(8,128)S(1)} %image.23), channel_id=1, source_target_pairs={{0,3},{1,2},{2,1},{3,0},{4,7},{5,6},{6,5},{7,4},{8,11},{9,10},{10,... | collective-permute-start | bytes 98312 | tf_op jit(solution)/shard_map/ppermute | solution.py:310
  56.3 5.2 %collective-permute-start.24 = (f32[8,1024]{1,0:T(8,128)S(1)}, f32[8,1024]{1,0:T(8,128)S(1)}, u32[]{:S(2)}, u32[]{:S(2)}) collective-permute-start(f32[8,1024]{1,0:T(8,128)S(1)} %image.23), channel_id=1, source_target_pairs={{0,2},{1,3},{2,0},{3,1},{4,6},{5,7},{6,4},{7,5},{8,10},{9,11},{10,... | collective-permute-start | bytes 98312 | tf_op jit(solution)/shard_map/ppermute | solution.py:310
  56.8 4.8 %collective-permute-start.23 = (f32[8,1024]{1,0:T(8,128)S(1)}, f32[8,1024]{1,0:T(8,128)S(1)}, u32[]{:S(2)}, u32[]{:S(2)}) collective-permute-start(f32[8,1024]{1,0:T(8,128)S(1)} %image.23), channel_id=1, source_target_pairs={{0,1},{1,0},{2,3},{3,2},{4,5},{5,4},{6,7},{7,6},{8,9},{9,8},{10,11... | collective-permute-start | bytes 98312 | tf_op jit(solution)/shard_map/ppermute | solution.py:310

commit v9 on v8

--- a/solution.py
+++ b/solution.py
@@ -247,6 +247,7 @@
     samp, snp = mesh.shape["samp"], mesh.shape["snp"]
     chips = samp // 2
     far = sorted(range(1, chips), key=lambda step: -bin(step).count("1"))
+    far_down = sorted(far, key=lambda step: (-bin(step).count("1"), -step))
     near = [1] + [step for step in far if step != 1]
     early = near[: chips // 2 - 1]
     late = near[chips // 2 - 1 :]
@@ -270,12 +271,13 @@
         return scaled.reshape(rows, columns)
 
     def reduce_panel(given, own, probes, exact):
+        order = far if exact else far_down
         width = own.shape[1] // chips
         rows = ENVS * probes
         pair = own + exchange(given, 1).astype(f32)
         sent = pack(pair) if exact else pair.astype(jnp.bfloat16)
         total = pair[:rows, :width]
-        for step in far:
+        for step in order:
             taken = between(sent[:, step * width : (step + 1) * width], step)
             total = total + (unpack(taken) if exact else taken.astype(f32))
         if exact:
@@ -288,11 +290,14 @@
             pieces[step] = between(mine, step)
         other = exchange(mine, 1)
         total = image([mine], held_own, [0])
-        total = image([other], held_other, [0], total)
+        mine_other = other
         for step in early:
             other = exchange(pieces[step], 1)
             total = image([pieces[step]], held_own, [step], total)
-            total = image([other], held_other, [step], total)
+            if step == early[-1]:
+                total = image([mine_other, other], held_other, [0, step], total)
+            else:
+                total = image([other], held_other, [step], total)
         late_pieces = [pieces[step] for step in late]
         other = exchange(jnp.concatenate(late_pieces, axis=1), 1)
         total = image(late_pieces, held_own, late, total)
@@ -308,7 +313,7 @@
         def spread(weighted):
             pieces = {
                 step: lax.ppermute(weighted, "snp", [(k, k ^ step) for k in range(snp)])
-                for step in range(snp - 1, 0, -1)
+                for step in range(1, snp)
             }
             return [weighted] + [pieces[step] for step in range(1, snp)]
 

time: 62.5 us -> 61.8 us (0.989)
  waiting for transfers between devices: 22 us -> 21.3 us
    pallas_call x12 -> x10, Pallas kernels: 6.55 us -> 6.3 us  [image(): pl.pallas_call(functools.partial(image_body, blocks=tuple(blocks), pieces...]
where the time goes in v9:
time: 61.8 us; the launch traced here: 61.5 us
  starting transfers between devices  24.9 us (40%)
  waiting for transfers between devices  21.3 us (34%)
  Pallas kernels  12.8 us (21%)
  other arithmetic  1.07 us (2%)
  between operations  0.85 us (1%)
  local copies, waits for them, and re-layouts  0.63 us (1%)
    ppermute x20, starting transfers between devices, exchange(): return lax.ppermute(block, 'samp', [(k, k ^ offset) for k in range(samp)])  16 us
    ppermute x20, waiting for transfers between devices, exchange(): return lax.ppermute(block, 'samp', [(k, k ^ offset) for k in range(samp)])  15.5 us
    ppermute x6, starting transfers between devices, spread(): lax.ppermute(weighted, 'snp', [(k, k ^ step) for k in range(snp)])  8.9 us
    pallas_call x10, Pallas kernels, image(): pl.pallas_call(functools.partial(image_body, blocks=tuple(blocks), pieces...  6.3 us
    ppermute x6, waiting for transfers between devices, spread(): lax.ppermute(weighted, 'snp', [(k, k ^ step) for k in range(snp)])  5.73 us
    pallas_call x1, Pallas kernels, load_first(): pl.pallas_call(functools.partial(first_body, snps=snps), in_specs=[HBM] *...  2.63 us
    pallas_call x1, Pallas kernels, load_second(): pl.pallas_call(second_body, in_specs=[VMEM, HBM, VMEM], out_specs=(VMEM,...  2.21 us
  transfers between devices with their start and end apart: 26, of which 18 were waited for; matrix products, arithmetic and copies ran while one was open for 1% of the time, Pallas kernels for 13%

profile of v9, /device:TPU:0, one launch (start us, length us, event | category | flops | bytes accessed | tf_op | source)
XLA Modules:
  0.0 61.5 jit_solution(14896751464872543107)
XLA Ops:
  0.6 2.6 %load_other.1 = (bf16[4,1024,512]{2,1,0:T(8,128)(2,1)S(1)}, bf16[4,1024,512]{2,1,0:T(8,128)(2,1)S(1)}, f32[72,2048]{1,0:T(8,128)S(1)}, bf16[64,1024]{1,0:T(8,128...) custom-call(bf16[8,1024]{1,0:T(8,128)(2,1)} %probes.1, ...), custom_call_target="tpu_custom_call" | custom-call | tf_op jit(solution)/shard_map/load_other/pallas_call | solution.py:95
  3.3 0.6 collective-permute-start
  3.8 2.2 %load_own.1 = (bf16[4,1024,512]{2,1,0:T(8,128)(2,1)S(1)}, f32[72,2048]{1,0:T(8,128)S(1)}) custom-call(bf16[64,1024]{1,0:T(8,128)(2,1)S(1)} %get-tuple-element.19.panel, bf16[1024,4096]{1,0:T(8,128)(2,1)} %genotypes.3, bf16[4,1024,512]{2,1,0:T(8,128)(2,1)S(1)} %get-tuple-element.20.begun), custom_call_target="tpu_custom_call", output_to_operand_aliasing={{0}: (2, {})} | custom-call | tf_op jit(solution)/shard_map/load_own/pallas_call | solution.py:134
  6.1 0.1 add.39
  6.2 0.1 pad_maximum_fusion.4
  6.3 3.6 %collective-permute-start.1 = (f16[72,512]{1,0:T(8,128)(2,1)S(1)}, f16[72,512]{1,0:T(8,128)(2,1)S(1)}, u32[]{:S(2)}, u32[]{:S(2)}) collective-permute-start(f16[72,512]{1,0:T(8,128)(2,1)S(1)} %get-tuple-element.34), channel_id=1, source_target_pairs={{0,28},{4,24},{8,20},{12,16},{16,12},{20,8},{24,4},{28,0},{1,29},{... | collective-permute-start | bytes 221192 | tf_op jit(solution)/shard_map/ppermute | solution.py:256
  9.9 0.2 collective-permute-start.2
  10.1 0.5 collective-permute-start.3
  10.5 2.0 %collective-permute-done.1 = f16[72,512]{1,0:T(8,128)(2,1)S(1)} collective-permute-done((f16[72,512]{1,0:T(8,128)(2,1)S(1)}, f16[72,512]{1,0:T(8,128)(2,1)S(1)}, u32[]{:S(2)}, u32[]{:S(2)}) %collective-permute-start.1) | collective-permute-done | bytes 73760 | tf_op jit(solution)/shard_map/ppermute | solution.py:256
  12.6 1.7 %collective-permute-done.2 = f16[72,512]{1,0:T(8,128)(2,1)S(1)} collective-permute-done((f16[72,512]{1,0:T(8,128)(2,1)S(1)}, f16[72,512]{1,0:T(8,128)(2,1)S(1)}, u32[]{:S(2)}, u32[]{:S(2)}) %collective-permute-start.2) | collective-permute-done | bytes 73760 | tf_op jit(solution)/shard_map/ppermute | solution.py:256
  14.3 0.4 collective-permute-done.3
  14.8 0.1 bitcast_reduce_fusion
  14.8 1.3 %collective-permute-start.5 = (bf16[72,512]{1,0:T(8,128)(2,1)S(1)}, bf16[72,512]{1,0:T(8,128)(2,1)S(1)}, u32[]{:S(2)}, u32[]{:S(2)}) collective-permute-start(bf16[72,512]{1,0:T(8,128)(2,1)S(1)} %pad_maximum_fusion.5.refs_0_), channel_id=1, source_target_pairs={{0,16},{4,20},{8,24},{12,28},{16,0},{20,4},{24,8},{28,12},{1,17},{... | collective-permute-start | bytes 221192 | tf_op jit(solution)/shard_map/ppermute | solution.py:256
  16.1 1.0 %collective-permute-start.4 = (bf16[72,512]{1,0:T(8,128)(2,1)S(1)}, bf16[72,512]{1,0:T(8,128)(2,1)S(1)}, u32[]{:S(2)}, u32[]{:S(2)}) collective-permute-start(bf16[72,512]{1,0:T(8,128)(2,1)S(1)} %pad_maximum_fusion.5.refs_0_), channel_id=1, source_target_pairs={{0,28},{4,24},{8,20},{12,16},{16,12},{20,8},{24,4},{28,0},{1,29},{... | collective-permute-start | bytes 221192 | tf_op jit(solution)/shard_map/ppermute | solution.py:256
  17.2 1.0 %collective-permute-start.8 = (bf16[72,512]{1,0:T(8,128)(2,1)S(1)}, bf16[72,512]{1,0:T(8,128)(2,1)S(1)}, u32[]{:S(2)}, u32[]{:S(2)}) collective-permute-start(bf16[72,512]{1,0:T(8,128)(2,1)S(1)} %pad_maximum_fusion.5.refs_0_), channel_id=1, source_target_pairs={{0,12},{4,8},{8,4},{12,0},{16,28},{20,24},{24,20},{28,16},{1,13},{... | collective-permute-start | bytes 221192 | tf_op jit(solution)/shard_map/ppermute | solution.py:256
  18.1 1.1 %collective-permute-done.5.refs_1_ = bf16[72,512]{1,0:T(8,128)(2,1)S(1)} collective-permute-done((bf16[72,512]{1,0:T(8,128)(2,1)S(1)}, bf16[72,512]{1,0:T(8,128)(2,1)S(1)}, u32[]{:S(2)}, u32[]{:S(2)}) %collective-permute-start.5) | collective-permute-done | bytes 73760 | tf_op jit(solution)/shard_map/ppermute | solution.py:256
  19.3 2.3 %collective-permute-done.4.refs_0_ = bf16[72,512]{1,0:T(8,128)(2,1)S(1)} collective-permute-done((bf16[72,512]{1,0:T(8,128)(2,1)S(1)}, bf16[72,512]{1,0:T(8,128)(2,1)S(1)}, u32[]{:S(2)}, u32[]{:S(2)}) %collective-permute-start.4) | collective-permute-done | bytes 73760 | tf_op jit(solution)/shard_map/ppermute | solution.py:256
  21.5 0.1 collective-permute-start.6
  21.7 0.4 collective-permute-start.7
  22.1 0.0 collective-permute-done.8.refs_0_
  22.1 0.1 collective-permute-start.9
  22.2 0.4 image.10.refs_2_
  22.6 0.5 image.11.refs_3_
  23.1 0.3 collective-permute-done.9.refs_1_
  23.4 0.8 %image.12.refs_3_ = f32[72,1024]{1,0:T(8,128)S(1)} custom-call(bf16[72,512]{1,0:T(8,128)(2,1)S(1)} %collective-permute-done.7.refs_0_, bf16[72,512]{1,0:T(8,128)(2,1)S(1)} %collective-permute-done.9.refs_1_, bf16[4,1024,512]{2,1,0:T(8,128)(2,1)S(1)} %get-tuple-element.18.refs_2_.refs_1_.held, f32[72,1024]{1,0:T(8,128)S(1)} %image.11.refs_3_), custom_call_target="tpu_custom_call" | custom-call | tf_op jit(solution)/shard_map/image/pallas_call | solution.py:236
  24.1 0.8 %image.13.refs_2_ = f32[72,1024]{1,0:T(8,128)S(1)} custom-call(bf16[72,512]{1,0:T(8,128)(2,1)S(1)} %collective-permute-done.4.refs_0_, bf16[72,512]{1,0:T(8,128)(2,1)S(1)} %collective-permute-done.5.refs_1_, bf16[4,1024,512]{2,1,0:T(8,128)(2,1)S(1)} %get-tuple-element.23.refs_1_.refs_2_.held, f32[72,1024]{1,0:T(8,128)S(1)} %image.12.refs_3_), custom_call_target="tpu_custom_call" | custom-call | tf_op jit(solution)/shard_map/image/pallas_call | solution.py:236
  24.9 0.8 %image.14.refs_0_ = f32[8,1024]{1,0:T(8,128)S(1)} custom-call(bf16[72,1024]{1,0:T(8,128)(2,1)S(1)} %collective-permute-done.6.refs_0_, bf16[4,1024,512]{2,1,0:T(8,128)(2,1)S(1)} %get-tuple-element.18.refs_2_.refs_1_.held, f32[72,1024]{1,0:T(8,128)S(1)} %image.13.refs_2_, s32[8,1024]{1,0:T(8,128)S(1)} %get-tuple-element.16.refs_3_.tags, ...), custom_call_target="tpu_custom_call" | custom-call | tf_op jit(solution)/shard_map/image/pallas_call | solution.py:236
  25.7 3.7 %collective-permute-start.12 = (f32[8,1024]{1,0:T(8,128)S(1)}, f32[8,1024]{1,0:T(8,128)S(1)}, u32[]{:S(2)}, u32[]{:S(2)}) collective-permute-start(f32[8,1024]{1,0:T(8,128)S(1)} %image.14.refs_0_), channel_id=1, source_target_pairs={{0,3},{1,2},{2,1},{3,0},{4,7},{5,6},{6,5},{7,4},{8,11},{9,10},{10,... | collective-permute-start | bytes 98312 | tf_op jit(solution)/shard_map/ppermute | solution.py:315
  29.4 0.8 %collective-permute-start.10 = (f32[8,1024]{1,0:T(8,128)S(1)}, f32[8,1024]{1,0:T(8,128)S(1)}, u32[]{:S(2)}, u32[]{:S(2)}) collective-permute-start(f32[8,1024]{1,0:T(8,128)S(1)} %image.14.refs_0_), channel_id=1, source_target_pairs={{0,1},{1,0},{2,3},{3,2},{4,5},{5,4},{6,7},{7,6},{8,9},{9,8},{10,11... | collective-permute-start | bytes 98312 | tf_op jit(solution)/shard_map/ppermute | solution.py:315
  30.1 1.3 %collective-permute-done.12.refs_3_ = f32[8,1024]{1,0:T(8,128)S(1)} collective-permute-done((f32[8,1024]{1,0:T(8,128)S(1)}, f32[8,1024]{1,0:T(8,128)S(1)}, u32[]{:S(2)}, u32[]{:S(2)}) %collective-permute-start.12) | collective-permute-done | bytes 32800 | tf_op jit(solution)/shard_map/ppermute | solution.py:315
  31.4 2.7 %collective-permute-done.11.refs_2_ = f32[8,1024]{1,0:T(8,128)S(1)} collective-permute-done((f32[8,1024]{1,0:T(8,128)S(1)}, f32[8,1024]{1,0:T(8,128)S(1)}, u32[]{:S(2)}, u32[]{:S(2)}) %collective-permute-start.11) | collective-permute-done | bytes 32800 | tf_op jit(solution)/shard_map/ppermute | solution.py:315
  34.2 0.8 %step_other.1 = (f32[8,1024]{1,0:T(8,128)S(1)}, f32[8,1024]{1,0:T(8,128)S(1)}, bf16[64,1024]{1,0:T(8,128)(2,1)S(1)}, bf16[64,2048]{1,0:T(8,128)(2,1)S(1)}) custom-call(bf16[8,1024]{1,0:T(8,128)(2,1)S(1)} %get-tuple-element.15.current, s32[8,1024]{1,0:T(8,128)S(1)} %get-tuple-element.16.refs_3_.tags, f32[3,8,1024]{2,1,0:T(8,128)S(1)} %get-tuple-element.17.refs_4_.scales, ...), custom_call_target="tpu_custom_call" | custom-call | tf_op jit(solution)/shard_map/step_other/pallas_call | solution.py:168
  35.0 0.1 collective-permute-start.13
  35.1 0.8 %step_own.1 = f32[64,2048]{1,0:T(8,128)S(1)} custom-call(bf16[64,1024]{1,0:T(8,128)(2,1)S(1)} %get-tuple-element.25.panel, bf16[4,1024,512]{2,1,0:T(8,128)(2,1)S(1)} %get-tuple-element.23.refs_1_.refs_2_.held), custom_call_target="tpu_custom_call" | custom-call | tf_op jit(solution)/shard_map/step_own/pallas_call | solution.py:189
  35.9 0.7 %collective-permute-done.13 = bf16[64,2048]{1,0:T(8,128)(2,1)S(1)} collective-permute-done((bf16[64,2048]{1,0:T(8,128)(2,1)S(1)}, bf16[64,2048]{1,0:T(8,128)(2,1)S(1)}, u32[]{:S(2)}, u32[]{:S(2)}) %collective-permute-start.13) | collective-permute-done | bytes 262176 | tf_op jit(solution)/shard_map/ppermute | solution.py:256
  36.6 0.1 fusion.17
  36.7 2.1 %collective-permute-start.14 = (bf16[64,512]{1,0:T(8,128)(2,1)S(1)}, bf16[64,512]{1,0:T(8,128)(2,1)S(1)}, u32[]{:S(2)}, u32[]{:S(2)}) collective-permute-start(bf16[64,512]{1,0:T(8,128)(2,1)S(1)} %get-tuple-element.37), channel_id=1, source_target_pairs={{0,28},{4,24},{8,20},{12,16},{16,12},{20,8},{24,4},{28,0},{1,29},{... | collective-permute-start | bytes 196616 | tf_op jit(solution)/shard_map/ppermute | solution.py:256
  38.8 0.5 collective-permute-start.16
  39.3 0.7 %collective-permute-start.15 = (bf16[64,512]{1,0:T(8,128)(2,1)S(1)}, bf16[64,512]{1,0:T(8,128)(2,1)S(1)}, u32[]{:S(2)}, u32[]{:S(2)}) collective-permute-start(bf16[64,512]{1,0:T(8,128)(2,1)S(1)} %get-tuple-element.39), channel_id=1, source_target_pairs={{0,16},{4,20},{8,24},{12,28},{16,0},{20,4},{24,8},{28,12},{1,17},{... | collective-permute-start | bytes 196616 | tf_op jit(solution)/shard_map/ppermute | solution.py:256
  40.0 1.8 %collective-permute-done.14 = bf16[64,512]{1,0:T(8,128)(2,1)S(1)} collective-permute-done((bf16[64,512]{1,0:T(8,128)(2,1)S(1)}, bf16[64,512]{1,0:T(8,128)(2,1)S(1)}, u32[]{:S(2)}, u32[]{:S(2)}) %collective-permute-start.14) | collective-permute-done | bytes 65568 | tf_op jit(solution)/shard_map/ppermute | solution.py:256
  41.7 1.1 %collective-permute-done.16 = bf16[64,512]{1,0:T(8,128)(2,1)S(1)} collective-permute-done((bf16[64,512]{1,0:T(8,128)(2,1)S(1)}, bf16[64,512]{1,0:T(8,128)(2,1)S(1)}, u32[]{:S(2)}, u32[]{:S(2)}) %collective-permute-start.16) | collective-permute-done | bytes 65568 | tf_op jit(solution)/shard_map/ppermute | solution.py:256
  42.9 0.7 %collective-permute-done.15 = bf16[64,512]{1,0:T(8,128)(2,1)S(1)} collective-permute-done((bf16[64,512]{1,0:T(8,128)(2,1)S(1)}, bf16[64,512]{1,0:T(8,128)(2,1)S(1)}, u32[]{:S(2)}, u32[]{:S(2)}) %collective-permute-start.15) | collective-permute-done | bytes 65568 | tf_op jit(solution)/shard_map/ppermute | solution.py:256
  43.6 1.3 %collective-permute-start.18 = (bf16[64,512]{1,0:T(8,128)(2,1)S(1)}, bf16[64,512]{1,0:T(8,128)(2,1)S(1)}, u32[]{:S(2)}, u32[]{:S(2)}) collective-permute-start(bf16[64,512]{1,0:T(8,128)(2,1)S(1)} %fusion.3.refs_0_), channel_id=1, source_target_pairs={{0,16},{4,20},{8,24},{12,28},{16,0},{20,4},{24,8},{28,12},{1,17},{... | collective-permute-start | bytes 196616 | tf_op jit(solution)/shard_map/ppermute | solution.py:256
  44.9 1.0 %collective-permute-start.17 = (bf16[64,512]{1,0:T(8,128)(2,1)S(1)}, bf16[64,512]{1,0:T(8,128)(2,1)S(1)}, u32[]{:S(2)}, u32[]{:S(2)}) collective-permute-start(bf16[64,512]{1,0:T(8,128)(2,1)S(1)} %fusion.3.refs_0_), channel_id=1, source_target_pairs={{0,28},{4,24},{8,20},{12,16},{16,12},{20,8},{24,4},{28,0},{1,29},{... | collective-permute-start | bytes 196616 | tf_op jit(solution)/shard_map/ppermute | solution.py:256
  45.9 1.0 %collective-permute-start.21 = (bf16[64,512]{1,0:T(8,128)(2,1)S(1)}, bf16[64,512]{1,0:T(8,128)(2,1)S(1)}, u32[]{:S(2)}, u32[]{:S(2)}) collective-permute-start(bf16[64,512]{1,0:T(8,128)(2,1)S(1)} %fusion.3.refs_0_), channel_id=1, source_target_pairs={{0,12},{4,8},{8,4},{12,0},{16,28},{20,24},{24,20},{28,16},{1,13},{... | collective-permute-start | bytes 196616 | tf_op jit(solution)/shard_map/ppermute | solution.py:256
  46.8 1.1 %collective-permute-done.18.refs_1_ = bf16[64,512]{1,0:T(8,128)(2,1)S(1)} collective-permute-done((bf16[64,512]{1,0:T(8,128)(2,1)S(1)}, bf16[64,512]{1,0:T(8,128)(2,1)S(1)}, u32[]{:S(2)}, u32[]{:S(2)}) %collective-permute-start.18) | collective-permute-done | bytes 65568 | tf_op jit(solution)/shard_map/ppermute | solution.py:256
  47.9 2.1 %collective-permute-done.17.refs_0_ = bf16[64,512]{1,0:T(8,128)(2,1)S(1)} collective-permute-done((bf16[64,512]{1,0:T(8,128)(2,1)S(1)}, bf16[64,512]{1,0:T(8,128)(2,1)S(1)}, u32[]{:S(2)}, u32[]{:S(2)}) %collective-permute-start.17) | collective-permute-done | bytes 65568 | tf_op jit(solution)/shard_map/ppermute | solution.py:256
  50.0 0.1 collective-permute-start.19
  50.1 0.5 collective-permute-start.20
  50.6 0.1 collective-permute-start.22
  50.7 0.4 image.15.refs_2_
  51.1 0.4 image.16.refs_3_
  51.6 0.3 collective-permute-done.22.refs_1_
  51.9 0.8 %image.17.refs_3_ = f32[64,1024]{1,0:T(8,128)S(1)} custom-call(bf16[64,512]{1,0:T(8,128)(2,1)S(1)} %collective-permute-done.20.refs_0_, bf16[64,512]{1,0:T(8,128)(2,1)S(1)} %collective-permute-done.22.refs_1_, bf16[4,1024,512]{2,1,0:T(8,128)(2,1)S(1)} %get-tuple-element.18.refs_2_.refs_1_.held, f32[64,1024]{1,0:T(8,128)S(1)} %image.16.refs_3_), custom_call_target="tpu_custom_call" | custom-call | tf_op jit(solution)/shard_map/image/pallas_call | solution.py:236
  52.6 0.8 %image.18.refs_2_ = f32[64,1024]{1,0:T(8,128)S(1)} custom-call(bf16[64,512]{1,0:T(8,128)(2,1)S(1)} %collective-permute-done.17.refs_0_, bf16[64,512]{1,0:T(8,128)(2,1)S(1)} %collective-permute-done.18.refs_1_, bf16[4,1024,512]{2,1,0:T(8,128)(2,1)S(1)} %get-tuple-element.23.refs_1_.refs_2_.held, f32[64,1024]{1,0:T(8,128)S(1)} %image.17.refs_3_), custom_call_target="tpu_custom_call" | custom-call | tf_op jit(solution)/shard_map/image/pallas_call | solution.py:236
  53.4 0.8 %image.19 = f32[8,1024]{1,0:T(8,128)S(1)} custom-call(bf16[64,1024]{1,0:T(8,128)(2,1)S(1)} %collective-permute-done.19.refs_0_, bf16[4,1024,512]{2,1,0:T(8,128)(2,1)S(1)} %get-tuple-element.18.refs_2_.refs_1_.held, f32[64,1024]{1,0:T(8,128)S(1)} %image.18.refs_2_, s32[8,1024]{1,0:T(8,128)S(1)} %get-tuple-element.16.refs_3_.tags, ...), custom_call_target="tpu_custom_call" | custom-call | tf_op jit(solution)/shard_map/image/pallas_call | solution.py:236
  54.1 1.5 %collective-permute-start.25 = (f32[8,1024]{1,0:T(8,128)S(1)}, f32[8,1024]{1,0:T(8,128)S(1)}, u32[]{:S(2)}, u32[]{:S(2)}) collective-permute-start(f32[8,1024]{1,0:T(8,128)S(1)} %image.19), channel_id=1, source_target_pairs={{0,3},{1,2},{2,1},{3,0},{4,7},{5,6},{6,5},{7,4},{8,11},{9,10},{10,... | collective-permute-start | bytes 98312 | tf_op jit(solution)/shard_map/ppermute | solution.py:315
  55.7 0.6 collective-permute-start.24
  56.3 2.3 %collective-permute-start.23 = (f32[8,1024]{1,0:T(8,128)S(1)}, f32[8,1024]{1,0:T(8,128)S(1)}, u32[]{:S(2)}, u32[]{:S(2)}) collective-permute-start(f32[8,1024]{1,0:T(8,128)S(1)} %image.19), channel_id=1, source_target_pairs={{0,1},{1,0},{2,3},{3,2},{4,5},{5,4},{6,7},{7,6},{8,9},{9,8},{10,11... | collective-permute-start | bytes 98312 | tf_op jit(solution)/shard_map/ppermute | solution.py:315
  58.6 0.6 copy.8
  59.2 1.0 %collective-permute-done.25 = f32[8,1024]{1,0:T(8,128)S(1)} collective-permute-done((f32[8,1024]{1,0:T(8,128)S(1)}, f32[8,1024]{1,0:T(8,128)S(1)}, u32[]{:S(2)}, u32[]{:S(2)}) %collective-permute-start.25) | collective-permute-done | bytes 32800 | tf_op jit(solution)/shard_map/ppermute | solution.py:315
  60.2 0.4 collective-permute-done.24
  60.6 0.3 collective-permute-done.23
  60.9 0.6 %add_add_fusion = f32[8,1024]{1,0:T(8,128)} fusion(f32[8,1024]{1,0:T(8,128)S(1)} %get-tuple-element.27, f32[8,1024]{1,0:T(8,128)S(1)} %collective-permute-done.24, f32[8,1024]{1,0:T(8,128)S(1)} %collective-permute-done.25, f32[8,1024]{1,0:T(8,128)S(1)} %image.19, f32[8,1024]{1,0:T(8,128)S(1)} %collective-permute-done.23), kind=kLoop, calls=%fused_computation.26 | loop fusion | flops 32768 | bytes 196608 | tf_op jit(solution)/shard_map/add | solution.py:330
  (21 shorter events, 0.2 us)
Async XLA Ops:
  3.3 2.8 %collective-permute-start = (f32[72,2048]{1,0:T(8,128)S(1)}, f32[72,2048]{1,0:T(8,128)S(1)}, u32[]{:S(2)}, u32[]{:S(2)}) collective-permute-start(f32[72,2048]{1,0:T(8,128)S(1)} %get-tuple-element.22), channel_id=1, source_target_pairs={{0,4},{4,0},{8,12},{12,8},{16,20},{20,16},{24,28},{28,24},{1,5},{5... | collective-permute-start | bytes 1769480 | tf_op jit(solution)/shard_map/ppermute | solution.py:256
  6.3 6.3 %collective-permute-start.1 = (f16[72,512]{1,0:T(8,128)(2,1)S(1)}, f16[72,512]{1,0:T(8,128)(2,1)S(1)}, u32[]{:S(2)}, u32[]{:S(2)}) collective-permute-start(f16[72,512]{1,0:T(8,128)(2,1)S(1)} %get-tuple-element.34), channel_id=1, source_target_pairs={{0,28},{4,24},{8,20},{12,16},{16,12},{20,8},{24,4},{28,0},{1,29},{... | collective-permute-start | bytes 221192 | tf_op jit(solution)/shard_map/ppermute | solution.py:256
  9.9 4.4 %collective-permute-start.2 = (f16[72,512]{1,0:T(8,128)(2,1)S(1)}, f16[72,512]{1,0:T(8,128)(2,1)S(1)}, u32[]{:S(2)}, u32[]{:S(2)}) collective-permute-start(f16[72,512]{1,0:T(8,128)(2,1)S(1)} %get-tuple-element.35), channel_id=1, source_target_pairs={{0,12},{4,8},{8,4},{12,0},{16,28},{20,24},{24,20},{28,16},{1,13},{... | collective-permute-start | bytes 221192 | tf_op jit(solution)/shard_map/ppermute | solution.py:256
  10.1 4.7 %collective-permute-start.3 = (f16[72,512]{1,0:T(8,128)(2,1)S(1)}, f16[72,512]{1,0:T(8,128)(2,1)S(1)}, u32[]{:S(2)}, u32[]{:S(2)}) collective-permute-start(f16[72,512]{1,0:T(8,128)(2,1)S(1)} %get-tuple-element.36), channel_id=1, source_target_pairs={{0,16},{4,20},{8,24},{12,28},{16,0},{20,4},{24,8},{28,12},{1,17},{... | collective-permute-start | bytes 221192 | tf_op jit(solution)/shard_map/ppermute | solution.py:256
  14.8 4.4 %collective-permute-start.5 = (bf16[72,512]{1,0:T(8,128)(2,1)S(1)}, bf16[72,512]{1,0:T(8,128)(2,1)S(1)}, u32[]{:S(2)}, u32[]{:S(2)}) collective-permute-start(bf16[72,512]{1,0:T(8,128)(2,1)S(1)} %pad_maximum_fusion.5.refs_0_), channel_id=1, source_target_pairs={{0,16},{4,20},{8,24},{12,28},{16,0},{20,4},{24,8},{28,12},{1,17},{... | collective-permute-start | bytes 221192 | tf_op jit(solution)/shard_map/ppermute | solution.py:256
  16.1 5.4 %collective-permute-start.4 = (bf16[72,512]{1,0:T(8,128)(2,1)S(1)}, bf16[72,512]{1,0:T(8,128)(2,1)S(1)}, u32[]{:S(2)}, u32[]{:S(2)}) collective-permute-start(bf16[72,512]{1,0:T(8,128)(2,1)S(1)} %pad_maximum_fusion.5.refs_0_), channel_id=1, source_target_pairs={{0,28},{4,24},{8,20},{12,16},{16,12},{20,8},{24,4},{28,0},{1,29},{... | collective-permute-start | bytes 221192 | tf_op jit(solution)/shard_map/ppermute | solution.py:256
  17.2 5.0 %collective-permute-start.8 = (bf16[72,512]{1,0:T(8,128)(2,1)S(1)}, bf16[72,512]{1,0:T(8,128)(2,1)S(1)}, u32[]{:S(2)}, u32[]{:S(2)}) collective-permute-start(bf16[72,512]{1,0:T(8,128)(2,1)S(1)} %pad_maximum_fusion.5.refs_0_), channel_id=1, source_target_pairs={{0,12},{4,8},{8,4},{12,0},{16,28},{20,24},{24,20},{28,16},{1,13},{... | collective-permute-start | bytes 221192 | tf_op jit(solution)/shard_map/ppermute | solution.py:256
  21.5 3.4 %collective-permute-start.6 = (bf16[72,1024]{1,0:T(8,128)(2,1)S(1)}, bf16[72,1024]{1,0:T(8,128)(2,1)S(1)}, u32[]{:S(2)}, u32[]{:S(2)}) collective-permute-start(bf16[72,1024]{1,0:T(8,128)(2,1)S(1)} %pad_maximum_fusion), channel_id=1, source_target_pairs={{0,4},{4,0},{8,12},{12,8},{16,20},{20,16},{24,28},{28,24},{1,5},{5... | collective-permute-start | bytes 442376 | tf_op jit(solution)/shard_map/ppermute | solution.py:256
  21.7 1.4 %collective-permute-start.7 = (bf16[72,512]{1,0:T(8,128)(2,1)S(1)}, bf16[72,512]{1,0:T(8,128)(2,1)S(1)}, u32[]{:S(2)}, u32[]{:S(2)}) collective-permute-start(bf16[72,512]{1,0:T(8,128)(2,1)S(1)} %pad_maximum_fusion.5.refs_0_), channel_id=1, source_target_pairs={{0,4},{4,0},{8,12},{12,8},{16,20},{20,16},{24,28},{28,24},{1,5},{5... | collective-permute-start | bytes 221192 | tf_op jit(solution)/shard_map/ppermute | solution.py:256
  22.1 1.3 %collective-permute-start.9 = (bf16[72,512]{1,0:T(8,128)(2,1)S(1)}, bf16[72,512]{1,0:T(8,128)(2,1)S(1)}, u32[]{:S(2)}, u32[]{:S(2)}) collective-permute-start(bf16[72,512]{1,0:T(8,128)(2,1)S(1)} %collective-permute-done.8.refs_0_), channel_id=1, source_target_pairs={{0,4},{4,0},{8,12},{12,8},{16,20},{20,16},{24,28},{28,24},{1,5},{5... | collective-permute-start | bytes 221192 | tf_op jit(solution)/shard_map/ppermute | solution.py:256
  25.7 5.8 %collective-permute-start.12 = (f32[8,1024]{1,0:T(8,128)S(1)}, f32[8,1024]{1,0:T(8,128)S(1)}, u32[]{:S(2)}, u32[]{:S(2)}) collective-permute-start(f32[8,1024]{1,0:T(8,128)S(1)} %image.14.refs_0_), channel_id=1, source_target_pairs={{0,3},{1,2},{2,1},{3,0},{4,7},{5,6},{6,5},{7,4},{8,11},{9,10},{10,... | collective-permute-start | bytes 98312 | tf_op jit(solution)/shard_map/ppermute | solution.py:315
  29.4 4.8 %collective-permute-start.11 = (f32[8,1024]{1,0:T(8,128)S(1)}, f32[8,1024]{1,0:T(8,128)S(1)}, u32[]{:S(2)}, u32[]{:S(2)}) collective-permute-start(f32[8,1024]{1,0:T(8,128)S(1)} %image.14.refs_0_), channel_id=1, source_target_pairs={{0,2},{1,3},{2,0},{3,1},{4,6},{5,7},{6,4},{7,5},{8,10},{9,11},{10,... | collective-permute-start | bytes 98312 | tf_op jit(solution)/shard_map/ppermute | solution.py:315
  29.4 4.8 %collective-permute-start.10 = (f32[8,1024]{1,0:T(8,128)S(1)}, f32[8,1024]{1,0:T(8,128)S(1)}, u32[]{:S(2)}, u32[]{:S(2)}) collective-permute-start(f32[8,1024]{1,0:T(8,128)S(1)} %image.14.refs_0_), channel_id=1, source_target_pairs={{0,1},{1,0},{2,3},{3,2},{4,5},{5,4},{6,7},{7,6},{8,9},{9,8},{10,11... | collective-permute-start | bytes 98312 | tf_op jit(solution)/shard_map/ppermute | solution.py:315
  35.0 1.6 %collective-permute-start.13 = (bf16[64,2048]{1,0:T(8,128)(2,1)S(1)}, bf16[64,2048]{1,0:T(8,128)(2,1)S(1)}, u32[]{:S(2)}, u32[]{:S(2)}) collective-permute-start(bf16[64,2048]{1,0:T(8,128)(2,1)S(1)} %get-tuple-element.26), channel_id=1, source_target_pairs={{0,4},{4,0},{8,12},{12,8},{16,20},{20,16},{24,28},{28,24},{1,5},{5... | collective-permute-start | bytes 786440 | tf_op jit(solution)/shard_map/ppermute | solution.py:256
  36.7 5.0 %collective-permute-start.14 = (bf16[64,512]{1,0:T(8,128)(2,1)S(1)}, bf16[64,512]{1,0:T(8,128)(2,1)S(1)}, u32[]{:S(2)}, u32[]{:S(2)}) collective-permute-start(bf16[64,512]{1,0:T(8,128)(2,1)S(1)} %get-tuple-element.37), channel_id=1, source_target_pairs={{0,28},{4,24},{8,20},{12,16},{16,12},{20,8},{24,4},{28,0},{1,29},{... | collective-permute-start | bytes 196616 | tf_op jit(solution)/shard_map/ppermute | solution.py:256
  38.8 4.1 %collective-permute-start.16 = (bf16[64,512]{1,0:T(8,128)(2,1)S(1)}, bf16[64,512]{1,0:T(8,128)(2,1)S(1)}, u32[]{:S(2)}, u32[]{:S(2)}) collective-permute-start(bf16[64,512]{1,0:T(8,128)(2,1)S(1)} %get-tuple-element.38), channel_id=1, source_target_pairs={{0,12},{4,8},{8,4},{12,0},{16,28},{20,24},{24,20},{28,16},{1,13},{... | collective-permute-start | bytes 196616 | tf_op jit(solution)/shard_map/ppermute | solution.py:256
  39.3 4.3 %collective-permute-start.15 = (bf16[64,512]{1,0:T(8,128)(2,1)S(1)}, bf16[64,512]{1,0:T(8,128)(2,1)S(1)}, u32[]{:S(2)}, u32[]{:S(2)}) collective-permute-start(bf16[64,512]{1,0:T(8,128)(2,1)S(1)} %get-tuple-element.39), channel_id=1, source_target_pairs={{0,16},{4,20},{8,24},{12,28},{16,0},{20,4},{24,8},{28,12},{1,17},{... | collective-permute-start | bytes 196616 | tf_op jit(solution)/shard_map/ppermute | solution.py:256
  43.6 4.3 %collective-permute-start.18 = (bf16[64,512]{1,0:T(8,128)(2,1)S(1)}, bf16[64,512]{1,0:T(8,128)(2,1)S(1)}, u32[]{:S(2)}, u32[]{:S(2)}) collective-permute-start(bf16[64,512]{1,0:T(8,128)(2,1)S(1)} %fusion.3.refs_0_), channel_id=1, source_target_pairs={{0,16},{4,20},{8,24},{12,28},{16,0},{20,4},{24,8},{28,12},{1,17},{... | collective-permute-start | bytes 196616 | tf_op jit(solution)/shard_map/ppermute | solution.py:256
  44.9 5.1 %collective-permute-start.17 = (bf16[64,512]{1,0:T(8,128)(2,1)S(1)}, bf16[64,512]{1,0:T(8,128)(2,1)S(1)}, u32[]{:S(2)}, u32[]{:S(2)}) collective-permute-start(bf16[64,512]{1,0:T(8,128)(2,1)S(1)} %fusion.3.refs_0_), channel_id=1, source_target_pairs={{0,28},{4,24},{8,20},{12,16},{16,12},{20,8},{24,4},{28,0},{1,29},{... | collective-permute-start | bytes 196616 | tf_op jit(solution)/shard_map/ppermute | solution.py:256
  45.9 4.7 %collective-permute-start.21 = (bf16[64,512]{1,0:T(8,128)(2,1)S(1)}, bf16[64,512]{1,0:T(8,128)(2,1)S(1)}, u32[]{:S(2)}, u32[]{:S(2)}) collective-permute-start(bf16[64,512]{1,0:T(8,128)(2,1)S(1)} %fusion.3.refs_0_), channel_id=1, source_target_pairs={{0,12},{4,8},{8,4},{12,0},{16,28},{20,24},{24,20},{28,16},{1,13},{... | collective-permute-start | bytes 196616 | tf_op jit(solution)/shard_map/ppermute | solution.py:256
  50.0 3.3 %collective-permute-start.19 = (bf16[64,1024]{1,0:T(8,128)(2,1)S(1)}, bf16[64,1024]{1,0:T(8,128)(2,1)S(1)}, u32[]{:S(2)}, u32[]{:S(2)}) collective-permute-start(bf16[64,1024]{1,0:T(8,128)(2,1)S(1)} %pad_maximum_fusion.1), channel_id=1, source_target_pairs={{0,4},{4,0},{8,12},{12,8},{16,20},{20,16},{24,28},{28,24},{1,5},{5... | collective-permute-start | bytes 393224 | tf_op jit(solution)/shard_map/ppermute | solution.py:256
  50.1 1.5 %collective-permute-start.20 = (bf16[64,512]{1,0:T(8,128)(2,1)S(1)}, bf16[64,512]{1,0:T(8,128)(2,1)S(1)}, u32[]{:S(2)}, u32[]{:S(2)}) collective-permute-start(bf16[64,512]{1,0:T(8,128)(2,1)S(1)} %fusion.3.refs_0_), channel_id=1, source_target_pairs={{0,4},{4,0},{8,12},{12,8},{16,20},{20,16},{24,28},{28,24},{1,5},{5... | collective-permute-start | bytes 196616 | tf_op jit(solution)/shard_map/ppermute | solution.py:256
  50.6 1.3 %collective-permute-start.22 = (bf16[64,512]{1,0:T(8,128)(2,1)S(1)}, bf16[64,512]{1,0:T(8,128)(2,1)S(1)}, u32[]{:S(2)}, u32[]{:S(2)}) collective-permute-start(bf16[64,512]{1,0:T(8,128)(2,1)S(1)} %collective-permute-done.21.refs_0_), channel_id=1, source_target_pairs={{0,4},{4,0},{8,12},{12,8},{16,20},{20,16},{24,28},{28,24},{1,5},{5... | collective-permute-start | bytes 196616 | tf_op jit(solution)/shard_map/ppermute | solution.py:256
  54.1 6.1 %collective-permute-start.25 = (f32[8,1024]{1,0:T(8,128)S(1)}, f32[8,1024]{1,0:T(8,128)S(1)}, u32[]{:S(2)}, u32[]{:S(2)}) collective-permute-start(f32[8,1024]{1,0:T(8,128)S(1)} %image.19), channel_id=1, source_target_pairs={{0,3},{1,2},{2,1},{3,0},{4,7},{5,6},{6,5},{7,4},{8,11},{9,10},{10,... | collective-permute-start | bytes 98312 | tf_op jit(solution)/shard_map/ppermute | solution.py:315
  55.7 4.9 %collective-permute-start.24 = (f32[8,1024]{1,0:T(8,128)S(1)}, f32[8,1024]{1,0:T(8,128)S(1)}, u32[]{:S(2)}, u32[]{:S(2)}) collective-permute-start(f32[8,1024]{1,0:T(8,128)S(1)} %image.19), channel_id=1, source_target_pairs={{0,2},{1,3},{2,0},{3,1},{4,6},{5,7},{6,4},{7,5},{8,10},{9,11},{10,... | collective-permute-start | bytes 98312 | tf_op jit(solution)/shard_map/ppermute | solution.py:315
  56.3 4.6 %collective-permute-start.23 = (f32[8,1024]{1,0:T(8,128)S(1)}, f32[8,1024]{1,0:T(8,128)S(1)}, u32[]{:S(2)}, u32[]{:S(2)}) collective-permute-start(f32[8,1024]{1,0:T(8,128)S(1)} %image.19), channel_id=1, source_target_pairs={{0,1},{1,0},{2,3},{3,2},{4,5},{5,4},{6,7},{7,6},{8,9},{9,8},{10,11... | collective-permute-start | bytes 98312 | tf_op jit(solution)/shard_map/ppermute | solution.py:315
